TPU v7x, 32 devices: a whole 2x2x4 slice. The times are simulated.
32 devices in a mesh: dp: 16 (over z, y, core), tensor: 2 (over x).
Axes of the slice: x: 2, y: 2, z: 4, core: 2. Of those that a mesh axis runs over, the one named last changes fastest.
Arguments:
- layer_input: bfloat16 [8192, 2048], P(('dp', 'tensor')), may hold values from -6 to 6
- teacher: bfloat16 [8192, 2048], P(('dp', 'tensor')), may hold values from -6 to 6
- lengths: int32 [16], replicated, may hold values from 32 to 512, as said below
- seq_order: int32 [16], replicated, may hold values from 0 to 15, as said below
- gain_attn: bfloat16 [2048], P('dp'), may hold values from 0.5 to 1.5
- w_query: bfloat16 [2048, 2048], P('dp', 'tensor'), may hold values from -0.25 to 0.25
- key_projection_weight: bfloat16 [2048, 1024], P('dp', 'tensor'), may hold values from -0.125 to 0.125
- value_projection_weight: bfloat16 [2048, 1024], P('dp', 'tensor'), may hold values from -0.125 to 0.125
- w_out: bfloat16 [2048, 2048], P('tensor', 'dp'), may hold values from -0.375 to 0.375
- gain_mlp: bfloat16 [2048], P('dp'), may hold values from 0.5 to 1.5
- w_gate: bfloat16 [2048, 8192], P('dp', 'tensor'), may hold values from -0.125 to 0.125
- w_up: bfloat16 [2048, 8192], P('dp', 'tensor'), may hold values from -0.125 to 0.125
- w_down: bfloat16 [8192, 2048], P('tensor', 'dp'), may hold values from -0.0625 to 0.0625
Outputs:
- activations: bfloat16 [8192, 2048], P(('dp', 'tensor'))
- input_grad: bfloat16 [8192, 2048], P(('dp', 'tensor'))
- gain_attn_grad: float32 [2048], P('dp')
- w_query_grad: float32 [2048, 2048], P('dp', 'tensor')
- w_key_grad: float32 [2048, 1024], P('dp', 'tensor')
- w_value_grad: float32 [2048, 1024], P('dp', 'tensor')
- w_out_grad: float32 [2048, 2048], P('tensor', 'dp')
- gain_mlp_grad: float32 [2048], P('dp')
- w_gate_grad: float32 [2048, 8192], P('dp', 'tensor')
- w_up_grad: float32 [2048, 8192], P('dp', 'tensor')
- w_down_grad: float32 [8192, 2048], P('tensor', 'dp')
- distill_loss: float32 [], replicated
Inputs may be any that keep to these rules, and one draw needn't show every extreme that they name: `lengths`: both ends are reached. `seq_order`: each number appears once.
All inputs are finite; a program needn't handle non-finite values.
Results may differ from a plain program's by a relative error of at most 0.014.
The roundings to bfloat16 on the way count: a program that leaves them out, or rounds other values in their place, can miss the bound.
Values may be sent and summed in bfloat16 or wider, within the bound.
No kernel may reach another device: no remote copies, remote signals or barrier semaphores. Data moves between devices by JAX's collectives and lax.ppermute only.
A program may use at most 256 MiB of HBM per device.

v0:
```python
import jax
import jax.numpy as jnp
from jax import lax
from jax.sharding import PartitionSpec as P

HEAD_SIZE = 256


EPS = 1e-06
ROPE_BASE = 1000042.0
over_rows = (((0,), (0,)), ((), ()))
over_last = (((1,), (1,)), ((), ()))


def rms_scale(value_rows):
    return lax.rsqrt(jnp.mean(value_rows * value_rows, axis=-1, keepdims=True) + EPS)


def rope_tables(position, width):
    half = width // 2
    exponent = jnp.arange(half, dtype=jnp.float32) * (-2.0 / width)
    frequency = jnp.exp(exponent * jnp.log(jnp.float32(ROPE_BASE)))
    angle = position.astype(jnp.float32)[:, None] * frequency[None, :]
    return (jnp.cos(angle), jnp.sin(angle))


def apply_rotary(heads, cosine_table, sine_table):
    half = heads.shape[-1] // 2
    first = heads[..., :half]
    second = heads[..., half:]
    cos_b = cosine_table[:, None, :]
    sin_b = sine_table[:, None, :]
    return jnp.concatenate(
        [first * cos_b - second * sin_b, second * cos_b + first * sin_b], axis=-1
    )


def unrotate(grads, cosine_table, sine_table):
    half = grads.shape[-1] // 2
    first = grads[..., :half]
    second = grads[..., half:]
    cos_b = cosine_table[:, None, :]
    sin_b = sine_table[:, None, :]
    return jnp.concatenate(
        [first * cos_b + second * sin_b, second * cos_b - first * sin_b], axis=-1
    )


def layout_of(length, slots):
    place = jnp.arange(slots, dtype=jnp.int32)
    inside = place < length
    sequence = jnp.where(inside, 0, 1 + place)
    position = jnp.where(inside, place, 0)
    return (sequence, position, inside)


def deal(first, second, source_of):
    token_rows, width = first.shape
    parts = lax.axis_size("dp")
    first_cut = first.reshape(token_rows, parts, width // parts)
    second_cut = second.reshape(token_rows, parts, width // parts)
    got_first, got_second = (
        lax.all_to_all(first_cut, "dp", split_axis=1, concat_axis=1, tiled=True),
        lax.all_to_all(second_cut, "dp", split_axis=1, concat_axis=1, tiled=True),
    )
    sent_first = jnp.take(got_first, source_of, axis=1)
    sent_second = jnp.take(got_second, source_of, axis=1)
    back_first, back_second = (
        lax.all_to_all(sent_first, "dp", split_axis=1, concat_axis=1, tiled=True),
        lax.all_to_all(sent_second, "dp", split_axis=1, concat_axis=1, tiled=True),
    )
    return (back_first.reshape(token_rows, width), back_second.reshape(token_rows, width))


def per_device(
    layer_input,
    teacher,
    lengths,
    seq_order,
    gain_attn,
    w_query,
    key_projection_weight,
    value_projection_weight,
    w_out,
    gain_mlp,
    w_gate,
    w_up,
    w_down,
):
    token_rows, width = layer_input.shape
    slots = token_rows * lax.axis_size("tensor")
    tokens_all = slots * lax.axis_size("dp")
    group = lax.axis_index("dp")
    numbers = jnp.arange(seq_order.shape[0], dtype=jnp.int32)
    inverse = jnp.sum(
        jnp.where(seq_order[None, :] == numbers[:, None], numbers[None, :], 0), axis=1
    )
    dealt_input, dealt_teacher = deal(layer_input, teacher, seq_order)
    sequence, position, inside = layout_of(lengths[group], slots)
    own_valid = lax.dynamic_slice_in_dim(
        inside, lax.axis_index("tensor") * token_rows, token_rows, 0
    ).astype(jnp.float32)
    allowed = (sequence[:, None] == sequence[None, :]) & (position[None, :] <= position[:, None])
    cosine_table, sine_table = rope_tables(position, HEAD_SIZE)
    scaling = HEAD_SIZE ** (-0.5)
    gathered = (
        lax.all_gather(gain_attn, "dp", axis=0, tiled=True),
        lax.all_gather(w_query, "dp", axis=0, tiled=True),
        lax.all_gather(key_projection_weight, "dp", axis=0, tiled=True),
        lax.all_gather(value_projection_weight, "dp", axis=0, tiled=True),
        lax.all_gather(w_out, "dp", axis=1, tiled=True),
        lax.all_gather(gain_mlp, "dp", axis=0, tiled=True),
        lax.all_gather(w_gate, "dp", axis=0, tiled=True),
        lax.all_gather(w_up, "dp", axis=0, tiled=True),
        lax.all_gather(w_down, "dp", axis=1, tiled=True),
    )
    (
        attn_gain,
        query_proj,
        key_proj,
        value_proj,
        out_proj,
        mlp_gain,
        gate_proj,
        up_proj,
        down_proj,
    ) = gathered
    attn_gain = attn_gain.astype(jnp.float32)
    mlp_gain = mlp_gain.astype(jnp.float32)
    query_heads = query_proj.shape[1] // HEAD_SIZE
    group_heads = key_proj.shape[1] // HEAD_SIZE
    group_portion = query_heads // group_heads
    inputs = dealt_input.astype(jnp.float32)
    attn_scale = rms_scale(inputs)
    normalized_rows = (inputs * attn_scale * attn_gain).astype(jnp.bfloat16)
    normed_all = lax.all_gather(normalized_rows, "tensor", axis=0, tiled=True)
    query_rows = jnp.dot(normed_all, query_proj, preferred_element_type=jnp.float32).reshape(
        slots, query_heads, HEAD_SIZE
    )
    key_rows = jnp.dot(normed_all, key_proj, preferred_element_type=jnp.float32).reshape(
        slots, group_heads, HEAD_SIZE
    )
    value_rows = (
        jnp.dot(normed_all, value_proj, preferred_element_type=jnp.float32)
        .astype(jnp.bfloat16)
        .reshape(slots, group_heads, HEAD_SIZE)
    )
    rot_queries = (
        apply_rotary(query_rows, cosine_table, sine_table)
        .astype(jnp.bfloat16)
        .reshape(slots, group_heads, group_portion, HEAD_SIZE)
    )
    rot_keys = apply_rotary(key_rows, cosine_table, sine_table).astype(jnp.bfloat16)

    def masked_scores():
        raw = (
            jnp.einsum("ikgd,jkd->kgij", rot_queries, rot_keys, preferred_element_type=jnp.float32)
            * scaling
        )
        return jnp.where(allowed, raw, -1e30)

    scores = masked_scores()
    highest = jnp.max(scores, axis=-1, keepdims=True)
    shifted = jnp.exp(scores - highest)
    row_total = jnp.sum(shifted, axis=-1, keepdims=True)
    probs = shifted / row_total
    log_total = highest + jnp.log(row_total)
    heads_out = jnp.einsum(
        "kgij,jkd->ikgd", probs.astype(jnp.bfloat16), value_rows, preferred_element_type=jnp.float32
    )
    attended = heads_out.reshape(slots, query_heads * HEAD_SIZE).astype(jnp.bfloat16)
    middle = inputs + lax.psum_scatter(
        jnp.dot(attended, out_proj, preferred_element_type=jnp.float32),
        "tensor",
        scatter_dimension=0,
        tiled=True,
    )
    mlp_scale = rms_scale(middle)
    normed_mlp = (middle * mlp_scale * mlp_gain).astype(jnp.bfloat16)
    mlp_all = lax.all_gather(normed_mlp, "tensor", axis=0, tiled=True)
    gate = jnp.dot(mlp_all, gate_proj, preferred_element_type=jnp.float32)
    up = jnp.dot(mlp_all, up_proj, preferred_element_type=jnp.float32)
    sigmoid_gate = jax.nn.sigmoid(gate)
    hidden = (gate * sigmoid_gate * up).astype(jnp.bfloat16)
    result = middle + lax.psum_scatter(
        jnp.dot(hidden, down_proj, preferred_element_type=jnp.float32),
        "tensor",
        scatter_dimension=0,
        tiled=True,
    )
    error = (result - dealt_teacher.astype(jnp.float32)) * own_valid[:, None]
    count = jnp.sum(lengths).astype(jnp.float32)
    delta_result = error * (tokens_all / count)
    branch_low = delta_result.astype(jnp.bfloat16)
    branch_all = lax.all_gather(branch_low, "tensor", axis=0, tiled=True)
    delta_hidden = lax.dot_general(
        branch_all, down_proj, over_last, preferred_element_type=jnp.float32
    )
    delta_gate = (delta_hidden * up * sigmoid_gate * (1.0 + gate * (1.0 - sigmoid_gate))).astype(
        jnp.bfloat16
    )
    delta_up = (delta_hidden * gate * sigmoid_gate).astype(jnp.bfloat16)
    grad_down_t = lax.dot_general(branch_all, hidden, over_rows, preferred_element_type=jnp.float32)
    grad_gate = lax.dot_general(mlp_all, delta_gate, over_rows, preferred_element_type=jnp.float32)
    grad_up = lax.dot_general(mlp_all, delta_up, over_rows, preferred_element_type=jnp.float32)
    from_gate = lax.dot_general(
        delta_gate, gate_proj, over_last, preferred_element_type=jnp.float32
    )
    from_up = lax.dot_general(delta_up, up_proj, over_last, preferred_element_type=jnp.float32)
    delta_normed_mlp = lax.psum_scatter(
        from_gate + from_up, "tensor", scatter_dimension=0, tiled=True
    )
    gain_mlp_part = jnp.sum(delta_normed_mlp * middle * mlp_scale, axis=0)
    weighted_mlp = mlp_gain * delta_normed_mlp
    delta_middle = (
        delta_result
        + mlp_scale * weighted_mlp
        - middle * mlp_scale**3 * jnp.mean(middle * weighted_mlp, axis=-1, keepdims=True)
    )
    attn_low = delta_middle.astype(jnp.bfloat16)
    attn_all = lax.all_gather(attn_low, "tensor", axis=0, tiled=True)
    grad_out_t = lax.dot_general(attn_all, attended, over_rows, preferred_element_type=jnp.float32)
    delta_mixed = lax.dot_general(attn_all, out_proj, over_last, preferred_element_type=jnp.float32)
    delta_mixed = delta_mixed.astype(jnp.bfloat16).reshape(
        slots, group_heads, group_portion, HEAD_SIZE
    )
    probs_back = jnp.exp(masked_scores() - log_total)
    delta_probs = jnp.einsum(
        "ikgd,jkd->kgij", delta_mixed, value_rows, preferred_element_type=jnp.float32
    )
    inner = jnp.sum(probs_back * delta_probs, axis=-1, keepdims=True)
    delta_scores = (probs_back * (delta_probs - inner)).astype(jnp.bfloat16)
    delta_values = jnp.einsum(
        "kgij,ikgd->jkd",
        probs_back.astype(jnp.bfloat16),
        delta_mixed,
        preferred_element_type=jnp.float32,
    )
    delta_values = delta_values.astype(jnp.bfloat16).reshape(slots, group_heads * HEAD_SIZE)
    delta_qrot = (
        jnp.einsum("kgij,jkd->ikgd", delta_scores, rot_keys, preferred_element_type=jnp.float32)
        * scaling
    )
    delta_krot = (
        jnp.einsum("kgij,ikgd->jkd", delta_scores, rot_queries, preferred_element_type=jnp.float32)
        * scaling
    )
    delta_queries = (
        unrotate(delta_qrot.reshape(slots, query_heads, HEAD_SIZE), cosine_table, sine_table)
        .astype(jnp.bfloat16)
        .reshape(slots, query_heads * HEAD_SIZE)
    )
    delta_keys = (
        unrotate(delta_krot, cosine_table, sine_table)
        .astype(jnp.bfloat16)
        .reshape(slots, group_heads * HEAD_SIZE)
    )
    grad_query = lax.dot_general(
        normed_all, delta_queries, over_rows, preferred_element_type=jnp.float32
    )
    grad_key = lax.dot_general(
        normed_all, delta_keys, over_rows, preferred_element_type=jnp.float32
    )
    grad_value = lax.dot_general(
        normed_all, delta_values, over_rows, preferred_element_type=jnp.float32
    )
    from_query = lax.dot_general(
        delta_queries, query_proj, over_last, preferred_element_type=jnp.float32
    )
    from_key = lax.dot_general(delta_keys, key_proj, over_last, preferred_element_type=jnp.float32)
    from_value = lax.dot_general(
        delta_values, value_proj, over_last, preferred_element_type=jnp.float32
    )
    delta_normed = lax.psum_scatter(
        (from_query + from_key + from_value).astype(jnp.bfloat16),
        "tensor",
        scatter_dimension=0,
        tiled=True,
    ).astype(jnp.float32)
    sum_query, sum_key, sum_value, sum_out_t, sum_gate, sum_up, sum_down_t = (
        lax.psum_scatter(grad_query, "dp", scatter_dimension=0, tiled=True),
        lax.psum_scatter(grad_key, "dp", scatter_dimension=0, tiled=True),
        lax.psum_scatter(grad_value, "dp", scatter_dimension=0, tiled=True),
        lax.psum_scatter(grad_out_t, "dp", scatter_dimension=0, tiled=True),
        lax.psum_scatter(grad_gate, "dp", scatter_dimension=0, tiled=True),
        lax.psum_scatter(grad_up, "dp", scatter_dimension=0, tiled=True),
        lax.psum_scatter(grad_down_t, "dp", scatter_dimension=0, tiled=True),
    )
    gain_attn_part = jnp.sum(delta_normed * inputs * attn_scale, axis=0)
    weighted_attn = attn_gain * delta_normed
    input_grad = (
        delta_middle
        + attn_scale * weighted_attn
        - inputs * attn_scale**3 * jnp.mean(inputs * weighted_attn, axis=-1, keepdims=True)
    )
    squared, gain_attn_sum, gain_mlp_sum = lax.psum(
        (jnp.sum(error * error), gain_attn_part, gain_mlp_part), ("dp", "tensor")
    )
    piece = gain_attn.shape[0]
    gain_attn_grad = lax.dynamic_slice_in_dim(gain_attn_sum, group * piece, piece, 0)
    gain_mlp_grad = lax.dynamic_slice_in_dim(gain_mlp_sum, group * piece, piece, 0)
    distill_loss = squared / (2.0 * width * count)
    placed_result, placed_grad = deal(
        result.astype(jnp.bfloat16), input_grad.astype(jnp.bfloat16), inverse
    )
    return (
        placed_result,
        placed_grad,
        gain_attn_grad,
        sum_query,
        sum_key,
        sum_value,
        sum_out_t.T,
        gain_mlp_grad,
        sum_gate,
        sum_up,
        sum_down_t.T,
        distill_loss,
    )


def solution(mesh):
    placed = (
        P(("dp", "tensor"), None),
        P(("dp", "tensor"), None),
        P(),
        P(),
        P("dp"),
        P("dp", "tensor"),
        P("dp", "tensor"),
        P("dp", "tensor"),
        P("tensor", "dp"),
        P("dp"),
        P("dp", "tensor"),
        P("dp", "tensor"),
        P("tensor", "dp"),
    )
    return jax.shard_map(
        per_device,
        mesh=mesh,
        in_specs=placed,
        out_specs=(
            P(("dp", "tensor"), None),
            P(("dp", "tensor"), None),
            P("dp"),
            P("dp", "tensor"),
            P("dp", "tensor"),
            P("dp", "tensor"),
            P("tensor", "dp"),
            P("dp"),
            P("dp", "tensor"),
            P("dp", "tensor"),
            P("tensor", "dp"),
            P(),
        ),
        check_vma=False,
    )
```

profile of v0, /device:TPU:0, one launch (start us, length us, event | category | flops | bytes accessed | tf_op | source)
XLA Modules:
  0.0 2515.5 jit_solution(9907472988749323498)
XLA Ops:
  83.6 38.9 %all-gather = bf16[16,1,128]{2,1,0:T(2,128)(2,1)S(1)} all-gather(bf16[1,1,128]{2,1,0:T(2,128)(2,1)S(1)} %bitcast.201), channel_id=1, replica_groups=mesh['dp'=16,'tensor'=2] {'dp'}, dimensions={0}, use_global_device_ids=true | all-gather | bytes 4352 | tf_op jit(solution)/shard_map/all_gather | solution.py:107
  131.9 27.6 %all-gather.14.cloned.1.call-done = bf16[512,2048]{1,0:T(8,128)(2,1)} async-done(((bf16[256,2048]{1,0:T(8,128)(2,1)}), bf16[512,2048]{1,0:T(8,128)(2,1)}) %all-gather.14.cloned.1.call-update) | async-done | bytes 2097168 | tf_op jit(solution)/shard_map/all_gather | solution.py:136
  170.6 32.6 %all-gather.16.cloned.1.call-done = bf16[2048,512]{1,0:T(8,128)(2,1)} async-done(((bf16[128,512]{1,0:T(8,128)(2,1)}), bf16[2048,512]{1,0:T(8,128)(2,1)}) %all-gather.16.cloned.1.call-update) | async-done | bytes 2097168 | tf_op jit(solution)/shard_map/all_gather | solution.py:110
  206.9 47.5 %all-gather.20.cloned.1.call-done = bf16[2048,1024]{1,0:T(8,128)(2,1)} async-done(((bf16[128,1024]{1,0:T(8,128)(2,1)}), bf16[2048,1024]{1,0:T(8,128)(2,1)}) %all-gather.20.cloned.1.call-update) | async-done | bytes 4194320 | tf_op jit(solution)/shard_map/all_gather | solution.py:108
  268.2 39.3 %all-gather.22.cloned.1.call-done = bf16[1024,2048]{1,0:T(8,128)(2,1)} async-done(((bf16[1024,128]{1,0:T(8,128)(2,1)}), bf16[1024,2048]{1,0:T(8,128)(2,1)}) %all-gather.22.cloned.1.call-update) | async-done | bytes 4194320 | tf_op jit(solution)/shard_map/all_gather | solution.py:111
  333.4 33.4 %reduce-scatter.12.cloned.1.call-done = f32[256,2048]{1,0:T(8,128)} async-done(((f32[512,2048]{1,0:T(8,128)}), f32[256,2048]{1,0:T(8,128)}) %reduce-scatter.12.cloned.1.call-update) | async-done | bytes 2097168 | tf_op jit(solution)/shard_map/reduce_scatter | solution.py:172
  372.1 31.1 %all-gather.24.cloned.1.call-done = bf16[512,2048]{1,0:T(8,128)(2,1)} async-done(((bf16[256,2048]{1,0:T(8,128)(2,1)}), bf16[512,2048]{1,0:T(8,128)(2,1)}) %all-gather.24.cloned.1.call-update) | async-done | bytes 2097168 | tf_op jit(solution)/shard_map/all_gather | solution.py:180
  403.2 128.6 %all-gather.26.cloned.1.call-done = bf16[2048,4096]{1,0:T(8,128)(2,1)} async-done(((bf16[128,4096]{1,0:T(8,128)(2,1)}), bf16[2048,4096]{1,0:T(8,128)(2,1)}) %all-gather.26.cloned.1.call-update) | async-done | bytes 16777232 | tf_op jit(solution)/shard_map/all_gather | solution.py:113
  546.8 111.8 %all-gather.28.cloned.1.call-done = bf16[2048,4096]{1,0:T(8,128)(2,1)} async-done(((bf16[128,4096]{1,0:T(8,128)(2,1)}), bf16[2048,4096]{1,0:T(8,128)(2,1)}) %all-gather.28.cloned.1.call-update) | async-done | bytes 16777232 | tf_op jit(solution)/shard_map/all_gather | solution.py:114
  678.6 110.1 %all-gather.30.cloned.1.call-done = bf16[4096,2048]{1,0:T(8,128)(2,1)} async-done(((bf16[4096,128]{1,0:T(8,128)(2,1)}), bf16[4096,2048]{1,0:T(8,128)(2,1)}) %all-gather.30.cloned.1.call-update) | async-done | bytes 16777232 | tf_op jit(solution)/shard_map/all_gather | solution.py:115
  830.3 26.2 %reduce-scatter.14.cloned.1.call-done = f32[256,2048]{1,0:T(8,128)} async-done(((f32[512,2048]{1,0:T(8,128)}), f32[256,2048]{1,0:T(8,128)}) %reduce-scatter.14.cloned.1.call-update) | async-done | bytes 2097168 | tf_op jit(solution)/shard_map/reduce_scatter | solution.py:185
  862.9 33.2 %all-gather.32.cloned.1.call-done = bf16[512,2048]{1,0:T(8,128)(2,1)} async-done(((bf16[256,2048]{1,0:T(8,128)(2,1)}), bf16[512,2048]{1,0:T(8,128)(2,1)}) %all-gather.32.cloned.1.call-update) | async-done | bytes 2097168 | tf_op jit(solution)/shard_map/all_gather | solution.py:195
  946.4 54.3 %reduce-scatter.16.cloned.1.call-done = f32[256,2048]{1,0:T(8,128)} async-done(((f32[512,2048]{1,0:T(8,128)}), f32[256,2048]{1,0:T(8,128)}) %reduce-scatter.16.cloned.1.call-update) | async-done | bytes 2097168 | tf_op jit(solution)/shard_map/reduce_scatter | solution.py:210
  1006.0 33.2 %all-gather.34.cloned.1.call-done = bf16[512,2048]{1,0:T(8,128)(2,1)} async-done(((bf16[256,2048]{1,0:T(8,128)(2,1)}), bf16[512,2048]{1,0:T(8,128)(2,1)}) %all-gather.34.cloned.1.call-update) | async-done | bytes 2097168 | tf_op jit(solution)/shard_map/all_gather | solution.py:221
  1164.5 29.3 %all-to-all-done.2 = bf16[256,16,128]{2,0,1:T(8,128)(2,1)} async-done(((bf16[256,16,128]{2,0,1:T(8,128)(2,1)}), bf16[256,16,128]{2,0,1:T(8,128)(2,1)}, u32[]{:S(2)}, u32[]{:S(2)}) %all-to-all-start.2) | async-done | bytes 1048608 | tf_op jit(solution)/shard_map/all_to_all | solution.py:63
  1202.9 33.4 %all-to-all-done.6 = bf16[256,16,128]{2,0,1:T(8,128)(2,1)S(1)} async-done(((bf16[256,16,128]{2,0,1:T(8,128)(2,1)}), bf16[256,16,128]{2,0,1:T(8,128)(2,1)S(1)}, u32[]{:S(2)}, u32[]{:S(2)}) %all-to-all-start.6) | async-done | bytes 1048608 | tf_op jit(solution)/shard_map/all_to_all | solution.py:64
  1238.3 35.4 %all_to_all.40 = bf16[256,16,128]{2,0,1:T(8,128)(2,1)S(1)} all-to-all(bf16[256,16,128]{2,0,1:T(8,128)(2,1)S(1)} %get-tuple-element.107), channel_id=1, replica_groups=mesh['dp'=16,'tensor'=2] {'dp'}, dimensions={1} | all-to-all | bytes 2097152 | tf_op jit(solution)/shard_map/all_to_all | solution.py:70
  1278.9 47.8 %all-reduce = (f32[2048]{0:T(1024)S(1)}, f32[2048]{0:T(1024)S(1)}, f32[]{:T(128)}) all-reduce(f32[2048]{0:T(1024)S(1)} %get-tuple-element.75, f32[2048]{0:T(1024)S(1)} %get-tuple-element.73, f32[]{:T(128)} %get-tuple-element.80), channel_id=1, replica_groups=mesh['dp'=16,'tensor'=2] {'dp','tensor'}, use_global_device_ids=true, to_apply=%region_14.16 | all-reduce | flops 4097 | bytes 32776 | tf_op jit(solution)/shard_map/psum | solution.py:296
  1334.5 243.6 %reduce-scatter.32.cloned.1.call-done = f32[128,4096]{1,0:T(8,128)} async-done(((f32[2048,4096]{1,0:T(8,128)}), f32[128,4096]{1,0:T(8,128)}) %reduce-scatter.32.cloned.1.call-update) | async-done | bytes 2097168 | tf_op jit(solution)/shard_map/reduce_scatter | solution.py:287
  1581.0 73.3 %reduce-scatter.24.cloned.1.call-done = f32[128,512]{1,0:T(8,128)} async-done(((f32[2048,512]{1,0:T(8,128)}), f32[128,512]{1,0:T(8,128)}) %reduce-scatter.24.cloned.1.call-update) | async-done | bytes 262160 | tf_op jit(solution)/shard_map/reduce_scatter | solution.py:283
  1654.4 76.3 %reduce-scatter.22.cloned.1.call-done = f32[128,512]{1,0:T(8,128)} async-done(((f32[2048,512]{1,0:T(8,128)}), f32[128,512]{1,0:T(8,128)}) %reduce-scatter.22.cloned.1.call-update) | async-done | bytes 262160 | tf_op jit(solution)/shard_map/reduce_scatter | solution.py:282
  1730.7 107.0 %reduce-scatter.20.cloned.1.call-done = f32[128,1024]{1,0:T(8,128)} async-done(((f32[2048,1024]{1,0:T(8,128)}), f32[128,1024]{1,0:T(8,128)}) %reduce-scatter.20.cloned.1.call-update) | async-done | bytes 524304 | tf_op jit(solution)/shard_map/reduce_scatter | solution.py:281
  1837.7 335.1 %reduce-scatter.30.cloned.1.call-done = f32[128,4096]{1,0:T(8,128)} async-done(((f32[2048,4096]{1,0:T(8,128)}), f32[128,4096]{1,0:T(8,128)}) %reduce-scatter.30.cloned.1.call-update) | async-done | bytes 2097168 | tf_op jit(solution)/shard_map/reduce_scatter | solution.py:286
  2172.7 334.5 %reduce-scatter.28.cloned.1.call-done = f32[128,4096]{1,0:T(8,128)} async-done(((f32[2048,4096]{1,0:T(8,128)}), f32[128,4096]{1,0:T(8,128)}) %reduce-scatter.28.cloned.1.call-update) | async-done | bytes 2097168 | tf_op jit(solution)/shard_map/reduce_scatter | solution.py:285
  (263 shorter events, 433.9 us)
Async XLA Ops:
  47.1 84.8 %all-gather.18.cloned.1.call-start = ((), (), s32[]{:S(2)}) async-start(), calls=%async_computation.21 | async-start | bytes 2228224 | tf_op jit(solution)/shard_map/all_gather | solution.py:109
  74.9 47.6 %all-to-all-start.1 = ((bf16[256,16,128]{2,0,1:T(8,128)(2,1)}), bf16[256,16,128]{2,0,1:T(8,128)(2,1)S(1)}, u32[]{:S(2)}, u32[]{:S(2)}) async-start(bf16[256,16,128]{2,0,1:T(8,128)(2,1)} %get-tuple-element.110), calls=%async_computation.1 | async-start | bytes 2097152 | tf_op jit(solution)/shard_map/all_to_all | solution.py:69
  83.5 76.0 %all-gather.14.cloned.1.call-start = ((), (), s32[]{:S(2)}) async-start(), calls=%async_computation.19 | async-start | bytes 3145728 | tf_op jit(solution)/shard_map/all_gather | solution.py:136
  124.8 78.4 %all-gather.16.cloned.1.call-start = ((), (), s32[]{:S(2)}) async-start(), calls=%async_computation.20 | async-start | bytes 2228224 | tf_op jit(solution)/shard_map/all_gather | solution.py:110
  125.5 128.8 %all-gather.20.cloned.1.call-start = ((), (), s32[]{:S(2)}) async-start(), calls=%async_computation.22 | async-start | bytes 4456448 | tf_op jit(solution)/shard_map/all_gather | solution.py:108
  126.1 181.3 %all-gather.22.cloned.1.call-start = ((), (), s32[]{:S(2)}) async-start(), calls=%async_computation.23 | async-start | bytes 4456448 | tf_op jit(solution)/shard_map/all_gather | solution.py:111
  126.7 240.0 %reduce-scatter.12.cloned.1.call-start = ((), (), s32[]{:S(2)}) async-start(), calls=%async_computation.24 | async-start | bytes 6291456 | tf_op jit(solution)/shard_map/reduce_scatter | solution.py:172
  314.0 89.2 %all-gather.24.cloned.1.call-start = ((), (), s32[]{:S(2)}) async-start(), calls=%async_computation.25 | async-start | bytes 3145728 | tf_op jit(solution)/shard_map/all_gather | solution.py:180
  370.0 161.9 %all-gather.26.cloned.1.call-start = ((), (), s32[]{:S(2)}) async-start(), calls=%async_computation.26 | async-start | bytes 17825792 | tf_op jit(solution)/shard_map/all_gather | solution.py:113
  370.7 287.9 %all-gather.28.cloned.1.call-start = ((), (), s32[]{:S(2)}) async-start(), calls=%async_computation.27 | async-start | bytes 17825792 | tf_op jit(solution)/shard_map/all_gather | solution.py:114
  371.4 417.3 %all-gather.30.cloned.1.call-start = ((), (), s32[]{:S(2)}) async-start(), calls=%async_computation.28 | async-start | bytes 17825792 | tf_op jit(solution)/shard_map/all_gather | solution.py:115
  372.0 484.4 %reduce-scatter.14.cloned.1.call-start = ((), (), s32[]{:S(2)}) async-start(), calls=%async_computation.29 | async-start | bytes 6291456 | tf_op jit(solution)/shard_map/reduce_scatter | solution.py:185
  807.4 88.6 %all-gather.32.cloned.1.call-start = ((), (), s32[]{:S(2)}) async-start(), calls=%async_computation.30 | async-start | bytes 3145728 | tf_op jit(solution)/shard_map/all_gather | solution.py:195
  862.8 137.9 %reduce-scatter.16.cloned.1.call-start = ((), (), s32[]{:S(2)}) async-start(), calls=%async_computation.31 | async-start | bytes 6291456 | tf_op jit(solution)/shard_map/reduce_scatter | solution.py:210
  946.2 93.0 %all-gather.34.cloned.1.call-start = ((), (), s32[]{:S(2)}) async-start(), calls=%async_computation.32 | async-start | bytes 3145728 | tf_op jit(solution)/shard_map/all_gather | solution.py:221
  1005.9 154.7 %reduce-scatter.18.cloned.1.call-start = ((), (), s32[]{:S(2)}) async-start(), calls=%async_computation.33 | async-start | bytes 3145728 | tf_op jit(solution)/shard_map/reduce_scatter | solution.py:274
  1070.3 262.2 %reduce-scatter.26.cloned.1.call-start = ((), (), s32[]{:S(2)}) async-start(), calls=%async_computation.37 | async-start | bytes 8912896 | tf_op jit(solution)/shard_map/reduce_scatter | solution.py:284
  1079.0 499.2 %reduce-scatter.32.cloned.1.call-start = ((), (), s32[]{:S(2)}) async-start(), calls=%async_computation.40 | async-start | bytes 35651584 | tf_op jit(solution)/shard_map/reduce_scatter | solution.py:287
  1098.2 556.2 %reduce-scatter.24.cloned.1.call-start = ((), (), s32[]{:S(2)}) async-start(), calls=%async_computation.36 | async-start | bytes 4456448 | tf_op jit(solution)/shard_map/reduce_scatter | solution.py:283
  1103.1 627.6 %reduce-scatter.22.cloned.1.call-start = ((), (), s32[]{:S(2)}) async-start(), calls=%async_computation.35 | async-start | bytes 4456448 | tf_op jit(solution)/shard_map/reduce_scatter | solution.py:282
  1106.5 731.2 %reduce-scatter.20.cloned.1.call-start = ((), (), s32[]{:S(2)}) async-start(), calls=%async_computation.34 | async-start | bytes 8912896 | tf_op jit(solution)/shard_map/reduce_scatter | solution.py:281
  1113.5 1059.2 %reduce-scatter.30.cloned.1.call-start = ((), (), s32[]{:S(2)}) async-start(), calls=%async_computation.39 | async-start | bytes 35651584 | tf_op jit(solution)/shard_map/reduce_scatter | solution.py:286
  1134.6 1372.7 %reduce-scatter.28.cloned.1.call-start = ((), (), s32[]{:S(2)}) async-start(), calls=%async_computation.38 | async-start | bytes 35651584 | tf_op jit(solution)/shard_map/reduce_scatter | solution.py:285
  1273.7 56.8 %all-to-all-start.3 = ((bf16[256,16,128]{2,0,1:T(8,128)(2,1)}), bf16[256,16,128]{2,0,1:T(8,128)(2,1)S(1)}, u32[]{:S(2)}, u32[]{:S(2)}) async-start(bf16[256,16,128]{2,0,1:T(8,128)(2,1)} %get-tuple-element.108), calls=%async_computation.5 | async-start | bytes 2097152 | tf_op jit(solution)/shard_map/all_to_all | solution.py:69
  (57 other events, 846.2 us)
Sparse Core Ops, SparseCore 0:
  50.1 57.1 all-gather.17
  124.9 34.6 all-gather.13
  161.7 41.4 all-gather.15
  205.3 49.0 all-gather.19
  256.4 50.9 all-gather.21
  314.2 52.5 reduce-scatter.11
  370.1 33.0 all-gather.23
  405.4 126.4 all-gather.25
  534.0 124.5 all-gather.27
  660.6 128.0 all-gather.29
  803.9 52.5 reduce-scatter.13
  862.9 33.0 all-gather.31
  946.3 54.3 reduce-scatter.15
  1006.1 33.0 all-gather.33
  1070.4 31.8 reduce-scatter.17
  1106.3 137.1 reduce-scatter.25
  1247.6 330.5 reduce-scatter.31
  1582.4 71.8 reduce-scatter.23
  1658.8 71.8 reduce-scatter.21
  1735.1 102.4 reduce-scatter.19
  1842.5 330.1 reduce-scatter.29
  2177.6 329.6 reduce-scatter.27
where the time goes:
time: 2520 us
  waiting for transfers between devices  2010 us (80%)
  matrix products  214 us (8%)
  blocking collectives  141 us (6%)
  local copies, waits for them, and re-layouts  49.6 us (2%)
  starting transfers between devices  47 us (2%)
  other arithmetic  34.8 us (1%)
    reduce_scatter x1, waiting for transfers between devices, per_device(): lax.psum_scatter(grad_up, 'dp', scatter_dimension=0, tiled=True)  335 us
    reduce_scatter x1, waiting for transfers between devices, per_device(): lax.psum_scatter(grad_gate, 'dp', scatter_dimension=0, tiled=True)  335 us
    reduce_scatter x1, waiting for transfers between devices, per_device(): lax.psum_scatter(grad_down_t, 'dp', scatter_dimension=0, tiled=True)  244 us
    all_gather x1, waiting for transfers between devices, per_device(): lax.all_gather(w_gate, 'dp', axis=0, tiled=True)  129 us
    all_gather x1, waiting for transfers between devices, per_device(): lax.all_gather(w_up, 'dp', axis=0, tiled=True)  112 us
    all_gather x1, waiting for transfers between devices, per_device(): lax.all_gather(w_down, 'dp', axis=1, tiled=True)  110 us
    reduce_scatter x1, waiting for transfers between devices, per_device(): lax.psum_scatter(grad_query, 'dp', scatter_dimension=0, tiled=True)  107 us
    reduce_scatter x1, waiting for transfers between devices, per_device(): lax.psum_scatter(grad_key, 'dp', scatter_dimension=0, tiled=True)  76.3 us
  transfers between devices with their start and end apart: 29, of which 24 were waited for; matrix products, arithmetic and copies ran while one was open for 7% of the time, Pallas kernels for 0%

commit v1 on v0

v1 whole, which is shorter than its diff:
```python
import jax
import jax.numpy as jnp
from jax import lax
from jax.experimental import pallas as pl
from jax.experimental.pallas import tpu as pltpu
from jax.sharding import PartitionSpec as P

HEAD_SIZE = 256
LANES = 128
EPS = 1e-06
ROPE_BASE = 1000042.0
over_rows = (((0,), (0,)), ((), ()))
over_last = (((1,), (1,)), ((), ()))
plain = (((1,), (0,)), ((), ()))
f32 = jnp.float32
bf16 = jnp.bfloat16


def rms_scale(value_rows):
    return lax.rsqrt(jnp.mean(value_rows * value_rows, axis=-1, keepdims=True) + EPS)


def rope_tables(position, width):
    half = width // 2
    exponent = jnp.arange(half, dtype=f32) * (-2.0 / width)
    frequency = jnp.exp(exponent * jnp.log(f32(ROPE_BASE)))
    angle = position.astype(f32)[..., None] * frequency
    return (jnp.cos(angle), jnp.sin(angle))


def rotate(heads, cosine, sine):
    half = heads.shape[-1] // 2
    first, second = heads[..., :half], heads[..., half:]
    return jnp.concatenate(
        [first * cosine - second * sine, second * cosine + first * sine], axis=-1
    )


def ring_order(chips):
    column = chips // 2
    return [2 * i for i in range(column)] + [2 * i + 1 for i in reversed(range(column))]


class Ring:
    def __init__(self, chips):
        self.chips = chips
        order = ring_order(chips)
        self.place = [order.index(c) for c in range(chips)]
        hop = [(order[i], order[(i + 1) % chips]) for i in range(chips)]
        self.up = [(2 * a + c, 2 * b + c) for a, b in hop for c in range(2)]
        self.down = [(b, a) for a, b in self.up]
        self.swap = [(d, d ^ 1) for d in range(2 * chips)]

    def ahead(self, v):
        return lax.ppermute(v, "dp", self.up)

    def back(self, v):
        return lax.ppermute(v, "dp", self.down)

    def other_core(self, v):
        return lax.ppermute(v, "dp", self.swap)


def other_tensor(v):
    return lax.ppermute(v, "tensor", [(0, 1), (1, 0)])


def gather_ring(ring, low, high):
    lows, highs = [low], [high]
    for _ in range(ring.chips - 1):
        low, high = ring.ahead(low), ring.back(high)
        lows.append(low)
        highs.append(high)
    return lows, highs


def scatter_ring(ring, grads, rows):
    half = ring.chips * rows

    def block(side, k):
        start = side * half + k * rows
        return grads[start : start + rows]

    last = ring.chips - 1
    low, high = block(0, last), block(1, last)
    for k in range(last - 1, -1, -1):
        low = ring.back(low.astype(bf16)).astype(f32) + block(0, k)
        high = ring.ahead(high.astype(bf16)).astype(f32) + block(1, k)
    return low, high


def gather_group(ring, rows):
    across = other_tensor(rows)
    beside = ring.other_core(rows)
    return jnp.concatenate([rows, across, beside, ring.other_core(across)], axis=0)


def scatter_group(ring, parts):
    quarter = parts.shape[0] // 4
    near = parts[: 2 * quarter] + ring.other_core(parts[2 * quarter :].astype(bf16)).astype(f32)
    return near[:quarter] + other_tensor(near[quarter:].astype(bf16)).astype(f32)


def copy_block(table, source, target):
    target[...] = source[...]


def reorder(rows, table):
    height, width = rows.shape
    return pl.pallas_call(
        copy_block,
        out_shape=jax.ShapeDtypeStruct(rows.shape, rows.dtype),
        grid_spec=pltpu.PrefetchScalarGridSpec(
            num_scalar_prefetch=1,
            grid=(width // LANES,),
            in_specs=[pl.BlockSpec((height, LANES), lambda k, t: (0, t[k]))],
            out_specs=pl.BlockSpec((height, LANES), lambda k, t: (0, k)),
        ),
        name="reorder",
    )(table, rows)


def sum_all(ring, v):
    v = v + other_tensor(v)
    devices = 2 * ring.chips
    step = 1
    while step < devices:
        v = v + lax.ppermute(v, "dp", [(d, d ^ step) for d in range(devices)])
        step *= 2
    return v


def per_device(
    layer_input,
    teacher,
    lengths,
    seq_order,
    gain_attn,
    w_query,
    key_projection_weight,
    value_projection_weight,
    w_out,
    gain_mlp,
    w_gate,
    w_up,
    w_down,
):
    token_rows, width = layer_input.shape
    slots = token_rows * lax.axis_size("tensor")
    devices = lax.axis_size("dp")
    tokens_all = slots * devices
    chips = devices // 2
    ring = Ring(chips)
    me = lax.axis_index("dp")
    side = lax.axis_index("tensor")
    chip, core = me // 2, me % 2
    first_core = core == 0
    place = jnp.array(ring.place, dtype=jnp.int32)
    here = place[chip]
    piece = gain_attn.shape[0]

    numbers = jnp.arange(chips, dtype=jnp.int32)
    order = jnp.array(ring_order(chips), dtype=jnp.int32)
    from_low = 2 * order[(here - numbers) % chips]
    from_high = 2 * order[(here + numbers) % chips] + 1
    to_relative = jnp.concatenate([from_low, from_high])
    to_natural = jnp.stack(
        [(here - place) % chips, chips + (place - here) % chips], axis=1
    ).reshape(devices)

    def split_cores(w):
        quarter = w.shape[1] // 2
        mine = lax.dynamic_slice_in_dim(w, core * quarter, quarter, 1)
        given = lax.dynamic_slice_in_dim(w, (1 - core) * quarter, quarter, 1)
        return mine, given

    def both_rows(weights, gains=None):
        mine, given = zip(*[split_cores(w) for w in weights])
        mine, given = jnp.concatenate(mine, axis=1), jnp.concatenate(given, axis=1)
        if gains is not None:
            extra = jnp.pad(gains, ((0, 16 - gains.shape[0]), (0, mine.shape[1] - gains.shape[1])))
            mine = jnp.concatenate([mine, extra], axis=0)
            given = jnp.concatenate([given, extra], axis=0)
        taken = ring.other_core(given)
        return (
            jnp.where(first_core, mine, taken),
            jnp.where(first_core, taken, mine),
        )

    own_input = reorder(layer_input, to_relative)
    own_teacher = reorder(teacher, to_relative)
    gains = jnp.stack([gain_attn, gain_mlp])
    attn_low, attn_high = gather_ring(
        ring,
        *both_rows([w_query, key_projection_weight, value_projection_weight, w_out.T], gains),
    )
    gate_low, gate_high = gather_ring(ring, *both_rows([w_gate]))
    up_low, up_high = gather_ring(ring, *both_rows([w_up]))
    down_low, down_high = gather_ring(ring, *both_rows([w_down.T]))

    pieces = attn_low + attn_high
    q_width = w_query.shape[1] // 2
    kv_width = key_projection_weight.shape[1] // 2
    qkv_width = q_width + 2 * kv_width
    qkv_proj = jnp.concatenate([p[:piece, :qkv_width] for p in pieces], axis=0)
    out_proj_t = jnp.concatenate([p[:piece, qkv_width:] for p in pieces], axis=0)
    gain_rows = jnp.concatenate([p[piece : piece + 2, :piece] for p in pieces], axis=1).astype(f32)
    attn_gain, mlp_gain = gain_rows[:1], gain_rows[1:]
    gate_proj = jnp.concatenate(gate_low + gate_high, axis=0)
    up_proj = jnp.concatenate(up_low + up_high, axis=0)
    down_proj_t = jnp.concatenate(down_low + down_high, axis=0)

    sequence_numbers = jnp.stack([me, me + 1 - 2 * core])
    length = jnp.sum(
        jnp.where(seq_order[None, :] == sequence_numbers[:, None], lengths[None, :], 0), axis=1
    )
    offsets = jnp.arange(token_rows, dtype=jnp.int32)
    slot = jnp.concatenate([side * token_rows + offsets, (1 - side) * token_rows + offsets])
    inside = slot[None, :] < length[:, None]
    sequence = jnp.where(inside, 0, 1 + slot[None, :])
    position = jnp.where(inside, slot[None, :], 0)
    own_valid = inside[0, :token_rows].astype(f32)[:, None]
    allowed = (sequence[:, :, None] == sequence[:, None, :]) & (
        position[:, None, :] <= position[:, :, None]
    )
    allowed = allowed[:, None]
    cosine, sine = rope_tables(position, HEAD_SIZE)
    cosine, sine = cosine[:, :, None, :], sine[:, :, None, :]
    scaling = HEAD_SIZE ** (-0.5)
    query_heads = q_width // HEAD_SIZE
    all_rows = 2 * slots

    group_input = gather_group(ring, own_input).astype(f32)
    group_scale = rms_scale(group_input)
    normed = (group_input * group_scale * attn_gain).astype(bf16)
    qkv = jnp.dot(normed, qkv_proj, preferred_element_type=f32)
    query_rows = qkv[:, :q_width].reshape(2, slots, query_heads, HEAD_SIZE)
    key_rows = qkv[:, q_width : q_width + kv_width].reshape(2, slots, 1, HEAD_SIZE)
    values = qkv[:, q_width + kv_width :].astype(bf16).reshape(2, slots, HEAD_SIZE)
    rot_queries = rotate(query_rows, cosine, sine).astype(bf16)
    rot_keys = rotate(key_rows, cosine, sine).astype(bf16)[:, :, 0]
    scores = (
        jnp.einsum("bigd,bjd->bgij", rot_queries, rot_keys, preferred_element_type=f32) * scaling
    )
    scores = jnp.where(allowed, scores, -1e30)
    highest = jnp.max(scores, axis=-1, keepdims=True)
    shifted = jnp.exp(scores - highest)
    probs = shifted / jnp.sum(shifted, axis=-1, keepdims=True)
    probs_low = probs.astype(bf16)
    mixed = (
        jnp.einsum("bgij,bjd->bigd", probs_low, values, preferred_element_type=f32)
        .reshape(all_rows, q_width)
        .astype(bf16)
    )
    own_rows = own_input.astype(f32)
    attn_scale = rms_scale(own_rows)
    middle = own_rows + scatter_group(
        ring, lax.dot_general(mixed, out_proj_t, over_last, preferred_element_type=f32)
    )
    mlp_scale = rms_scale(middle)
    normed_mlp = gather_group(ring, (middle * mlp_scale * mlp_gain).astype(bf16))
    gate = jnp.dot(normed_mlp, gate_proj, preferred_element_type=f32)
    up = jnp.dot(normed_mlp, up_proj, preferred_element_type=f32)
    sigmoid_gate = jax.nn.sigmoid(gate)
    hidden = (gate * sigmoid_gate * up).astype(bf16)
    result = middle + scatter_group(
        ring, lax.dot_general(hidden, down_proj_t, over_last, preferred_element_type=f32)
    )
    activations = reorder(result.astype(bf16), to_natural)
    error = (result - own_teacher.astype(f32)) * own_valid
    count = jnp.sum(lengths).astype(f32)
    delta_result = error * (tokens_all / count)
    branch = gather_group(ring, delta_result.astype(bf16))
    grad_down_t = lax.dot_general(branch, hidden, over_rows, preferred_element_type=f32)
    down_sum = scatter_ring(ring, grad_down_t, piece)
    delta_hidden = jnp.dot(branch, down_proj_t, preferred_element_type=f32)
    delta_gate = (delta_hidden * up * sigmoid_gate * (1.0 + gate * (1.0 - sigmoid_gate))).astype(
        bf16
    )
    delta_up = (delta_hidden * gate * sigmoid_gate).astype(bf16)
    grad_gate = lax.dot_general(normed_mlp, delta_gate, over_rows, preferred_element_type=f32)
    gate_sum = scatter_ring(ring, grad_gate, piece)
    grad_up = lax.dot_general(normed_mlp, delta_up, over_rows, preferred_element_type=f32)
    up_sum = scatter_ring(ring, grad_up, piece)
    delta_normed_mlp = scatter_group(
        ring,
        lax.dot_general(delta_gate, gate_proj, over_last, preferred_element_type=f32)
        + lax.dot_general(delta_up, up_proj, over_last, preferred_element_type=f32),
    )
    gain_mlp_part = jnp.sum(delta_normed_mlp * middle * mlp_scale, axis=0)
    weighted_mlp = mlp_gain * delta_normed_mlp
    delta_middle = (
        delta_result
        + mlp_scale * weighted_mlp
        - middle * mlp_scale**3 * jnp.mean(middle * weighted_mlp, axis=-1, keepdims=True)
    )
    attn_low_rows = gather_group(ring, delta_middle.astype(bf16))
    grad_out_t = lax.dot_general(attn_low_rows, mixed, over_rows, preferred_element_type=f32)
    delta_mixed = (
        jnp.dot(attn_low_rows, out_proj_t, preferred_element_type=f32)
        .astype(bf16)
        .reshape(2, slots, query_heads, HEAD_SIZE)
    )
    delta_probs = jnp.einsum("bigd,bjd->bgij", delta_mixed, values, preferred_element_type=f32)
    inner = jnp.sum(probs * delta_probs, axis=-1, keepdims=True)
    delta_scores = (probs * (delta_probs - inner)).astype(bf16)
    delta_values = jnp.einsum("bgij,bigd->bjd", probs_low, delta_mixed, preferred_element_type=f32)
    delta_qrot = (
        jnp.einsum("bgij,bjd->bigd", delta_scores, rot_keys, preferred_element_type=f32) * scaling
    )
    delta_krot = (
        jnp.einsum("bgij,bigd->bjd", delta_scores, rot_queries, preferred_element_type=f32)
        * scaling
    )
    delta_queries = rotate(delta_qrot, cosine, -sine).reshape(all_rows, q_width)
    delta_keys = rotate(delta_krot[:, :, None], cosine, -sine).reshape(all_rows, kv_width)
    delta_qkv = jnp.concatenate(
        [
            delta_queries.astype(bf16),
            delta_keys.astype(bf16),
            delta_values.astype(bf16).reshape(all_rows, kv_width),
        ],
        axis=1,
    )
    grad_qkv = lax.dot_general(normed, delta_qkv, over_rows, preferred_element_type=f32)
    attn_sum = scatter_ring(ring, jnp.concatenate([grad_qkv, grad_out_t], axis=1), piece)
    delta_normed = scatter_group(
        ring, lax.dot_general(delta_qkv, qkv_proj, over_last, preferred_element_type=f32)
    )
    gain_attn_part = jnp.sum(delta_normed * own_rows * attn_scale, axis=0)
    weighted_attn = attn_gain * delta_normed
    input_grad = (
        delta_middle
        + attn_scale * weighted_attn
        - own_rows * attn_scale**3 * jnp.mean(own_rows * weighted_attn, axis=-1, keepdims=True)
    )
    input_grad = reorder(input_grad.astype(bf16), to_natural)

    squared = jnp.sum(error * error)
    natural = jnp.stack([gain_mlp_part, gain_attn_part], axis=0).reshape(2, devices, piece)[
        :, to_natural
    ]
    totals = sum_all(
        ring,
        jnp.concatenate(
            [natural.reshape(2 * devices, piece), jnp.full((8, piece), squared)], axis=0
        ),
    )
    gain_mlp_grad = lax.dynamic_slice_in_dim(totals, me, 1, 0)[0]
    gain_attn_grad = lax.dynamic_slice_in_dim(totals, devices + me, 1, 0)[0]
    distill_loss = totals[2 * devices, 0] / (2.0 * width * count)

    def finish(sums):
        low, high = sums
        kept = jnp.where(first_core, low, high)
        taken = ring.other_core(jnp.where(first_core, high, low).astype(bf16)).astype(f32)
        return kept, taken

    def whole(kept, taken):
        return jnp.concatenate(
            [jnp.where(first_core, kept, taken), jnp.where(first_core, taken, kept)], axis=1
        )

    attn_kept, attn_taken = finish(attn_sum)
    cuts = [0, q_width, q_width + kv_width, qkv_width, attn_kept.shape[1]]
    query_grad, key_grad, value_grad, out_grad_t = [
        whole(attn_kept[:, a:b], attn_taken[:, a:b]) for a, b in zip(cuts[:-1], cuts[1:])
    ]
    return (
        activations,
        input_grad,
        gain_attn_grad,
        query_grad,
        key_grad,
        value_grad,
        out_grad_t.T,
        gain_mlp_grad,
        whole(*finish(gate_sum)),
        whole(*finish(up_sum)),
        whole(*finish(down_sum)).T,
        distill_loss,
    )


def solution(mesh):
    placed = (
        P(("dp", "tensor"), None),
        P(("dp", "tensor"), None),
        P(),
        P(),
        P("dp"),
        P("dp", "tensor"),
        P("dp", "tensor"),
        P("dp", "tensor"),
        P("tensor", "dp"),
        P("dp"),
        P("dp", "tensor"),
        P("dp", "tensor"),
        P("tensor", "dp"),
    )
    return jax.shard_map(
        per_device,
        mesh=mesh,
        in_specs=placed,
        out_specs=(
            P(("dp", "tensor"), None),
            P(("dp", "tensor"), None),
            P("dp"),
            P("dp", "tensor"),
            P("dp", "tensor"),
            P("dp", "tensor"),
            P("tensor", "dp"),
            P("dp"),
            P("dp", "tensor"),
            P("dp", "tensor"),
            P("tensor", "dp"),
            P(),
        ),
        check_vma=False,
    )
```

time: 2520 us -> 1200 us (0.48)
  waiting for transfers between devices: 2010 us -> 594 us
  blocking collectives: 141 us -> 0 us
  starting transfers between devices: 47 us -> 154 us
  other arithmetic: 34.8 us -> 112 us
  local copies, waits for them, and re-layouts: 49.6 us -> 117 us
  Pallas kernels: 0 us -> 38.3 us
  matrix products: 214 us -> 176 us
    reduce_scatter x11 -> x0, waiting for transfers between devices: 1280 us -> none  [the longest x1 335 us: per_device(): lax.psum_scatter(grad_up, 'dp', scatter_dimension=0, tiled=True)]
    all_gather x11 -> x0, waiting for transfers between devices: 595 us -> none  [the longest x1 129 us: per_device(): lax.all_gather(w_gate, 'dp', axis=0, tiled=True)]
    ppermute x0 -> x145, waiting for transfers between devices: none -> 594 us  [the longest x56 323 us: ahead(): return lax.ppermute(v, 'dp', self.up)]
    ppermute x0 -> x145, starting transfers between devices: none -> 154 us  [the longest x56 86.4 us: ahead(): return lax.ppermute(v, 'dp', self.up)]
    all_to_all x7 -> x0, waiting for transfers between devices: 128 us -> none  [the longest x2 57.4 us: deal(): lax.all_to_all(second_cut, 'dp', split_axis=1, concat_axis=1, tiled=True)]
    all_gather x2 -> x0, blocking collectives: 57.6 us -> none  [the longest x1 38.9 us: per_device(): lax.all_gather(gain_attn, 'dp', axis=0, tiled=True)]
    unnamed x115 -> x337, local copies, waits for them, and re-layouts: 31.9 us -> 80.6 us
    psum x1 -> x0, blocking collectives: 47.8 us -> none  [per_device(): lax.psum((jnp.sum(error * error), gain_attn_part, gain_mlp_part), ('dp',...]
  transfers between devices with their start and end apart: 29 -> 145, of which waited for: 24 -> 78; matrix products, arithmetic and copies ran while one was open for 7% -> 24% of each run, Pallas kernels for 0% -> 3%
where the time goes in v1:
time: 1200 us
  waiting for transfers between devices  594 us (50%)
  matrix products  176 us (15%)
  starting transfers between devices  154 us (13%)
  local copies, waits for them, and re-layouts  117 us (10%)
  other arithmetic  112 us (9%)
  Pallas kernels  38.3 us (3%)
    ppermute x56, waiting for transfers between devices, ahead(): return lax.ppermute(v, 'dp', self.up)  323 us
    ppermute x56, waiting for transfers between devices, back(): return lax.ppermute(v, 'dp', self.down)  221 us
    ppermute x56, starting transfers between devices, ahead(): return lax.ppermute(v, 'dp', self.up)  86.4 us
    unnamed x337, local copies, waits for them, and re-layouts  80.6 us
    ppermute x56, starting transfers between devices, back(): return lax.ppermute(v, 'dp', self.down)  53.5 us
    ppermute x9, waiting for transfers between devices, other_tensor(): return lax.ppermute(v, 'tensor', [(0, 1), (1, 0)])  44 us
    pallas_call x4, Pallas kernels, reorder(): pl.pallas_call(copy_block, out_shape=jax.ShapeDtypeStruct(rows.shape, row...  38.3 us
    convert_element_type x24, other arithmetic, scatter_ring(): high = ring.ahead(high.astype(bf16)).astype(f32) + block(1, k)  32.9 us
  transfers between devices with their start and end apart: 145, of which 78 were waited for; matrix products, arithmetic and copies ran while one was open for 24% of the time, Pallas kernels for 3%

profile of v1, /device:TPU:0, one launch (start us, length us, event | category | flops | bytes accessed | tf_op | source)
XLA Modules:
  0.0 1195.7 jit_solution(5435719185326328952)
XLA Ops:
  226.3 39.8 %collective-permute-done.9 = bf16[144,1536]{1,0:T(8,128)(2,1)S(1)} collective-permute-done((bf16[144,1536]{1,0:T(8,128)(2,1)S(1)}, bf16[144,1536]{1,0:T(8,128)(2,1)S(1)}, u32[]{:S(2)}, u32[]{:S(2)}) %collective-permute-start.9) | collective-permute-done | bytes 442400 | tf_op jit(solution)/shard_map/ppermute | solution.py:55
  340.4 9.8 collective-permute-done.45
  352.1 12.4 %collective-permute-start.46 = (bf16[128,2048]{0,1:T(8,128)(2,1)S(1)}, bf16[128,2048]{0,1:T(8,128)(2,1)S(1)}, u32[]{:S(2)}, u32[]{:S(2)}) collective-permute-start(bf16[128,2048]{0,1:T(8,128)(2,1)S(1)} %get-tuple-element.94), channel_id=1, source_target_pairs={{8,0},{10,2},{16,8},{18,10},{24,16},{26,18},{28,24},{30,26},{20,28... | collective-permute-start | bytes 1572872 | tf_op jit(solution)/shard_map/ppermute | solution.py:58
  379.3 10.3 collective-permute-done.61
  401.8 10.3 collective-permute-done.47
  413.0 10.3 collective-permute-done.62
  435.5 10.3 collective-permute-done.48
  446.7 10.3 collective-permute-done.63
  469.2 10.3 collective-permute-done.49
  480.4 10.3 collective-permute-done.64
  503.1 10.1 collective-permute-done.50
  536.8 10.1 collective-permute-done.51
  569.6 11.0 collective-permute-done.52
  592.9 11.1 fusion.172
  604.0 18.3 %multiply_convert_fusion.2 = (bf16[1024,2048]{1,0:T(8,128)(2,1)}, f32[1024,2048]{1,0:T(8,128)}) fusion(f32[1024,2048]{1,0:T(8,128)} %fusion.172, bf16[2048,2048]{0,1:T(8,128)(2,1)} %constant_dynamic-update-slice_fusion.48, bf16[256,2048]{1,0:T(8,128)(2,1)} %copy-done.104, bf16[256,2048]{1,0:T(8,128)(2,1)} %copy-done.102, bf16[256,2048]{1,0:T(8,128)(2,1)} %copy-done.100, ...), kind=kOutput, calls=%fused_computation.41 | convolution fusion | flops 8619294720 | bytes 33554432 | tf_op jit(solution)/shard_map/dot_general | solution.py:263
  622.3 12.7 %fusion.187 = f32[1024,2048]{1,0:T(8,128)S(1)} fusion(bf16[1024,2048]{1,0:T(8,128)(2,1)} %get-tuple-element.205, bf16[2048,2048]{0,1:T(8,128)(2,1)} %constant_dynamic-update-slice_fusion.64), kind=kOutput, calls=%fused_computation.513 | convolution fusion | flops 8589934592 | bytes 20971520 | tf_op jit(solution)/shard_map/dot_general | solution.py:267
  655.0 13.9 %collective-permute-done.69 = bf16[256,2048]{1,0:T(8,128)(2,1)S(1)} collective-permute-done((bf16[256,2048]{1,0:T(8,128)(2,1)}, bf16[256,2048]{1,0:T(8,128)(2,1)S(1)}, u32[]{:S(2)}, u32[]{:S(2)}) %collective-permute-start.69) | collective-permute-done | bytes 1048608 | tf_op jit(solution)/shard_map/ppermute | solution.py:65
  675.2 23.9 %collective-permute-done.70 = bf16[256,2048]{1,0:T(8,128)(2,1)} collective-permute-done((bf16[256,2048]{1,0:T(8,128)(2,1)S(1)}, bf16[256,2048]{1,0:T(8,128)(2,1)}, u32[]{:S(2)}, u32[]{:S(2)}) %collective-permute-start.70) | collective-permute-done | bytes 1048608 | tf_op jit(solution)/shard_map/ppermute | solution.py:65
  711.3 18.7 %multiply_convert_fusion.1 = (bf16[1024,2048]{1,0:T(8,128)(2,1)}, bf16[1024,2048]{1,0:T(8,128)(2,1)}) fusion(f32[1024,2048]{1,0:T(8,128)} %fusion.172, f32[1024,2048]{1,0:T(8,128)} %get-tuple-element.206, bf16[2048,2048]{0,1:T(8,128)(2,1)} %constant_dynamic-update-slice_fusion.64, bf16[256,2048]{1,0:T(8,128)(2,1)} %collective-permute-done.72, ...), kind=kOutput, calls=%fused_computation.40 | convolution fusion | flops 8633974784 | bytes 37748736 | tf_op jit(solution)/shard_map/dot_general | solution.py:276
  730.1 12.6 %fusion.188 = f32[1024,2048]{1,0:T(8,128)S(1)} fusion(bf16[1024,2048]{1,0:T(8,128)(2,1)} %get-tuple-element.140, bf16[2048,2048]{0,1:T(8,128)(2,1)} %constant_dynamic-update-slice_fusion.48), kind=kOutput, calls=%fused_computation.514 | convolution fusion | flops 8589934592 | bytes 20971520 | tf_op jit(solution)/shard_map/dot_general | solution.py:288
  742.7 11.6 convolution_add_fusion
  760.2 16.1 %fusion.183 = (bf16[2048,2048]{0,1:T(8,128)(2,1)}, f32[2048,2048]{0,1:T(8,128)}) fusion(bf16[1024,2048]{1,0:T(8,128)(2,1)} %get-tuple-element.139, bf16[256,2048]{1,0:T(8,128)(2,1)} %copy-done.104, bf16[256,2048]{1,0:T(8,128)(2,1)S(1)} %copy-done.103, bf16[256,2048]{1,0:T(8,128)(2,1)S(1)} %copy-done.101, bf16[256,2048]{1,0:T(8,128)(2,1)S(1)} %copy-done.56), kind=kOutput, calls=%fused_computation.509 | convolution fusion | flops 8610906112 | bytes 33554432 | tf_op jit(solution)/shard_map/dot_general | solution.py:281
  779.6 16.6 %fusion.184 = (bf16[2048,2048]{0,1:T(8,128)(2,1)}, f32[2048,2048]{0,1:T(8,128)}) fusion(bf16[1024,2048]{1,0:T(8,128)(2,1)} %get-tuple-element.140, bf16[256,2048]{1,0:T(8,128)(2,1)} %copy-done.104, bf16[256,2048]{1,0:T(8,128)(2,1)} %copy-done.102, bf16[256,2048]{1,0:T(8,128)(2,1)} %copy-done.100, bf16[256,2048]{1,0:T(8,128)(2,1)S(1)} %copy-done.56), kind=kOutput, calls=%fused_computation.510 | convolution fusion | flops 8610906112 | bytes 33554432 | tf_op jit(solution)/shard_map/dot_general | solution.py:283
  799.6 16.5 %fusion.185 = (bf16[2048,2048]{0,1:T(8,128)(2,1)}, f32[2048,2048]{0,1:T(8,128)}) fusion(bf16[1024,2048]{1,0:T(8,128)(2,1)} %get-tuple-element.205, bf16[256,2048]{1,0:T(8,128)(2,1)} %collective-permute-done.72, bf16[256,2048]{1,0:T(8,128)(2,1)} %collective-permute-done.71, bf16[256,2048]{1,0:T(8,128)(2,1)} %collective-permute-done.70, ...), kind=kOutput, calls=%fused_computation.511 | convolution fusion | flops 8610906112 | bytes 33554432 | tf_op jit(solution)/shard_map/dot_general | solution.py:274
  (784 shorter events, 852.4 us)
Async XLA Ops:
  21.3 75.1 %collective-permute-start = (bf16[256,2048]{1,0:T(8,128)(2,1)}, bf16[256,2048]{1,0:T(8,128)(2,1)}, u32[]{:S(2)}, u32[]{:S(2)}) collective-permute-start(bf16[256,2048]{1,0:T(8,128)(2,1)} %reorder.4), channel_id=1, source_target_pairs={{0,1},{1,0},{2,3},{3,2},{4,5},{5,4},{6,7},{7,6},{8,9},{9,8},{10,11... | collective-permute-start | bytes 3145736 | tf_op jit(solution)/shard_map/ppermute | solution.py:65
  62.1 44.0 %collective-permute-start.12 = (bf16[144,1536]{1,0:T(8,128)(2,1)S(1)}, bf16[144,1536]{1,0:T(8,128)(2,1)S(1)}, u32[]{:S(2)}, u32[]{:S(2)}) collective-permute-start(bf16[144,1536]{1,0:T(8,128)(2,1)S(1)} %collective-permute-done.11), channel_id=1, source_target_pairs={{8,0},{10,2},{16,8},{18,10},{24,16},{26,18},{28,24},{30,26},{20,28... | collective-permute-start | bytes 1327112 | tf_op jit(solution)/shard_map/ppermute | solution.py:58
  96.3 65.7 %collective-permute-start.1 = (bf16[256,2048]{1,0:T(8,128)(2,1)S(1)}, bf16[256,2048]{1,0:T(8,128)(2,1)S(1)}, u32[]{:S(2)}, u32[]{:S(2)}) collective-permute-start(bf16[256,2048]{1,0:T(8,128)(2,1)S(1)} %copy-done.3), channel_id=1, source_target_pairs={{0,2},{2,0},{4,6},{6,4},{8,10},{10,8},{12,14},{14,12},{16,18},{18,... | collective-permute-start | bytes 3145736 | tf_op jit(solution)/shard_map/ppermute | solution.py:61
  105.3 57.3 %collective-permute-start.2 = (bf16[256,2048]{1,0:T(8,128)(2,1)}, bf16[256,2048]{1,0:T(8,128)(2,1)S(1)}, u32[]{:S(2)}, u32[]{:S(2)}) collective-permute-start(bf16[256,2048]{1,0:T(8,128)(2,1)} %collective-permute-done), channel_id=1, source_target_pairs={{0,2},{2,0},{4,6},{6,4},{8,10},{10,8},{12,14},{14,12},{16,18},{18,... | collective-permute-start | bytes 3145736 | tf_op jit(solution)/shard_map/ppermute | solution.py:61
  170.9 43.2 %collective-permute-start.57 = (bf16[128,2048]{0,1:T(8,128)(2,1)S(1)}, bf16[128,2048]{0,1:T(8,128)(2,1)S(1)}, u32[]{:S(2)}, u32[]{:S(2)}) collective-permute-start(bf16[128,2048]{0,1:T(8,128)(2,1)S(1)} %collective-permute-done.56), channel_id=1, source_target_pairs={{0,8},{2,10},{8,16},{10,18},{16,24},{18,26},{24,28},{26,30},{28,20... | collective-permute-start | bytes 1572872 | tf_op jit(solution)/shard_map/ppermute | solution.py:55
  180.4 43.2 %collective-permute-start.8 = (bf16[144,1536]{1,0:T(8,128)(2,1)S(1)}, bf16[144,1536]{1,0:T(8,128)(2,1)S(1)}, u32[]{:S(2)}, u32[]{:S(2)}) collective-permute-start(bf16[144,1536]{1,0:T(8,128)(2,1)S(1)} %collective-permute-done.7), channel_id=1, source_target_pairs={{0,8},{2,10},{8,16},{10,18},{16,24},{18,26},{24,28},{26,30},{28,20... | collective-permute-start | bytes 1327112 | tf_op jit(solution)/shard_map/ppermute | solution.py:55
  191.6 77.2 %collective-permute-start.28 = (bf16[128,2048]{0,1:T(8,128)(2,1)S(1)}, bf16[128,2048]{0,1:T(8,128)(2,1)}, u32[]{:S(2)}, u32[]{:S(2)}) collective-permute-start(bf16[128,2048]{0,1:T(8,128)(2,1)S(1)} %collective-permute-done.27), channel_id=1, source_target_pairs={{0,8},{2,10},{8,16},{10,18},{16,24},{18,26},{24,28},{26,30},{28,20... | collective-permute-start | bytes 1572872 | tf_op jit(solution)/shard_map/ppermute | solution.py:55
  202.9 67.6 %collective-permute-start.43 = (bf16[128,2048]{0,1:T(8,128)(2,1)S(1)}, bf16[128,2048]{0,1:T(8,128)(2,1)}, u32[]{:S(2)}, u32[]{:S(2)}) collective-permute-start(bf16[128,2048]{0,1:T(8,128)(2,1)S(1)} %collective-permute-done.42), channel_id=1, source_target_pairs={{0,8},{2,10},{8,16},{10,18},{16,24},{18,26},{24,28},{26,30},{28,20... | collective-permute-start | bytes 1572872 | tf_op jit(solution)/shard_map/ppermute | solution.py:55
  214.1 59.8 %collective-permute-start.58 = (bf16[128,2048]{0,1:T(8,128)(2,1)S(1)}, bf16[128,2048]{0,1:T(8,128)(2,1)}, u32[]{:S(2)}, u32[]{:S(2)}) collective-permute-start(bf16[128,2048]{0,1:T(8,128)(2,1)S(1)} %collective-permute-done.57), channel_id=1, source_target_pairs={{0,8},{2,10},{8,16},{10,18},{16,24},{18,26},{24,28},{26,30},{28,20... | collective-permute-start | bytes 1572872 | tf_op jit(solution)/shard_map/ppermute | solution.py:55
  268.8 55.1 %collective-permute-start.29 = (bf16[128,2048]{0,1:T(8,128)(2,1)}, bf16[128,2048]{0,1:T(8,128)(2,1)}, u32[]{:S(2)}, u32[]{:S(2)}) collective-permute-start(bf16[128,2048]{0,1:T(8,128)(2,1)} %collective-permute-done.28), channel_id=1, source_target_pairs={{0,8},{2,10},{8,16},{10,18},{16,24},{18,26},{24,28},{26,30},{28,20... | collective-permute-start | bytes 1572872 | tf_op jit(solution)/shard_map/ppermute | solution.py:55
  270.5 56.3 %collective-permute-start.44 = (bf16[128,2048]{0,1:T(8,128)(2,1)}, bf16[128,2048]{0,1:T(8,128)(2,1)}, u32[]{:S(2)}, u32[]{:S(2)}) collective-permute-start(bf16[128,2048]{0,1:T(8,128)(2,1)} %collective-permute-done.43), channel_id=1, source_target_pairs={{0,8},{2,10},{8,16},{10,18},{16,24},{18,26},{24,28},{26,30},{28,20... | collective-permute-start | bytes 1572872 | tf_op jit(solution)/shard_map/ppermute | solution.py:55
  274.0 53.9 %collective-permute-start.59 = (bf16[128,2048]{0,1:T(8,128)(2,1)}, bf16[128,2048]{0,1:T(8,128)(2,1)}, u32[]{:S(2)}, u32[]{:S(2)}) collective-permute-start(bf16[128,2048]{0,1:T(8,128)(2,1)} %collective-permute-done.58), channel_id=1, source_target_pairs={{0,8},{2,10},{8,16},{10,18},{16,24},{18,26},{24,28},{26,30},{28,20... | collective-permute-start | bytes 1572872 | tf_op jit(solution)/shard_map/ppermute | solution.py:55
  323.8 102.4 %collective-permute-start.18 = (bf16[512,2048]{1,0:T(8,128)(2,1)S(1)}, bf16[512,2048]{1,0:T(8,128)(2,1)S(1)}, u32[]{:S(2)}, u32[]{:S(2)}) collective-permute-start(bf16[512,2048]{1,0:T(8,128)(2,1)S(1)} %slice.1267), channel_id=1, source_target_pairs={{0,2},{2,0},{4,6},{6,4},{8,10},{10,8},{12,14},{14,12},{16,18},{18,... | collective-permute-start | bytes 6291464 | tf_op jit(solution)/shard_map/ppermute | solution.py:61
  427.3 65.5 %collective-permute-start.19 = (bf16[256,2048]{1,0:T(8,128)(2,1)S(1)}, bf16[256,2048]{1,0:T(8,128)(2,1)S(1)}, u32[]{:S(2)}, u32[]{:S(2)}) collective-permute-start(bf16[256,2048]{1,0:T(8,128)(2,1)S(1)} %slice.1271), channel_id=1, source_target_pairs={{0,1},{1,0},{2,3},{3,2},{4,5},{5,4},{6,7},{7,6},{8,9},{9,8},{10,11... | collective-permute-start | bytes 3145736 | tf_op jit(solution)/shard_map/ppermute | solution.py:65
  494.3 53.6 %collective-permute-start.20 = (bf16[256,2048]{1,0:T(8,128)(2,1)S(1)}, bf16[256,2048]{1,0:T(8,128)(2,1)S(1)}, u32[]{:S(2)}, u32[]{:S(2)}) collective-permute-start(bf16[256,2048]{1,0:T(8,128)(2,1)S(1)} %multiply_convert_fusion.3), channel_id=1, source_target_pairs={{0,1},{1,0},{2,3},{3,2},{4,5},{5,4},{6,7},{7,6},{8,9},{9,8},{10,11... | collective-permute-start | bytes 3145736 | tf_op jit(solution)/shard_map/ppermute | solution.py:65
  495.7 95.1 %collective-permute-start.21 = (bf16[256,2048]{1,0:T(8,128)(2,1)S(1)}, bf16[256,2048]{1,0:T(8,128)(2,1)S(1)}, u32[]{:S(2)}, u32[]{:S(2)}) collective-permute-start(bf16[256,2048]{1,0:T(8,128)(2,1)S(1)} %multiply_convert_fusion.3), channel_id=1, source_target_pairs={{0,2},{2,0},{4,6},{6,4},{8,10},{10,8},{12,14},{14,12},{16,18},{18,... | collective-permute-start | bytes 3145736 | tf_op jit(solution)/shard_map/ppermute | solution.py:61
  759.2 143.7 %collective-permute-start.73 = (bf16[512,2048]{1,0:T(8,128)(2,1)}, bf16[512,2048]{1,0:T(8,128)(2,1)}, u32[]{:S(2)}, u32[]{:S(2)}) collective-permute-start(bf16[512,2048]{1,0:T(8,128)(2,1)} %slice.1265), channel_id=1, source_target_pairs={{0,2},{2,0},{4,6},{6,4},{8,10},{10,8},{12,14},{14,12},{16,18},{18,... | collective-permute-start | bytes 6291464 | tf_op jit(solution)/shard_map/ppermute | solution.py:61
  912.6 47.3 %collective-permute-start.74 = (bf16[256,2048]{1,0:T(8,128)(2,1)S(1)}, bf16[256,2048]{1,0:T(8,128)(2,1)S(1)}, u32[]{:S(2)}, u32[]{:S(2)}) collective-permute-start(bf16[256,2048]{1,0:T(8,128)(2,1)S(1)} %slice.1269), channel_id=1, source_target_pairs={{0,1},{1,0},{2,3},{3,2},{4,5},{5,4},{6,7},{7,6},{8,9},{9,8},{10,11... | collective-permute-start | bytes 3145736 | tf_op jit(solution)/shard_map/ppermute | solution.py:65
  1002.4 55.5 %collective-permute-start.121 = (bf16[128,2048]{0,1:T(8,128)(2,1)}, bf16[128,2048]{0,1:T(8,128)(2,1)S(1)}, u32[]{:S(2)}, u32[]{:S(2)}) collective-permute-start(bf16[128,2048]{0,1:T(8,128)(2,1)} %get-tuple-element.116), channel_id=1, source_target_pairs={{8,0},{10,2},{16,8},{18,10},{24,16},{26,18},{28,24},{30,26},{20,28... | collective-permute-start | bytes 1572872 | tf_op jit(solution)/shard_map/ppermute | solution.py:58
  1013.6 45.8 %collective-permute-start.128 = (bf16[128,2048]{0,1:T(8,128)(2,1)}, bf16[128,2048]{0,1:T(8,128)(2,1)}, u32[]{:S(2)}, u32[]{:S(2)}) collective-permute-start(bf16[128,2048]{0,1:T(8,128)(2,1)} %get-tuple-element.115), channel_id=1, source_target_pairs={{0,8},{2,10},{8,16},{10,18},{16,24},{18,26},{24,28},{26,30},{28,20... | collective-permute-start | bytes 1572872 | tf_op jit(solution)/shard_map/ppermute | solution.py:55
  1014.6 55.6 %collective-permute-start.136 = (bf16[128,2048]{0,1:T(8,128)(2,1)}, bf16[128,2048]{0,1:T(8,128)(2,1)S(1)}, u32[]{:S(2)}, u32[]{:S(2)}) collective-permute-start(bf16[128,2048]{0,1:T(8,128)(2,1)} %get-tuple-element.104), channel_id=1, source_target_pairs={{8,0},{10,2},{16,8},{18,10},{24,16},{26,18},{28,24},{30,26},{20,28... | collective-permute-start | bytes 1572872 | tf_op jit(solution)/shard_map/ppermute | solution.py:58
  1018.2 52.0 %collective-permute-start.143 = (bf16[128,2048]{0,1:T(8,128)(2,1)}, bf16[128,2048]{0,1:T(8,128)(2,1)S(1)}, u32[]{:S(2)}, u32[]{:S(2)}) collective-permute-start(bf16[128,2048]{0,1:T(8,128)(2,1)} %get-tuple-element.103), channel_id=1, source_target_pairs={{0,8},{2,10},{8,16},{10,18},{16,24},{18,26},{24,28},{26,30},{28,20... | collective-permute-start | bytes 1572872 | tf_op jit(solution)/shard_map/ppermute | solution.py:55
  1019.7 70.7 %collective-permute-start.114 = (bf16[128,2048]{0,1:T(8,128)(2,1)}, bf16[128,2048]{0,1:T(8,128)(2,1)}, u32[]{:S(2)}, u32[]{:S(2)}) collective-permute-start(bf16[128,2048]{0,1:T(8,128)(2,1)} %select_convert_fusion.2), channel_id=1, source_target_pairs={{0,2},{2,0},{4,6},{6,4},{8,10},{10,8},{12,14},{14,12},{16,18},{18,... | collective-permute-start | bytes 1572872 | tf_op jit(solution)/shard_map/ppermute | solution.py:61
  1072.8 48.9 %collective-permute-start.144 = (bf16[128,2048]{0,1:T(8,128)(2,1)}, bf16[128,2048]{0,1:T(8,128)(2,1)S(1)}, u32[]{:S(2)}, u32[]{:S(2)}) collective-permute-start(bf16[128,2048]{0,1:T(8,128)(2,1)} %select_convert_fusion), channel_id=1, source_target_pairs={{0,2},{2,0},{4,6},{6,4},{8,10},{10,8},{12,14},{14,12},{16,18},{18,... | collective-permute-start | bytes 1572872 | tf_op jit(solution)/shard_map/ppermute | solution.py:61
  (242 other events, 6223.6 us)

commit v2 on v1

v2 whole, which is shorter than its diff:
```python
import jax
import jax.numpy as jnp
from jax import lax
from jax.experimental import pallas as pl
from jax.experimental.pallas import tpu as pltpu
from jax.sharding import PartitionSpec as P

HEAD_SIZE = 256
LANES = 128
EPS = 1e-06
ROPE_BASE = 1000042.0
over_rows = (((0,), (0,)), ((), ()))
over_last = (((1,), (1,)), ((), ()))
plain = (((1,), (0,)), ((), ()))
f32 = jnp.float32
bf16 = jnp.bfloat16


def rms_scale(value_rows):
    return lax.rsqrt(jnp.mean(value_rows * value_rows, axis=-1, keepdims=True) + EPS)


def rope_tables(position, width):
    half = width // 2
    exponent = jnp.arange(half, dtype=f32) * (-2.0 / width)
    frequency = jnp.exp(exponent * jnp.log(f32(ROPE_BASE)))
    angle = position.astype(f32)[..., None] * frequency
    return (jnp.cos(angle), jnp.sin(angle))


def rotate(heads, cosine, sine):
    half = heads.shape[-1] // 2
    first, second = heads[..., :half], heads[..., half:]
    return jnp.concatenate(
        [first * cosine - second * sine, second * cosine + first * sine], axis=-1
    )


def ring_order(chips):
    column = chips // 2
    return [2 * i for i in range(column)] + [2 * i + 1 for i in reversed(range(column))]


class Ring:
    def __init__(self, chips):
        self.chips = chips
        order = ring_order(chips)
        self.place = [order.index(c) for c in range(chips)]
        hop = [(order[i], order[(i + 1) % chips]) for i in range(chips)]
        self.up = [(2 * a + c, 2 * b + c) for a, b in hop for c in range(2)]
        self.down = [(b, a) for a, b in self.up]
        self.swap = [(d, d ^ 1) for d in range(2 * chips)]

    def ahead(self, v):
        return lax.ppermute(v, "dp", self.up)

    def back(self, v):
        return lax.ppermute(v, "dp", self.down)

    def other_core(self, v):
        return lax.ppermute(v, "dp", self.swap)


def other_tensor(v):
    return lax.ppermute(v, "tensor", [(0, 1), (1, 0)])


def together(values):
    return lax.optimization_barrier(values)


class Gather:
    def __init__(self, ring, low, high):
        self.ring = ring
        self.now = (low, high)
        self.lows, self.highs = [low], [high]

    def move(self):
        return self.ring.ahead(self.now[0]), self.ring.back(self.now[1])

    def take(self, moved):
        self.now = moved
        self.lows.append(moved[0])
        self.highs.append(moved[1])

    def rows(self):
        return self.lows + self.highs


class Scatter:
    def __init__(self, ring, grads, rows):
        self.ring, self.grads, self.size = ring, grads, rows
        self.left = ring.chips - 1
        self.now = (self.block(0), self.block(1))

    def block(self, half):
        start = (half * self.ring.chips + self.left) * self.size
        return jnp.concatenate([g[start : start + self.size] for g in self.grads], axis=1)

    def move(self):
        return self.ring.back(self.now[0]), self.ring.ahead(self.now[1])

    def take(self, moved):
        self.left -= 1
        sums = [m.astype(f32) + self.block(half).astype(f32) for half, m in enumerate(moved)]
        self.now = tuple(sums if self.left == 0 else [v.astype(bf16) for v in sums])


def turn(lane, other=None, values=()):
    moved, _, values = together((lane.move(), other.now if other else (), values))
    lane.take(moved)
    return values


class Stages:
    def __init__(self, generator):
        self.generator = generator
        self.result = None
        self.value = ()
        self.over = False
        self.advance(None)

    def advance(self, value):
        if not self.over:
            try:
                self.value = self.generator.send(value)
            except StopIteration as end:
                self.result, self.over, self.value = end.value, True, ()

    def turn(self, lane, other=None):
        self.advance(turn(lane, other, self.value))

    def finish(self):
        while not self.over:
            self.advance(self.value)
        return self.result


def gather_group(ring, rows):
    across = other_tensor(rows)
    beside = ring.other_core(rows)
    return jnp.concatenate([rows, across, beside, ring.other_core(across)], axis=0)


def scatter_group(ring, parts):
    quarter = parts.shape[0] // 4
    near = parts[: 2 * quarter] + ring.other_core(parts[2 * quarter :].astype(bf16)).astype(f32)
    return near[:quarter] + other_tensor(near[quarter:].astype(bf16)).astype(f32)


def copy_blocks(table, source, target):
    for k in range(target.shape[1] // LANES):
        start = pl.multiple_of(table[k] * LANES, LANES)
        target[:, k * LANES : (k + 1) * LANES] = source[:, pl.ds(start, LANES)]


def reorder(rows, table):
    height, width = rows.shape
    step = height // 4
    return pl.pallas_call(
        copy_blocks,
        out_shape=jax.ShapeDtypeStruct(rows.shape, rows.dtype),
        grid_spec=pltpu.PrefetchScalarGridSpec(
            num_scalar_prefetch=1,
            grid=(height // step,),
            in_specs=[pl.BlockSpec((step, width), lambda k, t: (k, 0))],
            out_specs=pl.BlockSpec((step, width), lambda k, t: (k, 0)),
        ),
        name="reorder",
    )(table, rows)


def sum_all(ring, v):
    v = v + other_tensor(v)
    devices = 2 * ring.chips
    step = 1
    while step < devices:
        v = v + lax.ppermute(v, "dp", [(d, d ^ step) for d in range(devices)])
        step *= 2
    return v


def per_device(
    layer_input,
    teacher,
    lengths,
    seq_order,
    gain_attn,
    w_query,
    key_projection_weight,
    value_projection_weight,
    w_out,
    gain_mlp,
    w_gate,
    w_up,
    w_down,
):
    token_rows, width = layer_input.shape
    slots = token_rows * lax.axis_size("tensor")
    devices = lax.axis_size("dp")
    tokens_all = slots * devices
    chips = devices // 2
    ring = Ring(chips)
    me = lax.axis_index("dp")
    side = lax.axis_index("tensor")
    chip, core = me // 2, me % 2
    first_core = core == 0
    place = jnp.array(ring.place, dtype=jnp.int32)
    here = place[chip]
    piece = gain_attn.shape[0]

    numbers = jnp.arange(chips, dtype=jnp.int32)
    order = jnp.array(ring_order(chips), dtype=jnp.int32)
    from_low = 2 * order[(here - numbers) % chips]
    from_high = 2 * order[(here + numbers) % chips] + 1
    to_relative = jnp.concatenate([from_low, from_high])
    to_natural = jnp.stack(
        [(here - place) % chips, chips + (place - here) % chips], axis=1
    ).reshape(devices)

    def split_cores(w):
        quarter = w.shape[1] // 2
        mine = lax.dynamic_slice_in_dim(w, core * quarter, quarter, 1)
        given = lax.dynamic_slice_in_dim(w, (1 - core) * quarter, quarter, 1)
        return mine, given

    def both_rows(weights, gains=None):
        mine, given = zip(*[split_cores(w) for w in weights])
        mine, given = jnp.concatenate(mine, axis=1), jnp.concatenate(given, axis=1)
        if gains is not None:
            extra = jnp.pad(gains, ((0, 16 - gains.shape[0]), (0, mine.shape[1] - gains.shape[1])))
            mine = jnp.concatenate([mine, extra], axis=0)
            given = jnp.concatenate([given, extra], axis=0)
        taken = ring.other_core(given)
        return (
            jnp.where(first_core, mine, taken),
            jnp.where(first_core, taken, mine),
        )

    gains = jnp.stack([gain_attn, gain_mlp])
    hops = ring.chips - 1
    attn_weights = Gather(
        ring,
        *both_rows([w_query, key_projection_weight, value_projection_weight, w_out.T], gains),
    )
    gate_weights = Gather(ring, *both_rows([w_gate]))
    own_input = reorder(layer_input, to_relative)
    group_rows = gather_group(ring, own_input)
    for k in range(hops):
        turn(attn_weights, gate_weights)
        turn(gate_weights, attn_weights)
    up_weights = Gather(ring, *together((both_rows([w_up]), attn_weights.now))[0])
    down_weights = Gather(ring, *together((both_rows([w_down.T]), gate_weights.now))[0])

    sequence_numbers = jnp.stack([me, me + 1 - 2 * core])
    length = jnp.sum(
        jnp.where(seq_order[None, :] == sequence_numbers[:, None], lengths[None, :], 0), axis=1
    )
    offsets = jnp.arange(token_rows, dtype=jnp.int32)
    slot = jnp.concatenate([side * token_rows + offsets, (1 - side) * token_rows + offsets])
    inside = slot[None, :] < length[:, None]
    sequence = jnp.where(inside, 0, 1 + slot[None, :])
    position = jnp.where(inside, slot[None, :], 0)
    own_valid = inside[0, :token_rows].astype(f32)[:, None]
    allowed = (sequence[:, :, None] == sequence[:, None, :]) & (
        position[:, None, :] <= position[:, :, None]
    )
    allowed = allowed[:, None]
    cosine, sine = rope_tables(position, HEAD_SIZE)
    cosine, sine = cosine[:, :, None, :], sine[:, :, None, :]
    scaling = HEAD_SIZE ** (-0.5)
    q_width = w_query.shape[1] // 2
    kv_width = key_projection_weight.shape[1] // 2
    qkv_width = q_width + 2 * kv_width
    query_heads = q_width // HEAD_SIZE
    all_rows = 2 * slots
    own_rows = own_input.astype(f32)
    attn_scale = rms_scale(own_rows)

    pieces = attn_weights.rows()
    qkv_proj = jnp.concatenate([p[:piece, :qkv_width] for p in pieces], axis=0)
    out_proj_t = jnp.concatenate([p[:piece, qkv_width:] for p in pieces], axis=0)
    gain_rows = jnp.concatenate([p[piece : piece + 2, :piece] for p in pieces], axis=1).astype(f32)
    attn_gain, mlp_gain = gain_rows[:1], gain_rows[1:]
    gate_proj = jnp.concatenate(gate_weights.rows(), axis=0)

    def forward():
        group_input = group_rows.astype(f32)
        normed = (group_input * rms_scale(group_input) * attn_gain).astype(bf16)
        qkv = jnp.dot(normed, qkv_proj, preferred_element_type=f32)
        normed, qkv = yield normed, qkv
        query_rows = qkv[:, :q_width].reshape(2, slots, query_heads, HEAD_SIZE)
        key_rows = qkv[:, q_width : q_width + kv_width].reshape(2, slots, 1, HEAD_SIZE)
        values = qkv[:, q_width + kv_width :].astype(bf16).reshape(2, slots, HEAD_SIZE)
        rot_queries = rotate(query_rows, cosine, sine).astype(bf16)
        rot_keys = rotate(key_rows, cosine, sine).astype(bf16)[:, :, 0]
        rot_queries, rot_keys, values = yield rot_queries, rot_keys, values
        scores = (
            jnp.einsum("bigd,bjd->bgij", rot_queries, rot_keys, preferred_element_type=f32)
            * scaling
        )
        scores = jnp.where(allowed, scores, -1e30)
        shifted = jnp.exp(scores - jnp.max(scores, axis=-1, keepdims=True))
        probs = shifted / jnp.sum(shifted, axis=-1, keepdims=True)
        probs = yield probs
        mixed = (
            jnp.einsum("bgij,bjd->bigd", probs.astype(bf16), values, preferred_element_type=f32)
            .reshape(all_rows, q_width)
            .astype(bf16)
        )
        parts = lax.dot_general(mixed, out_proj_t, over_last, preferred_element_type=f32)
        mixed, parts = yield mixed, parts
        shared = scatter_group(ring, parts)
        yield ()
        yield ()
        shared = yield shared
        middle = own_rows + shared
        mlp_scale = rms_scale(middle)
        normed_mlp = gather_group(ring, (middle * mlp_scale * mlp_gain).astype(bf16))
        yield ()
        yield ()
        normed_mlp = yield normed_mlp
        gate = jnp.dot(normed_mlp, gate_proj, preferred_element_type=f32)
        gate = yield gate
        return normed, rot_queries, rot_keys, values, probs, mixed, middle, mlp_scale, normed_mlp, gate

    stages = Stages(forward())
    for k in range(hops):
        stages.turn(up_weights, down_weights)
        stages.turn(down_weights, up_weights)
    (normed, rot_queries, rot_keys, values, probs, mixed, middle, mlp_scale, normed_mlp, gate) = (
        stages.finish()
    )
    up_proj = jnp.concatenate(up_weights.rows(), axis=0)
    down_proj_t = jnp.concatenate(down_weights.rows(), axis=0)
    own_teacher = reorder(teacher, to_relative)

    up = jnp.dot(normed_mlp, up_proj, preferred_element_type=f32)
    sigmoid_gate = jax.nn.sigmoid(gate)
    hidden = (gate * sigmoid_gate * up).astype(bf16)
    result = middle + scatter_group(
        ring, lax.dot_general(hidden, down_proj_t, over_last, preferred_element_type=f32)
    )
    error = (result - own_teacher.astype(f32)) * own_valid
    count = jnp.sum(lengths).astype(f32)
    delta_result = error * (tokens_all / count)
    branch = gather_group(ring, delta_result.astype(bf16))
    grad_down_t = lax.dot_general(branch, hidden, over_rows, preferred_element_type=f32)
    down_sums = Scatter(ring, [grad_down_t.astype(bf16)], piece)

    def backward():
        activations = reorder(result.astype(bf16), to_natural)
        delta_hidden = jnp.dot(branch, down_proj_t, preferred_element_type=f32)
        delta_gate = (
            delta_hidden * up * sigmoid_gate * (1.0 + gate * (1.0 - sigmoid_gate))
        ).astype(bf16)
        delta_up = (delta_hidden * gate * sigmoid_gate).astype(bf16)
        activations, delta_gate, delta_up = yield activations, delta_gate, delta_up
        grad_gate = lax.dot_general(
            normed_mlp, delta_gate, over_rows, preferred_element_type=f32
        ).astype(bf16)
        grad_gate, delta_gate = yield grad_gate, delta_gate
        grad_up = lax.dot_general(
            normed_mlp, delta_up, over_rows, preferred_element_type=f32
        ).astype(bf16)
        grad_up, delta_up = yield grad_up, delta_up
        gate_up.append(grad_gate)
        gate_up.append(grad_up)
        from_gate = lax.dot_general(delta_gate, gate_proj, over_last, preferred_element_type=f32)
        from_gate, delta_up = yield from_gate, delta_up
        parts = from_gate + lax.dot_general(
            delta_up, up_proj, over_last, preferred_element_type=f32
        )
        parts = yield parts
        delta_normed_mlp = scatter_group(ring, parts)
        yield ()
        delta_normed_mlp = yield delta_normed_mlp
        gain_mlp_part = jnp.sum(delta_normed_mlp * middle * mlp_scale, axis=0)
        weighted_mlp = mlp_gain * delta_normed_mlp
        delta_middle = (
            delta_result
            + mlp_scale * weighted_mlp
            - middle * mlp_scale**3 * jnp.mean(middle * weighted_mlp, axis=-1, keepdims=True)
        )
        attn_low_rows = gather_group(ring, delta_middle.astype(bf16))
        yield ()
        attn_low_rows = yield attn_low_rows
        grad_out_t = lax.dot_general(attn_low_rows, mixed, over_rows, preferred_element_type=f32)
        delta_mixed = (
            jnp.dot(attn_low_rows, out_proj_t, preferred_element_type=f32)
            .astype(bf16)
            .reshape(2, slots, query_heads, HEAD_SIZE)
        )
        grad_out_t, delta_mixed = yield grad_out_t.astype(bf16), delta_mixed
        probs_low = probs.astype(bf16)
        delta_probs = jnp.einsum("bigd,bjd->bgij", delta_mixed, values, preferred_element_type=f32)
        inner = jnp.sum(probs * delta_probs, axis=-1, keepdims=True)
        delta_scores = (probs * (delta_probs - inner)).astype(bf16)
        delta_values = jnp.einsum(
            "bgij,bigd->bjd", probs_low, delta_mixed, preferred_element_type=f32
        )
        delta_scores, delta_values = yield delta_scores, delta_values
        delta_qrot = (
            jnp.einsum("bgij,bjd->bigd", delta_scores, rot_keys, preferred_element_type=f32)
            * scaling
        )
        delta_krot = (
            jnp.einsum("bgij,bigd->bjd", delta_scores, rot_queries, preferred_element_type=f32)
            * scaling
        )
        delta_queries = rotate(delta_qrot, cosine, -sine).reshape(all_rows, q_width)
        delta_keys = rotate(delta_krot[:, :, None], cosine, -sine).reshape(all_rows, kv_width)
        delta_qkv = jnp.concatenate(
            [
                delta_queries.astype(bf16),
                delta_keys.astype(bf16),
                delta_values.astype(bf16).reshape(all_rows, kv_width),
            ],
            axis=1,
        )
        delta_qkv = yield delta_qkv
        grad_qkv = lax.dot_general(normed, delta_qkv, over_rows, preferred_element_type=f32)
        return (
            activations,
            gain_mlp_part,
            delta_middle,
            delta_qkv,
            [grad_qkv.astype(bf16), grad_out_t],
        )

    gate_up = []
    stages = Stages(backward())
    for k in range(3):
        stages.turn(down_sums)
    gate_up_sums = Scatter(ring, gate_up, piece)
    for k in range(hops):
        stages.turn(gate_up_sums, down_sums)
        if down_sums.left:
            stages.turn(down_sums, gate_up_sums)
    activations, gain_mlp_part, delta_middle, delta_qkv, attn_grads = stages.finish()
    attn_sums = Scatter(ring, attn_grads, piece)
    squared = jnp.sum(error * error)

    def finish(sums):
        low, high = sums.now
        kept = jnp.where(first_core, low, high)
        taken = ring.other_core(jnp.where(first_core, high, low).astype(bf16)).astype(f32)
        return kept, taken

    def whole(kept, taken):
        return jnp.concatenate(
            [jnp.where(first_core, kept, taken), jnp.where(first_core, taken, kept)], axis=1
        )

    def closing():
        delta_normed = scatter_group(
            ring, lax.dot_general(delta_qkv, qkv_proj, over_last, preferred_element_type=f32)
        )
        down_grad = whole(*finish(down_sums)).T
        down_grad = yield down_grad
        kept, taken = finish(gate_up_sums)
        gate_width = w_gate.shape[1] // 2
        gate_grad = whole(kept[:, :gate_width], taken[:, :gate_width])
        up_grad = whole(kept[:, gate_width:], taken[:, gate_width:])
        gate_grad, up_grad, delta_normed = yield gate_grad, up_grad, delta_normed
        gain_attn_part = jnp.sum(delta_normed * own_rows * attn_scale, axis=0)
        weighted_attn = attn_gain * delta_normed
        input_grad = (
            delta_middle
            + attn_scale * weighted_attn
            - own_rows * attn_scale**3 * jnp.mean(own_rows * weighted_attn, axis=-1, keepdims=True)
        )
        input_grad = reorder(input_grad.astype(bf16), to_natural)
        natural = jnp.stack([gain_mlp_part, gain_attn_part], axis=0).reshape(2, devices, piece)[
            :, to_natural
        ]
        sums = jnp.concatenate(
            [natural.reshape(2 * devices, piece), jnp.full((8, piece), squared)], axis=0
        )
        input_grad, sums = yield input_grad, sums
        totals = yield sum_all(ring, sums)
        return down_grad, gate_grad, up_grad, input_grad, totals

    stages = Stages(closing())
    for k in range(hops):
        stages.turn(attn_sums)
    down_grad, gate_grad, up_grad, input_grad, totals = stages.finish()
    gain_mlp_grad = lax.dynamic_slice_in_dim(totals, me, 1, 0)[0]
    gain_attn_grad = lax.dynamic_slice_in_dim(totals, devices + me, 1, 0)[0]
    distill_loss = totals[2 * devices, 0] / (2.0 * width * count)
    attn_kept, attn_taken = finish(attn_sums)
    cuts = [0, q_width, q_width + kv_width, qkv_width, attn_kept.shape[1]]
    query_grad, key_grad, value_grad, out_grad_t = [
        whole(attn_kept[:, a:b], attn_taken[:, a:b]) for a, b in zip(cuts[:-1], cuts[1:])
    ]
    return (
        activations,
        input_grad,
        gain_attn_grad,
        query_grad,
        key_grad,
        value_grad,
        out_grad_t.T,
        gain_mlp_grad,
        gate_grad,
        up_grad,
        down_grad,
        distill_loss,
    )


def solution(mesh):
    placed = (
        P(("dp", "tensor"), None),
        P(("dp", "tensor"), None),
        P(),
        P(),
        P("dp"),
        P("dp", "tensor"),
        P("dp", "tensor"),
        P("dp", "tensor"),
        P("tensor", "dp"),
        P("dp"),
        P("dp", "tensor"),
        P("dp", "tensor"),
        P("tensor", "dp"),
    )
    return jax.shard_map(
        per_device,
        mesh=mesh,
        in_specs=placed,
        out_specs=(
            P(("dp", "tensor"), None),
            P(("dp", "tensor"), None),
            P("dp"),
            P("dp", "tensor"),
            P("dp", "tensor"),
            P("dp", "tensor"),
            P("tensor", "dp"),
            P("dp"),
            P("dp", "tensor"),
            P("dp", "tensor"),
            P("tensor", "dp"),
            P(),
        ),
        check_vma=False,
    )
```

time: 1200 us -> 989 us (0.82)
  waiting for transfers between devices: 594 us -> 398 us
  starting transfers between devices: 154 us -> 125 us
  other arithmetic: 112 us -> 138 us
  Pallas kernels: 38.3 us -> 16.7 us
  local copies, waits for them, and re-layouts: 117 us -> 138 us
  matrix products: 176 us -> 158 us
    ppermute x56 -> x49, waiting for transfers between devices: 221 us -> 82.7 us  [back(): return lax.ppermute(v, 'dp', self.down)]
    ppermute x56 -> x49, waiting for transfers between devices: 323 us -> 192 us  [ahead(): return lax.ppermute(v, 'dp', self.up)]
    ppermute x9, waiting for transfers between devices: 44 us -> 111 us  [other_tensor(): return lax.ppermute(v, 'tensor', [(0, 1), (1, 0)])]
    pallas_call x4, Pallas kernels: 38.3 us -> 16.7 us  [reorder(): pl.pallas_call(copy_blocks, out_shape=jax.ShapeDtypeStruct(rows.shape, ro...]
    ppermute x56 -> x49, starting transfers between devices: 86.4 us -> 67.6 us  [ahead(): return lax.ppermute(v, 'dp', self.up)]
    ppermute x56 -> x49, starting transfers between devices: 53.5 us -> 37.4 us  [back(): return lax.ppermute(v, 'dp', self.down)]
    convert_element_type x32 -> x34, other arithmetic: 41.1 us -> 55.1 us  [the longest x30 42.4 us: take(): self.now = tuple(sums if self.left == 0 else [v.astype(bf16) for v in sums])]
    slice x8 -> x24, local copies, waits for them, and re-layouts: 8.1 us -> 21.1 us  [the longest x21 19.3 us: block(): g[start:start + self.size]]
  transfers between devices with their start and end apart: 145 -> 130, of which waited for: 78 -> 72; matrix products, arithmetic and copies ran while one was open for 24% -> 34% of each run, Pallas kernels for 3% -> 2%
where the time goes in v2:
time: 989 us; the launch traced here: 980 us
  waiting for transfers between devices  398 us (40%)
  matrix products  158 us (16%)
  local copies, waits for them, and re-layouts  138 us (14%)
  other arithmetic  138 us (14%)
  starting transfers between devices  125 us (13%)
  Pallas kernels  16.7 us (2%)
    ppermute x49, waiting for transfers between devices, ahead(): return lax.ppermute(v, 'dp', self.up)  192 us
    ppermute x9, waiting for transfers between devices, other_tensor(): return lax.ppermute(v, 'tensor', [(0, 1), (1, 0)])  111 us
    ppermute x49, waiting for transfers between devices, back(): return lax.ppermute(v, 'dp', self.down)  82.7 us
    unnamed x400, local copies, waits for them, and re-layouts  82.6 us
    ppermute x49, starting transfers between devices, ahead(): return lax.ppermute(v, 'dp', self.up)  67.6 us
    convert_element_type x30, other arithmetic, take(): self.now = tuple(sums if self.left == 0 else [v.astype(bf16) for v in sums])  42.4 us
    ppermute x49, starting transfers between devices, back(): return lax.ppermute(v, 'dp', self.down)  37.4 us
  transfers between devices with their start and end apart: 130, of which 72 were waited for; matrix products, arithmetic and copies ran while one was open for 34% of the time, Pallas kernels for 2%

profile of v2, /device:TPU:0, one launch (start us, length us, event | category | flops | bytes accessed | tf_op | source)
XLA Modules:
  0.0 980.1 jit_solution(12756161669953122610)
XLA Ops:
  82.7 8.3 collective-permute-done.15
  216.6 8.4 fusion.9
  257.4 8.3 collective-permute-done.41
  278.4 8.4 collective-permute-done.45
  300.8 12.3 %collective-permute-done.59 = bf16[256,2048]{1,0:T(8,128)(2,1)S(1)} collective-permute-done((bf16[256,2048]{1,0:T(8,128)(2,1)S(1)}, bf16[256,2048]{1,0:T(8,128)(2,1)S(1)}, u32[]{:S(2)}, u32[]{:S(2)}) %collective-permute-start.59) | collective-permute-done | bytes 1048608 | tf_op jit(solution)/shard_map/ppermute | solution.py:65
  321.4 8.5 collective-permute-done.51
  347.1 11.1 %fusion.94 = f32[1024,2048]{1,0:T(8,128)} fusion(bf16[1024,2048]{1,0:T(8,128)(2,1)S(1)} %pad_maximum_fusion.1, bf16[2048,2048]{0,1:T(8,128)(2,1)S(1)} %bitcast.166), kind=kOutput, calls=%fused_computation.404 | convolution fusion | flops 8589934592 | bytes 20971520 | tf_op jit(solution)/shard_map/dot_general | solution.py:323
  388.5 16.1 %multiply_convert_fusion.2 = (bf16[1024,2048]{1,0:T(8,128)(2,1)}, f32[1024,2048]{1,0:T(8,128)}) fusion(f32[1024,2048]{1,0:T(8,128)} %fusion.94, bf16[1024,2048]{1,0:T(8,128)(2,1)S(1)} %pad_maximum_fusion.1, bf16[2048,2048]{0,1:T(8,128)(2,1)} %constant_dynamic-update-slice_fusion.48), kind=kOutput, calls=%fused_computation.13 | convolution fusion | flops 8602517504 | bytes 33554432 | tf_op jit(solution)/shard_map/dot_general | solution.py:338
  415.9 11.3 %fusion.95 = f32[1024,2048]{1,0:T(8,128)S(1)} fusion(bf16[1024,2048]{1,0:T(8,128)(2,1)S(1)} %copy-done.143, bf16[2048,2048]{0,1:T(8,128)(2,1)} %constant_dynamic-update-slice_fusion.64), kind=kOutput, calls=%fused_computation.405 | convolution fusion | flops 8589934592 | bytes 20971520 | tf_op jit(solution)/shard_map/dot_general | solution.py:342
  442.8 18.4 %collective-permute-done.69 = bf16[256,2048]{1,0:T(8,128)(2,1)S(1)} collective-permute-done((bf16[256,2048]{1,0:T(8,128)(2,1)}, bf16[256,2048]{1,0:T(8,128)(2,1)S(1)}, u32[]{:S(2)}, u32[]{:S(2)}) %collective-permute-start.69) | collective-permute-done | bytes 1048608 | tf_op jit(solution)/shard_map/ppermute | solution.py:65
  468.5 22.8 %collective-permute-done.70 = bf16[256,2048]{1,0:T(8,128)(2,1)S(1)} collective-permute-done((bf16[256,2048]{1,0:T(8,128)(2,1)S(1)}, bf16[256,2048]{1,0:T(8,128)(2,1)S(1)}, u32[]{:S(2)}, u32[]{:S(2)}) %collective-permute-start.70) | collective-permute-done | bytes 1048608 | tf_op jit(solution)/shard_map/ppermute | solution.py:65
  496.9 11.9 %convolution_convert_fusion.2 = bf16[2048,2048]{0,1:T(8,128)(2,1)S(1)} fusion(bf16[1024,2048]{1,0:T(8,128)(2,1)} %get-tuple-element.507, bf16[256,2048]{1,0:T(8,128)(2,1)} %collective-permute-done.72, bf16[256,2048]{1,0:T(8,128)(2,1)} %collective-permute-done.71, bf16[256,2048]{1,0:T(8,128)(2,1)S(1)} %collective-permute-done.70, ...), kind=kOutput, calls=%fused_computation.17 | convolution fusion | flops 8610906112 | bytes 16777216 | tf_op jit(solution)/shard_map/dot_general | solution.py:348
  514.4 18.8 %multiply_convert_fusion = (bf16[1024,2048]{1,0:T(8,128)(2,1)}, bf16[1024,2048]{1,0:T(8,128)(2,1)}) fusion(f32[1024,2048]{1,0:T(8,128)} %fusion.94, f32[1024,2048]{1,0:T(8,128)} %get-tuple-element.508, bf16[2048,2048]{0,1:T(8,128)(2,1)} %constant_dynamic-update-slice_fusion.64, bf16[256,2048]{1,0:T(8,128)(2,1)} %collective-permute-done.72, ...), kind=kOutput, calls=%fused_computation.11 | convolution fusion | flops 8633974784 | bytes 37748736 | tf_op jit(solution)/shard_map/dot_general | solution.py:353
  533.1 12.1 %convolution_convert_fusion.1 = bf16[2048,2048]{0,1:T(8,128)(2,1)S(1)} fusion(bf16[1024,2048]{1,0:T(8,128)(2,1)} %copy-done.21, bf16[1024,2048]{1,0:T(8,128)(2,1)} %get-tuple-element.230), kind=kOutput, calls=%fused_computation.16 | convolution fusion | flops 8594128896 | bytes 16777216 | tf_op jit(solution)/shard_map/dot_general | solution.py:359
  548.9 11.1 %convolution_convert_fusion = bf16[2048,2048]{0,1:T(8,128)(2,1)S(1)} fusion(bf16[1024,2048]{1,0:T(8,128)(2,1)S(1)} %copy-done.22, bf16[1024,2048]{1,0:T(8,128)(2,1)} %get-tuple-element.235), kind=kOutput, calls=%fused_computation.15 | convolution fusion | flops 8594128896 | bytes 16777216 | tf_op jit(solution)/shard_map/dot_general | solution.py:363
  582.0 13.4 %fusion.96 = f32[1024,2048]{1,0:T(8,128)} fusion(bf16[1024,2048]{1,0:T(8,128)(2,1)S(1)} %copy-done.144, bf16[2048,2048]{0,1:T(8,128)(2,1)} %constant_dynamic-update-slice_fusion.32), kind=kOutput, calls=%fused_computation.406 | convolution fusion | flops 8589934592 | bytes 20971520 | tf_op jit(solution)/shard_map/dot_general | solution.py:369
  606.9 13.6 %fusion.97 = f32[1024,2048]{1,0:T(8,128)} fusion(bf16[1024,2048]{1,0:T(8,128)(2,1)S(1)} %copy-done.142, bf16[2048,2048]{0,1:T(8,128)(2,1)} %constant_dynamic-update-slice_fusion.48), kind=kOutput, calls=%fused_computation.407 | convolution fusion | flops 8589934592 | bytes 20971520 | tf_op jit(solution)/shard_map/dot_general | solution.py:371
  620.5 11.7 %add.434 = f32[1024,2048]{1,0:T(8,128)} add(f32[1024,2048]{1,0:T(8,128)} %fusion.96, f32[1024,2048]{1,0:T(8,128)} %fusion.97) | non-fusion elementwise | flops 2097152 | bytes 25165824 | tf_op jit(solution)/shard_map/add | solution.py:371
  644.5 20.3 %collective-permute-done.82 = bf16[128,4096]{0,1:T(8,128)(2,1)} collective-permute-done((bf16[128,4096]{0,1:T(8,128)(2,1)}, bf16[128,4096]{0,1:T(8,128)(2,1)}, u32[]{:S(2)}, u32[]{:S(2)}) %collective-permute-start.82) | collective-permute-done | bytes 1048608 | tf_op jit(solution)/shard_map/ppermute | solution.py:55
  675.9 16.9 %collective-permute-done.90 = bf16[256,2048]{1,0:T(8,128)(2,1)S(1)} collective-permute-done((bf16[256,2048]{1,0:T(8,128)(2,1)S(1)}, bf16[256,2048]{1,0:T(8,128)(2,1)S(1)}, u32[]{:S(2)}, u32[]{:S(2)}) %collective-permute-start.90) | collective-permute-done | bytes 1048608 | tf_op jit(solution)/shard_map/ppermute | solution.py:65
  702.1 16.6 %collective-permute-done.95 = bf16[256,2048]{1,0:T(8,128)(2,1)S(1)} collective-permute-done((bf16[256,2048]{1,0:T(8,128)(2,1)S(1)}, bf16[256,2048]{1,0:T(8,128)(2,1)S(1)}, u32[]{:S(2)}, u32[]{:S(2)}) %collective-permute-start.95) | collective-permute-done | bytes 1048608 | tf_op jit(solution)/shard_map/ppermute | solution.py:65
  809.1 13.7 %collective-permute-done.108 = bf16[128,4096]{0,1:T(8,128)(2,1)S(1)} collective-permute-done((bf16[128,4096]{0,1:T(8,128)(2,1)S(1)}, bf16[128,4096]{0,1:T(8,128)(2,1)S(1)}, u32[]{:S(2)}, u32[]{:S(2)}) %collective-permute-start.108) | collective-permute-done | bytes 1048608 | tf_op jit(solution)/shard_map/ppermute | solution.py:55
  836.6 17.0 %collective-permute-done.110 = bf16[128,4096]{0,1:T(8,128)(2,1)S(1)} collective-permute-done((bf16[128,4096]{0,1:T(8,128)(2,1)S(1)}, bf16[128,4096]{0,1:T(8,128)(2,1)S(1)}, u32[]{:S(2)}, u32[]{:S(2)}) %collective-permute-start.110) | collective-permute-done | bytes 1048608 | tf_op jit(solution)/shard_map/ppermute | solution.py:55
  860.6 21.8 %collective-permute-done.113 = bf16[256,2048]{1,0:T(8,128)(2,1)S(1)} collective-permute-done((bf16[256,2048]{1,0:T(8,128)(2,1)S(1)}, bf16[256,2048]{1,0:T(8,128)(2,1)S(1)}, u32[]{:S(2)}, u32[]{:S(2)}) %collective-permute-start.113) | collective-permute-done | bytes 1048608 | tf_op jit(solution)/shard_map/ppermute | solution.py:65
  (843 shorter events, 641.4 us)
Async XLA Ops:
  12.4 40.0 %collective-permute-start.34 = (bf16[256,2048]{1,0:T(8,128)(2,1)}, bf16[256,2048]{1,0:T(8,128)(2,1)S(1)}, u32[]{:S(2)}, u32[]{:S(2)}) collective-permute-start(bf16[256,2048]{1,0:T(8,128)(2,1)} %reorder.4), channel_id=1, source_target_pairs={{0,1},{1,0},{2,3},{3,2},{4,5},{5,4},{6,7},{7,6},{8,9},{9,8},{10,11... | collective-permute-start | bytes 3145736 | tf_op jit(solution)/shard_map/ppermute | solution.py:65
  38.3 55.0 %collective-permute-start.35 = (bf16[256,2048]{1,0:T(8,128)(2,1)S(1)}, bf16[256,2048]{1,0:T(8,128)(2,1)S(1)}, u32[]{:S(2)}, u32[]{:S(2)}) collective-permute-start(bf16[256,2048]{1,0:T(8,128)(2,1)S(1)} %copy-done.3), channel_id=1, source_target_pairs={{0,2},{2,0},{4,6},{6,4},{8,10},{10,8},{12,14},{14,12},{16,18},{18,... | collective-permute-start | bytes 3145736 | tf_op jit(solution)/shard_map/ppermute | solution.py:61
  59.0 35.5 %collective-permute-start.36 = (bf16[256,2048]{1,0:T(8,128)(2,1)S(1)}, bf16[256,2048]{1,0:T(8,128)(2,1)S(1)}, u32[]{:S(2)}, u32[]{:S(2)}) collective-permute-start(bf16[256,2048]{1,0:T(8,128)(2,1)S(1)} %collective-permute-done.34), channel_id=1, source_target_pairs={{0,2},{2,0},{4,6},{6,4},{8,10},{10,8},{12,14},{14,12},{16,18},{18,... | collective-permute-start | bytes 3145736 | tf_op jit(solution)/shard_map/ppermute | solution.py:61
  247.9 30.2 %collective-permute-start.50 = (bf16[256,2048]{1,0:T(8,128)(2,1)S(1)}, bf16[256,2048]{1,0:T(8,128)(2,1)S(1)}, u32[]{:S(2)}, u32[]{:S(2)}) collective-permute-start(bf16[256,2048]{1,0:T(8,128)(2,1)S(1)} %slice.912), channel_id=1, source_target_pairs={{0,1},{1,0},{2,3},{3,2},{4,5},{5,4},{6,7},{7,6},{8,9},{9,8},{10,11... | collective-permute-start | bytes 3145736 | tf_op jit(solution)/shard_map/ppermute | solution.py:65
  300.8 32.5 %collective-permute-start.60 = (bf16[256,2048]{1,0:T(8,128)(2,1)S(1)}, bf16[256,2048]{1,0:T(8,128)(2,1)S(1)}, u32[]{:S(2)}, u32[]{:S(2)}) collective-permute-start(bf16[256,2048]{1,0:T(8,128)(2,1)S(1)} %multiply_convert_fusion.3), channel_id=1, source_target_pairs={{0,2},{2,0},{4,6},{6,4},{8,10},{10,8},{12,14},{14,12},{16,18},{18,... | collective-permute-start | bytes 3145736 | tf_op jit(solution)/shard_map/ppermute | solution.py:61
  331.7 26.6 %collective-permute-start.55 = (bf16[128,2048]{0,1:T(8,128)(2,1)S(1)}, bf16[128,2048]{0,1:T(8,128)(2,1)S(1)}, u32[]{:S(2)}, u32[]{:S(2)}) collective-permute-start(bf16[128,2048]{0,1:T(8,128)(2,1)S(1)} %collective-permute-done.51), channel_id=1, source_target_pairs={{0,8},{2,10},{8,16},{10,18},{16,24},{18,26},{24,28},{26,30},{28,20... | collective-permute-start | bytes 1572872 | tf_op jit(solution)/shard_map/ppermute | solution.py:55
  367.2 38.3 %collective-permute-start.66 = (bf16[128,2048]{0,1:T(8,128)(2,1)S(1)}, bf16[128,2048]{0,1:T(8,128)(2,1)S(1)}, u32[]{:S(2)}, u32[]{:S(2)}) collective-permute-start(bf16[128,2048]{0,1:T(8,128)(2,1)S(1)} %collective-permute-done.64), channel_id=1, source_target_pairs={{0,8},{2,10},{8,16},{10,18},{16,24},{18,26},{24,28},{26,30},{28,20... | collective-permute-start | bytes 1572872 | tf_op jit(solution)/shard_map/ppermute | solution.py:55
  368.7 36.8 %collective-permute-start.67 = (bf16[128,2048]{0,1:T(8,128)(2,1)S(1)}, bf16[128,2048]{0,1:T(8,128)(2,1)S(1)}, u32[]{:S(2)}, u32[]{:S(2)}) collective-permute-start(bf16[128,2048]{0,1:T(8,128)(2,1)S(1)} %collective-permute-done.65), channel_id=1, source_target_pairs={{8,0},{10,2},{16,8},{18,10},{24,16},{26,18},{28,24},{30,26},{20,28... | collective-permute-start | bytes 1572872 | tf_op jit(solution)/shard_map/ppermute | solution.py:58
  468.5 28.4 %collective-permute-start.71 = (bf16[256,2048]{1,0:T(8,128)(2,1)S(1)}, bf16[256,2048]{1,0:T(8,128)(2,1)}, u32[]{:S(2)}, u32[]{:S(2)}) collective-permute-start(bf16[256,2048]{1,0:T(8,128)(2,1)S(1)} %multiply_convert_fusion.4), channel_id=1, source_target_pairs={{0,2},{2,0},{4,6},{6,4},{8,10},{10,8},{12,14},{14,12},{16,18},{18,... | collective-permute-start | bytes 3145736 | tf_op jit(solution)/shard_map/ppermute | solution.py:61
  597.9 36.7 %collective-permute-start.83 = (bf16[128,2048]{0,1:T(8,128)(2,1)}, bf16[128,2048]{0,1:T(8,128)(2,1)}, u32[]{:S(2)}, u32[]{:S(2)}) collective-permute-start(bf16[128,2048]{0,1:T(8,128)(2,1)} %get-tuple-element.403), channel_id=1, source_target_pairs={{8,0},{10,2},{16,8},{18,10},{24,16},{26,18},{28,24},{30,26},{20,28... | collective-permute-start | bytes 1572872 | tf_op jit(solution)/shard_map/ppermute | solution.py:58
  599.5 35.2 %collective-permute-start.84 = (bf16[128,2048]{0,1:T(8,128)(2,1)}, bf16[128,2048]{0,1:T(8,128)(2,1)}, u32[]{:S(2)}, u32[]{:S(2)}) collective-permute-start(bf16[128,2048]{0,1:T(8,128)(2,1)} %get-tuple-element.402), channel_id=1, source_target_pairs={{0,8},{2,10},{8,16},{10,18},{16,24},{18,26},{24,28},{26,30},{28,20... | collective-permute-start | bytes 1572872 | tf_op jit(solution)/shard_map/ppermute | solution.py:55
  638.5 27.6 %collective-permute-start.89 = (bf16[512,2048]{1,0:T(8,128)(2,1)}, bf16[512,2048]{1,0:T(8,128)(2,1)S(1)}, u32[]{:S(2)}, u32[]{:S(2)}) collective-permute-start(bf16[512,2048]{1,0:T(8,128)(2,1)} %slice.906), channel_id=1, source_target_pairs={{0,2},{2,0},{4,6},{6,4},{8,10},{10,8},{12,14},{14,12},{16,18},{18,... | collective-permute-start | bytes 6291464 | tf_op jit(solution)/shard_map/ppermute | solution.py:61
  642.4 50.7 %collective-permute-start.87 = (bf16[128,2048]{0,1:T(8,128)(2,1)S(1)}, bf16[128,2048]{0,1:T(8,128)(2,1)S(1)}, u32[]{:S(2)}, u32[]{:S(2)}) collective-permute-start(bf16[128,2048]{0,1:T(8,128)(2,1)S(1)} %get-tuple-element.401), channel_id=1, source_target_pairs={{8,0},{10,2},{16,8},{18,10},{24,16},{26,18},{28,24},{30,26},{20,28... | collective-permute-start | bytes 1572872 | tf_op jit(solution)/shard_map/ppermute | solution.py:58
  643.6 49.5 %collective-permute-start.88 = (bf16[128,2048]{0,1:T(8,128)(2,1)S(1)}, bf16[128,2048]{0,1:T(8,128)(2,1)S(1)}, u32[]{:S(2)}, u32[]{:S(2)}) collective-permute-start(bf16[128,2048]{0,1:T(8,128)(2,1)S(1)} %get-tuple-element.400), channel_id=1, source_target_pairs={{0,8},{2,10},{8,16},{10,18},{16,24},{18,26},{24,28},{26,30},{28,20... | collective-permute-start | bytes 1572872 | tf_op jit(solution)/shard_map/ppermute | solution.py:55
  672.1 28.5 %collective-permute-start.86 = (bf16[128,4096]{0,1:T(8,128)(2,1)S(1)}, bf16[128,4096]{0,1:T(8,128)(2,1)S(1)}, u32[]{:S(2)}, u32[]{:S(2)}) collective-permute-start(bf16[128,4096]{0,1:T(8,128)(2,1)S(1)} %add_convert_fusion.8), channel_id=1, source_target_pairs={{0,8},{2,10},{8,16},{10,18},{16,24},{18,26},{24,28},{26,30},{28,20... | collective-permute-start | bytes 3145736 | tf_op jit(solution)/shard_map/ppermute | solution.py:55
  675.4 26.7 %collective-permute-start.85 = (bf16[128,4096]{0,1:T(8,128)(2,1)S(1)}, bf16[128,4096]{0,1:T(8,128)(2,1)S(1)}, u32[]{:S(2)}, u32[]{:S(2)}) collective-permute-start(bf16[128,4096]{0,1:T(8,128)(2,1)S(1)} %add_convert_fusion.9), channel_id=1, source_target_pairs={{8,0},{10,2},{16,8},{18,10},{24,16},{26,18},{28,24},{30,26},{20,28... | collective-permute-start | bytes 3145736 | tf_op jit(solution)/shard_map/ppermute | solution.py:58
  756.0 32.9 %collective-permute-start.99 = (bf16[128,4096]{0,1:T(8,128)(2,1)}, bf16[128,4096]{0,1:T(8,128)(2,1)}, u32[]{:S(2)}, u32[]{:S(2)}) collective-permute-start(bf16[128,4096]{0,1:T(8,128)(2,1)} %add_convert_fusion.4), channel_id=1, source_target_pairs={{0,8},{2,10},{8,16},{10,18},{16,24},{18,26},{24,28},{26,30},{28,20... | collective-permute-start | bytes 3145736 | tf_op jit(solution)/shard_map/ppermute | solution.py:55
  759.9 28.9 %collective-permute-start.98 = (bf16[128,4096]{0,1:T(8,128)(2,1)}, bf16[128,4096]{0,1:T(8,128)(2,1)}, u32[]{:S(2)}, u32[]{:S(2)}) collective-permute-start(bf16[128,4096]{0,1:T(8,128)(2,1)} %add_convert_fusion.5), channel_id=1, source_target_pairs={{8,0},{10,2},{16,8},{18,10},{24,16},{26,18},{28,24},{30,26},{20,28... | collective-permute-start | bytes 3145736 | tf_op jit(solution)/shard_map/ppermute | solution.py:58
  783.8 44.0 %collective-permute-start.104 = (bf16[128,2048]{0,1:T(8,128)(2,1)S(1)}, bf16[128,2048]{0,1:T(8,128)(2,1)S(1)}, u32[]{:S(2)}, u32[]{:S(2)}) collective-permute-start(bf16[128,2048]{0,1:T(8,128)(2,1)S(1)} %select_convert_fusion.1), channel_id=1, source_target_pairs={{0,2},{2,0},{4,6},{6,4},{8,10},{10,8},{12,14},{14,12},{16,18},{18,... | collective-permute-start | bytes 1572872 | tf_op jit(solution)/shard_map/ppermute | solution.py:61
  793.8 62.3 %collective-permute-start.112 = (bf16[512,2048]{1,0:T(8,128)(2,1)S(1)}, bf16[512,2048]{1,0:T(8,128)(2,1)S(1)}, u32[]{:S(2)}, u32[]{:S(2)}) collective-permute-start(bf16[512,2048]{1,0:T(8,128)(2,1)S(1)} %slice.905), channel_id=1, source_target_pairs={{0,2},{2,0},{4,6},{6,4},{8,10},{10,8},{12,14},{14,12},{16,18},{18,... | collective-permute-start | bytes 6291464 | tf_op jit(solution)/shard_map/ppermute | solution.py:61
  826.0 27.6 %collective-permute-start.110 = (bf16[128,4096]{0,1:T(8,128)(2,1)S(1)}, bf16[128,4096]{0,1:T(8,128)(2,1)S(1)}, u32[]{:S(2)}, u32[]{:S(2)}) collective-permute-start(bf16[128,4096]{0,1:T(8,128)(2,1)S(1)} %add_convert_fusion), channel_id=1, source_target_pairs={{0,8},{2,10},{8,16},{10,18},{16,24},{18,26},{24,28},{26,30},{28,20... | collective-permute-start | bytes 3145736 | tf_op jit(solution)/shard_map/ppermute | solution.py:55
  827.9 26.8 %collective-permute-start.109 = (bf16[128,4096]{0,1:T(8,128)(2,1)S(1)}, bf16[128,4096]{0,1:T(8,128)(2,1)S(1)}, u32[]{:S(2)}, u32[]{:S(2)}) collective-permute-start(bf16[128,4096]{0,1:T(8,128)(2,1)S(1)} %add_convert_fusion.1), channel_id=1, source_target_pairs={{8,0},{10,2},{16,8},{18,10},{24,16},{26,18},{28,24},{30,26},{20,28... | collective-permute-start | bytes 3145736 | tf_op jit(solution)/shard_map/ppermute | solution.py:58
  834.8 49.3 %collective-permute-start.106 = (bf16[128,1536]{0,1:T(8,128)(2,1)S(1)}, bf16[128,1536]{0,1:T(8,128)(2,1)}, u32[]{:S(2)}, u32[]{:S(2)}) collective-permute-start(bf16[128,1536]{0,1:T(8,128)(2,1)S(1)} %add_convert_fusion.36), channel_id=1, source_target_pairs={{0,8},{2,10},{8,16},{10,18},{16,24},{18,26},{24,28},{26,30},{28,20... | collective-permute-start | bytes 1179656 | tf_op jit(solution)/shard_map/ppermute | solution.py:55
  855.6 28.6 %collective-permute-start.105 = (bf16[128,1536]{0,1:T(8,128)(2,1)S(1)}, bf16[128,1536]{0,1:T(8,128)(2,1)}, u32[]{:S(2)}, u32[]{:S(2)}) collective-permute-start(bf16[128,1536]{0,1:T(8,128)(2,1)S(1)} %add_convert_fusion.37), channel_id=1, source_target_pairs={{8,0},{10,2},{16,8},{18,10},{24,16},{26,18},{28,24},{30,26},{20,28... | collective-permute-start | bytes 1179656 | tf_op jit(solution)/shard_map/ppermute | solution.py:58
  (253 other events, 5220.4 us)

commit v3 on v2

--- a/solution.py
+++ b/solution.py
@@ -83,33 +83,50 @@
         self.lows.append(moved[0])
         self.highs.append(moved[1])
 
+    def far(self):
+        half = self.ring.chips // 2
+        return jnp.concatenate(self.lows[half:] + self.highs[half:], axis=0)
+
+    def near(self):
+        half = self.ring.chips // 2
+        return jnp.concatenate(self.lows[:half] + self.highs[:half], axis=0)
+
     def rows(self):
-        return self.lows + self.highs
+        half = self.ring.chips // 2
+        return self.lows[half:] + self.highs[half:] + self.lows[:half] + self.highs[:half]
 
 
 class Scatter:
-    def __init__(self, ring, grads, rows):
-        self.ring, self.grads, self.size = ring, grads, rows
+    def __init__(self, ring, far, near, rows):
+        self.ring, self.parts, self.size = ring, (near, far), rows
         self.left = ring.chips - 1
         self.now = (self.block(0), self.block(1))
 
-    def block(self, half):
-        start = (half * self.ring.chips + self.left) * self.size
-        return jnp.concatenate([g[start : start + self.size] for g in self.grads], axis=1)
+    def block(self, side):
+        half = self.ring.chips // 2
+        grads = self.parts[self.left // half]
+        start = (side * half + self.left % half) * self.size
+        return jnp.concatenate([g[start : start + self.size] for g in grads], axis=1)
 
     def move(self):
         return self.ring.back(self.now[0]), self.ring.ahead(self.now[1])
 
     def take(self, moved):
         self.left -= 1
-        sums = [m.astype(f32) + self.block(half).astype(f32) for half, m in enumerate(moved)]
+        sums = [m.astype(f32) + self.block(side).astype(f32) for side, m in enumerate(moved)]
         self.now = tuple(sums if self.left == 0 else [v.astype(bf16) for v in sums])
 
 
-def turn(lane, other=None, values=()):
-    moved, _, values = together((lane.move(), other.now if other else (), values))
+class Held:
+    def __init__(self, *value):
+        self.value = value if len(value) > 1 else value[0]
+
+
+def turn(lane, other=None, values=(), held=()):
+    moved, _, held = together((lane.move(), other.now if other else (), held))
+    values = together((values, moved))[0]
     lane.take(moved)
-    return values
+    return values, held
 
 
 class Stages:
@@ -127,12 +144,17 @@
             except StopIteration as end:
                 self.result, self.over, self.value = end.value, True, ()
 
-    def turn(self, lane, other=None):
-        self.advance(turn(lane, other, self.value))
+    def turn(self, lane, other=None, extra=()):
+        if isinstance(self.value, Held):
+            extra, value = turn(lane, other, extra, self.value.value)
+        else:
+            (value, extra), _ = turn(lane, other, (self.value, extra))
+        self.advance(value)
+        return extra
 
     def finish(self):
         while not self.over:
-            self.advance(self.value)
+            self.advance(self.value.value if isinstance(self.value, Held) else self.value)
         return self.result
 
 
@@ -213,9 +235,17 @@
     order = jnp.array(ring_order(chips), dtype=jnp.int32)
     from_low = 2 * order[(here - numbers) % chips]
     from_high = 2 * order[(here + numbers) % chips] + 1
-    to_relative = jnp.concatenate([from_low, from_high])
+    half = chips // 2
+    to_relative = jnp.concatenate(
+        [from_low[half:], from_high[half:], from_low[:half], from_high[:half]]
+    )
+    behind, before = (here - place) % chips, (place - here) % chips
     to_natural = jnp.stack(
-        [(here - place) % chips, chips + (place - here) % chips], axis=1
+        [
+            jnp.where(behind < half, behind + 2 * half, behind - half),
+            jnp.where(before < half, before + 3 * half, before),
+        ],
+        axis=1,
     ).reshape(devices)
 
     def split_cores(w):
@@ -332,30 +362,46 @@
         stages.finish()
     )
     up_proj = jnp.concatenate(up_weights.rows(), axis=0)
-    down_proj_t = jnp.concatenate(down_weights.rows(), axis=0)
+    down_far, down_near = down_weights.far(), down_weights.near()
     own_teacher = reorder(teacher, to_relative)
+    count = jnp.sum(lengths).astype(f32)
 
     up = jnp.dot(normed_mlp, up_proj, preferred_element_type=f32)
     sigmoid_gate = jax.nn.sigmoid(gate)
     hidden = (gate * sigmoid_gate * up).astype(bf16)
-    result = middle + scatter_group(
-        ring, lax.dot_general(hidden, down_proj_t, over_last, preferred_element_type=f32)
-    )
-    error = (result - own_teacher.astype(f32)) * own_valid
-    count = jnp.sum(lengths).astype(f32)
-    delta_result = error * (tokens_all / count)
-    branch = gather_group(ring, delta_result.astype(bf16))
-    grad_down_t = lax.dot_general(branch, hidden, over_rows, preferred_element_type=f32)
-    down_sums = Scatter(ring, [grad_down_t.astype(bf16)], piece)
+    cut = width // 2
+
+    def output(proj_t, columns, before=()):
+        parts = lax.dot_general(hidden, proj_t, over_last, preferred_element_type=f32)
+        shared = together((scatter_group(ring, parts), before))[0]
+        result = middle[:, columns] + shared
+        error = (result - own_teacher[:, columns].astype(f32)) * own_valid
+        delta = error * (tokens_all / count)
+        return result, error, delta, gather_group(ring, delta.astype(bf16))
+
+    def down_grad_of(branch):
+        return lax.dot_general(branch, hidden, over_rows, preferred_element_type=f32).astype(bf16)
+
+    result_far, error_far, delta_far, branch_far = output(down_far, slice(0, cut))
+    result_near, error_near, delta_near, branch_near = output(down_near, slice(cut, width), delta_far)
+    down_sums = Scatter(ring, [down_grad_of(branch_far)], [down_grad_of(branch_near)], piece)
+    result = jnp.concatenate([result_far, result_near], axis=1)
+    delta_result = jnp.concatenate([delta_far, delta_near], axis=1)
+    squared = jnp.sum(error_far * error_far) + jnp.sum(error_near * error_near)
 
     def backward():
         activations = reorder(result.astype(bf16), to_natural)
-        delta_hidden = jnp.dot(branch, down_proj_t, preferred_element_type=f32)
+        delta_hidden = jnp.dot(branch_far, down_far, preferred_element_type=f32) + jnp.dot(
+            branch_near, down_near, preferred_element_type=f32
+        )
         delta_gate = (
             delta_hidden * up * sigmoid_gate * (1.0 + gate * (1.0 - sigmoid_gate))
         ).astype(bf16)
         delta_up = (delta_hidden * gate * sigmoid_gate).astype(bf16)
-        activations, delta_gate, delta_up = yield activations, delta_gate, delta_up
+        activations, delta_gate, delta_up, near = (
+            yield activations, delta_gate, delta_up, down_sums.parts[0]
+        )
+        down_sums.parts = (near, down_sums.parts[1])
         grad_gate = lax.dot_general(
             normed_mlp, delta_gate, over_rows, preferred_element_type=f32
         ).astype(bf16)
@@ -366,15 +412,13 @@
         grad_up, delta_up = yield grad_up, delta_up
         gate_up.append(grad_gate)
         gate_up.append(grad_up)
-        from_gate = lax.dot_general(delta_gate, gate_proj, over_last, preferred_element_type=f32)
-        from_gate, delta_up = yield from_gate, delta_up
-        parts = from_gate + lax.dot_general(
-            delta_up, up_proj, over_last, preferred_element_type=f32
-        )
+        parts = lax.dot_general(
+            delta_gate, gate_proj, over_last, preferred_element_type=f32
+        ) + lax.dot_general(delta_up, up_proj, over_last, preferred_element_type=f32)
         parts = yield parts
         delta_normed_mlp = scatter_group(ring, parts)
         yield ()
-        delta_normed_mlp = yield delta_normed_mlp
+        delta_normed_mlp = yield Held(delta_normed_mlp)
         gain_mlp_part = jnp.sum(delta_normed_mlp * middle * mlp_scale, axis=0)
         weighted_mlp = mlp_gain * delta_normed_mlp
         delta_middle = (
@@ -384,14 +428,14 @@
         )
         attn_low_rows = gather_group(ring, delta_middle.astype(bf16))
         yield ()
-        attn_low_rows = yield attn_low_rows
+        attn_low_rows = yield Held(attn_low_rows)
         grad_out_t = lax.dot_general(attn_low_rows, mixed, over_rows, preferred_element_type=f32)
         delta_mixed = (
             jnp.dot(attn_low_rows, out_proj_t, preferred_element_type=f32)
             .astype(bf16)
             .reshape(2, slots, query_heads, HEAD_SIZE)
         )
-        grad_out_t, delta_mixed = yield grad_out_t.astype(bf16), delta_mixed
+        grad_out_t, delta_mixed = yield Held(grad_out_t.astype(bf16), delta_mixed)
         probs_low = probs.astype(bf16)
         delta_probs = jnp.einsum("bigd,bjd->bgij", delta_mixed, values, preferred_element_type=f32)
         inner = jnp.sum(probs * delta_probs, axis=-1, keepdims=True)
@@ -399,7 +443,7 @@
         delta_values = jnp.einsum(
             "bgij,bigd->bjd", probs_low, delta_mixed, preferred_element_type=f32
         )
-        delta_scores, delta_values = yield delta_scores, delta_values
+        delta_scores, delta_values = yield Held(delta_scores, delta_values)
         delta_qrot = (
             jnp.einsum("bgij,bjd->bigd", delta_scores, rot_keys, preferred_element_type=f32)
             * scaling
@@ -428,19 +472,6 @@
             [grad_qkv.astype(bf16), grad_out_t],
         )
 
-    gate_up = []
-    stages = Stages(backward())
-    for k in range(3):
-        stages.turn(down_sums)
-    gate_up_sums = Scatter(ring, gate_up, piece)
-    for k in range(hops):
-        stages.turn(gate_up_sums, down_sums)
-        if down_sums.left:
-            stages.turn(down_sums, gate_up_sums)
-    activations, gain_mlp_part, delta_middle, delta_qkv, attn_grads = stages.finish()
-    attn_sums = Scatter(ring, attn_grads, piece)
-    squared = jnp.sum(error * error)
-
     def finish(sums):
         low, high = sums.now
         kept = jnp.where(first_core, low, high)
@@ -452,17 +483,31 @@
             [jnp.where(first_core, kept, taken), jnp.where(first_core, taken, kept)], axis=1
         )
 
+    def halves(grads):
+        return [g[: width // 2] for g in grads], [g[width // 2 :] for g in grads]
+
+    gate_up = []
+    stages = Stages(backward())
+    for k in range(3):
+        stages.turn(down_sums)
+    gate_up_sums = Scatter(ring, *halves(gate_up), piece)
+    while down_sums.left:
+        if gate_up_sums.left:
+            stages.turn(gate_up_sums, down_sums)
+        stages.turn(down_sums, gate_up_sums)
+    down_grad = whole(*finish(down_sums)).T
+    while not stages.over and gate_up_sums.left:
+        down_grad = stages.turn(gate_up_sums, None, down_grad)
+    assert stages.over
+    activations, gain_mlp_part, delta_middle, delta_qkv, attn_grads = stages.finish()
+    attn_sums = Scatter(ring, *halves(attn_grads), piece)
+
     def closing():
         delta_normed = scatter_group(
             ring, lax.dot_general(delta_qkv, qkv_proj, over_last, preferred_element_type=f32)
         )
-        down_grad = whole(*finish(down_sums)).T
-        down_grad = yield down_grad
-        kept, taken = finish(gate_up_sums)
-        gate_width = w_gate.shape[1] // 2
-        gate_grad = whole(kept[:, :gate_width], taken[:, :gate_width])
-        up_grad = whole(kept[:, gate_width:], taken[:, gate_width:])
-        gate_grad, up_grad, delta_normed = yield gate_grad, up_grad, delta_normed
+        yield ()
+        delta_normed = yield delta_normed
         gain_attn_part = jnp.sum(delta_normed * own_rows * attn_scale, axis=0)
         weighted_attn = attn_gain * delta_normed
         input_grad = (
@@ -479,12 +524,20 @@
         )
         input_grad, sums = yield input_grad, sums
         totals = yield sum_all(ring, sums)
-        return down_grad, gate_grad, up_grad, input_grad, totals
+        return input_grad, totals
 
     stages = Stages(closing())
-    for k in range(hops):
-        stages.turn(attn_sums)
-    down_grad, gate_grad, up_grad, input_grad, totals = stages.finish()
+    while gate_up_sums.left:
+        down_grad = stages.turn(gate_up_sums, attn_sums, down_grad)
+        stages.turn(attn_sums, gate_up_sums)
+    kept, taken = finish(gate_up_sums)
+    gate_width = w_gate.shape[1] // 2
+    gate_grad = whole(kept[:, :gate_width], taken[:, :gate_width])
+    up_grad = whole(kept[:, gate_width:], taken[:, gate_width:])
+    stages.turn(attn_sums)
+    while attn_sums.left:
+        gate_grad, up_grad = stages.turn(attn_sums, None, (gate_grad, up_grad))
+    input_grad, totals = stages.finish()
     gain_mlp_grad = lax.dynamic_slice_in_dim(totals, me, 1, 0)[0]
     gain_attn_grad = lax.dynamic_slice_in_dim(totals, devices + me, 1, 0)[0]
     distill_loss = totals[2 * devices, 0] / (2.0 * width * count)

time: 989 us -> 933 us (0.943)
  waiting for transfers between devices: 398 us -> 361 us
  other arithmetic: 138 us -> 110 us
    ppermute x49, waiting for transfers between devices: 192 us -> 157 us  [ahead(): return lax.ppermute(v, 'dp', self.up)]
    ppermute x49, waiting for transfers between devices: 82.7 us -> 115 us  [back(): return lax.ppermute(v, 'dp', self.down)]
    ppermute x9 -> x11, waiting for transfers between devices: 111 us -> 80.9 us  [other_tensor(): return lax.ppermute(v, 'tensor', [(0, 1), (1, 0)])]
    convert_element_type x30, other arithmetic: 42.4 us -> 27.7 us  [take(): self.now = tuple(sums if self.left == 0 else [v.astype(bf16) for v in sums])]
    add x1 -> x0, other arithmetic: 11.7 us -> none  [backward(): from_gate + lax.dot_general(delta_up, up_proj, over_last, preferred_eleme...]
    dot_general x3 -> x6, matrix products: 41.9 us -> 50.3 us  [the longest x2 16.9 us: down_grad_of(): lax.dot_general(branch, hidden, over_rows, preferred_element_type=f32)]
    slice x21 -> x23, local copies, waits for them, and re-layouts: 19.3 us -> 26.7 us  [the longest x21 26.6 us: block(): return jnp.concatenate([g[start:start + self.size] for g in grads], axis=1)]
    unnamed x400 -> x383, local copies, waits for them, and re-layouts: 82.6 us -> 82.6 us
  transfers between devices with their start and end apart: 130 -> 135, of which waited for: 72 -> 76; matrix products, arithmetic and copies ran while one was open for 34% -> 37% of each run, Pallas kernels for 2% -> 2%
where the time goes in v3:
time: 933 us; the launch traced here: 924 us
  waiting for transfers between devices  361 us (39%)
  matrix products  163 us (17%)
  local copies, waits for them, and re-layouts  144 us (15%)
  starting transfers between devices  122 us (13%)
  other arithmetic  110 us (12%)
  Pallas kernels  16.7 us (2%)
    ppermute x49, waiting for transfers between devices, ahead(): return lax.ppermute(v, 'dp', self.up)  157 us
    ppermute x49, waiting for transfers between devices, back(): return lax.ppermute(v, 'dp', self.down)  115 us
    unnamed x383, local copies, waits for them, and re-layouts  82.6 us
    ppermute x11, waiting for transfers between devices, other_tensor(): return lax.ppermute(v, 'tensor', [(0, 1), (1, 0)])  80.9 us
    ppermute x49, starting transfers between devices, ahead(): return lax.ppermute(v, 'dp', self.up)  61.8 us
    ppermute x49, starting transfers between devices, back(): return lax.ppermute(v, 'dp', self.down)  42.8 us
    convert_element_type x30, other arithmetic, take(): self.now = tuple(sums if self.left == 0 else [v.astype(bf16) for v in sums])  27.7 us
    slice x21, local copies, waits for them, and re-layouts, block(): return jnp.concatenate([g[start:start + self.size] for g in grads], axis=1)  26.6 us
  transfers between devices with their start and end apart: 135, of which 76 were waited for; matrix products, arithmetic and copies ran while one was open for 37% of the time, Pallas kernels for 2%

profile of v3, /device:TPU:0, one launch (start us, length us, event | category | flops | bytes accessed | tf_op | source)
XLA Modules:
  0.0 924.2 jit_solution(6328245141507670485)
XLA Ops:
  83.4 10.4 %collective-permute-done.12 = bf16[144,1536]{1,0:T(8,128)(2,1)S(1)} collective-permute-done((bf16[144,1536]{1,0:T(8,128)(2,1)}, bf16[144,1536]{1,0:T(8,128)(2,1)S(1)}, u32[]{:S(2)}, u32[]{:S(2)}) %collective-permute-start.12) | collective-permute-done | bytes 442400 | tf_op jit(solution)/shard_map/ppermute | solution.py:58
  242.7 8.4 fusion.9
  273.7 7.8 collective-permute-done.47
  296.2 7.8 collective-permute-done.58
  318.7 7.8 collective-permute-done.60
  370.8 9.4 %collective-permute-done.51 = bf16[256,2048]{1,0:T(8,128)(2,1)S(1)} collective-permute-done((bf16[256,2048]{1,0:T(8,128)(2,1)S(1)}, bf16[256,2048]{1,0:T(8,128)(2,1)S(1)}, u32[]{:S(2)}, u32[]{:S(2)}) %collective-permute-start.51) | collective-permute-done | bytes 1048608 | tf_op jit(solution)/shard_map/ppermute | solution.py:65
  384.2 11.1 %fusion.105 = f32[1024,2048]{1,0:T(8,128)} fusion(bf16[1024,2048]{1,0:T(8,128)(2,1)S(1)} %pad_maximum_fusion.1, bf16[2048,2048]{1,0:T(8,128)(2,1)S(1)} %bitcast.169), kind=kOutput, calls=%fused_computation.423 | convolution fusion | flops 8589934592 | bytes 20971520 | tf_op jit(solution)/shard_map/dot_general | solution.py:353
  395.3 15.3 %multiply_convert_fusion.2 = (bf16[1024,2048]{1,0:T(8,128)(2,1)S(1)}, f32[1024,2048]{1,0:T(8,128)}) fusion(f32[1024,2048]{1,0:T(8,128)} %fusion.105, bf16[1024,2048]{1,0:T(8,128)(2,1)S(1)} %pad_maximum_fusion.1, bf16[2048,2048]{1,0:T(8,128)(2,1)} %constant_dynamic-update-slice_fusion.48), kind=kOutput, calls=%fused_computation.13 | convolution fusion | flops 8602517504 | bytes 33554432 | tf_op jit(solution)/shard_map/dot_general | solution.py:369
  436.1 12.3 %collective-permute-done.69 = bf16[256,1024]{1,0:T(8,128)(2,1)S(1)} collective-permute-done((bf16[256,1024]{1,0:T(8,128)(2,1)S(1)}, bf16[256,1024]{1,0:T(8,128)(2,1)S(1)}, u32[]{:S(2)}, u32[]{:S(2)}) %collective-permute-start.69) | collective-permute-done | bytes 524320 | tf_op jit(solution)/shard_map/ppermute | solution.py:65
  450.2 9.5 %collective-permute-done.71 = bf16[256,1024]{1,0:T(8,128)(2,1)S(1)} collective-permute-done((bf16[256,1024]{1,0:T(8,128)(2,1)S(1)}, bf16[256,1024]{1,0:T(8,128)(2,1)S(1)}, u32[]{:S(2)}, u32[]{:S(2)}) %collective-permute-start.71) | collective-permute-done | bytes 524320 | tf_op jit(solution)/shard_map/ppermute | solution.py:65
  462.9 8.1 collective-permute-done.72
  492.3 8.3 fusion.56
  500.7 16.0 %multiply_convert_fusion = (bf16[1024,2048]{1,0:T(8,128)(2,1)}, bf16[1024,2048]{1,0:T(8,128)(2,1)}) fusion(f32[1024,2048]{1,0:T(8,128)} %fusion.105, f32[1024,2048]{1,0:T(8,128)} %get-tuple-element.526, f32[1024,2048]{1,0:T(8,128)} %fusion.56, bf16[1024,2048]{1,0:T(8,128)(2,1)} %copy-done.118, bf16[256,1024]{1,0:T(8,128)(2,1)} %collective-permute-done.74, ...), kind=kOutput, calls=%fused_computation.11 | convolution fusion | flops 4332716032 | bytes 39845888 | tf_op jit(solution)/shard_map/dot_general | solution.py:394
  516.7 9.5 %convolution_convert_fusion.4 = bf16[1024,2048]{1,0:T(8,128)(2,1)} fusion(bf16[1024,2048]{1,0:T(8,128)(2,1)} %copy-done.135, bf16[256,1024]{1,0:T(8,128)(2,1)} %copy-done.134, bf16[256,1024]{1,0:T(8,128)(2,1)} %collective-permute-done.76, bf16[256,1024]{1,0:T(8,128)(2,1)} %collective-permute-done.75, bf16[256,1024]{1,0:T(8,128)(2,1)} %get-tuple-element.408), kind=kOutput, calls=%fused_computation.41 | convolution fusion | flops 4305453056 | bytes 10485760 | tf_op jit(solution)/shard_map/dot_general | solution.py:383
  527.3 10.2 %convolution_convert_fusion = bf16[2048,2048]{1,0:T(8,128)(2,1)S(1)} fusion(bf16[1024,2048]{1,0:T(8,128)(2,1)S(1)} %copy-done.23, bf16[1024,2048]{1,0:T(8,128)(2,1)S(1)} %copy-done.136), kind=kOutput, calls=%fused_computation.15 | convolution fusion | flops 8594128896 | bytes 16777216 | tf_op jit(solution)/shard_map/dot_general | solution.py:409
  539.6 11.0 %convolution_convert_fusion.1 = bf16[2048,2048]{1,0:T(8,128)(2,1)S(1)} fusion(bf16[1024,2048]{1,0:T(8,128)(2,1)S(1)} %copy-done.23, bf16[1024,2048]{1,0:T(8,128)(2,1)} %get-tuple-element.241), kind=kOutput, calls=%fused_computation.16 | convolution fusion | flops 8594128896 | bytes 16777216 | tf_op jit(solution)/shard_map/dot_general | solution.py:405
  557.2 7.7 collective-permute-done.82
  573.1 13.5 %fusion.108 = f32[1024,2048]{1,0:T(8,128)} fusion(bf16[1024,2048]{1,0:T(8,128)(2,1)S(1)} %copy-done.137, bf16[2048,2048]{1,0:T(8,128)(2,1)} %constant_dynamic-update-slice_fusion.48), kind=kOutput, calls=%fused_computation.426 | convolution fusion | flops 8589934592 | bytes 20971520 | tf_op jit(solution)/shard_map/dot_general | solution.py:417
  586.5 13.8 %convolution_add_fusion.1 = f32[1024,2048]{1,0:T(8,128)S(1)} fusion(f32[1024,2048]{1,0:T(8,128)} %fusion.108, bf16[1024,2048]{1,0:T(8,128)(2,1)} %get-tuple-element.241, bf16[2048,2048]{1,0:T(8,128)(2,1)} %constant_dynamic-update-slice_fusion.32), kind=kOutput, calls=%fused_computation.38 | convolution fusion | flops 8592031744 | bytes 29360128 | tf_op jit(solution)/shard_map/dot_general | solution.py:415
  623.7 15.3 %collective-permute-done.91 = bf16[256,2048]{1,0:T(8,128)(2,1)S(1)} collective-permute-done((bf16[256,2048]{1,0:T(8,128)(2,1)S(1)}, bf16[256,2048]{1,0:T(8,128)(2,1)S(1)}, u32[]{:S(2)}, u32[]{:S(2)}) %collective-permute-start.91) | collective-permute-done | bytes 1048608 | tf_op jit(solution)/shard_map/ppermute | solution.py:65
  651.0 20.5 %collective-permute-done.96 = bf16[256,2048]{1,0:T(8,128)(2,1)} collective-permute-done((bf16[256,2048]{1,0:T(8,128)(2,1)}, bf16[256,2048]{1,0:T(8,128)(2,1)}, u32[]{:S(2)}, u32[]{:S(2)}) %collective-permute-start.96) | collective-permute-done | bytes 1048608 | tf_op jit(solution)/shard_map/ppermute | solution.py:65
  684.1 15.8 %collective-permute-done.93 = bf16[128,4096]{1,0:T(8,128)(2,1)S(1)} collective-permute-done((bf16[128,4096]{1,0:T(8,128)(2,1)}, bf16[128,4096]{1,0:T(8,128)(2,1)S(1)}, u32[]{:S(2)}, u32[]{:S(2)}) %collective-permute-start.93) | collective-permute-done | bytes 1048608 | tf_op jit(solution)/shard_map/ppermute | solution.py:55
  793.1 17.1 %collective-permute-done.112 = bf16[128,4096]{1,0:T(8,128)(2,1)S(1)} collective-permute-done((bf16[128,4096]{1,0:T(8,128)(2,1)S(1)}, bf16[128,4096]{1,0:T(8,128)(2,1)S(1)}, u32[]{:S(2)}, u32[]{:S(2)}) %collective-permute-start.112) | collective-permute-done | bytes 1048608 | tf_op jit(solution)/shard_map/ppermute | solution.py:58
  845.2 16.8 %collective-permute-done.123 = bf16[128,4096]{1,0:T(8,128)(2,1)S(1)} collective-permute-done((bf16[128,4096]{1,0:T(8,128)(2,1)S(1)}, bf16[128,4096]{1,0:T(8,128)(2,1)S(1)}, u32[]{:S(2)}, u32[]{:S(2)}) %collective-permute-start.123) | collective-permute-done | bytes 1048608 | tf_op jit(solution)/shard_map/ppermute | solution.py:58
  (849 shorter events, 633.6 us)
Async XLA Ops:
  33.0 35.6 %collective-permute-start.31 = (bf16[128,2048]{1,0:T(8,128)(2,1)}, bf16[128,2048]{1,0:T(8,128)(2,1)}, u32[]{:S(2)}, u32[]{:S(2)}) collective-permute-start(bf16[128,2048]{1,0:T(8,128)(2,1)} %constant_dynamic-slice_fusion.4), channel_id=1, source_target_pairs={{0,2},{2,0},{4,6},{6,4},{8,10},{10,8},{12,14},{14,12},{16,18},{18,... | collective-permute-start | bytes 1572872 | tf_op jit(solution)/shard_map/ppermute | solution.py:61
  58.1 39.2 %collective-permute-start.1 = (bf16[256,2048]{1,0:T(8,128)(2,1)S(1)}, bf16[256,2048]{1,0:T(8,128)(2,1)S(1)}, u32[]{:S(2)}, u32[]{:S(2)}) collective-permute-start(bf16[256,2048]{1,0:T(8,128)(2,1)S(1)} %copy-done.1), channel_id=1, source_target_pairs={{0,2},{2,0},{4,6},{6,4},{8,10},{10,8},{12,14},{14,12},{16,18},{18,... | collective-permute-start | bytes 3145736 | tf_op jit(solution)/shard_map/ppermute | solution.py:61
  63.8 34.0 %collective-permute-start.2 = (bf16[256,2048]{1,0:T(8,128)(2,1)S(1)}, bf16[256,2048]{1,0:T(8,128)(2,1)}, u32[]{:S(2)}, u32[]{:S(2)}) collective-permute-start(bf16[256,2048]{1,0:T(8,128)(2,1)S(1)} %collective-permute-done), channel_id=1, source_target_pairs={{0,2},{2,0},{4,6},{6,4},{8,10},{10,8},{12,14},{14,12},{16,18},{18,... | collective-permute-start | bytes 3145736 | tf_op jit(solution)/shard_map/ppermute | solution.py:61
  161.0 32.3 %collective-permute-start.35 = (bf16[128,2048]{1,0:T(8,128)(2,1)S(1)}, bf16[128,2048]{1,0:T(8,128)(2,1)S(1)}, u32[]{:S(2)}, u32[]{:S(2)}) collective-permute-start(bf16[128,2048]{1,0:T(8,128)(2,1)S(1)} %collective-permute-done.29), channel_id=1, source_target_pairs={{0,8},{2,10},{8,16},{10,18},{16,24},{18,26},{24,28},{26,30},{28,20... | collective-permute-start | bytes 1572872 | tf_op jit(solution)/shard_map/ppermute | solution.py:55
  194.3 41.3 %collective-permute-start.37 = (bf16[128,2048]{1,0:T(8,128)(2,1)}, bf16[128,2048]{1,0:T(8,128)(2,1)}, u32[]{:S(2)}, u32[]{:S(2)}) collective-permute-start(bf16[128,2048]{1,0:T(8,128)(2,1)} %get-tuple-element.185), channel_id=1, source_target_pairs={{0,8},{2,10},{8,16},{10,18},{16,24},{18,26},{24,28},{26,30},{28,20... | collective-permute-start | bytes 1572872 | tf_op jit(solution)/shard_map/ppermute | solution.py:55
  195.8 39.8 %collective-permute-start.38 = (bf16[128,2048]{1,0:T(8,128)(2,1)}, bf16[128,2048]{1,0:T(8,128)(2,1)}, u32[]{:S(2)}, u32[]{:S(2)}) collective-permute-start(bf16[128,2048]{1,0:T(8,128)(2,1)} %get-tuple-element.186), channel_id=1, source_target_pairs={{8,0},{10,2},{16,8},{18,10},{24,16},{26,18},{28,24},{30,26},{20,28... | collective-permute-start | bytes 1572872 | tf_op jit(solution)/shard_map/ppermute | solution.py:58
  196.3 41.3 %collective-permute-start.39 = (bf16[128,2048]{1,0:T(8,128)(2,1)}, bf16[128,2048]{1,0:T(8,128)(2,1)}, u32[]{:S(2)}, u32[]{:S(2)}) collective-permute-start(bf16[128,2048]{1,0:T(8,128)(2,1)} %collective-permute-done.32), channel_id=1, source_target_pairs={{0,8},{2,10},{8,16},{10,18},{16,24},{18,26},{24,28},{26,30},{28,20... | collective-permute-start | bytes 1572872 | tf_op jit(solution)/shard_map/ppermute | solution.py:55
  197.9 39.8 %collective-permute-start.40 = (bf16[128,2048]{1,0:T(8,128)(2,1)}, bf16[128,2048]{1,0:T(8,128)(2,1)}, u32[]{:S(2)}, u32[]{:S(2)}) collective-permute-start(bf16[128,2048]{1,0:T(8,128)(2,1)} %collective-permute-done.33), channel_id=1, source_target_pairs={{8,0},{10,2},{16,8},{18,10},{24,16},{26,18},{28,24},{30,26},{20,28... | collective-permute-start | bytes 1572872 | tf_op jit(solution)/shard_map/ppermute | solution.py:58
  268.0 62.8 %collective-permute-start.43 = (bf16[512,2048]{1,0:T(8,128)(2,1)S(1)}, bf16[512,2048]{1,0:T(8,128)(2,1)S(1)}, u32[]{:S(2)}, u32[]{:S(2)}) collective-permute-start(bf16[512,2048]{1,0:T(8,128)(2,1)S(1)} %slice.1043), channel_id=1, source_target_pairs={{0,2},{2,0},{4,6},{6,4},{8,10},{10,8},{12,14},{14,12},{16,18},{18,... | collective-permute-start | bytes 6291464 | tf_op jit(solution)/shard_map/ppermute | solution.py:61
  490.3 35.9 %collective-permute-start.78 = (bf16[128,2048]{1,0:T(8,128)(2,1)}, bf16[128,2048]{1,0:T(8,128)(2,1)S(1)}, u32[]{:S(2)}, u32[]{:S(2)}) collective-permute-start(bf16[128,2048]{1,0:T(8,128)(2,1)} %get-tuple-element.445), channel_id=1, source_target_pairs={{8,0},{10,2},{16,8},{18,10},{24,16},{26,18},{28,24},{30,26},{20,28... | collective-permute-start | bytes 1572872 | tf_op jit(solution)/shard_map/ppermute | solution.py:58
  490.8 35.4 %collective-permute-start.79 = (bf16[128,2048]{1,0:T(8,128)(2,1)S(1)}, bf16[128,2048]{1,0:T(8,128)(2,1)S(1)}, u32[]{:S(2)}, u32[]{:S(2)}) collective-permute-start(bf16[128,2048]{1,0:T(8,128)(2,1)S(1)} %get-tuple-element.444), channel_id=1, source_target_pairs={{0,8},{2,10},{8,16},{10,18},{16,24},{18,26},{24,28},{26,30},{28,20... | collective-permute-start | bytes 1572872 | tf_op jit(solution)/shard_map/ppermute | solution.py:55
  570.0 33.8 %collective-permute-start.84 = (bf16[128,4096]{1,0:T(8,128)(2,1)}, bf16[128,4096]{1,0:T(8,128)(2,1)}, u32[]{:S(2)}, u32[]{:S(2)}) collective-permute-start(bf16[128,4096]{1,0:T(8,128)(2,1)} %pad_maximum_fusion.10), channel_id=1, source_target_pairs={{8,0},{10,2},{16,8},{18,10},{24,16},{26,18},{28,24},{30,26},{20,28... | collective-permute-start | bytes 3145736 | tf_op jit(solution)/shard_map/ppermute | solution.py:58
  609.6 33.2 %collective-permute-start.86 = (bf16[128,4096]{1,0:T(8,128)(2,1)S(1)}, bf16[128,4096]{1,0:T(8,128)(2,1)S(1)}, u32[]{:S(2)}, u32[]{:S(2)}) collective-permute-start(bf16[128,4096]{1,0:T(8,128)(2,1)S(1)} %add_convert_fusion.11), channel_id=1, source_target_pairs={{8,0},{10,2},{16,8},{18,10},{24,16},{26,18},{28,24},{30,26},{20,28... | collective-permute-start | bytes 3145736 | tf_op jit(solution)/shard_map/ppermute | solution.py:58
  650.4 33.7 %collective-permute-start.92 = (bf16[128,4096]{1,0:T(8,128)(2,1)S(1)}, bf16[128,4096]{1,0:T(8,128)(2,1)S(1)}, u32[]{:S(2)}, u32[]{:S(2)}) collective-permute-start(bf16[128,4096]{1,0:T(8,128)(2,1)S(1)} %add_convert_fusion.9), channel_id=1, source_target_pairs={{8,0},{10,2},{16,8},{18,10},{24,16},{26,18},{28,24},{30,26},{20,28... | collective-permute-start | bytes 3145736 | tf_op jit(solution)/shard_map/ppermute | solution.py:58
  679.3 36.8 %collective-permute-start.101 = (bf16[128,2048]{1,0:T(8,128)(2,1)}, bf16[128,2048]{1,0:T(8,128)(2,1)}, u32[]{:S(2)}, u32[]{:S(2)}) collective-permute-start(bf16[128,2048]{1,0:T(8,128)(2,1)} %get-tuple-element.435), channel_id=1, source_target_pairs={{8,0},{10,2},{16,8},{18,10},{24,16},{26,18},{28,24},{30,26},{20,28... | collective-permute-start | bytes 1572872 | tf_op jit(solution)/shard_map/ppermute | solution.py:58
  679.9 36.2 %collective-permute-start.102 = (bf16[128,2048]{1,0:T(8,128)(2,1)}, bf16[128,2048]{1,0:T(8,128)(2,1)}, u32[]{:S(2)}, u32[]{:S(2)}) collective-permute-start(bf16[128,2048]{1,0:T(8,128)(2,1)} %get-tuple-element.434), channel_id=1, source_target_pairs={{0,8},{2,10},{8,16},{10,18},{16,24},{18,26},{24,28},{26,30},{28,20... | collective-permute-start | bytes 1572872 | tf_op jit(solution)/shard_map/ppermute | solution.py:55
  702.1 41.5 %collective-permute-start.99 = (bf16[128,4096]{1,0:T(8,128)(2,1)}, bf16[128,4096]{1,0:T(8,128)(2,1)S(1)}, u32[]{:S(2)}, u32[]{:S(2)}) collective-permute-start(bf16[128,4096]{1,0:T(8,128)(2,1)} %add_convert_fusion.7), channel_id=1, source_target_pairs={{8,0},{10,2},{16,8},{18,10},{24,16},{26,18},{28,24},{30,26},{20,28... | collective-permute-start | bytes 3145736 | tf_op jit(solution)/shard_map/ppermute | solution.py:58
  705.1 38.5 %collective-permute-start.100 = (bf16[128,4096]{1,0:T(8,128)(2,1)}, bf16[128,4096]{1,0:T(8,128)(2,1)}, u32[]{:S(2)}, u32[]{:S(2)}) collective-permute-start(bf16[128,4096]{1,0:T(8,128)(2,1)} %add_convert_fusion.6), channel_id=1, source_target_pairs={{0,8},{2,10},{8,16},{10,18},{16,24},{18,26},{24,28},{26,30},{28,20... | collective-permute-start | bytes 3145736 | tf_op jit(solution)/shard_map/ppermute | solution.py:55
  719.0 39.1 %collective-permute-start.103 = (bf16[128,2048]{1,0:T(8,128)(2,1)}, bf16[128,2048]{1,0:T(8,128)(2,1)}, u32[]{:S(2)}, u32[]{:S(2)}) collective-permute-start(bf16[128,2048]{1,0:T(8,128)(2,1)} %get-tuple-element.433), channel_id=1, source_target_pairs={{8,0},{10,2},{16,8},{18,10},{24,16},{26,18},{28,24},{30,26},{20,28... | collective-permute-start | bytes 1572872 | tf_op jit(solution)/shard_map/ppermute | solution.py:58
  719.6 38.5 %collective-permute-start.104 = (bf16[128,2048]{1,0:T(8,128)(2,1)}, bf16[128,2048]{1,0:T(8,128)(2,1)}, u32[]{:S(2)}, u32[]{:S(2)}) collective-permute-start(bf16[128,2048]{1,0:T(8,128)(2,1)} %get-tuple-element.432), channel_id=1, source_target_pairs={{0,8},{2,10},{8,16},{10,18},{16,24},{18,26},{24,28},{26,30},{28,20... | collective-permute-start | bytes 1572872 | tf_op jit(solution)/shard_map/ppermute | solution.py:55
  763.3 57.7 %collective-permute-start.105 = (bf16[512,2048]{1,0:T(8,128)(2,1)S(1)}, bf16[512,2048]{1,0:T(8,128)(2,1)S(1)}, u32[]{:S(2)}, u32[]{:S(2)}) collective-permute-start(bf16[512,2048]{1,0:T(8,128)(2,1)S(1)} %slice.1041), channel_id=1, source_target_pairs={{0,2},{2,0},{4,6},{6,4},{8,10},{10,8},{12,14},{14,12},{16,18},{18,... | collective-permute-start | bytes 6291464 | tf_op jit(solution)/shard_map/ppermute | solution.py:61
  872.9 42.5 %collective-permute-start.134 = (bf16[128,4096]{1,0:T(8,128)(2,1)}, bf16[128,4096]{1,0:T(8,128)(2,1)S(1)}, u32[]{:S(2)}, u32[]{:S(2)}) collective-permute-start(bf16[128,4096]{1,0:T(8,128)(2,1)} %get-tuple-element.415), channel_id=1, source_target_pairs={{0,2},{2,0},{4,6},{6,4},{8,10},{10,8},{12,14},{14,12},{16,18},{18,... | collective-permute-start | bytes 3145736 | tf_op jit(solution)/shard_map/ppermute | solution.py:61
  878.6 35.2 %collective-permute-start.131 = (bf16[128,1536]{0,1:T(8,128)(2,1)}, bf16[128,1536]{0,1:T(8,128)(2,1)}, u32[]{:S(2)}, u32[]{:S(2)}) collective-permute-start(bf16[128,1536]{0,1:T(8,128)(2,1)} %add_convert_fusion.27), channel_id=1, source_target_pairs={{8,0},{10,2},{16,8},{18,10},{24,16},{26,18},{28,24},{30,26},{20,28... | collective-permute-start | bytes 1179656 | tf_op jit(solution)/shard_map/ppermute | solution.py:58
  881.5 32.3 %collective-permute-start.132 = (bf16[128,1536]{0,1:T(8,128)(2,1)}, bf16[128,1536]{0,1:T(8,128)(2,1)}, u32[]{:S(2)}, u32[]{:S(2)}) collective-permute-start(bf16[128,1536]{0,1:T(8,128)(2,1)} %add_convert_fusion.26), channel_id=1, source_target_pairs={{0,8},{2,10},{8,16},{10,18},{16,24},{18,26},{24,28},{26,30},{28,20... | collective-permute-start | bytes 1179656 | tf_op jit(solution)/shard_map/ppermute | solution.py:55
  (252 other events, 4930.8 us)

commit v4 on v3

--- a/solution.py
+++ b/solution.py
@@ -70,35 +70,55 @@
 
 
 class Gather:
-    def __init__(self, ring, low, high):
-        self.ring = ring
+    def __init__(self, ring, low, high, rows, cuts=None, split=False, below=0):
+        self.ring, self.size, self.split, self.below = ring, rows, split, below
         self.now = (low, high)
-        self.lows, self.highs = [low], [high]
+        self.cuts = cuts or [(0, low.shape[1])]
+        height = 2 * ring.chips * rows
+        if split:
+            self.buffers = [jnp.zeros((height // 2, low.shape[1]), bf16)] * 2
+        else:
+            self.buffers = [jnp.zeros((height, b - a), bf16) for a, b in self.cuts]
+        if below:
+            self.buffers.append(jnp.zeros((below, height), bf16))
+        self.hops = 0
+        self.store()
+
+    def store(self):
+        half = self.ring.chips // 2
+        k, self.hops = self.hops, self.hops + 1
+        for side, rows in enumerate(self.now):
+            at = k + (side - 1) * half if k >= half else k + (side + 2) * half
+            if self.split:
+                which = int(k < half)
+                start = (at - which * 2 * half) * self.size
+                self.buffers[which] = lax.dynamic_update_slice(
+                    self.buffers[which], rows[: self.size], (start, 0)
+                )
+                continue
+            for i, (a, b) in enumerate(self.cuts):
+                self.buffers[i] = lax.dynamic_update_slice(
+                    self.buffers[i], rows[: self.size, a:b], (at * self.size, 0)
+                )
+            if self.below:
+                self.buffers[-1] = lax.dynamic_update_slice(
+                    self.buffers[-1],
+                    rows[self.size : self.size + self.below, : self.size],
+                    (0, at * self.size),
+                )
 
     def move(self):
         return self.ring.ahead(self.now[0]), self.ring.back(self.now[1])
 
     def take(self, moved):
         self.now = moved
-        self.lows.append(moved[0])
-        self.highs.append(moved[1])
-
-    def far(self):
-        half = self.ring.chips // 2
-        return jnp.concatenate(self.lows[half:] + self.highs[half:], axis=0)
-
-    def near(self):
-        half = self.ring.chips // 2
-        return jnp.concatenate(self.lows[:half] + self.highs[:half], axis=0)
-
-    def rows(self):
-        half = self.ring.chips // 2
-        return self.lows[half:] + self.highs[half:] + self.lows[:half] + self.highs[:half]
+        self.store()
 
 
 class Scatter:
     def __init__(self, ring, far, near, rows):
         self.ring, self.parts, self.size = ring, (near, far), rows
+        self.buffers = []
         self.left = ring.chips - 1
         self.now = (self.block(0), self.block(1))
 
@@ -123,9 +143,11 @@
 
 
 def turn(lane, other=None, values=(), held=()):
-    moved, _, held = together((lane.move(), other.now if other else (), held))
-    values = together((values, moved))[0]
+    moved, _, held, lane.buffers = together(
+        (lane.move(), other.now if other else (), held, lane.buffers)
+    )
     lane.take(moved)
+    values, held, _ = together((values, held, lane.now))
     return values, held
 
 
@@ -164,9 +186,10 @@
     return jnp.concatenate([rows, across, beside, ring.other_core(across)], axis=0)
 
 
-def scatter_group(ring, parts):
+def scatter_group(ring, parts, before=()):
     quarter = parts.shape[0] // 4
     near = parts[: 2 * quarter] + ring.other_core(parts[2 * quarter :].astype(bf16)).astype(f32)
+    near = together((near, before))[0]
     return near[:quarter] + other_tensor(near[quarter:].astype(bf16)).astype(f32)
 
 
@@ -269,18 +292,27 @@
 
     gains = jnp.stack([gain_attn, gain_mlp])
     hops = ring.chips - 1
+    q_width = w_query.shape[1] // 2
+    kv_width = key_projection_weight.shape[1] // 2
+    qkv_width = q_width + 2 * kv_width
+    out_width = w_out.shape[0] // 2
     attn_weights = Gather(
         ring,
         *both_rows([w_query, key_projection_weight, value_projection_weight, w_out.T], gains),
-    )
-    gate_weights = Gather(ring, *both_rows([w_gate]))
+        piece,
+        [(0, qkv_width), (qkv_width, qkv_width + out_width)],
+        below=16,
+    )
+    gate_weights = Gather(ring, *both_rows([w_gate]), piece)
     own_input = reorder(layer_input, to_relative)
     group_rows = gather_group(ring, own_input)
     for k in range(hops):
         turn(attn_weights, gate_weights)
         turn(gate_weights, attn_weights)
-    up_weights = Gather(ring, *together((both_rows([w_up]), attn_weights.now))[0])
-    down_weights = Gather(ring, *together((both_rows([w_down.T]), gate_weights.now))[0])
+    up_weights = Gather(ring, *together((both_rows([w_up]), attn_weights.now))[0], piece)
+    down_weights = Gather(
+        ring, *together((both_rows([w_down.T]), gate_weights.now))[0], piece, split=True
+    )
 
     sequence_numbers = jnp.stack([me, me + 1 - 2 * core])
     length = jnp.sum(
@@ -299,32 +331,27 @@
     cosine, sine = rope_tables(position, HEAD_SIZE)
     cosine, sine = cosine[:, :, None, :], sine[:, :, None, :]
     scaling = HEAD_SIZE ** (-0.5)
-    q_width = w_query.shape[1] // 2
-    kv_width = key_projection_weight.shape[1] // 2
-    qkv_width = q_width + 2 * kv_width
     query_heads = q_width // HEAD_SIZE
     all_rows = 2 * slots
     own_rows = own_input.astype(f32)
     attn_scale = rms_scale(own_rows)
 
-    pieces = attn_weights.rows()
-    qkv_proj = jnp.concatenate([p[:piece, :qkv_width] for p in pieces], axis=0)
-    out_proj_t = jnp.concatenate([p[:piece, qkv_width:] for p in pieces], axis=0)
-    gain_rows = jnp.concatenate([p[piece : piece + 2, :piece] for p in pieces], axis=1).astype(f32)
+    qkv_proj, out_proj_t, gain_rows = attn_weights.buffers
+    gain_rows = gain_rows[:2].astype(f32)
     attn_gain, mlp_gain = gain_rows[:1], gain_rows[1:]
-    gate_proj = jnp.concatenate(gate_weights.rows(), axis=0)
+    gate_proj = gate_weights.buffers[0]
 
     def forward():
         group_input = group_rows.astype(f32)
         normed = (group_input * rms_scale(group_input) * attn_gain).astype(bf16)
         qkv = jnp.dot(normed, qkv_proj, preferred_element_type=f32)
-        normed, qkv = yield normed, qkv
+        normed, qkv = yield Held(normed, qkv)
         query_rows = qkv[:, :q_width].reshape(2, slots, query_heads, HEAD_SIZE)
         key_rows = qkv[:, q_width : q_width + kv_width].reshape(2, slots, 1, HEAD_SIZE)
         values = qkv[:, q_width + kv_width :].astype(bf16).reshape(2, slots, HEAD_SIZE)
         rot_queries = rotate(query_rows, cosine, sine).astype(bf16)
         rot_keys = rotate(key_rows, cosine, sine).astype(bf16)[:, :, 0]
-        rot_queries, rot_keys, values = yield rot_queries, rot_keys, values
+        rot_queries, rot_keys, values = yield Held(rot_queries, rot_keys, values)
         scores = (
             jnp.einsum("bigd,bjd->bgij", rot_queries, rot_keys, preferred_element_type=f32)
             * scaling
@@ -332,38 +359,41 @@
         scores = jnp.where(allowed, scores, -1e30)
         shifted = jnp.exp(scores - jnp.max(scores, axis=-1, keepdims=True))
         probs = shifted / jnp.sum(shifted, axis=-1, keepdims=True)
-        probs = yield probs
+        probs = yield Held(probs)
         mixed = (
             jnp.einsum("bgij,bjd->bigd", probs.astype(bf16), values, preferred_element_type=f32)
             .reshape(all_rows, q_width)
             .astype(bf16)
         )
         parts = lax.dot_general(mixed, out_proj_t, over_last, preferred_element_type=f32)
-        mixed, parts = yield mixed, parts
+        mixed, parts = yield Held(mixed, parts)
         shared = scatter_group(ring, parts)
+        own_teacher = yield Held(reorder(teacher, to_relative))
         yield ()
-        yield ()
-        shared = yield shared
+        shared = yield Held(shared)
         middle = own_rows + shared
         mlp_scale = rms_scale(middle)
         normed_mlp = gather_group(ring, (middle * mlp_scale * mlp_gain).astype(bf16))
         yield ()
         yield ()
-        normed_mlp = yield normed_mlp
+        normed_mlp = yield Held(normed_mlp)
         gate = jnp.dot(normed_mlp, gate_proj, preferred_element_type=f32)
-        gate = yield gate
-        return normed, rot_queries, rot_keys, values, probs, mixed, middle, mlp_scale, normed_mlp, gate
+        gate = yield Held(gate)
+        return (
+            own_teacher,
+            (normed, rot_queries, rot_keys, values, probs, mixed),
+            (middle, mlp_scale, normed_mlp, gate),
+        )
 
     stages = Stages(forward())
     for k in range(hops):
         stages.turn(up_weights, down_weights)
         stages.turn(down_weights, up_weights)
-    (normed, rot_queries, rot_keys, values, probs, mixed, middle, mlp_scale, normed_mlp, gate) = (
-        stages.finish()
-    )
-    up_proj = jnp.concatenate(up_weights.rows(), axis=0)
-    down_far, down_near = down_weights.far(), down_weights.near()
-    own_teacher = reorder(teacher, to_relative)
+    own_teacher, attn_kept, mlp_kept = stages.finish()
+    normed, rot_queries, rot_keys, values, probs, mixed = attn_kept
+    middle, mlp_scale, normed_mlp, gate = mlp_kept
+    up_proj = up_weights.buffers[0]
+    down_far, down_near = down_weights.buffers
     count = jnp.sum(lengths).astype(f32)
 
     up = jnp.dot(normed_mlp, up_proj, preferred_element_type=f32)
@@ -373,8 +403,7 @@
 
     def output(proj_t, columns, before=()):
         parts = lax.dot_general(hidden, proj_t, over_last, preferred_element_type=f32)
-        shared = together((scatter_group(ring, parts), before))[0]
-        result = middle[:, columns] + shared
+        result = middle[:, columns] + scatter_group(ring, parts, before)
         error = (result - own_teacher[:, columns].astype(f32)) * own_valid
         delta = error * (tokens_all / count)
         return result, error, delta, gather_group(ring, delta.astype(bf16))
@@ -384,40 +413,39 @@
 
     result_far, error_far, delta_far, branch_far = output(down_far, slice(0, cut))
     result_near, error_near, delta_near, branch_near = output(down_near, slice(cut, width), delta_far)
-    down_sums = Scatter(ring, [down_grad_of(branch_far)], [down_grad_of(branch_near)], piece)
+    down_sums = Scatter(ring, [down_grad_of(branch_far)], None, piece)
     result = jnp.concatenate([result_far, result_near], axis=1)
     delta_result = jnp.concatenate([delta_far, delta_near], axis=1)
     squared = jnp.sum(error_far * error_far) + jnp.sum(error_near * error_near)
 
     def backward():
-        activations = reorder(result.astype(bf16), to_natural)
-        delta_hidden = jnp.dot(branch_far, down_far, preferred_element_type=f32) + jnp.dot(
-            branch_near, down_near, preferred_element_type=f32
-        )
+        first = jnp.dot(branch_far, down_far, preferred_element_type=f32)
+        first = yield Held(first)
+        delta_hidden = first + jnp.dot(branch_near, down_near, preferred_element_type=f32)
         delta_gate = (
             delta_hidden * up * sigmoid_gate * (1.0 + gate * (1.0 - sigmoid_gate))
         ).astype(bf16)
         delta_up = (delta_hidden * gate * sigmoid_gate).astype(bf16)
-        activations, delta_gate, delta_up, near = (
-            yield activations, delta_gate, delta_up, down_sums.parts[0]
-        )
-        down_sums.parts = (near, down_sums.parts[1])
+        delta_gate, delta_up = yield Held(delta_gate, delta_up)
+        near = yield Held(down_grad_of(branch_near))
+        down_sums.parts = ([near], down_sums.parts[1])
         grad_gate = lax.dot_general(
             normed_mlp, delta_gate, over_rows, preferred_element_type=f32
         ).astype(bf16)
-        grad_gate, delta_gate = yield grad_gate, delta_gate
+        grad_gate = yield Held(grad_gate)
         grad_up = lax.dot_general(
             normed_mlp, delta_up, over_rows, preferred_element_type=f32
         ).astype(bf16)
-        grad_up, delta_up = yield grad_up, delta_up
+        grad_up = yield Held(grad_up)
         gate_up.append(grad_gate)
         gate_up.append(grad_up)
         parts = lax.dot_general(
             delta_gate, gate_proj, over_last, preferred_element_type=f32
         ) + lax.dot_general(delta_up, up_proj, over_last, preferred_element_type=f32)
-        parts = yield parts
+        parts = yield Held(parts)
         delta_normed_mlp = scatter_group(ring, parts)
-        yield ()
+        placed = together((result.astype(bf16), parts))[0]
+        activations = yield Held(reorder(placed, to_natural))
         delta_normed_mlp = yield Held(delta_normed_mlp)
         gain_mlp_part = jnp.sum(delta_normed_mlp * middle * mlp_scale, axis=0)
         weighted_mlp = mlp_gain * delta_normed_mlp
@@ -435,7 +463,7 @@
             .astype(bf16)
             .reshape(2, slots, query_heads, HEAD_SIZE)
         )
-        grad_out_t, delta_mixed = yield Held(grad_out_t.astype(bf16), delta_mixed)
+        grad_out_t = grad_out_t.astype(bf16)
         probs_low = probs.astype(bf16)
         delta_probs = jnp.einsum("bigd,bjd->bgij", delta_mixed, values, preferred_element_type=f32)
         inner = jnp.sum(probs * delta_probs, axis=-1, keepdims=True)
@@ -443,7 +471,7 @@
         delta_values = jnp.einsum(
             "bgij,bigd->bjd", probs_low, delta_mixed, preferred_element_type=f32
         )
-        delta_scores, delta_values = yield Held(delta_scores, delta_values)
+        grad_out_t, delta_scores, delta_values = yield Held(grad_out_t, delta_scores, delta_values)
         delta_qrot = (
             jnp.einsum("bgij,bjd->bigd", delta_scores, rot_keys, preferred_element_type=f32)
             * scaling
@@ -462,14 +490,14 @@
             ],
             axis=1,
         )
-        delta_qkv = yield delta_qkv
+        delta_qkv = yield Held(delta_qkv)
         grad_qkv = lax.dot_general(normed, delta_qkv, over_rows, preferred_element_type=f32)
         return (
             activations,
             gain_mlp_part,
             delta_middle,
             delta_qkv,
-            [grad_qkv.astype(bf16), grad_out_t],
+            [jnp.concatenate([grad_qkv.astype(bf16), grad_out_t], axis=1)],
         )
 
     def finish(sums):
@@ -488,7 +516,7 @@
 
     gate_up = []
     stages = Stages(backward())
-    for k in range(3):
+    for k in range(5):
         stages.turn(down_sums)
     gate_up_sums = Scatter(ring, *halves(gate_up), piece)
     while down_sums.left:

time: 933 us -> 930 us (level)
  waiting for transfers between devices: 361 us -> 344 us
  other arithmetic: 110 us -> 123 us
    dynamic_update_slice x0 -> x95, local copies, waits for them, and re-layouts: none -> 59.2 us  [the longest x63 37.1 us: store(): lax.dynamic_update_slice(self.buffers[i], rows[:self.size, a:b], (at * se...]
    unnamed x383 -> x252, local copies, waits for them, and re-layouts: 82.6 us -> 30.1 us
    ppermute x49, waiting for transfers between devices: 157 us -> 127 us  [ahead(): return lax.ppermute(v, 'dp', self.up)]
    ppermute x49, waiting for transfers between devices: 115 us -> 142 us  [back(): return lax.ppermute(v, 'dp', self.down)]
    slice x21 -> x3, local copies, waits for them, and re-layouts: 26.6 us -> 6.21 us  [block(): return jnp.concatenate([g[start:start + self.size] for g in grads], axis=1)]
    convert_element_type x30 -> x24, other arithmetic: 27.7 us -> 29.5 us  [take(): self.now = tuple(sums if self.left == 0 else [v.astype(bf16) for v in sums])]
  transfers between devices with their start and end apart: 135 -> 135, of which waited for: 76 -> 75; matrix products, arithmetic and copies ran while one was open for 37% -> 39% of each run, Pallas kernels for 2% -> 1%
where the time goes in v4:
time: 930 us; the launch traced here: 919 us
  waiting for transfers between devices  344 us (37%)
  matrix products  166 us (18%)
  local copies, waits for them, and re-layouts  140 us (15%)
  other arithmetic  123 us (13%)
  starting transfers between devices  122 us (13%)
  Pallas kernels  16.5 us (2%)
    ppermute x49, waiting for transfers between devices, back(): return lax.ppermute(v, 'dp', self.down)  142 us
    ppermute x49, waiting for transfers between devices, ahead(): return lax.ppermute(v, 'dp', self.up)  127 us
    ppermute x11, waiting for transfers between devices, other_tensor(): return lax.ppermute(v, 'tensor', [(0, 1), (1, 0)])  73 us
    ppermute x49, starting transfers between devices, ahead(): return lax.ppermute(v, 'dp', self.up)  61.7 us
    ppermute x49, starting transfers between devices, back(): return lax.ppermute(v, 'dp', self.down)  44 us
    dynamic_update_slice x63, local copies, waits for them, and re-layouts, store(): lax.dynamic_update_slice(self.buffers[i], rows[:self.size, a:b], (at * se...  37.1 us
    unnamed x252, local copies, waits for them, and re-layouts  30.1 us
    convert_element_type x24, other arithmetic, take(): self.now = tuple(sums if self.left == 0 else [v.astype(bf16) for v in sums])  29.5 us
  transfers between devices with their start and end apart: 135, of which 75 were waited for; matrix products, arithmetic and copies ran while one was open for 39% of the time, Pallas kernels for 1%

profile of v4, /device:TPU:0, one launch (start us, length us, event | category | flops | bytes accessed | tf_op | source)
XLA Modules:
  0.0 919.3 jit_solution(3308625735115086501)
XLA Ops:
  68.4 7.5 collective-permute-done.6
  184.6 7.1 fusion.5
  250.6 8.3 fusion.9
  296.9 7.5 collective-permute-done.47
  327.2 7.8 collective-permute-done.53
  350.3 7.2 collective-permute-done.57
  363.1 11.1 %fusion.118 = f32[1024,2048]{1,0:T(8,128)} fusion(bf16[1024,2048]{1,0:T(8,128)(2,1)S(1)} %pad_maximum_fusion.1, bf16[2048,2048]{1,0:T(8,128)(2,1)S(1)} %constant_dynamic-update-slice_fusion.12), kind=kOutput, calls=%fused_computation.456 | convolution fusion | flops 8589934592 | bytes 20971520 | tf_op jit(solution)/shard_map/dot_general | solution.py:380
  394.8 15.4 %multiply_convert_fusion.2 = (bf16[1024,2048]{1,0:T(8,128)(2,1)}, f32[1024,2048]{1,0:T(8,128)}) fusion(f32[1024,2048]{1,0:T(8,128)} %fusion.118, bf16[1024,2048]{1,0:T(8,128)(2,1)S(1)} %pad_maximum_fusion.1, bf16[2048,2048]{1,0:T(8,128)(2,1)S(1)} %constant_dynamic-update-slice_fusion.4), kind=kOutput, calls=%fused_computation.43 | convolution fusion | flops 8602517504 | bytes 33554432 | tf_op jit(solution)/shard_map/dot_general | solution.py:399
  435.5 11.9 %collective-permute-done.69 = bf16[256,1024]{1,0:T(8,128)(2,1)S(1)} collective-permute-done((bf16[256,1024]{1,0:T(8,128)(2,1)S(1)}, bf16[256,1024]{1,0:T(8,128)(2,1)S(1)}, u32[]{:S(2)}, u32[]{:S(2)}) %collective-permute-start.69) | collective-permute-done | bytes 524320 | tf_op jit(solution)/shard_map/ppermute | solution.py:65
  451.8 12.6 %collective-permute-done.70 = bf16[256,1024]{1,0:T(8,128)(2,1)S(1)} collective-permute-done((bf16[256,1024]{1,0:T(8,128)(2,1)S(1)}, bf16[256,1024]{1,0:T(8,128)(2,1)S(1)}, u32[]{:S(2)}, u32[]{:S(2)}) %collective-permute-start.70) | collective-permute-done | bytes 524320 | tf_op jit(solution)/shard_map/ppermute | solution.py:65
  464.4 9.4 %collective-permute-done.78 = bf16[256,1024]{1,0:T(8,128)(2,1)S(1)} collective-permute-done((bf16[256,1024]{1,0:T(8,128)(2,1)S(1)}, bf16[256,1024]{1,0:T(8,128)(2,1)S(1)}, u32[]{:S(2)}, u32[]{:S(2)}) %collective-permute-start.78) | collective-permute-done | bytes 524320 | tf_op jit(solution)/shard_map/ppermute | solution.py:65
  488.4 8.6 fusion.71
  502.2 16.4 %multiply_convert_fusion = (bf16[1024,2048]{1,0:T(8,128)(2,1)}, bf16[1024,2048]{1,0:T(8,128)(2,1)}) fusion(f32[1024,2048]{1,0:T(8,128)} %fusion.118, f32[1024,2048]{1,0:T(8,128)} %get-tuple-element.667, f32[1024,2048]{1,0:T(8,128)} %fusion.71, bf16[1024,2048]{1,0:T(8,128)(2,1)} %constant_dynamic-update-slice_fusion.18, bf16[256,1024]{1,0:T(8,128)(2,1)} %copy-done.111, ...), kind=kOutput, calls=%fused_computation.41 | convolution fusion | flops 4332716032 | bytes 39845888 | tf_op jit(solution)/shard_map/dot_general | solution.py:424
  518.6 7.4 convolution_convert_fusion.3
  530.9 9.9 %convolution_convert_fusion.1 = bf16[2048,2048]{1,0:T(8,128)(2,1)S(1)} fusion(bf16[1024,2048]{1,0:T(8,128)(2,1)S(1)} %copy-done.35, bf16[1024,2048]{1,0:T(8,128)(2,1)S(1)} %copy-done.114), kind=kOutput, calls=%fused_computation.46 | convolution fusion | flops 8594128896 | bytes 16777216 | tf_op jit(solution)/shard_map/dot_general | solution.py:432
  540.8 12.0 %convolution_convert_fusion = bf16[2048,2048]{1,0:T(8,128)(2,1)S(1)} fusion(bf16[1024,2048]{1,0:T(8,128)(2,1)} %copy-done.34, bf16[1024,2048]{1,0:T(8,128)(2,1)} %get-tuple-element.381), kind=kOutput, calls=%fused_computation.45 | convolution fusion | flops 8594128896 | bytes 16777216 | tf_op jit(solution)/shard_map/dot_general | solution.py:436
  557.1 14.6 %fusion.121 = f32[1024,2048]{1,0:T(8,128)} fusion(bf16[1024,2048]{1,0:T(8,128)(2,1)} %get-tuple-element.381, bf16[2048,2048]{1,0:T(8,128)(2,1)} %copy-done.13), kind=kOutput, calls=%fused_computation.459 | convolution fusion | flops 8589934592 | bytes 20971520 | tf_op jit(solution)/shard_map/dot_general | solution.py:444
  594.6 13.9 %convolution_add_fusion.1 = f32[1024,2048]{1,0:T(8,128)} fusion(f32[1024,2048]{1,0:T(8,128)} %fusion.121, bf16[1024,2048]{1,0:T(8,128)(2,1)} %get-tuple-element.376, bf16[2048,2048]{1,0:T(8,128)(2,1)S(1)} %bitcast.149), kind=kOutput, calls=%fused_computation.68 | convolution fusion | flops 8592031744 | bytes 29360128 | tf_op jit(solution)/shard_map/dot_general | solution.py:442
  645.6 9.8 %collective-permute-done.95 = bf16[256,2048]{1,0:T(8,128)(2,1)} collective-permute-done((bf16[256,2048]{1,0:T(8,128)(2,1)}, bf16[256,2048]{1,0:T(8,128)(2,1)}, u32[]{:S(2)}, u32[]{:S(2)}) %collective-permute-start.95) | collective-permute-done | bytes 1048608 | tf_op jit(solution)/shard_map/ppermute | solution.py:65
  680.8 13.2 %collective-permute-done.101 = bf16[256,2048]{1,0:T(8,128)(2,1)S(1)} collective-permute-done((bf16[256,2048]{1,0:T(8,128)(2,1)}, bf16[256,2048]{1,0:T(8,128)(2,1)S(1)}, u32[]{:S(2)}, u32[]{:S(2)}) %collective-permute-start.101) | collective-permute-done | bytes 1048608 | tf_op jit(solution)/shard_map/ppermute | solution.py:65
  724.9 16.7 %collective-permute-done.105 = bf16[128,4096]{1,0:T(8,128)(2,1)S(1)} collective-permute-done((bf16[128,4096]{1,0:T(8,128)(2,1)S(1)}, bf16[128,4096]{1,0:T(8,128)(2,1)S(1)}, u32[]{:S(2)}, u32[]{:S(2)}) %collective-permute-start.105) | collective-permute-done | bytes 1048608 | tf_op jit(solution)/shard_map/ppermute | solution.py:55
  781.6 15.2 %collective-permute-done.113 = bf16[128,4096]{1,0:T(8,128)(2,1)S(1)} collective-permute-done((bf16[128,4096]{1,0:T(8,128)(2,1)S(1)}, bf16[128,4096]{1,0:T(8,128)(2,1)S(1)}, u32[]{:S(2)}, u32[]{:S(2)}) %collective-permute-start.113) | collective-permute-done | bytes 1048608 | tf_op jit(solution)/shard_map/ppermute | solution.py:55
  809.8 17.8 %collective-permute-done.115 = bf16[128,4096]{1,0:T(8,128)(2,1)S(1)} collective-permute-done((bf16[128,4096]{1,0:T(8,128)(2,1)S(1)}, bf16[128,4096]{1,0:T(8,128)(2,1)S(1)}, u32[]{:S(2)}, u32[]{:S(2)}) %collective-permute-start.115) | collective-permute-done | bytes 1048608 | tf_op jit(solution)/shard_map/ppermute | solution.py:55
  887.2 8.3 collective-permute-done.129
  (790 shorter events, 642.5 us)
Async XLA Ops:
  10.2 54.7 %collective-permute-start.34 = (bf16[256,2048]{1,0:T(8,128)(2,1)}, bf16[256,2048]{1,0:T(8,128)(2,1)S(1)}, u32[]{:S(2)}, u32[]{:S(2)}) collective-permute-start(bf16[256,2048]{1,0:T(8,128)(2,1)} %reorder.4), channel_id=1, source_target_pairs={{0,1},{1,0},{2,3},{3,2},{4,5},{5,4},{6,7},{7,6},{8,9},{9,8},{10,11... | collective-permute-start | bytes 3145736 | tf_op jit(solution)/shard_map/ppermute | solution.py:65
  13.2 98.3 %collective-permute-start.35 = (bf16[256,2048]{1,0:T(8,128)(2,1)}, bf16[256,2048]{1,0:T(8,128)(2,1)S(1)}, u32[]{:S(2)}, u32[]{:S(2)}) collective-permute-start(bf16[256,2048]{1,0:T(8,128)(2,1)} %reorder.4), channel_id=1, source_target_pairs={{0,2},{2,0},{4,6},{6,4},{8,10},{10,8},{12,14},{14,12},{16,18},{18,... | collective-permute-start | bytes 3145736 | tf_op jit(solution)/shard_map/ppermute | solution.py:61
  68.4 43.7 %collective-permute-start.36 = (bf16[256,2048]{1,0:T(8,128)(2,1)S(1)}, bf16[256,2048]{1,0:T(8,128)(2,1)S(1)}, u32[]{:S(2)}, u32[]{:S(2)}) collective-permute-start(bf16[256,2048]{1,0:T(8,128)(2,1)S(1)} %collective-permute-done.34), channel_id=1, source_target_pairs={{0,2},{2,0},{4,6},{6,4},{8,10},{10,8},{12,14},{14,12},{16,18},{18,... | collective-permute-start | bytes 3145736 | tf_op jit(solution)/shard_map/ppermute | solution.py:61
  172.2 35.2 %collective-permute-start.32 = (bf16[128,2048]{1,0:T(8,128)(2,1)}, bf16[128,2048]{1,0:T(8,128)(2,1)}, u32[]{:S(2)}, u32[]{:S(2)}) collective-permute-start(bf16[128,2048]{1,0:T(8,128)(2,1)} %collective-permute-done.27), channel_id=1, source_target_pairs={{0,8},{2,10},{8,16},{10,18},{16,24},{18,26},{24,28},{26,30},{28,20... | collective-permute-start | bytes 1572872 | tf_op jit(solution)/shard_map/ppermute | solution.py:55
  173.7 33.7 %collective-permute-start.33 = (bf16[128,2048]{1,0:T(8,128)(2,1)}, bf16[128,2048]{1,0:T(8,128)(2,1)}, u32[]{:S(2)}, u32[]{:S(2)}) collective-permute-start(bf16[128,2048]{1,0:T(8,128)(2,1)} %collective-permute-done.28), channel_id=1, source_target_pairs={{8,0},{10,2},{16,8},{18,10},{24,16},{26,18},{28,24},{30,26},{20,28... | collective-permute-start | bytes 1572872 | tf_op jit(solution)/shard_map/ppermute | solution.py:58
  181.7 31.4 %collective-permute-start.29 = (bf16[128,2048]{1,0:T(8,128)(2,1)}, bf16[128,2048]{1,0:T(8,128)(2,1)}, u32[]{:S(2)}, u32[]{:S(2)}) collective-permute-start(bf16[128,2048]{1,0:T(8,128)(2,1)} %get-tuple-element.283), channel_id=1, source_target_pairs={{0,8},{2,10},{8,16},{10,18},{16,24},{18,26},{24,28},{26,30},{28,20... | collective-permute-start | bytes 1572872 | tf_op jit(solution)/shard_map/ppermute | solution.py:55
  183.3 29.8 %collective-permute-start.30 = (bf16[128,2048]{1,0:T(8,128)(2,1)}, bf16[128,2048]{1,0:T(8,128)(2,1)}, u32[]{:S(2)}, u32[]{:S(2)}) collective-permute-start(bf16[128,2048]{1,0:T(8,128)(2,1)} %get-tuple-element.284), channel_id=1, source_target_pairs={{8,0},{10,2},{16,8},{18,10},{24,16},{26,18},{28,24},{30,26},{20,28... | collective-permute-start | bytes 1572872 | tf_op jit(solution)/shard_map/ppermute | solution.py:58
  213.4 30.2 %collective-permute-start.39 = (bf16[128,2048]{1,0:T(8,128)(2,1)}, bf16[128,2048]{1,0:T(8,128)(2,1)}, u32[]{:S(2)}, u32[]{:S(2)}) collective-permute-start(bf16[128,2048]{1,0:T(8,128)(2,1)} %get-tuple-element.288), channel_id=1, source_target_pairs={{0,8},{2,10},{8,16},{10,18},{16,24},{18,26},{24,28},{26,30},{28,20... | collective-permute-start | bytes 1572872 | tf_op jit(solution)/shard_map/ppermute | solution.py:55
  215.0 28.6 %collective-permute-start.40 = (bf16[128,2048]{1,0:T(8,128)(2,1)}, bf16[128,2048]{1,0:T(8,128)(2,1)}, u32[]{:S(2)}, u32[]{:S(2)}) collective-permute-start(bf16[128,2048]{1,0:T(8,128)(2,1)} %get-tuple-element.289), channel_id=1, source_target_pairs={{8,0},{10,2},{16,8},{18,10},{24,16},{26,18},{28,24},{30,26},{20,28... | collective-permute-start | bytes 1572872 | tf_op jit(solution)/shard_map/ppermute | solution.py:58
  215.5 43.5 %collective-permute-start.37 = (bf16[128,2048]{1,0:T(8,128)(2,1)}, bf16[128,2048]{1,0:T(8,128)(2,1)}, u32[]{:S(2)}, u32[]{:S(2)}) collective-permute-start(bf16[128,2048]{1,0:T(8,128)(2,1)} %collective-permute-done.29), channel_id=1, source_target_pairs={{0,8},{2,10},{8,16},{10,18},{16,24},{18,26},{24,28},{26,30},{28,20... | collective-permute-start | bytes 1572872 | tf_op jit(solution)/shard_map/ppermute | solution.py:55
  217.0 41.9 %collective-permute-start.38 = (bf16[128,2048]{1,0:T(8,128)(2,1)}, bf16[128,2048]{1,0:T(8,128)(2,1)}, u32[]{:S(2)}, u32[]{:S(2)}) collective-permute-start(bf16[128,2048]{1,0:T(8,128)(2,1)} %collective-permute-done.30), channel_id=1, source_target_pairs={{8,0},{10,2},{16,8},{18,10},{24,16},{26,18},{28,24},{30,26},{20,28... | collective-permute-start | bytes 1572872 | tf_op jit(solution)/shard_map/ppermute | solution.py:58
  346.7 27.6 %collective-permute-start.55 = (bf16[128,2048]{1,0:T(8,128)(2,1)S(1)}, bf16[128,2048]{1,0:T(8,128)(2,1)S(1)}, u32[]{:S(2)}, u32[]{:S(2)}) collective-permute-start(bf16[128,2048]{1,0:T(8,128)(2,1)S(1)} %collective-permute-done.51), channel_id=1, source_target_pairs={{0,8},{2,10},{8,16},{10,18},{16,24},{18,26},{24,28},{26,30},{28,20... | collective-permute-start | bytes 1572872 | tf_op jit(solution)/shard_map/ppermute | solution.py:55
  383.6 29.2 %collective-permute-start.66 = (bf16[128,2048]{1,0:T(8,128)(2,1)}, bf16[128,2048]{1,0:T(8,128)(2,1)S(1)}, u32[]{:S(2)}, u32[]{:S(2)}) collective-permute-start(bf16[128,2048]{1,0:T(8,128)(2,1)} %collective-permute-done.64), channel_id=1, source_target_pairs={{0,8},{2,10},{8,16},{10,18},{16,24},{18,26},{24,28},{26,30},{28,20... | collective-permute-start | bytes 1572872 | tf_op jit(solution)/shard_map/ppermute | solution.py:55
  385.2 27.6 %collective-permute-start.67 = (bf16[128,2048]{1,0:T(8,128)(2,1)}, bf16[128,2048]{1,0:T(8,128)(2,1)S(1)}, u32[]{:S(2)}, u32[]{:S(2)}) collective-permute-start(bf16[128,2048]{1,0:T(8,128)(2,1)} %collective-permute-done.65), channel_id=1, source_target_pairs={{8,0},{10,2},{16,8},{18,10},{24,16},{26,18},{28,24},{30,26},{20,28... | collective-permute-start | bytes 1572872 | tf_op jit(solution)/shard_map/ppermute | solution.py:58
  499.2 26.8 %collective-permute-start.75 = (bf16[128,2048]{1,0:T(8,128)(2,1)}, bf16[128,2048]{1,0:T(8,128)(2,1)S(1)}, u32[]{:S(2)}, u32[]{:S(2)}) collective-permute-start(bf16[128,2048]{1,0:T(8,128)(2,1)} %get-tuple-element.605), channel_id=1, source_target_pairs={{8,0},{10,2},{16,8},{18,10},{24,16},{26,18},{28,24},{30,26},{20,28... | collective-permute-start | bytes 1572872 | tf_op jit(solution)/shard_map/ppermute | solution.py:58
  643.6 29.5 %collective-permute-start.96 = (bf16[128,2048]{1,0:T(8,128)(2,1)S(1)}, bf16[128,2048]{1,0:T(8,128)(2,1)S(1)}, u32[]{:S(2)}, u32[]{:S(2)}) collective-permute-start(bf16[128,2048]{1,0:T(8,128)(2,1)S(1)} %get-tuple-element.595), channel_id=1, source_target_pairs={{8,0},{10,2},{16,8},{18,10},{24,16},{26,18},{28,24},{30,26},{20,28... | collective-permute-start | bytes 1572872 | tf_op jit(solution)/shard_map/ppermute | solution.py:58
  644.1 29.0 %collective-permute-start.97 = (bf16[128,2048]{1,0:T(8,128)(2,1)S(1)}, bf16[128,2048]{1,0:T(8,128)(2,1)S(1)}, u32[]{:S(2)}, u32[]{:S(2)}) collective-permute-start(bf16[128,2048]{1,0:T(8,128)(2,1)S(1)} %get-tuple-element.594), channel_id=1, source_target_pairs={{0,8},{2,10},{8,16},{10,18},{16,24},{18,26},{24,28},{26,30},{28,20... | collective-permute-start | bytes 1572872 | tf_op jit(solution)/shard_map/ppermute | solution.py:55
  779.5 28.0 %collective-permute-start.110 = (bf16[128,1536]{0,1:T(8,128)(2,1)S(1)}, bf16[128,1536]{0,1:T(8,128)(2,1)S(1)}, u32[]{:S(2)}, u32[]{:S(2)}) collective-permute-start(bf16[128,1536]{0,1:T(8,128)(2,1)S(1)} %get-tuple-element.585), channel_id=1, source_target_pairs={{8,0},{10,2},{16,8},{18,10},{24,16},{26,18},{28,24},{30,26},{20,28... | collective-permute-start | bytes 1179656 | tf_op jit(solution)/shard_map/ppermute | solution.py:58
  780.7 26.9 %collective-permute-start.111 = (bf16[128,1536]{0,1:T(8,128)(2,1)S(1)}, bf16[128,1536]{0,1:T(8,128)(2,1)S(1)}, u32[]{:S(2)}, u32[]{:S(2)}) collective-permute-start(bf16[128,1536]{0,1:T(8,128)(2,1)S(1)} %get-tuple-element.584), channel_id=1, source_target_pairs={{0,8},{2,10},{8,16},{10,18},{16,24},{18,26},{24,28},{26,30},{28,20... | collective-permute-start | bytes 1179656 | tf_op jit(solution)/shard_map/ppermute | solution.py:55
  799.4 28.2 %collective-permute-start.115 = (bf16[128,4096]{1,0:T(8,128)(2,1)S(1)}, bf16[128,4096]{1,0:T(8,128)(2,1)S(1)}, u32[]{:S(2)}, u32[]{:S(2)}) collective-permute-start(bf16[128,4096]{1,0:T(8,128)(2,1)S(1)} %add_convert_fusion), channel_id=1, source_target_pairs={{0,8},{2,10},{8,16},{10,18},{16,24},{18,26},{24,28},{26,30},{28,20... | collective-permute-start | bytes 3145736 | tf_op jit(solution)/shard_map/ppermute | solution.py:55
  800.1 30.0 %collective-permute-start.114 = (bf16[128,4096]{1,0:T(8,128)(2,1)S(1)}, bf16[128,4096]{1,0:T(8,128)(2,1)S(1)}, u32[]{:S(2)}, u32[]{:S(2)}) collective-permute-start(bf16[128,4096]{1,0:T(8,128)(2,1)S(1)} %add_convert_fusion.1), channel_id=1, source_target_pairs={{8,0},{10,2},{16,8},{18,10},{24,16},{26,18},{28,24},{30,26},{20,28... | collective-permute-start | bytes 3145736 | tf_op jit(solution)/shard_map/ppermute | solution.py:58
  806.7 31.2 %collective-permute-start.108 = (bf16[512,2048]{1,0:T(8,128)(2,1)S(1)}, bf16[512,2048]{1,0:T(8,128)(2,1)S(1)}, u32[]{:S(2)}, u32[]{:S(2)}) collective-permute-start(bf16[512,2048]{1,0:T(8,128)(2,1)S(1)} %slice.1103), channel_id=1, source_target_pairs={{0,2},{2,0},{4,6},{6,4},{8,10},{10,8},{12,14},{14,12},{16,18},{18,... | collective-permute-start | bytes 6291464 | tf_op jit(solution)/shard_map/ppermute | solution.py:61
  807.8 27.7 %collective-permute-start.121 = (bf16[128,1536]{0,1:T(8,128)(2,1)S(1)}, bf16[128,1536]{0,1:T(8,128)(2,1)S(1)}, u32[]{:S(2)}, u32[]{:S(2)}) collective-permute-start(bf16[128,1536]{0,1:T(8,128)(2,1)S(1)} %get-tuple-element.583), channel_id=1, source_target_pairs={{8,0},{10,2},{16,8},{18,10},{24,16},{26,18},{28,24},{30,26},{20,28... | collective-permute-start | bytes 1179656 | tf_op jit(solution)/shard_map/ppermute | solution.py:58
  852.6 27.8 %collective-permute-start.134 = (bf16[128,4096]{1,0:T(8,128)(2,1)}, bf16[128,4096]{1,0:T(8,128)(2,1)}, u32[]{:S(2)}, u32[]{:S(2)}) collective-permute-start(bf16[128,4096]{1,0:T(8,128)(2,1)} %get-tuple-element.593), channel_id=1, source_target_pairs={{0,2},{2,0},{4,6},{6,4},{8,10},{10,8},{12,14},{14,12},{16,18},{18,... | collective-permute-start | bytes 3145736 | tf_op jit(solution)/shard_map/ppermute | solution.py:61
  (231 other events, 3846.7 us)

commit v5 on v4

--- a/solution.py
+++ b/solution.py
@@ -28,14 +28,6 @@
     return (jnp.cos(angle), jnp.sin(angle))
 
 
-def rotate(heads, cosine, sine):
-    half = heads.shape[-1] // 2
-    first, second = heads[..., :half], heads[..., half:]
-    return jnp.concatenate(
-        [first * cosine - second * sine, second * cosine + first * sine], axis=-1
-    )
-
-
 def ring_order(chips):
     column = chips // 2
     return [2 * i for i in range(column)] + [2 * i + 1 for i in reversed(range(column))]
@@ -69,18 +61,27 @@
     return lax.optimization_barrier(values)
 
 
+def unfilled(shape, name):
+    return pl.pallas_call(
+        lambda out: None,
+        out_shape=jax.ShapeDtypeStruct(shape, bf16),
+        out_specs=pl.BlockSpec(memory_space=pl.ANY),
+        name=name,
+    )()
+
+
 class Gather:
-    def __init__(self, ring, low, high, rows, cuts=None, split=False, below=0):
+    def __init__(self, ring, name, low, high, rows, cuts=None, split=False, below=0):
         self.ring, self.size, self.split, self.below = ring, rows, split, below
         self.now = (low, high)
         self.cuts = cuts or [(0, low.shape[1])]
         height = 2 * ring.chips * rows
+        shapes = [(height, b - a) for a, b in self.cuts]
         if split:
-            self.buffers = [jnp.zeros((height // 2, low.shape[1]), bf16)] * 2
-        else:
-            self.buffers = [jnp.zeros((height, b - a), bf16) for a, b in self.cuts]
+            shapes = [(height // 2, low.shape[1])] * 2
         if below:
-            self.buffers.append(jnp.zeros((below, height), bf16))
+            shapes.append((below, height))
+        self.buffers = [unfilled(v, f"{name}_{i}") for i, v in enumerate(shapes)]
         self.hops = 0
         self.store()
 
@@ -213,6 +214,99 @@
         ),
         name="reorder",
     )(table, rows)
+
+
+def visible(numbers, shape):
+    def slot(axis):
+        offset = lax.broadcasted_iota(jnp.int32, shape, axis)
+        start = numbers[2] * (shape[0] // 2)
+        return jnp.where(offset < shape[0] // 2, offset + start, offset - start)
+
+    query, key = slot(0), slot(1)
+    inside = query < numbers[pl.program_id(0)]
+    return jnp.where(inside, key - query, jnp.abs(key - query)) <= 0
+
+
+def turned(heads, cosine, sine):
+    half = heads.shape[1] // 2
+    first, second = heads[:, :half], heads[:, half:]
+    return first * cosine - second * sine, second * cosine + first * sine
+
+
+def weights_of(queries, keys, allowed):
+    scores = lax.dot_general(queries, keys, over_last, preferred_element_type=f32)
+    scores = jnp.where(allowed, scores * HEAD_SIZE ** (-0.5), -1e30)
+    shifted = jnp.exp(scores - jnp.max(scores, axis=-1, keepdims=True))
+    return shifted / jnp.sum(shifted, axis=-1, keepdims=True)
+
+
+def attend_body(numbers, qkv, cosine, sine, queries, keys, values, mixed):
+    rows, width = queries.shape
+    half = HEAD_SIZE // 2
+    cosine, sine = cosine[...], sine[...]
+    key_low, key_high = turned(qkv[:, width : width + HEAD_SIZE], cosine, sine)
+    keys[:, :half] = key_low.astype(bf16)
+    keys[:, half:] = key_high.astype(bf16)
+    values[...] = qkv[:, width + HEAD_SIZE :].astype(bf16)
+    allowed = visible(numbers, (rows, rows))
+    for start in range(0, width, HEAD_SIZE):
+        low, high = turned(qkv[:, start : start + HEAD_SIZE], cosine, sine)
+        queries[:, start : start + half] = low.astype(bf16)
+        queries[:, start + half : start + HEAD_SIZE] = high.astype(bf16)
+        probs = weights_of(queries[:, start : start + HEAD_SIZE], keys[...], allowed)
+        mixed[:, start : start + HEAD_SIZE] = jnp.dot(
+            probs.astype(bf16), values[...], preferred_element_type=f32
+        ).astype(bf16)
+
+
+def attend_back_body(numbers, queries, keys, values, delta, cosine, sine, out):
+    rows, width = queries.shape
+    half = HEAD_SIZE // 2
+    scaling = HEAD_SIZE ** (-0.5)
+    cosine, sine = cosine[...], sine[...]
+    allowed = visible(numbers, (rows, rows))
+    delta_keys = jnp.zeros((rows, HEAD_SIZE), f32)
+    delta_values = jnp.zeros((rows, HEAD_SIZE), f32)
+    for start in range(0, width, HEAD_SIZE):
+        head = queries[:, start : start + HEAD_SIZE]
+        delta_mixed = delta[:, start : start + HEAD_SIZE]
+        probs = weights_of(head, keys[...], allowed)
+        delta_probs = lax.dot_general(
+            delta_mixed, values[...], over_last, preferred_element_type=f32
+        )
+        inner = jnp.sum(probs * delta_probs, axis=-1, keepdims=True)
+        delta_scores = (probs * (delta_probs - inner)).astype(bf16)
+        delta_values += lax.dot_general(
+            probs.astype(bf16), delta_mixed, over_rows, preferred_element_type=f32
+        )
+        delta_keys += lax.dot_general(delta_scores, head, over_rows, preferred_element_type=f32)
+        delta_head = jnp.dot(delta_scores, keys[...], preferred_element_type=f32) * scaling
+        low, high = turned(delta_head, cosine, -sine)
+        out[:, start : start + half] = low.astype(bf16)
+        out[:, start + half : start + HEAD_SIZE] = high.astype(bf16)
+    low, high = turned(delta_keys * scaling, cosine, -sine)
+    out[:, width : width + half] = low.astype(bf16)
+    out[:, width + half : width + HEAD_SIZE] = high.astype(bf16)
+    out[:, width + HEAD_SIZE :] = delta_values.astype(bf16)
+
+
+def by_sequence(body, numbers, arrays, widths, name):
+    rows = arrays[0].shape[0] // 2
+
+    def spec(columns):
+        return pl.BlockSpec((rows, columns), lambda b, n: (b, 0))
+
+    return pl.pallas_call(
+        body,
+        out_shape=[jax.ShapeDtypeStruct((2 * rows, w), bf16) for w in widths],
+        grid_spec=pltpu.PrefetchScalarGridSpec(
+            num_scalar_prefetch=1,
+            grid=(2,),
+            in_specs=[spec(v.shape[1]) for v in arrays],
+            out_specs=[spec(w) for w in widths],
+        ),
+        name=name,
+    )(numbers, *arrays)
 
 
 def sum_all(ring, v):
@@ -298,20 +392,26 @@
     out_width = w_out.shape[0] // 2
     attn_weights = Gather(
         ring,
+        "attn_rows",
         *both_rows([w_query, key_projection_weight, value_projection_weight, w_out.T], gains),
         piece,
         [(0, qkv_width), (qkv_width, qkv_width + out_width)],
         below=16,
     )
-    gate_weights = Gather(ring, *both_rows([w_gate]), piece)
+    w_gate, layer_input, to_relative, lengths, _ = together(
+        (w_gate, layer_input, to_relative, lengths, attn_weights.now)
+    )
+    gate_weights = Gather(ring, "gate_rows", *both_rows([w_gate]), piece)
     own_input = reorder(layer_input, to_relative)
     group_rows = gather_group(ring, own_input)
     for k in range(hops):
         turn(attn_weights, gate_weights)
         turn(gate_weights, attn_weights)
-    up_weights = Gather(ring, *together((both_rows([w_up]), attn_weights.now))[0], piece)
+    up_weights = Gather(
+        ring, "up_rows", *together((both_rows([w_up]), attn_weights.now))[0], piece
+    )
     down_weights = Gather(
-        ring, *together((both_rows([w_down.T]), gate_weights.now))[0], piece, split=True
+        ring, "down_rows", *together((both_rows([w_down.T]), gate_weights.now))[0], piece, split=True
     )
 
     sequence_numbers = jnp.stack([me, me + 1 - 2 * core])
@@ -321,18 +421,10 @@
     offsets = jnp.arange(token_rows, dtype=jnp.int32)
     slot = jnp.concatenate([side * token_rows + offsets, (1 - side) * token_rows + offsets])
     inside = slot[None, :] < length[:, None]
-    sequence = jnp.where(inside, 0, 1 + slot[None, :])
     position = jnp.where(inside, slot[None, :], 0)
     own_valid = inside[0, :token_rows].astype(f32)[:, None]
-    allowed = (sequence[:, :, None] == sequence[:, None, :]) & (
-        position[:, None, :] <= position[:, :, None]
-    )
-    allowed = allowed[:, None]
-    cosine, sine = rope_tables(position, HEAD_SIZE)
-    cosine, sine = cosine[:, :, None, :], sine[:, :, None, :]
-    scaling = HEAD_SIZE ** (-0.5)
-    query_heads = q_width // HEAD_SIZE
-    all_rows = 2 * slots
+    cosine, sine = rope_tables(position.reshape(-1), HEAD_SIZE)
+    numbers = jnp.concatenate([length, side[None]]).astype(jnp.int32)
     own_rows = own_input.astype(f32)
     attn_scale = rms_scale(own_rows)
 
@@ -346,27 +438,16 @@
         normed = (group_input * rms_scale(group_input) * attn_gain).astype(bf16)
         qkv = jnp.dot(normed, qkv_proj, preferred_element_type=f32)
         normed, qkv = yield Held(normed, qkv)
-        query_rows = qkv[:, :q_width].reshape(2, slots, query_heads, HEAD_SIZE)
-        key_rows = qkv[:, q_width : q_width + kv_width].reshape(2, slots, 1, HEAD_SIZE)
-        values = qkv[:, q_width + kv_width :].astype(bf16).reshape(2, slots, HEAD_SIZE)
-        rot_queries = rotate(query_rows, cosine, sine).astype(bf16)
-        rot_keys = rotate(key_rows, cosine, sine).astype(bf16)[:, :, 0]
-        rot_queries, rot_keys, values = yield Held(rot_queries, rot_keys, values)
-        scores = (
-            jnp.einsum("bigd,bjd->bgij", rot_queries, rot_keys, preferred_element_type=f32)
-            * scaling
-        )
-        scores = jnp.where(allowed, scores, -1e30)
-        shifted = jnp.exp(scores - jnp.max(scores, axis=-1, keepdims=True))
-        probs = shifted / jnp.sum(shifted, axis=-1, keepdims=True)
-        probs = yield Held(probs)
-        mixed = (
-            jnp.einsum("bgij,bjd->bigd", probs.astype(bf16), values, preferred_element_type=f32)
-            .reshape(all_rows, q_width)
-            .astype(bf16)
-        )
-        parts = lax.dot_general(mixed, out_proj_t, over_last, preferred_element_type=f32)
-        mixed, parts = yield Held(mixed, parts)
+        attended = by_sequence(
+            attend_body,
+            numbers,
+            [qkv, cosine, sine],
+            [q_width, kv_width, kv_width, q_width],
+            "attend",
+        )
+        attended = yield Held(attended)
+        parts = lax.dot_general(attended[3], out_proj_t, over_last, preferred_element_type=f32)
+        parts = yield Held(parts)
         shared = scatter_group(ring, parts)
         own_teacher = yield Held(reorder(teacher, to_relative))
         yield ()
@@ -381,7 +462,7 @@
         gate = yield Held(gate)
         return (
             own_teacher,
-            (normed, rot_queries, rot_keys, values, probs, mixed),
+            (normed, *attended),
             (middle, mlp_scale, normed_mlp, gate),
         )
 
@@ -390,7 +471,7 @@
         stages.turn(up_weights, down_weights)
         stages.turn(down_weights, up_weights)
     own_teacher, attn_kept, mlp_kept = stages.finish()
-    normed, rot_queries, rot_keys, values, probs, mixed = attn_kept
+    normed, rot_queries, rot_keys, values, mixed = attn_kept
     middle, mlp_scale, normed_mlp, gate = mlp_kept
     up_proj = up_weights.buffers[0]
     down_far, down_near = down_weights.buffers
@@ -458,39 +539,16 @@
         yield ()
         attn_low_rows = yield Held(attn_low_rows)
         grad_out_t = lax.dot_general(attn_low_rows, mixed, over_rows, preferred_element_type=f32)
-        delta_mixed = (
-            jnp.dot(attn_low_rows, out_proj_t, preferred_element_type=f32)
-            .astype(bf16)
-            .reshape(2, slots, query_heads, HEAD_SIZE)
-        )
+        delta_mixed = jnp.dot(attn_low_rows, out_proj_t, preferred_element_type=f32).astype(bf16)
         grad_out_t = grad_out_t.astype(bf16)
-        probs_low = probs.astype(bf16)
-        delta_probs = jnp.einsum("bigd,bjd->bgij", delta_mixed, values, preferred_element_type=f32)
-        inner = jnp.sum(probs * delta_probs, axis=-1, keepdims=True)
-        delta_scores = (probs * (delta_probs - inner)).astype(bf16)
-        delta_values = jnp.einsum(
-            "bgij,bigd->bjd", probs_low, delta_mixed, preferred_element_type=f32
-        )
-        grad_out_t, delta_scores, delta_values = yield Held(grad_out_t, delta_scores, delta_values)
-        delta_qrot = (
-            jnp.einsum("bgij,bjd->bigd", delta_scores, rot_keys, preferred_element_type=f32)
-            * scaling
-        )
-        delta_krot = (
-            jnp.einsum("bgij,bigd->bjd", delta_scores, rot_queries, preferred_element_type=f32)
-            * scaling
-        )
-        delta_queries = rotate(delta_qrot, cosine, -sine).reshape(all_rows, q_width)
-        delta_keys = rotate(delta_krot[:, :, None], cosine, -sine).reshape(all_rows, kv_width)
-        delta_qkv = jnp.concatenate(
-            [
-                delta_queries.astype(bf16),
-                delta_keys.astype(bf16),
-                delta_values.astype(bf16).reshape(all_rows, kv_width),
-            ],
-            axis=1,
-        )
-        delta_qkv = yield Held(delta_qkv)
+        delta_qkv = by_sequence(
+            attend_back_body,
+            numbers,
+            [rot_queries, rot_keys, values, delta_mixed, cosine, sine],
+            [qkv_width],
+            "attend_back",
+        )[0]
+        delta_qkv, grad_out_t = yield Held(delta_qkv, grad_out_t)
         grad_qkv = lax.dot_general(normed, delta_qkv, over_rows, preferred_element_type=f32)
         return (
             activations,

time: 930 us -> 872 us (0.938)
  other arithmetic: 123 us -> 88.3 us
  local copies, waits for them, and re-layouts: 140 us -> 112 us
  Pallas kernels: 16.5 us -> 31.1 us
    ppermute x49, waiting for transfers between devices: 142 us -> 99.9 us  [back(): return lax.ppermute(v, 'dp', self.down)]
    ppermute x49, waiting for transfers between devices: 127 us -> 155 us  [ahead(): return lax.ppermute(v, 'dp', self.up)]
    pallas_call x0 -> x9, Pallas kernels: none -> 14.2 us  [the longest x2 14.2 us: by_sequence(): pl.pallas_call(body, out_shape=[jax.ShapeDtypeStruct((2 * rows, w), bf16)...]
    dynamic_update_slice x16, local copies, waits for them, and re-layouts: 21.2 us -> 9.14 us  [store(): lax.dynamic_update_slice(self.buffers[which], rows[:self.size], (start, 0))]
    unnamed x252 -> x202, local copies, waits for them, and re-layouts: 30.1 us -> 18.8 us
    dot_general x7 -> x1, matrix products: 15.9 us -> 4.64 us  [forward(): lax.dot_general(attended[3], out_proj_t, over_last, preferred_element_typ...]
    dynamic_update_slice x63 -> x62, local copies, waits for them, and re-layouts: 37.1 us -> 48.1 us  [store(): lax.dynamic_update_slice(self.buffers[i], rows[:self.size, a:b], (at * se...]
    ppermute x4, waiting for transfers between devices: 0.01 us -> 9.66 us  [sum_all(): v = v + lax.ppermute(v, 'dp', [(d, d ^ step) for d in range(devices)])]
  transfers between devices with their start and end apart: 135 -> 135, of which waited for: 75 -> 78; matrix products, arithmetic and copies ran while one was open for 39% -> 34% of each run, Pallas kernels for 1% -> 4%
where the time goes in v5:
time: 872 us; the launch traced here: 864 us
  waiting for transfers between devices  348 us (40%)
  matrix products  160 us (18%)
  starting transfers between devices  118 us (14%)
  local copies, waits for them, and re-layouts  112 us (13%)
  other arithmetic  88.3 us (10%)
  Pallas kernels  31.1 us (4%)
    ppermute x49, waiting for transfers between devices, ahead(): return lax.ppermute(v, 'dp', self.up)  155 us
    ppermute x49, waiting for transfers between devices, back(): return lax.ppermute(v, 'dp', self.down)  99.9 us
    ppermute x11, waiting for transfers between devices, other_tensor(): return lax.ppermute(v, 'tensor', [(0, 1), (1, 0)])  81.3 us
    ppermute x49, starting transfers between devices, ahead(): return lax.ppermute(v, 'dp', self.up)  52.1 us
    ppermute x49, starting transfers between devices, back(): return lax.ppermute(v, 'dp', self.down)  50.5 us
    dynamic_update_slice x62, local copies, waits for them, and re-layouts, store(): lax.dynamic_update_slice(self.buffers[i], rows[:self.size, a:b], (at * se...  48.1 us
    convert_element_type x24, other arithmetic, take(): self.now = tuple(sums if self.left == 0 else [v.astype(bf16) for v in sums])  22 us
    unnamed x202, local copies, waits for them, and re-layouts  18.8 us
  transfers between devices with their start and end apart: 135, of which 78 were waited for; matrix products, arithmetic and copies ran while one was open for 34% of the time, Pallas kernels for 4%

profile of v5, /device:TPU:0, one launch (start us, length us, event | category | flops | bytes accessed | tf_op | source)
XLA Modules:
  0.0 863.5 jit_solution(6786667169671724934)
XLA Ops:
  74.5 7.7 collective-permute-done.7
  82.8 9.0 %collective-permute-done.13 = bf16[144,1536]{1,0:T(8,128)(2,1)S(1)} collective-permute-done((bf16[144,1536]{1,0:T(8,128)(2,1)S(1)}, bf16[144,1536]{1,0:T(8,128)(2,1)S(1)}, u32[]{:S(2)}, u32[]{:S(2)}) %collective-permute-start.13) | collective-permute-done | bytes 442400 | tf_op jit(solution)/shard_map/ppermute | solution.py:47
  245.8 8.2 collective-permute-done.45
  274.9 7.7 collective-permute-done.51
  282.6 8.8 %collective-permute-done.57 = bf16[256,2048]{1,0:T(8,128)(2,1)S(1)} collective-permute-done((bf16[256,2048]{1,0:T(8,128)(2,1)S(1)}, bf16[256,2048]{1,0:T(8,128)(2,1)S(1)}, u32[]{:S(2)}, u32[]{:S(2)}) %collective-permute-start.57) | collective-permute-done | bytes 1048608 | tf_op jit(solution)/shard_map/ppermute | solution.py:57
  298.7 8.4 collective-permute-done.55
  312.4 10.9 %fusion.70 = f32[1024,2048]{1,0:T(8,128)} fusion(bf16[1024,2048]{1,0:T(8,128)(2,1)S(1)} %pad_maximum_fusion.1, bf16[2048,2048]{1,0:T(8,128)(2,1)S(1)} %constant_dynamic-update-slice_fusion.14), kind=kOutput, calls=%fused_computation.393 | convolution fusion | flops 8589934592 | bytes 20971520 | tf_op jit(solution)/shard_map/dot_general | solution.py:461
  367.5 15.0 %multiply_convert_fusion.2 = (bf16[1024,2048]{1,0:T(8,128)(2,1)S(1)}, f32[1024,2048]{1,0:T(8,128)}) fusion(f32[1024,2048]{1,0:T(8,128)} %fusion.70, bf16[1024,2048]{1,0:T(8,128)(2,1)S(1)} %pad_maximum_fusion.1, bf16[2048,2048]{1,0:T(8,128)(2,1)} %constant_dynamic-update-slice_fusion.4), kind=kOutput, calls=%fused_computation.40 | convolution fusion | flops 8602517504 | bytes 33554432 | tf_op jit(solution)/shard_map/dot_general | solution.py:480
  403.8 12.9 %collective-permute-done.69 = bf16[256,1024]{1,0:T(8,128)(2,1)S(1)} collective-permute-done((bf16[256,1024]{1,0:T(8,128)(2,1)S(1)}, bf16[256,1024]{1,0:T(8,128)(2,1)S(1)}, u32[]{:S(2)}, u32[]{:S(2)}) %collective-permute-start.69) | collective-permute-done | bytes 524320 | tf_op jit(solution)/shard_map/ppermute | solution.py:57
  421.2 12.6 %collective-permute-done.70 = bf16[256,1024]{1,0:T(8,128)(2,1)S(1)} collective-permute-done((bf16[256,1024]{1,0:T(8,128)(2,1)S(1)}, bf16[256,1024]{1,0:T(8,128)(2,1)S(1)}, u32[]{:S(2)}, u32[]{:S(2)}) %collective-permute-start.70) | collective-permute-done | bytes 524320 | tf_op jit(solution)/shard_map/ppermute | solution.py:57
  433.8 9.9 %collective-permute-done.78 = bf16[256,1024]{1,0:T(8,128)(2,1)S(1)} collective-permute-done((bf16[256,1024]{1,0:T(8,128)(2,1)S(1)}, bf16[256,1024]{1,0:T(8,128)(2,1)S(1)}, u32[]{:S(2)}, u32[]{:S(2)}) %collective-permute-start.78) | collective-permute-done | bytes 524320 | tf_op jit(solution)/shard_map/ppermute | solution.py:57
  458.6 8.6 fusion.30
  471.3 16.5 %multiply_convert_fusion = (bf16[1024,2048]{1,0:T(8,128)(2,1)}, bf16[1024,2048]{1,0:T(8,128)(2,1)}) fusion(f32[1024,2048]{1,0:T(8,128)} %fusion.70, f32[1024,2048]{1,0:T(8,128)} %get-tuple-element.639, f32[1024,2048]{1,0:T(8,128)} %fusion.30, bf16[1024,2048]{1,0:T(8,128)(2,1)} %constant_dynamic-update-slice_fusion.18, bf16[256,1024]{1,0:T(8,128)(2,1)} %copy-done.86, ...), kind=kOutput, calls=%fused_computation.38 | convolution fusion | flops 4332716032 | bytes 39845888 | tf_op jit(solution)/shard_map/dot_general | solution.py:505
  497.5 10.9 %convolution_convert_fusion.1 = bf16[2048,2048]{1,0:T(8,128)(2,1)S(1)} fusion(bf16[1024,2048]{1,0:T(8,128)(2,1)S(1)} %copy-done.21, bf16[1024,2048]{1,0:T(8,128)(2,1)} %get-tuple-element.380), kind=kOutput, calls=%fused_computation.43 | convolution fusion | flops 8594128896 | bytes 16777216 | tf_op jit(solution)/shard_map/dot_general | solution.py:513
  508.5 13.4 %convolution_convert_fusion = bf16[2048,2048]{1,0:T(8,128)(2,1)} fusion(bf16[1024,2048]{1,0:T(8,128)(2,1)S(1)} %copy-done.21, bf16[1024,2048]{1,0:T(8,128)(2,1)} %get-tuple-element.385), kind=kOutput, calls=%fused_computation.42 | convolution fusion | flops 8594128896 | bytes 16777216 | tf_op jit(solution)/shard_map/dot_general | solution.py:517
  524.4 14.7 %fusion.73 = f32[1024,2048]{1,0:T(8,128)} fusion(bf16[1024,2048]{1,0:T(8,128)(2,1)} %get-tuple-element.385, bf16[2048,2048]{1,0:T(8,128)(2,1)} %constant_dynamic-update-slice_fusion.4), kind=kOutput, calls=%fused_computation.396 | convolution fusion | flops 8589934592 | bytes 20971520 | tf_op jit(solution)/shard_map/dot_general | solution.py:525
  544.7 7.5 collective-permute-done.86
  560.2 14.0 %convolution_add_fusion.1 = f32[1024,2048]{1,0:T(8,128)} fusion(f32[1024,2048]{1,0:T(8,128)} %fusion.73, bf16[1024,2048]{1,0:T(8,128)(2,1)} %get-tuple-element.380, bf16[2048,2048]{1,0:T(8,128)(2,1)S(1)} %bitcast.80), kind=kOutput, calls=%fused_computation.59 | convolution fusion | flops 8592031744 | bytes 29360128 | tf_op jit(solution)/shard_map/dot_general | solution.py:523
  611.6 10.3 %collective-permute-done.95 = bf16[256,2048]{1,0:T(8,128)(2,1)} collective-permute-done((bf16[256,2048]{1,0:T(8,128)(2,1)}, bf16[256,2048]{1,0:T(8,128)(2,1)}, u32[]{:S(2)}, u32[]{:S(2)}) %collective-permute-start.95) | collective-permute-done | bytes 1048608 | tf_op jit(solution)/shard_map/ppermute | solution.py:57
  645.7 14.4 %collective-permute-done.101 = bf16[256,2048]{1,0:T(8,128)(2,1)S(1)} collective-permute-done((bf16[256,2048]{1,0:T(8,128)(2,1)}, bf16[256,2048]{1,0:T(8,128)(2,1)S(1)}, u32[]{:S(2)}, u32[]{:S(2)}) %collective-permute-start.101) | collective-permute-done | bytes 1048608 | tf_op jit(solution)/shard_map/ppermute | solution.py:57
  677.1 7.9 attend_back.1
  714.4 10.4 %collective-permute-done.111 = bf16[128,4096]{1,0:T(8,128)(2,1)S(1)} collective-permute-done((bf16[128,4096]{1,0:T(8,128)(2,1)}, bf16[128,4096]{1,0:T(8,128)(2,1)S(1)}, u32[]{:S(2)}, u32[]{:S(2)}) %collective-permute-start.111) | collective-permute-done | bytes 1048608 | tf_op jit(solution)/shard_map/ppermute | solution.py:47
  737.9 17.8 %collective-permute-done.113 = bf16[128,4096]{1,0:T(8,128)(2,1)S(1)} collective-permute-done((bf16[128,4096]{1,0:T(8,128)(2,1)S(1)}, bf16[128,4096]{1,0:T(8,128)(2,1)S(1)}, u32[]{:S(2)}, u32[]{:S(2)}) %collective-permute-start.113) | collective-permute-done | bytes 1048608 | tf_op jit(solution)/shard_map/ppermute | solution.py:47
  770.5 16.1 %collective-permute-done.124 = bf16[128,4096]{1,0:T(8,128)(2,1)S(1)} collective-permute-done((bf16[128,4096]{1,0:T(8,128)(2,1)S(1)}, bf16[128,4096]{1,0:T(8,128)(2,1)S(1)}, u32[]{:S(2)}, u32[]{:S(2)}) %collective-permute-start.124) | collective-permute-done | bytes 1048608 | tf_op jit(solution)/shard_map/ppermute | solution.py:47
  (718 shorter events, 583.4 us)
Async XLA Ops:
  8.7 31.8 %collective-permute-start.1 = (bf16[128,2048]{1,0:T(8,128)(2,1)}, bf16[128,2048]{1,0:T(8,128)(2,1)S(1)}, u32[]{:S(2)}, u32[]{:S(2)}) collective-permute-start(bf16[128,2048]{1,0:T(8,128)(2,1)} %bitcast.8), channel_id=1, source_target_pairs={{0,2},{2,0},{4,6},{6,4},{8,10},{10,8},{12,14},{14,12},{16,18},{18,... | collective-permute-start | bytes 1572872 | tf_op jit(solution)/shard_map/ppermute | solution.py:53
  9.6 27.7 %collective-permute-start.33 = (bf16[128,2048]{1,0:T(8,128)(2,1)}, bf16[128,2048]{1,0:T(8,128)(2,1)}, u32[]{:S(2)}, u32[]{:S(2)}) collective-permute-start(bf16[128,2048]{1,0:T(8,128)(2,1)} %constant_dynamic-slice_fusion.2), channel_id=1, source_target_pairs={{0,2},{2,0},{4,6},{6,4},{8,10},{10,8},{12,14},{14,12},{16,18},{18,... | collective-permute-start | bytes 1572872 | tf_op jit(solution)/shard_map/ppermute | solution.py:53
  16.5 30.7 %collective-permute-start.5 = (bf16[144,1536]{1,0:T(8,128)(2,1)}, bf16[144,1536]{1,0:T(8,128)(2,1)}, u32[]{:S(2)}, u32[]{:S(2)}) collective-permute-start(bf16[144,1536]{1,0:T(8,128)(2,1)} %get-tuple-element.615), channel_id=1, source_target_pairs={{0,8},{2,10},{8,16},{10,18},{16,24},{18,26},{24,28},{26,30},{28,20... | collective-permute-start | bytes 1327112 | tf_op jit(solution)/shard_map/ppermute | solution.py:47
  19.1 28.2 %collective-permute-start.6 = (bf16[144,1536]{1,0:T(8,128)(2,1)}, bf16[144,1536]{1,0:T(8,128)(2,1)}, u32[]{:S(2)}, u32[]{:S(2)}) collective-permute-start(bf16[144,1536]{1,0:T(8,128)(2,1)} %get-tuple-element.614), channel_id=1, source_target_pairs={{8,0},{10,2},{16,8},{18,10},{24,16},{26,18},{28,24},{30,26},{20,28... | collective-permute-start | bytes 1327112 | tf_op jit(solution)/shard_map/ppermute | solution.py:50
  37.2 37.2 %collective-permute-start.36 = (bf16[256,2048]{1,0:T(8,128)(2,1)}, bf16[256,2048]{1,0:T(8,128)(2,1)S(1)}, u32[]{:S(2)}, u32[]{:S(2)}) collective-permute-start(bf16[256,2048]{1,0:T(8,128)(2,1)} %reorder.4), channel_id=1, source_target_pairs={{0,1},{1,0},{2,3},{3,2},{4,5},{5,4},{6,7},{7,6},{8,9},{9,8},{10,11... | collective-permute-start | bytes 3145736 | tf_op jit(solution)/shard_map/ppermute | solution.py:57
  168.7 28.3 %collective-permute-start.27 = (bf16[128,2048]{1,0:T(8,128)(2,1)S(1)}, bf16[128,2048]{1,0:T(8,128)(2,1)S(1)}, u32[]{:S(2)}, u32[]{:S(2)}) collective-permute-start(bf16[128,2048]{1,0:T(8,128)(2,1)S(1)} %collective-permute-done.23), channel_id=1, source_target_pairs={{0,8},{2,10},{8,16},{10,18},{16,24},{18,26},{24,28},{26,30},{28,20... | collective-permute-start | bytes 1572872 | tf_op jit(solution)/shard_map/ppermute | solution.py:47
  169.2 27.8 %collective-permute-start.28 = (bf16[128,2048]{1,0:T(8,128)(2,1)S(1)}, bf16[128,2048]{1,0:T(8,128)(2,1)S(1)}, u32[]{:S(2)}, u32[]{:S(2)}) collective-permute-start(bf16[128,2048]{1,0:T(8,128)(2,1)S(1)} %collective-permute-done.24), channel_id=1, source_target_pairs={{8,0},{10,2},{16,8},{18,10},{24,16},{26,18},{28,24},{30,26},{20,28... | collective-permute-start | bytes 1572872 | tf_op jit(solution)/shard_map/ppermute | solution.py:50
  296.1 27.3 %collective-permute-start.53 = (bf16[128,2048]{1,0:T(8,128)(2,1)S(1)}, bf16[128,2048]{1,0:T(8,128)(2,1)S(1)}, u32[]{:S(2)}, u32[]{:S(2)}) collective-permute-start(bf16[128,2048]{1,0:T(8,128)(2,1)S(1)} %collective-permute-done.49), channel_id=1, source_target_pairs={{0,8},{2,10},{8,16},{10,18},{16,24},{18,26},{24,28},{26,30},{28,20... | collective-permute-start | bytes 1572872 | tf_op jit(solution)/shard_map/ppermute | solution.py:47
  467.6 27.4 %collective-permute-start.75 = (bf16[128,2048]{1,0:T(8,128)(2,1)S(1)}, bf16[128,2048]{1,0:T(8,128)(2,1)S(1)}, u32[]{:S(2)}, u32[]{:S(2)}) collective-permute-start(bf16[128,2048]{1,0:T(8,128)(2,1)S(1)} %get-tuple-element.595), channel_id=1, source_target_pairs={{8,0},{10,2},{16,8},{18,10},{24,16},{26,18},{28,24},{30,26},{20,28... | collective-permute-start | bytes 1572872 | tf_op jit(solution)/shard_map/ppermute | solution.py:50
  468.6 26.5 %collective-permute-start.76 = (bf16[128,2048]{1,0:T(8,128)(2,1)S(1)}, bf16[128,2048]{1,0:T(8,128)(2,1)S(1)}, u32[]{:S(2)}, u32[]{:S(2)}) collective-permute-start(bf16[128,2048]{1,0:T(8,128)(2,1)S(1)} %get-tuple-element.594), channel_id=1, source_target_pairs={{0,8},{2,10},{8,16},{10,18},{16,24},{18,26},{24,28},{26,30},{28,20... | collective-permute-start | bytes 1572872 | tf_op jit(solution)/shard_map/ppermute | solution.py:47
  495.5 26.4 %collective-permute-start.82 = (bf16[128,2048]{1,0:T(8,128)(2,1)S(1)}, bf16[128,2048]{1,0:T(8,128)(2,1)S(1)}, u32[]{:S(2)}, u32[]{:S(2)}) collective-permute-start(bf16[128,2048]{1,0:T(8,128)(2,1)S(1)} %get-tuple-element.593), channel_id=1, source_target_pairs={{8,0},{10,2},{16,8},{18,10},{24,16},{26,18},{28,24},{30,26},{20,28... | collective-permute-start | bytes 1572872 | tf_op jit(solution)/shard_map/ppermute | solution.py:50
  609.5 29.1 %collective-permute-start.96 = (bf16[128,2048]{1,0:T(8,128)(2,1)S(1)}, bf16[128,2048]{1,0:T(8,128)(2,1)S(1)}, u32[]{:S(2)}, u32[]{:S(2)}) collective-permute-start(bf16[128,2048]{1,0:T(8,128)(2,1)S(1)} %get-tuple-element.585), channel_id=1, source_target_pairs={{8,0},{10,2},{16,8},{18,10},{24,16},{26,18},{28,24},{30,26},{20,28... | collective-permute-start | bytes 1572872 | tf_op jit(solution)/shard_map/ppermute | solution.py:50
  610.0 28.6 %collective-permute-start.97 = (bf16[128,2048]{1,0:T(8,128)(2,1)S(1)}, bf16[128,2048]{1,0:T(8,128)(2,1)S(1)}, u32[]{:S(2)}, u32[]{:S(2)}) collective-permute-start(bf16[128,2048]{1,0:T(8,128)(2,1)S(1)} %get-tuple-element.584), channel_id=1, source_target_pairs={{0,8},{2,10},{8,16},{10,18},{16,24},{18,26},{24,28},{26,30},{28,20... | collective-permute-start | bytes 1572872 | tf_op jit(solution)/shard_map/ppermute | solution.py:47
  698.4 26.4 %collective-permute-start.111 = (bf16[128,4096]{1,0:T(8,128)(2,1)}, bf16[128,4096]{1,0:T(8,128)(2,1)S(1)}, u32[]{:S(2)}, u32[]{:S(2)}) collective-permute-start(bf16[128,4096]{1,0:T(8,128)(2,1)} %add_convert_fusion.4), channel_id=1, source_target_pairs={{0,8},{2,10},{8,16},{10,18},{16,24},{18,26},{24,28},{26,30},{28,20... | collective-permute-start | bytes 3145736 | tf_op jit(solution)/shard_map/ppermute | solution.py:47
  726.9 28.7 %collective-permute-start.113 = (bf16[128,4096]{1,0:T(8,128)(2,1)S(1)}, bf16[128,4096]{1,0:T(8,128)(2,1)S(1)}, u32[]{:S(2)}, u32[]{:S(2)}) collective-permute-start(bf16[128,4096]{1,0:T(8,128)(2,1)S(1)} %add_convert_fusion.2), channel_id=1, source_target_pairs={{0,8},{2,10},{8,16},{10,18},{16,24},{18,26},{24,28},{26,30},{28,20... | collective-permute-start | bytes 3145736 | tf_op jit(solution)/shard_map/ppermute | solution.py:47
  728.8 28.7 %collective-permute-start.112 = (bf16[128,4096]{1,0:T(8,128)(2,1)S(1)}, bf16[128,4096]{1,0:T(8,128)(2,1)S(1)}, u32[]{:S(2)}, u32[]{:S(2)}) collective-permute-start(bf16[128,4096]{1,0:T(8,128)(2,1)S(1)} %add_convert_fusion.3), channel_id=1, source_target_pairs={{8,0},{10,2},{16,8},{18,10},{24,16},{26,18},{28,24},{30,26},{20,28... | collective-permute-start | bytes 3145736 | tf_op jit(solution)/shard_map/ppermute | solution.py:50
  735.5 30.4 %collective-permute-start.106 = (bf16[512,2048]{1,0:T(8,128)(2,1)S(1)}, bf16[512,2048]{1,0:T(8,128)(2,1)S(1)}, u32[]{:S(2)}, u32[]{:S(2)}) collective-permute-start(bf16[512,2048]{1,0:T(8,128)(2,1)S(1)} %slice.1043), channel_id=1, source_target_pairs={{0,2},{2,0},{4,6},{6,4},{8,10},{10,8},{12,14},{14,12},{16,18},{18,... | collective-permute-start | bytes 6291464 | tf_op jit(solution)/shard_map/ppermute | solution.py:53
  735.8 30.1 %collective-permute-start.119 = (bf16[128,1536]{0,1:T(8,128)(2,1)S(1)}, bf16[128,1536]{0,1:T(8,128)(2,1)S(1)}, u32[]{:S(2)}, u32[]{:S(2)}) collective-permute-start(bf16[128,1536]{0,1:T(8,128)(2,1)S(1)} %get-tuple-element.573), channel_id=1, source_target_pairs={{8,0},{10,2},{16,8},{18,10},{24,16},{26,18},{28,24},{30,26},{20,28... | collective-permute-start | bytes 1179656 | tf_op jit(solution)/shard_map/ppermute | solution.py:50
  737.3 28.6 %collective-permute-start.120 = (bf16[128,1536]{0,1:T(8,128)(2,1)S(1)}, bf16[128,1536]{0,1:T(8,128)(2,1)S(1)}, u32[]{:S(2)}, u32[]{:S(2)}) collective-permute-start(bf16[128,1536]{0,1:T(8,128)(2,1)S(1)} %get-tuple-element.572), channel_id=1, source_target_pairs={{0,8},{2,10},{8,16},{10,18},{16,24},{18,26},{24,28},{26,30},{28,20... | collective-permute-start | bytes 1179656 | tf_op jit(solution)/shard_map/ppermute | solution.py:47
  757.7 28.8 %collective-permute-start.124 = (bf16[128,4096]{1,0:T(8,128)(2,1)S(1)}, bf16[128,4096]{1,0:T(8,128)(2,1)S(1)}, u32[]{:S(2)}, u32[]{:S(2)}) collective-permute-start(bf16[128,4096]{1,0:T(8,128)(2,1)S(1)} %add_convert_fusion), channel_id=1, source_target_pairs={{0,8},{2,10},{8,16},{10,18},{16,24},{18,26},{24,28},{26,30},{28,20... | collective-permute-start | bytes 3145736 | tf_op jit(solution)/shard_map/ppermute | solution.py:47
  758.4 30.0 %collective-permute-start.123 = (bf16[128,4096]{1,0:T(8,128)(2,1)S(1)}, bf16[128,4096]{1,0:T(8,128)(2,1)S(1)}, u32[]{:S(2)}, u32[]{:S(2)}) collective-permute-start(bf16[128,4096]{1,0:T(8,128)(2,1)S(1)} %add_convert_fusion.1), channel_id=1, source_target_pairs={{8,0},{10,2},{16,8},{18,10},{24,16},{26,18},{28,24},{30,26},{20,28... | collective-permute-start | bytes 3145736 | tf_op jit(solution)/shard_map/ppermute | solution.py:50
  791.1 49.8 %collective-permute-start.134 = (bf16[128,4096]{1,0:T(8,128)(2,1)}, bf16[128,4096]{1,0:T(8,128)(2,1)S(1)}, u32[]{:S(2)}, u32[]{:S(2)}) collective-permute-start(bf16[128,4096]{1,0:T(8,128)(2,1)} %get-tuple-element.583), channel_id=1, source_target_pairs={{0,2},{2,0},{4,6},{6,4},{8,10},{10,8},{12,14},{14,12},{16,18},{18,... | collective-permute-start | bytes 3145736 | tf_op jit(solution)/shard_map/ppermute | solution.py:53
  805.2 32.0 %collective-permute-start.127 = (bf16[128,1536]{0,1:T(8,128)(2,1)}, bf16[128,1536]{0,1:T(8,128)(2,1)S(1)}, u32[]{:S(2)}, u32[]{:S(2)}) collective-permute-start(bf16[128,1536]{0,1:T(8,128)(2,1)} %get-tuple-element.567), channel_id=1, source_target_pairs={{8,0},{10,2},{16,8},{18,10},{24,16},{26,18},{28,24},{30,26},{20,28... | collective-permute-start | bytes 1179656 | tf_op jit(solution)/shard_map/ppermute | solution.py:50
  805.8 31.4 %collective-permute-start.128 = (bf16[128,1536]{0,1:T(8,128)(2,1)}, bf16[128,1536]{0,1:T(8,128)(2,1)}, u32[]{:S(2)}, u32[]{:S(2)}) collective-permute-start(bf16[128,1536]{0,1:T(8,128)(2,1)} %get-tuple-element.566), channel_id=1, source_target_pairs={{0,8},{2,10},{8,16},{10,18},{16,24},{18,26},{24,28},{26,30},{28,20... | collective-permute-start | bytes 1179656 | tf_op jit(solution)/shard_map/ppermute | solution.py:47
  (207 other events, 3630.3 us)

commit v6 on v5

--- a/solution.py
+++ b/solution.py
@@ -187,11 +187,18 @@
     return jnp.concatenate([rows, across, beside, ring.other_core(across)], axis=0)
 
 
-def scatter_group(ring, parts, before=()):
-    quarter = parts.shape[0] // 4
-    near = parts[: 2 * quarter] + ring.other_core(parts[2 * quarter :].astype(bf16)).astype(f32)
-    near = together((near, before))[0]
-    return near[:quarter] + other_tensor(near[quarter:].astype(bf16)).astype(f32)
+def core_sum(ring, parts):
+    half = parts.shape[0] // 2
+    return parts[:half] + ring.other_core(parts[half:].astype(bf16)).astype(f32)
+
+
+def tensor_sum(rows):
+    half = rows.shape[0] // 2
+    return rows[:half] + other_tensor(rows[half:].astype(bf16)).astype(f32)
+
+
+def scatter_group(ring, parts):
+    return tensor_sum(core_sum(ring, parts))
 
 
 def copy_blocks(table, source, target):
@@ -307,16 +314,6 @@
         ),
         name=name,
     )(numbers, *arrays)
-
-
-def sum_all(ring, v):
-    v = v + other_tensor(v)
-    devices = 2 * ring.chips
-    step = 1
-    while step < devices:
-        v = v + lax.ppermute(v, "dp", [(d, d ^ step) for d in range(devices)])
-        step *= 2
-    return v
 
 
 def per_device(
@@ -482,19 +479,29 @@
     hidden = (gate * sigmoid_gate * up).astype(bf16)
     cut = width // 2
 
-    def output(proj_t, columns, before=()):
-        parts = lax.dot_general(hidden, proj_t, over_last, preferred_element_type=f32)
-        result = middle[:, columns] + scatter_group(ring, parts, before)
+    def half_sum(rows, proj_t):
+        parts = lax.dot_general(rows, proj_t, over_last, preferred_element_type=f32)
+        return core_sum(ring, parts)
+
+    def output(shared, columns):
+        result = middle[:, columns] + shared
         error = (result - own_teacher[:, columns].astype(f32)) * own_valid
         delta = error * (tokens_all / count)
-        return result, error, delta, gather_group(ring, delta.astype(bf16))
+        return result, error, delta, delta.astype(bf16)
 
     def down_grad_of(branch):
         return lax.dot_general(branch, hidden, over_rows, preferred_element_type=f32).astype(bf16)
 
-    result_far, error_far, delta_far, branch_far = output(down_far, slice(0, cut))
-    result_near, error_near, delta_near, branch_near = output(down_near, slice(cut, width), delta_far)
-    down_sums = Scatter(ring, [down_grad_of(branch_far)], None, piece)
+    half_far = half_sum(hidden, down_far)
+    half_near = half_sum(together((hidden, half_far))[0], down_near)
+    result_far, error_far, delta_far, low_far = output(tensor_sum(half_far), slice(0, cut))
+    half_near, low_far = together((half_near, low_far))
+    branch_far = gather_group(ring, low_far)
+    grad_far = down_grad_of(branch_far)
+    shared_near, branch_far, _ = together((tensor_sum(half_near), branch_far, grad_far))
+    result_near, error_near, delta_near, low_near = output(shared_near, slice(cut, width))
+    branch_near = gather_group(ring, low_near)
+    down_sums = Scatter(ring, [grad_far], None, piece)
     result = jnp.concatenate([result_far, result_near], axis=1)
     delta_result = jnp.concatenate([delta_far, delta_near], axis=1)
     squared = jnp.sum(error_far * error_far) + jnp.sum(error_near * error_near)
@@ -507,17 +514,17 @@
             delta_hidden * up * sigmoid_gate * (1.0 + gate * (1.0 - sigmoid_gate))
         ).astype(bf16)
         delta_up = (delta_hidden * gate * sigmoid_gate).astype(bf16)
-        delta_gate, delta_up = yield Held(delta_gate, delta_up)
-        near = yield Held(down_grad_of(branch_near))
+        delta_gate, delta_up, branch = yield Held(delta_gate, delta_up, branch_near)
+        near, delta_gate = yield Held(down_grad_of(branch), delta_gate)
         down_sums.parts = ([near], down_sums.parts[1])
         grad_gate = lax.dot_general(
             normed_mlp, delta_gate, over_rows, preferred_element_type=f32
         ).astype(bf16)
-        grad_gate = yield Held(grad_gate)
+        grad_gate, delta_up = yield Held(grad_gate, delta_up)
         grad_up = lax.dot_general(
             normed_mlp, delta_up, over_rows, preferred_element_type=f32
         ).astype(bf16)
-        grad_up = yield Held(grad_up)
+        grad_up, delta_gate, delta_up = yield Held(grad_up, delta_gate, delta_up)
         gate_up.append(grad_gate)
         gate_up.append(grad_up)
         parts = lax.dot_general(
@@ -593,7 +600,7 @@
             ring, lax.dot_general(delta_qkv, qkv_proj, over_last, preferred_element_type=f32)
         )
         yield ()
-        delta_normed = yield delta_normed
+        delta_normed = yield Held(delta_normed)
         gain_attn_part = jnp.sum(delta_normed * own_rows * attn_scale, axis=0)
         weighted_attn = attn_gain * delta_normed
         input_grad = (
@@ -601,16 +608,20 @@
             + attn_scale * weighted_attn
             - own_rows * attn_scale**3 * jnp.mean(own_rows * weighted_attn, axis=-1, keepdims=True)
         )
-        input_grad = reorder(input_grad.astype(bf16), to_natural)
         natural = jnp.stack([gain_mlp_part, gain_attn_part], axis=0).reshape(2, devices, piece)[
             :, to_natural
         ]
         sums = jnp.concatenate(
             [natural.reshape(2 * devices, piece), jnp.full((8, piece), squared)], axis=0
         )
-        input_grad, sums = yield input_grad, sums
-        totals = yield sum_all(ring, sums)
-        return input_grad, totals
+        input_grad, sums = yield Held(input_grad.astype(bf16), sums)
+        sums = yield Held(sums + other_tensor(sums))
+        step = 1
+        while step < devices:
+            pairs = [(d, d ^ step) for d in range(devices)]
+            sums = yield Held(sums + lax.ppermute(sums, "dp", pairs))
+            step *= 2
+        return reorder(input_grad, to_natural), sums
 
     stages = Stages(closing())
     while gate_up_sums.left:

time: 872 us -> 866 us (level)
  waiting for transfers between devices: 348 us -> 332 us
  other arithmetic: 88.3 us -> 98.1 us
    ppermute x49, waiting for transfers between devices: 155 us -> 98.1 us  [ahead(): return lax.ppermute(v, 'dp', self.up)]
    ppermute x49, waiting for transfers between devices: 99.9 us -> 122 us  [back(): return lax.ppermute(v, 'dp', self.down)]
    ppermute x49, starting transfers between devices: 52.1 us -> 68.3 us  [ahead(): return lax.ppermute(v, 'dp', self.up)]
    ppermute x49, starting transfers between devices: 50.5 us -> 35.1 us  [back(): return lax.ppermute(v, 'dp', self.down)]
    ppermute x11, waiting for transfers between devices: 81.3 us -> 91.2 us  [other_tensor(): return lax.ppermute(v, 'tensor', [(0, 1), (1, 0)])]
    unnamed x202 -> x219, local copies, waits for them, and re-layouts: 18.8 us -> 23.1 us
  transfers between devices with their start and end apart: 135 -> 135, of which waited for: 78 -> 76; matrix products, arithmetic and copies ran while one was open for 34% -> 34% of each run, Pallas kernels for 4% -> 4%
where the time goes in v6:
time: 866 us; the launch traced here: 857 us
  waiting for transfers between devices  332 us (38%)
  matrix products  156 us (18%)
  starting transfers between devices  119 us (14%)
  local copies, waits for them, and re-layouts  115 us (13%)
  other arithmetic  98.1 us (11%)
  Pallas kernels  30.7 us (4%)
    ppermute x49, waiting for transfers between devices, back(): return lax.ppermute(v, 'dp', self.down)  122 us
    ppermute x49, waiting for transfers between devices, ahead(): return lax.ppermute(v, 'dp', self.up)  98.1 us
    ppermute x11, waiting for transfers between devices, other_tensor(): return lax.ppermute(v, 'tensor', [(0, 1), (1, 0)])  91.2 us
    ppermute x49, starting transfers between devices, ahead(): return lax.ppermute(v, 'dp', self.up)  68.3 us
    dynamic_update_slice x62, local copies, waits for them, and re-layouts, store(): lax.dynamic_update_slice(self.buffers[i], rows[:self.size, a:b], (at * se...  48 us
    ppermute x49, starting transfers between devices, back(): return lax.ppermute(v, 'dp', self.down)  35.1 us
    convert_element_type x24, other arithmetic, take(): self.now = tuple(sums if self.left == 0 else [v.astype(bf16) for v in sums])  28.8 us
    unnamed x219, local copies, waits for them, and re-layouts  23.1 us
  transfers between devices with their start and end apart: 135, of which 76 were waited for; matrix products, arithmetic and copies ran while one was open for 34% of the time, Pallas kernels for 4%

profile of v6, /device:TPU:0, one launch (start us, length us, event | category | flops | bytes accessed | tf_op | source)
XLA Modules:
  0.0 857.3 jit_solution(17386971935187254234)
XLA Ops:
  177.0 7.3 fusion.2
  242.2 7.2 collective-permute-done.45
  272.1 7.7 collective-permute-done.51
  279.9 8.6 %collective-permute-done.57 = bf16[256,2048]{1,0:T(8,128)(2,1)S(1)} collective-permute-done((bf16[256,2048]{1,0:T(8,128)(2,1)S(1)}, bf16[256,2048]{1,0:T(8,128)(2,1)S(1)}, u32[]{:S(2)}, u32[]{:S(2)}) %collective-permute-start.57) | collective-permute-done | bytes 1048608 | tf_op jit(solution)/shard_map/ppermute | solution.py:57
  295.7 8.5 collective-permute-done.55
  309.5 11.1 %fusion.66 = f32[1024,2048]{1,0:T(8,128)} fusion(bf16[1024,2048]{1,0:T(8,128)(2,1)S(1)} %pad_maximum_fusion.1, bf16[2048,2048]{1,0:T(8,128)(2,1)S(1)} %constant_dynamic-update-slice_fusion.14), kind=kOutput, calls=%fused_computation.393 | convolution fusion | flops 8589934592 | bytes 20971520 | tf_op jit(solution)/shard_map/dot_general | solution.py:458
  362.9 15.3 %multiply_convert_fusion.2 = (bf16[1024,2048]{1,0:T(8,128)(2,1)S(1)}, f32[1024,2048]{1,0:T(8,128)}) fusion(f32[1024,2048]{1,0:T(8,128)} %fusion.66, bf16[1024,2048]{1,0:T(8,128)(2,1)S(1)} %pad_maximum_fusion.1, bf16[2048,2048]{1,0:T(8,128)(2,1)} %constant_dynamic-update-slice_fusion.4), kind=kOutput, calls=%fused_computation.40 | convolution fusion | flops 8602517504 | bytes 33554432 | tf_op jit(solution)/shard_map/dot_general | solution.py:477
  410.3 12.6 %collective-permute-done.71 = bf16[256,1024]{1,0:T(8,128)(2,1)S(1)} collective-permute-done((bf16[256,1024]{1,0:T(8,128)(2,1)S(1)}, bf16[256,1024]{1,0:T(8,128)(2,1)S(1)}, u32[]{:S(2)}, u32[]{:S(2)}) %collective-permute-start.71) | collective-permute-done | bytes 524320 | tf_op jit(solution)/shard_map/ppermute | solution.py:57
  423.0 9.5 %collective-permute-done.76 = bf16[256,1024]{1,0:T(8,128)(2,1)S(1)} collective-permute-done((bf16[256,1024]{1,0:T(8,128)(2,1)S(1)}, bf16[256,1024]{1,0:T(8,128)(2,1)S(1)}, u32[]{:S(2)}, u32[]{:S(2)}) %collective-permute-start.76) | collective-permute-done | bytes 524320 | tf_op jit(solution)/shard_map/ppermute | solution.py:57
  443.3 9.1 %collective-permute-done.79 = bf16[256,1024]{1,0:T(8,128)(2,1)S(1)} collective-permute-done((bf16[256,1024]{1,0:T(8,128)(2,1)S(1)}, bf16[256,1024]{1,0:T(8,128)(2,1)S(1)}, u32[]{:S(2)}, u32[]{:S(2)}) %collective-permute-start.79) | collective-permute-done | bytes 524320 | tf_op jit(solution)/shard_map/ppermute | solution.py:57
  462.6 16.3 %multiply_convert_fusion = (bf16[1024,2048]{1,0:T(8,128)(2,1)}, bf16[1024,2048]{1,0:T(8,128)(2,1)}) fusion(f32[1024,2048]{1,0:T(8,128)} %fusion.66, f32[1024,2048]{1,0:T(8,128)} %get-tuple-element.692, f32[1024,2048]{1,0:T(8,128)} %fusion.69, bf16[1024,2048]{1,0:T(8,128)(2,1)} %constant_dynamic-update-slice_fusion.18, bf16[256,1024]{1,0:T(8,128)(2,1)} %copy-done.71, ...), kind=kOutput, calls=%fused_computation.38 | convolution fusion | flops 4332716032 | bytes 39845888 | tf_op jit(solution)/shard_map/dot_general | solution.py:512
  484.0 7.4 convolution_convert_fusion.3
  498.4 11.0 %convolution_convert_fusion.1 = bf16[2048,2048]{1,0:T(8,128)(2,1)S(1)} fusion(bf16[1024,2048]{1,0:T(8,128)(2,1)S(1)} %copy-done.26, bf16[1024,2048]{1,0:T(8,128)(2,1)} %get-tuple-element.430), kind=kOutput, calls=%fused_computation.43 | convolution fusion | flops 8594128896 | bytes 16777216 | tf_op jit(solution)/shard_map/dot_general | solution.py:520
  511.9 11.0 %convolution_convert_fusion = bf16[2048,2048]{1,0:T(8,128)(2,1)S(1)} fusion(bf16[1024,2048]{1,0:T(8,128)(2,1)S(1)} %copy-done.27, bf16[1024,2048]{1,0:T(8,128)(2,1)} %get-tuple-element.431), kind=kOutput, calls=%fused_computation.42 | convolution fusion | flops 8594128896 | bytes 16777216 | tf_op jit(solution)/shard_map/dot_general | solution.py:524
  533.7 14.2 %fusion.70 = f32[1024,2048]{1,0:T(8,128)} fusion(bf16[1024,2048]{1,0:T(8,128)(2,1)S(1)} %copy-done.97, bf16[2048,2048]{1,0:T(8,128)(2,1)} %constant_dynamic-update-slice_fusion.4), kind=kOutput, calls=%fused_computation.397 | convolution fusion | flops 8589934592 | bytes 20971520 | tf_op jit(solution)/shard_map/dot_general | solution.py:532
  548.0 14.0 %convolution_add_fusion.1 = f32[1024,2048]{1,0:T(8,128)} fusion(f32[1024,2048]{1,0:T(8,128)} %fusion.70, bf16[1024,2048]{1,0:T(8,128)(2,1)} %get-tuple-element.430, bf16[2048,2048]{1,0:T(8,128)(2,1)S(1)} %bitcast.83), kind=kOutput, calls=%fused_computation.59 | convolution fusion | flops 8592031744 | bytes 29360128 | tf_op jit(solution)/shard_map/dot_general | solution.py:530
  591.3 10.1 %collective-permute-done.97 = bf16[256,2048]{1,0:T(8,128)(2,1)} collective-permute-done((bf16[256,2048]{1,0:T(8,128)(2,1)}, bf16[256,2048]{1,0:T(8,128)(2,1)}, u32[]{:S(2)}, u32[]{:S(2)}) %collective-permute-start.97) | collective-permute-done | bytes 1048608 | tf_op jit(solution)/shard_map/ppermute | solution.py:57
  620.7 16.0 %collective-permute-done.101 = bf16[256,2048]{1,0:T(8,128)(2,1)S(1)} collective-permute-done((bf16[256,2048]{1,0:T(8,128)(2,1)S(1)}, bf16[256,2048]{1,0:T(8,128)(2,1)S(1)}, u32[]{:S(2)}, u32[]{:S(2)}) %collective-permute-start.101) | collective-permute-done | bytes 1048608 | tf_op jit(solution)/shard_map/ppermute | solution.py:57
  652.3 7.9 attend_back.1
  693.9 7.6 convolution_convert_fusion.2
  703.6 11.5 %collective-permute-done.106 = bf16[128,4096]{1,0:T(8,128)(2,1)} collective-permute-done((bf16[128,4096]{1,0:T(8,128)(2,1)}, bf16[128,4096]{1,0:T(8,128)(2,1)}, u32[]{:S(2)}, u32[]{:S(2)}) %collective-permute-start.106) | collective-permute-done | bytes 1048608 | tf_op jit(solution)/shard_map/ppermute | solution.py:50
  727.1 15.8 %collective-permute-done.113 = bf16[256,2048]{1,0:T(8,128)(2,1)S(1)} collective-permute-done((bf16[256,2048]{1,0:T(8,128)(2,1)S(1)}, bf16[256,2048]{1,0:T(8,128)(2,1)S(1)}, u32[]{:S(2)}, u32[]{:S(2)}) %collective-permute-start.113) | collective-permute-done | bytes 1048608 | tf_op jit(solution)/shard_map/ppermute | solution.py:57
  765.6 22.0 %collective-permute-done.116 = bf16[128,1536]{0,1:T(8,128)(2,1)S(1)} collective-permute-done((bf16[128,1536]{0,1:T(8,128)(2,1)S(1)}, bf16[128,1536]{0,1:T(8,128)(2,1)S(1)}, u32[]{:S(2)}, u32[]{:S(2)}) %collective-permute-start.116) | collective-permute-done | bytes 393248 | tf_op jit(solution)/shard_map/ppermute | solution.py:50
  792.6 9.5 %collective-permute-done.123 = f32[40,128]{1,0:T(8,128)S(1)} collective-permute-done((f32[40,128]{1,0:T(8,128)S(1)}, f32[40,128]{1,0:T(8,128)S(1)}, u32[]{:S(2)}, u32[]{:S(2)}) %collective-permute-start.123) | collective-permute-done | bytes 20512 | tf_op jit(solution)/shard_map/ppermute | solution.py:622
  (735 shorter events, 579.5 us)
Async XLA Ops:
  3.1 34.9 %collective-permute-start = (bf16[128,2048]{1,0:T(8,128)(2,1)}, bf16[128,2048]{1,0:T(8,128)(2,1)S(1)}, u32[]{:S(2)}, u32[]{:S(2)}) collective-permute-start(bf16[128,2048]{1,0:T(8,128)(2,1)} %bitcast.1), channel_id=1, source_target_pairs={{0,2},{2,0},{4,6},{6,4},{8,10},{10,8},{12,14},{14,12},{16,18},{18,... | collective-permute-start | bytes 1572872 | tf_op jit(solution)/shard_map/ppermute | solution.py:53
  7.2 27.7 %collective-permute-start.33 = (bf16[128,2048]{1,0:T(8,128)(2,1)}, bf16[128,2048]{1,0:T(8,128)(2,1)}, u32[]{:S(2)}, u32[]{:S(2)}) collective-permute-start(bf16[128,2048]{1,0:T(8,128)(2,1)} %constant_dynamic-slice_fusion.2), channel_id=1, source_target_pairs={{0,2},{2,0},{4,6},{6,4},{8,10},{10,8},{12,14},{14,12},{16,18},{18,... | collective-permute-start | bytes 1572872 | tf_op jit(solution)/shard_map/ppermute | solution.py:53
  14.0 30.6 %collective-permute-start.5 = (bf16[144,1536]{1,0:T(8,128)(2,1)}, bf16[144,1536]{1,0:T(8,128)(2,1)}, u32[]{:S(2)}, u32[]{:S(2)}) collective-permute-start(bf16[144,1536]{1,0:T(8,128)(2,1)} %get-tuple-element.668), channel_id=1, source_target_pairs={{0,8},{2,10},{8,16},{10,18},{16,24},{18,26},{24,28},{26,30},{28,20... | collective-permute-start | bytes 1327112 | tf_op jit(solution)/shard_map/ppermute | solution.py:47
  16.6 28.0 %collective-permute-start.6 = (bf16[144,1536]{1,0:T(8,128)(2,1)}, bf16[144,1536]{1,0:T(8,128)(2,1)}, u32[]{:S(2)}, u32[]{:S(2)}) collective-permute-start(bf16[144,1536]{1,0:T(8,128)(2,1)} %get-tuple-element.667), channel_id=1, source_target_pairs={{8,0},{10,2},{16,8},{18,10},{24,16},{26,18},{28,24},{30,26},{20,28... | collective-permute-start | bytes 1327112 | tf_op jit(solution)/shard_map/ppermute | solution.py:50
  34.8 38.8 %collective-permute-start.36 = (bf16[256,2048]{1,0:T(8,128)(2,1)}, bf16[256,2048]{1,0:T(8,128)(2,1)S(1)}, u32[]{:S(2)}, u32[]{:S(2)}) collective-permute-start(bf16[256,2048]{1,0:T(8,128)(2,1)} %reorder.4), channel_id=1, source_target_pairs={{0,1},{1,0},{2,3},{3,2},{4,5},{5,4},{6,7},{7,6},{8,9},{9,8},{10,11... | collective-permute-start | bytes 3145736 | tf_op jit(solution)/shard_map/ppermute | solution.py:57
  162.6 29.9 %collective-permute-start.27 = (bf16[128,2048]{1,0:T(8,128)(2,1)S(1)}, bf16[128,2048]{1,0:T(8,128)(2,1)S(1)}, u32[]{:S(2)}, u32[]{:S(2)}) collective-permute-start(bf16[128,2048]{1,0:T(8,128)(2,1)S(1)} %collective-permute-done.23), channel_id=1, source_target_pairs={{0,8},{2,10},{8,16},{10,18},{16,24},{18,26},{24,28},{26,30},{28,20... | collective-permute-start | bytes 1572872 | tf_op jit(solution)/shard_map/ppermute | solution.py:47
  164.2 28.3 %collective-permute-start.28 = (bf16[128,2048]{1,0:T(8,128)(2,1)S(1)}, bf16[128,2048]{1,0:T(8,128)(2,1)S(1)}, u32[]{:S(2)}, u32[]{:S(2)}) collective-permute-start(bf16[128,2048]{1,0:T(8,128)(2,1)S(1)} %collective-permute-done.24), channel_id=1, source_target_pairs={{8,0},{10,2},{16,8},{18,10},{24,16},{26,18},{28,24},{30,26},{20,28... | collective-permute-start | bytes 1572872 | tf_op jit(solution)/shard_map/ppermute | solution.py:50
  293.1 29.2 %collective-permute-start.53 = (bf16[128,2048]{1,0:T(8,128)(2,1)S(1)}, bf16[128,2048]{1,0:T(8,128)(2,1)S(1)}, u32[]{:S(2)}, u32[]{:S(2)}) collective-permute-start(bf16[128,2048]{1,0:T(8,128)(2,1)S(1)} %collective-permute-done.49), channel_id=1, source_target_pairs={{0,8},{2,10},{8,16},{10,18},{16,24},{18,26},{24,28},{26,30},{28,20... | collective-permute-start | bytes 1572872 | tf_op jit(solution)/shard_map/ppermute | solution.py:47
  294.8 27.5 %collective-permute-start.54 = (bf16[128,2048]{1,0:T(8,128)(2,1)S(1)}, bf16[128,2048]{1,0:T(8,128)(2,1)S(1)}, u32[]{:S(2)}, u32[]{:S(2)}) collective-permute-start(bf16[128,2048]{1,0:T(8,128)(2,1)S(1)} %collective-permute-done.50), channel_id=1, source_target_pairs={{8,0},{10,2},{16,8},{18,10},{24,16},{26,18},{28,24},{30,26},{20,28... | collective-permute-start | bytes 1572872 | tf_op jit(solution)/shard_map/ppermute | solution.py:50
  530.6 31.3 %collective-permute-start.90 = (bf16[128,4096]{1,0:T(8,128)(2,1)S(1)}, bf16[128,4096]{1,0:T(8,128)(2,1)S(1)}, u32[]{:S(2)}, u32[]{:S(2)}) collective-permute-start(bf16[128,4096]{1,0:T(8,128)(2,1)S(1)} %pad_maximum_fusion.6), channel_id=1, source_target_pairs={{8,0},{10,2},{16,8},{18,10},{24,16},{26,18},{28,24},{30,26},{20,28... | collective-permute-start | bytes 3145736 | tf_op jit(solution)/shard_map/ppermute | solution.py:50
  533.1 28.9 %collective-permute-start.91 = (bf16[128,4096]{1,0:T(8,128)(2,1)}, bf16[128,4096]{1,0:T(8,128)(2,1)S(1)}, u32[]{:S(2)}, u32[]{:S(2)}) collective-permute-start(bf16[128,4096]{1,0:T(8,128)(2,1)} %pad_maximum_fusion.7), channel_id=1, source_target_pairs={{0,8},{2,10},{8,16},{10,18},{16,24},{18,26},{24,28},{26,30},{28,20... | collective-permute-start | bytes 3145736 | tf_op jit(solution)/shard_map/ppermute | solution.py:47
  588.9 28.2 %collective-permute-start.92 = (bf16[128,2048]{1,0:T(8,128)(2,1)S(1)}, bf16[128,2048]{1,0:T(8,128)(2,1)S(1)}, u32[]{:S(2)}, u32[]{:S(2)}) collective-permute-start(bf16[128,2048]{1,0:T(8,128)(2,1)S(1)} %get-tuple-element.638), channel_id=1, source_target_pairs={{8,0},{10,2},{16,8},{18,10},{24,16},{26,18},{28,24},{30,26},{20,28... | collective-permute-start | bytes 1572872 | tf_op jit(solution)/shard_map/ppermute | solution.py:50
  590.3 27.9 %collective-permute-start.93 = (bf16[128,2048]{1,0:T(8,128)(2,1)S(1)}, bf16[128,2048]{1,0:T(8,128)(2,1)S(1)}, u32[]{:S(2)}, u32[]{:S(2)}) collective-permute-start(bf16[128,2048]{1,0:T(8,128)(2,1)S(1)} %get-tuple-element.637), channel_id=1, source_target_pairs={{0,8},{2,10},{8,16},{10,18},{16,24},{18,26},{24,28},{26,30},{28,20... | collective-permute-start | bytes 1572872 | tf_op jit(solution)/shard_map/ppermute | solution.py:47
  686.2 30.4 %collective-permute-start.112 = (bf16[512,2048]{1,0:T(8,128)(2,1)}, bf16[512,2048]{1,0:T(8,128)(2,1)}, u32[]{:S(2)}, u32[]{:S(2)}) collective-permute-start(bf16[512,2048]{1,0:T(8,128)(2,1)} %slice.1049), channel_id=1, source_target_pairs={{0,2},{2,0},{4,6},{6,4},{8,10},{10,8},{12,14},{14,12},{16,18},{18,... | collective-permute-start | bytes 6291464 | tf_op jit(solution)/shard_map/ppermute | solution.py:53
  688.7 26.4 %collective-permute-start.106 = (bf16[128,4096]{1,0:T(8,128)(2,1)}, bf16[128,4096]{1,0:T(8,128)(2,1)}, u32[]{:S(2)}, u32[]{:S(2)}) collective-permute-start(bf16[128,4096]{1,0:T(8,128)(2,1)} %add_convert_fusion.5), channel_id=1, source_target_pairs={{8,0},{10,2},{16,8},{18,10},{24,16},{26,18},{28,24},{30,26},{20,28... | collective-permute-start | bytes 3145736 | tf_op jit(solution)/shard_map/ppermute | solution.py:50
  690.1 26.5 %collective-permute-start.107 = (bf16[128,4096]{1,0:T(8,128)(2,1)}, bf16[128,4096]{1,0:T(8,128)(2,1)}, u32[]{:S(2)}, u32[]{:S(2)}) collective-permute-start(bf16[128,4096]{1,0:T(8,128)(2,1)} %add_convert_fusion.4), channel_id=1, source_target_pairs={{0,8},{2,10},{8,16},{10,18},{16,24},{18,26},{24,28},{26,30},{28,20... | collective-permute-start | bytes 3145736 | tf_op jit(solution)/shard_map/ppermute | solution.py:47
  701.5 41.8 %collective-permute-start.110 = (bf16[128,1536]{0,1:T(8,128)(2,1)S(1)}, bf16[128,1536]{0,1:T(8,128)(2,1)S(1)}, u32[]{:S(2)}, u32[]{:S(2)}) collective-permute-start(bf16[128,1536]{0,1:T(8,128)(2,1)S(1)} %get-tuple-element.626), channel_id=1, source_target_pairs={{8,0},{10,2},{16,8},{18,10},{24,16},{26,18},{28,24},{30,26},{20,28... | collective-permute-start | bytes 1179656 | tf_op jit(solution)/shard_map/ppermute | solution.py:50
  702.9 40.5 %collective-permute-start.111 = (bf16[128,1536]{0,1:T(8,128)(2,1)S(1)}, bf16[128,1536]{0,1:T(8,128)(2,1)S(1)}, u32[]{:S(2)}, u32[]{:S(2)}) collective-permute-start(bf16[128,1536]{0,1:T(8,128)(2,1)S(1)} %get-tuple-element.625), channel_id=1, source_target_pairs={{0,8},{2,10},{8,16},{10,18},{16,24},{18,26},{24,28},{26,30},{28,20... | collective-permute-start | bytes 1179656 | tf_op jit(solution)/shard_map/ppermute | solution.py:47
  722.7 31.8 %collective-permute-start.108 = (bf16[128,4096]{1,0:T(8,128)(2,1)}, bf16[128,4096]{1,0:T(8,128)(2,1)}, u32[]{:S(2)}, u32[]{:S(2)}) collective-permute-start(bf16[128,4096]{1,0:T(8,128)(2,1)} %add_convert_fusion.3), channel_id=1, source_target_pairs={{8,0},{10,2},{16,8},{18,10},{24,16},{26,18},{28,24},{30,26},{20,28... | collective-permute-start | bytes 3145736 | tf_op jit(solution)/shard_map/ppermute | solution.py:50
  725.8 28.7 %collective-permute-start.109 = (bf16[128,4096]{1,0:T(8,128)(2,1)}, bf16[128,4096]{1,0:T(8,128)(2,1)}, u32[]{:S(2)}, u32[]{:S(2)}) collective-permute-start(bf16[128,4096]{1,0:T(8,128)(2,1)} %add_convert_fusion.2), channel_id=1, source_target_pairs={{0,8},{2,10},{8,16},{10,18},{16,24},{18,26},{24,28},{26,30},{28,20... | collective-permute-start | bytes 3145736 | tf_op jit(solution)/shard_map/ppermute | solution.py:47
  756.1 35.8 %collective-permute-start.114 = (bf16[128,4096]{1,0:T(8,128)(2,1)S(1)}, bf16[128,4096]{1,0:T(8,128)(2,1)S(1)}, u32[]{:S(2)}, u32[]{:S(2)}) collective-permute-start(bf16[128,4096]{1,0:T(8,128)(2,1)S(1)} %add_convert_fusion.1), channel_id=1, source_target_pairs={{8,0},{10,2},{16,8},{18,10},{24,16},{26,18},{28,24},{30,26},{20,28... | collective-permute-start | bytes 3145736 | tf_op jit(solution)/shard_map/ppermute | solution.py:50
  758.4 33.6 %collective-permute-start.115 = (bf16[128,4096]{1,0:T(8,128)(2,1)S(1)}, bf16[128,4096]{1,0:T(8,128)(2,1)S(1)}, u32[]{:S(2)}, u32[]{:S(2)}) collective-permute-start(bf16[128,4096]{1,0:T(8,128)(2,1)S(1)} %add_convert_fusion), channel_id=1, source_target_pairs={{0,8},{2,10},{8,16},{10,18},{16,24},{18,26},{24,28},{26,30},{28,20... | collective-permute-start | bytes 3145736 | tf_op jit(solution)/shard_map/ppermute | solution.py:47
  759.8 27.8 %collective-permute-start.116 = (bf16[128,1536]{0,1:T(8,128)(2,1)S(1)}, bf16[128,1536]{0,1:T(8,128)(2,1)S(1)}, u32[]{:S(2)}, u32[]{:S(2)}) collective-permute-start(bf16[128,1536]{0,1:T(8,128)(2,1)S(1)} %copy-done.72), channel_id=1, source_target_pairs={{8,0},{10,2},{16,8},{18,10},{24,16},{26,18},{28,24},{30,26},{20,28... | collective-permute-start | bytes 1179656 | tf_op jit(solution)/shard_map/ppermute | solution.py:50
  760.5 29.1 %collective-permute-start.117 = (bf16[128,1536]{0,1:T(8,128)(2,1)S(1)}, bf16[128,1536]{0,1:T(8,128)(2,1)S(1)}, u32[]{:S(2)}, u32[]{:S(2)}) collective-permute-start(bf16[128,1536]{0,1:T(8,128)(2,1)S(1)} %get-tuple-element.623), channel_id=1, source_target_pairs={{0,8},{2,10},{8,16},{10,18},{16,24},{18,26},{24,28},{26,30},{28,20... | collective-permute-start | bytes 1179656 | tf_op jit(solution)/shard_map/ppermute | solution.py:47
  (213 other events, 2998.7 us)

commit v7 on v6

--- a/solution.py
+++ b/solution.py
@@ -495,10 +495,9 @@
     half_far = half_sum(hidden, down_far)
     half_near = half_sum(together((hidden, half_far))[0], down_near)
     result_far, error_far, delta_far, low_far = output(tensor_sum(half_far), slice(0, cut))
-    half_near, low_far = together((half_near, low_far))
     branch_far = gather_group(ring, low_far)
     grad_far = down_grad_of(branch_far)
-    shared_near, branch_far, _ = together((tensor_sum(half_near), branch_far, grad_far))
+    shared_near = together((tensor_sum(half_near), low_far))[0]
     result_near, error_near, delta_near, low_near = output(shared_near, slice(cut, width))
     branch_near = gather_group(ring, low_near)
     down_sums = Scatter(ring, [grad_far], None, piece)
@@ -507,7 +506,8 @@
     squared = jnp.sum(error_far * error_far) + jnp.sum(error_near * error_near)
 
     def backward():
-        first = jnp.dot(branch_far, down_far, preferred_element_type=f32)
+        branch = together((branch_far, grad_far))[0]
+        first = jnp.dot(branch, down_far, preferred_element_type=f32)
         first = yield Held(first)
         delta_hidden = first + jnp.dot(branch_near, down_near, preferred_element_type=f32)
         delta_gate = (
@@ -527,11 +527,17 @@
         grad_up, delta_gate, delta_up = yield Held(grad_up, delta_gate, delta_up)
         gate_up.append(grad_gate)
         gate_up.append(grad_up)
-        parts = lax.dot_general(
-            delta_gate, gate_proj, over_last, preferred_element_type=f32
-        ) + lax.dot_general(delta_up, up_proj, over_last, preferred_element_type=f32)
-        parts = yield Held(parts)
-        delta_normed_mlp = scatter_group(ring, parts)
+        def from_hidden(rows):
+            return lax.dot_general(
+                delta_gate[rows], gate_proj, over_last, preferred_element_type=f32
+            ) + lax.dot_general(delta_up[rows], up_proj, over_last, preferred_element_type=f32)
+
+        given, delta_gate, delta_up = yield Held(
+            from_hidden(slice(slots, None)).astype(bf16), delta_gate, delta_up
+        )
+        taken = ring.other_core(given)
+        parts = yield Held(from_hidden(slice(0, slots)))
+        delta_normed_mlp = tensor_sum(parts + taken.astype(f32))
         placed = together((result.astype(bf16), parts))[0]
         activations = yield Held(reorder(placed, to_natural))
         delta_normed_mlp = yield Held(delta_normed_mlp)
@@ -585,9 +591,8 @@
         stages.turn(down_sums)
     gate_up_sums = Scatter(ring, *halves(gate_up), piece)
     while down_sums.left:
-        if gate_up_sums.left:
-            stages.turn(gate_up_sums, down_sums)
         stages.turn(down_sums, gate_up_sums)
+        stages.turn(gate_up_sums, down_sums)
     down_grad = whole(*finish(down_sums)).T
     while not stages.over and gate_up_sums.left:
         down_grad = stages.turn(gate_up_sums, None, down_grad)
@@ -597,8 +602,16 @@
 
     def closing():
         delta_normed = scatter_group(
-            ring, lax.dot_general(delta_qkv, qkv_proj, over_last, preferred_element_type=f32)
-        )
+            ring,
+            lax.dot_general(
+                together((delta_qkv, attn_sums.now))[0],
+                qkv_proj,
+                over_last,
+                preferred_element_type=f32,
+            ),
+        )
+        yield ()
+        yield ()
         yield ()
         delta_normed = yield Held(delta_normed)
         gain_attn_part = jnp.sum(delta_normed * own_rows * attn_scale, axis=0)
@@ -614,8 +627,8 @@
         sums = jnp.concatenate(
             [natural.reshape(2 * devices, piece), jnp.full((8, piece), squared)], axis=0
         )
-        input_grad, sums = yield Held(input_grad.astype(bf16), sums)
-        sums = yield Held(sums + other_tensor(sums))
+        input_grad = input_grad.astype(bf16)
+        sums, input_grad = yield Held(sums + other_tensor(sums), input_grad)
         step = 1
         while step < devices:
             pairs = [(d, d ^ step) for d in range(devices)]

time: 866 us -> 834 us (0.963)
  waiting for transfers between devices: 332 us -> 297 us
    ppermute x11, waiting for transfers between devices: 91.2 us -> 51.7 us  [other_tensor(): return lax.ppermute(v, 'tensor', [(0, 1), (1, 0)])]
    dot_general x4 -> x6, matrix products: 39.5 us -> 46.9 us  [the longest x2 21.2 us: from_hidden(): lax.dot_general(delta_up[rows], up_proj, over_last, preferred_element_typ...]
    unnamed x219 -> x204, local copies, waits for them, and re-layouts: 23.1 us -> 22.7 us
  transfers between devices with their start and end apart: 135 -> 135, of which waited for: 76 -> 74; matrix products, arithmetic and copies ran while one was open for 34% -> 38% of each run, Pallas kernels for 4% -> 4%
where the time goes in v7:
time: 834 us; the launch traced here: 826 us
  waiting for transfers between devices  297 us (36%)
  matrix products  162 us (19%)
  starting transfers between devices  123 us (15%)
  local copies, waits for them, and re-layouts  110 us (13%)
  other arithmetic  95.1 us (11%)
  Pallas kernels  30.7 us (4%)
    ppermute x49, waiting for transfers between devices, back(): return lax.ppermute(v, 'dp', self.down)  125 us
    ppermute x49, waiting for transfers between devices, ahead(): return lax.ppermute(v, 'dp', self.up)  101 us
    ppermute x49, starting transfers between devices, ahead(): return lax.ppermute(v, 'dp', self.up)  69.6 us
    ppermute x11, waiting for transfers between devices, other_tensor(): return lax.ppermute(v, 'tensor', [(0, 1), (1, 0)])  51.7 us
    dynamic_update_slice x62, local copies, waits for them, and re-layouts, store(): lax.dynamic_update_slice(self.buffers[i], rows[:self.size, a:b], (at * se...  48.2 us
    ppermute x49, starting transfers between devices, back(): return lax.ppermute(v, 'dp', self.down)  35.3 us
    convert_element_type x24, other arithmetic, take(): self.now = tuple(sums if self.left == 0 else [v.astype(bf16) for v in sums])  26.6 us
    unnamed x204, local copies, waits for them, and re-layouts  22.7 us
  transfers between devices with their start and end apart: 135, of which 74 were waited for; matrix products, arithmetic and copies ran while one was open for 38% of the time, Pallas kernels for 4%

profile of v7, /device:TPU:0, one launch (start us, length us, event | category | flops | bytes accessed | tf_op | source)
XLA Modules:
  0.0 825.6 jit_solution(8377737865029529254)
XLA Ops:
  177.0 7.3 fusion.2
  242.4 7.1 collective-permute-done.45
  271.1 7.7 collective-permute-done.51
  278.8 8.6 %collective-permute-done.57 = bf16[256,2048]{1,0:T(8,128)(2,1)S(1)} collective-permute-done((bf16[256,2048]{1,0:T(8,128)(2,1)S(1)}, bf16[256,2048]{1,0:T(8,128)(2,1)S(1)}, u32[]{:S(2)}, u32[]{:S(2)}) %collective-permute-start.57) | collective-permute-done | bytes 1048608 | tf_op jit(solution)/shard_map/ppermute | solution.py:57
  294.6 8.4 %collective-permute-done.55 = bf16[128,2048]{1,0:T(8,128)(2,1)S(1)} collective-permute-done((bf16[128,2048]{1,0:T(8,128)(2,1)S(1)}, bf16[128,2048]{1,0:T(8,128)(2,1)S(1)}, u32[]{:S(2)}, u32[]{:S(2)}) %collective-permute-start.55) | collective-permute-done | bytes 524320 | tf_op jit(solution)/shard_map/ppermute | solution.py:47
  308.4 11.0 %fusion.71 = f32[1024,2048]{1,0:T(8,128)} fusion(bf16[1024,2048]{1,0:T(8,128)(2,1)S(1)} %pad_maximum_fusion.1, bf16[2048,2048]{1,0:T(8,128)(2,1)S(1)} %constant_dynamic-update-slice_fusion.14), kind=kOutput, calls=%fused_computation.397 | convolution fusion | flops 8589934592 | bytes 20971520 | tf_op jit(solution)/shard_map/dot_general | solution.py:458
  361.8 15.0 %multiply_convert_fusion.2 = (bf16[1024,2048]{1,0:T(8,128)(2,1)S(1)}, f32[1024,2048]{1,0:T(8,128)}) fusion(f32[1024,2048]{1,0:T(8,128)} %fusion.71, bf16[1024,2048]{1,0:T(8,128)(2,1)S(1)} %pad_maximum_fusion.1, bf16[2048,2048]{1,0:T(8,128)(2,1)} %constant_dynamic-update-slice_fusion.4), kind=kOutput, calls=%fused_computation.40 | convolution fusion | flops 8602517504 | bytes 33554432 | tf_op jit(solution)/shard_map/dot_general | solution.py:477
  410.1 9.8 %collective-permute-done.70 = bf16[256,1024]{1,0:T(8,128)(2,1)S(1)} collective-permute-done((bf16[256,1024]{1,0:T(8,128)(2,1)S(1)}, bf16[256,1024]{1,0:T(8,128)(2,1)S(1)}, u32[]{:S(2)}, u32[]{:S(2)}) %collective-permute-start.70) | collective-permute-done | bytes 524320 | tf_op jit(solution)/shard_map/ppermute | solution.py:57
  420.0 9.7 %collective-permute-done.78 = bf16[256,1024]{1,0:T(8,128)(2,1)S(1)} collective-permute-done((bf16[256,1024]{1,0:T(8,128)(2,1)S(1)}, bf16[256,1024]{1,0:T(8,128)(2,1)S(1)}, u32[]{:S(2)}, u32[]{:S(2)}) %collective-permute-start.78) | collective-permute-done | bytes 524320 | tf_op jit(solution)/shard_map/ppermute | solution.py:57
  444.6 6.6 fusion.73
  456.4 16.4 %multiply_convert_fusion = (bf16[1024,2048]{1,0:T(8,128)(2,1)}, bf16[1024,2048]{1,0:T(8,128)(2,1)}) fusion(f32[1024,2048]{1,0:T(8,128)} %fusion.71, f32[1024,2048]{1,0:T(8,128)} %get-tuple-element.704, f32[1024,2048]{1,0:T(8,128)} %fusion.73, bf16[1024,2048]{1,0:T(8,128)(2,1)} %constant_dynamic-update-slice_fusion.18, bf16[256,1024]{1,0:T(8,128)(2,1)} %copy-done.68, ...), kind=kOutput, calls=%fused_computation.38 | convolution fusion | flops 4332716032 | bytes 39845888 | tf_op jit(solution)/shard_map/dot_general | solution.py:512
  477.8 7.0 convolution_convert_fusion.3
  491.2 11.2 %convolution_convert_fusion.1 = bf16[2048,2048]{1,0:T(8,128)(2,1)S(1)} fusion(bf16[1024,2048]{1,0:T(8,128)(2,1)S(1)} %copy-done.21, bf16[1024,2048]{1,0:T(8,128)(2,1)} %get-tuple-element.440), kind=kOutput, calls=%fused_computation.43 | convolution fusion | flops 8594128896 | bytes 16777216 | tf_op jit(solution)/shard_map/dot_general | solution.py:520
  505.1 11.0 %convolution_convert_fusion = bf16[2048,2048]{1,0:T(8,128)(2,1)S(1)} fusion(bf16[1024,2048]{1,0:T(8,128)(2,1)S(1)} %copy-done.22, bf16[1024,2048]{1,0:T(8,128)(2,1)} %get-tuple-element.441), kind=kOutput, calls=%fused_computation.42 | convolution fusion | flops 8594128896 | bytes 16777216 | tf_op jit(solution)/shard_map/dot_general | solution.py:524
  526.9 10.7 %fusion.14 = f32[512,2048]{1,0:T(8,128)} fusion(bf16[2048,2048]{1,0:T(8,128)(2,1)} %constant_dynamic-update-slice_fusion.4, bf16[1024,2048]{1,0:T(8,128)(2,1)} %get-tuple-element.441), kind=kOutput, calls=%fused_computation.108 | convolution fusion | flops 4294967296 | bytes 14680064 | tf_op jit(solution)/shard_map/dot_general | solution.py:533
  541.9 7.4 add_convert_fusion
  554.2 10.5 %fusion.11 = f32[512,2048]{1,0:T(8,128)} fusion(bf16[2048,2048]{1,0:T(8,128)(2,1)} %constant_dynamic-update-slice_fusion.4, bf16[1024,2048]{1,0:T(8,128)(2,1)} %get-tuple-element.441), kind=kOutput, calls=%fused_computation.105 | convolution fusion | flops 4294967296 | bytes 14680064 | tf_op jit(solution)/shard_map/dot_general | solution.py:533
  564.7 7.1 convolution_add_fusion.1
  592.2 14.5 %collective-permute-done.98 = bf16[256,2048]{1,0:T(8,128)(2,1)} collective-permute-done((bf16[256,2048]{1,0:T(8,128)(2,1)}, bf16[256,2048]{1,0:T(8,128)(2,1)}, u32[]{:S(2)}, u32[]{:S(2)}) %collective-permute-start.98) | collective-permute-done | bytes 1048608 | tf_op jit(solution)/shard_map/ppermute | solution.py:57
  620.2 16.2 %collective-permute-done.99 = bf16[128,4096]{1,0:T(8,128)(2,1)S(1)} collective-permute-done((bf16[128,4096]{1,0:T(8,128)(2,1)S(1)}, bf16[128,4096]{1,0:T(8,128)(2,1)S(1)}, u32[]{:S(2)}, u32[]{:S(2)}) %collective-permute-start.99) | collective-permute-done | bytes 1048608 | tf_op jit(solution)/shard_map/ppermute | solution.py:50
  646.7 16.2 %collective-permute-done.101 = bf16[128,4096]{1,0:T(8,128)(2,1)S(1)} collective-permute-done((bf16[128,4096]{1,0:T(8,128)(2,1)S(1)}, bf16[128,4096]{1,0:T(8,128)(2,1)S(1)}, u32[]{:S(2)}, u32[]{:S(2)}) %collective-permute-start.101) | collective-permute-done | bytes 1048608 | tf_op jit(solution)/shard_map/ppermute | solution.py:50
  672.3 7.9 attend_back.1
  697.5 7.4 convolution_convert_fusion.2
  729.3 16.9 %collective-permute-done.114 = bf16[128,4096]{1,0:T(8,128)(2,1)S(1)} collective-permute-done((bf16[128,4096]{1,0:T(8,128)(2,1)S(1)}, bf16[128,4096]{1,0:T(8,128)(2,1)S(1)}, u32[]{:S(2)}, u32[]{:S(2)}) %collective-permute-start.114) | collective-permute-done | bytes 1048608 | tf_op jit(solution)/shard_map/ppermute | solution.py:50
  (721 shorter events, 567.2 us)
Async XLA Ops:
  3.1 34.8 %collective-permute-start.1 = (bf16[128,2048]{1,0:T(8,128)(2,1)}, bf16[128,2048]{1,0:T(8,128)(2,1)S(1)}, u32[]{:S(2)}, u32[]{:S(2)}) collective-permute-start(bf16[128,2048]{1,0:T(8,128)(2,1)} %bitcast.8), channel_id=1, source_target_pairs={{0,2},{2,0},{4,6},{6,4},{8,10},{10,8},{12,14},{14,12},{16,18},{18,... | collective-permute-start | bytes 1572872 | tf_op jit(solution)/shard_map/ppermute | solution.py:53
  7.2 27.6 %collective-permute-start.33 = (bf16[128,2048]{1,0:T(8,128)(2,1)}, bf16[128,2048]{1,0:T(8,128)(2,1)}, u32[]{:S(2)}, u32[]{:S(2)}) collective-permute-start(bf16[128,2048]{1,0:T(8,128)(2,1)} %constant_dynamic-slice_fusion.2), channel_id=1, source_target_pairs={{0,2},{2,0},{4,6},{6,4},{8,10},{10,8},{12,14},{14,12},{16,18},{18,... | collective-permute-start | bytes 1572872 | tf_op jit(solution)/shard_map/ppermute | solution.py:53
  14.0 30.6 %collective-permute-start.5 = (bf16[144,1536]{1,0:T(8,128)(2,1)}, bf16[144,1536]{1,0:T(8,128)(2,1)}, u32[]{:S(2)}, u32[]{:S(2)}) collective-permute-start(bf16[144,1536]{1,0:T(8,128)(2,1)} %get-tuple-element.680), channel_id=1, source_target_pairs={{0,8},{2,10},{8,16},{10,18},{16,24},{18,26},{24,28},{26,30},{28,20... | collective-permute-start | bytes 1327112 | tf_op jit(solution)/shard_map/ppermute | solution.py:47
  16.6 28.0 %collective-permute-start.6 = (bf16[144,1536]{1,0:T(8,128)(2,1)}, bf16[144,1536]{1,0:T(8,128)(2,1)}, u32[]{:S(2)}, u32[]{:S(2)}) collective-permute-start(bf16[144,1536]{1,0:T(8,128)(2,1)} %get-tuple-element.679), channel_id=1, source_target_pairs={{8,0},{10,2},{16,8},{18,10},{24,16},{26,18},{28,24},{30,26},{20,28... | collective-permute-start | bytes 1327112 | tf_op jit(solution)/shard_map/ppermute | solution.py:50
  34.8 38.9 %collective-permute-start.36 = (bf16[256,2048]{1,0:T(8,128)(2,1)}, bf16[256,2048]{1,0:T(8,128)(2,1)S(1)}, u32[]{:S(2)}, u32[]{:S(2)}) collective-permute-start(bf16[256,2048]{1,0:T(8,128)(2,1)} %reorder.4), channel_id=1, source_target_pairs={{0,1},{1,0},{2,3},{3,2},{4,5},{5,4},{6,7},{7,6},{8,9},{9,8},{10,11... | collective-permute-start | bytes 3145736 | tf_op jit(solution)/shard_map/ppermute | solution.py:57
  162.5 30.0 %collective-permute-start.27 = (bf16[128,2048]{1,0:T(8,128)(2,1)S(1)}, bf16[128,2048]{1,0:T(8,128)(2,1)S(1)}, u32[]{:S(2)}, u32[]{:S(2)}) collective-permute-start(bf16[128,2048]{1,0:T(8,128)(2,1)S(1)} %collective-permute-done.23), channel_id=1, source_target_pairs={{0,8},{2,10},{8,16},{10,18},{16,24},{18,26},{24,28},{26,30},{28,20... | collective-permute-start | bytes 1572872 | tf_op jit(solution)/shard_map/ppermute | solution.py:47
  164.1 28.4 %collective-permute-start.28 = (bf16[128,2048]{1,0:T(8,128)(2,1)S(1)}, bf16[128,2048]{1,0:T(8,128)(2,1)S(1)}, u32[]{:S(2)}, u32[]{:S(2)}) collective-permute-start(bf16[128,2048]{1,0:T(8,128)(2,1)S(1)} %collective-permute-done.24), channel_id=1, source_target_pairs={{8,0},{10,2},{16,8},{18,10},{24,16},{26,18},{28,24},{30,26},{20,28... | collective-permute-start | bytes 1572872 | tf_op jit(solution)/shard_map/ppermute | solution.py:50
  292.1 29.1 %collective-permute-start.53 = (bf16[128,2048]{1,0:T(8,128)(2,1)S(1)}, bf16[128,2048]{1,0:T(8,128)(2,1)S(1)}, u32[]{:S(2)}, u32[]{:S(2)}) collective-permute-start(bf16[128,2048]{1,0:T(8,128)(2,1)S(1)} %collective-permute-done.49), channel_id=1, source_target_pairs={{0,8},{2,10},{8,16},{10,18},{16,24},{18,26},{24,28},{26,30},{28,20... | collective-permute-start | bytes 1572872 | tf_op jit(solution)/shard_map/ppermute | solution.py:47
  293.7 27.4 %collective-permute-start.54 = (bf16[128,2048]{1,0:T(8,128)(2,1)S(1)}, bf16[128,2048]{1,0:T(8,128)(2,1)S(1)}, u32[]{:S(2)}, u32[]{:S(2)}) collective-permute-start(bf16[128,2048]{1,0:T(8,128)(2,1)S(1)} %collective-permute-done.50), channel_id=1, source_target_pairs={{8,0},{10,2},{16,8},{18,10},{24,16},{26,18},{28,24},{30,26},{20,28... | collective-permute-start | bytes 1572872 | tf_op jit(solution)/shard_map/ppermute | solution.py:50
  521.2 28.1 %collective-permute-start.88 = (bf16[128,2048]{1,0:T(8,128)(2,1)}, bf16[128,2048]{1,0:T(8,128)(2,1)}, u32[]{:S(2)}, u32[]{:S(2)}) collective-permute-start(bf16[128,2048]{1,0:T(8,128)(2,1)} %get-tuple-element.652), channel_id=1, source_target_pairs={{8,0},{10,2},{16,8},{18,10},{24,16},{26,18},{28,24},{30,26},{20,28... | collective-permute-start | bytes 1572872 | tf_op jit(solution)/shard_map/ppermute | solution.py:50
  522.7 26.6 %collective-permute-start.89 = (bf16[128,2048]{1,0:T(8,128)(2,1)}, bf16[128,2048]{1,0:T(8,128)(2,1)}, u32[]{:S(2)}, u32[]{:S(2)}) collective-permute-start(bf16[128,2048]{1,0:T(8,128)(2,1)} %get-tuple-element.651), channel_id=1, source_target_pairs={{0,8},{2,10},{8,16},{10,18},{16,24},{18,26},{24,28},{26,30},{28,20... | collective-permute-start | bytes 1572872 | tf_op jit(solution)/shard_map/ppermute | solution.py:47
  538.7 33.2 %collective-permute-start.92 = (bf16[128,4096]{1,0:T(8,128)(2,1)}, bf16[128,4096]{1,0:T(8,128)(2,1)}, u32[]{:S(2)}, u32[]{:S(2)}) collective-permute-start(bf16[128,4096]{1,0:T(8,128)(2,1)} %pad_maximum_fusion.7), channel_id=1, source_target_pairs={{8,0},{10,2},{16,8},{18,10},{24,16},{26,18},{28,24},{30,26},{20,28... | collective-permute-start | bytes 3145736 | tf_op jit(solution)/shard_map/ppermute | solution.py:50
  541.2 30.7 %collective-permute-start.93 = (bf16[128,4096]{1,0:T(8,128)(2,1)}, bf16[128,4096]{1,0:T(8,128)(2,1)}, u32[]{:S(2)}, u32[]{:S(2)}) collective-permute-start(bf16[128,4096]{1,0:T(8,128)(2,1)} %pad_maximum_fusion.8), channel_id=1, source_target_pairs={{0,8},{2,10},{8,16},{10,18},{16,24},{18,26},{24,28},{26,30},{28,20... | collective-permute-start | bytes 3145736 | tf_op jit(solution)/shard_map/ppermute | solution.py:47
  552.2 38.0 %collective-permute-start.90 = (bf16[128,2048]{1,0:T(8,128)(2,1)}, bf16[128,2048]{1,0:T(8,128)(2,1)}, u32[]{:S(2)}, u32[]{:S(2)}) collective-permute-start(bf16[128,2048]{1,0:T(8,128)(2,1)} %get-tuple-element.650), channel_id=1, source_target_pairs={{8,0},{10,2},{16,8},{18,10},{24,16},{26,18},{28,24},{30,26},{20,28... | collective-permute-start | bytes 1572872 | tf_op jit(solution)/shard_map/ppermute | solution.py:50
  553.7 36.5 %collective-permute-start.91 = (bf16[128,2048]{1,0:T(8,128)(2,1)}, bf16[128,2048]{1,0:T(8,128)(2,1)}, u32[]{:S(2)}, u32[]{:S(2)}) collective-permute-start(bf16[128,2048]{1,0:T(8,128)(2,1)} %get-tuple-element.649), channel_id=1, source_target_pairs={{0,8},{2,10},{8,16},{10,18},{16,24},{18,26},{24,28},{26,30},{28,20... | collective-permute-start | bytes 1572872 | tf_op jit(solution)/shard_map/ppermute | solution.py:47
  580.9 25.8 %collective-permute-start.98 = (bf16[256,2048]{1,0:T(8,128)(2,1)}, bf16[256,2048]{1,0:T(8,128)(2,1)}, u32[]{:S(2)}, u32[]{:S(2)}) collective-permute-start(bf16[256,2048]{1,0:T(8,128)(2,1)} %slice.1067), channel_id=1, source_target_pairs={{0,1},{1,0},{2,3},{3,2},{4,5},{5,4},{6,7},{7,6},{8,9},{9,8},{10,11... | collective-permute-start | bytes 3145736 | tf_op jit(solution)/shard_map/ppermute | solution.py:57
  584.0 25.6 %collective-permute-start.95 = (bf16[128,4096]{1,0:T(8,128)(2,1)}, bf16[128,4096]{1,0:T(8,128)(2,1)}, u32[]{:S(2)}, u32[]{:S(2)}) collective-permute-start(bf16[128,4096]{1,0:T(8,128)(2,1)} %add_convert_fusion.12), channel_id=1, source_target_pairs={{8,0},{10,2},{16,8},{18,10},{24,16},{26,18},{28,24},{30,26},{20,28... | collective-permute-start | bytes 3145736 | tf_op jit(solution)/shard_map/ppermute | solution.py:50
  592.2 50.4 %collective-permute-start.94 = (bf16[128,2048]{1,0:T(8,128)(2,1)S(1)}, bf16[128,2048]{1,0:T(8,128)(2,1)S(1)}, u32[]{:S(2)}, u32[]{:S(2)}) collective-permute-start(bf16[128,2048]{1,0:T(8,128)(2,1)S(1)} %select_convert_fusion.1), channel_id=1, source_target_pairs={{0,2},{2,0},{4,6},{6,4},{8,10},{10,8},{12,14},{14,12},{16,18},{18,... | collective-permute-start | bytes 1572872 | tf_op jit(solution)/shard_map/ppermute | solution.py:53
  620.2 25.8 %collective-permute-start.104 = (bf16[256,2048]{1,0:T(8,128)(2,1)S(1)}, bf16[256,2048]{1,0:T(8,128)(2,1)S(1)}, u32[]{:S(2)}, u32[]{:S(2)}) collective-permute-start(bf16[256,2048]{1,0:T(8,128)(2,1)S(1)} %get-tuple-element.575), channel_id=1, source_target_pairs={{0,2},{2,0},{4,6},{6,4},{8,10},{10,8},{12,14},{14,12},{16,18},{18,... | collective-permute-start | bytes 3145736 | tf_op jit(solution)/shard_map/ppermute | solution.py:53
  693.5 25.2 %collective-permute-start.111 = (bf16[128,4096]{1,0:T(8,128)(2,1)}, bf16[128,4096]{1,0:T(8,128)(2,1)}, u32[]{:S(2)}, u32[]{:S(2)}) collective-permute-start(bf16[128,4096]{1,0:T(8,128)(2,1)} %add_convert_fusion.3), channel_id=1, source_target_pairs={{0,8},{2,10},{8,16},{10,18},{16,24},{18,26},{24,28},{26,30},{28,20... | collective-permute-start | bytes 3145736 | tf_op jit(solution)/shard_map/ppermute | solution.py:47
  720.2 26.1 %collective-permute-start.114 = (bf16[128,4096]{1,0:T(8,128)(2,1)S(1)}, bf16[128,4096]{1,0:T(8,128)(2,1)S(1)}, u32[]{:S(2)}, u32[]{:S(2)}) collective-permute-start(bf16[128,4096]{1,0:T(8,128)(2,1)S(1)} %add_convert_fusion.2), channel_id=1, source_target_pairs={{8,0},{10,2},{16,8},{18,10},{24,16},{26,18},{28,24},{30,26},{20,28... | collective-permute-start | bytes 3145736 | tf_op jit(solution)/shard_map/ppermute | solution.py:50
  722.4 26.1 %collective-permute-start.115 = (bf16[128,4096]{1,0:T(8,128)(2,1)S(1)}, bf16[128,4096]{1,0:T(8,128)(2,1)S(1)}, u32[]{:S(2)}, u32[]{:S(2)}) collective-permute-start(bf16[128,4096]{1,0:T(8,128)(2,1)S(1)} %add_convert_fusion.1), channel_id=1, source_target_pairs={{0,8},{2,10},{8,16},{10,18},{16,24},{18,26},{24,28},{26,30},{28,20... | collective-permute-start | bytes 3145736 | tf_op jit(solution)/shard_map/ppermute | solution.py:47
  724.6 26.7 %collective-permute-start.112 = (bf16[128,1536]{0,1:T(8,128)(2,1)S(1)}, bf16[128,1536]{0,1:T(8,128)(2,1)S(1)}, u32[]{:S(2)}, u32[]{:S(2)}) collective-permute-start(bf16[128,1536]{0,1:T(8,128)(2,1)S(1)} %get-tuple-element.634), channel_id=1, source_target_pairs={{8,0},{10,2},{16,8},{18,10},{24,16},{26,18},{28,24},{30,26},{20,28... | collective-permute-start | bytes 1179656 | tf_op jit(solution)/shard_map/ppermute | solution.py:50
  725.3 28.4 %collective-permute-start.113 = (bf16[128,1536]{0,1:T(8,128)(2,1)S(1)}, bf16[128,1536]{0,1:T(8,128)(2,1)S(1)}, u32[]{:S(2)}, u32[]{:S(2)}) collective-permute-start(bf16[128,1536]{0,1:T(8,128)(2,1)S(1)} %get-tuple-element.633), channel_id=1, source_target_pairs={{0,8},{2,10},{8,16},{10,18},{16,24},{18,26},{24,28},{26,30},{28,20... | collective-permute-start | bytes 1179656 | tf_op jit(solution)/shard_map/ppermute | solution.py:47
  (207 other events, 3065.8 us)

commit v8 on v7

--- a/solution.py
+++ b/solution.py
@@ -169,11 +169,10 @@
 
     def turn(self, lane, other=None, extra=()):
         if isinstance(self.value, Held):
-            extra, value = turn(lane, other, extra, self.value.value)
+            value = turn(lane, other, (), (self.value.value, extra))[1][0]
         else:
-            (value, extra), _ = turn(lane, other, (self.value, extra))
+            value = turn(lane, other, self.value, extra)[0]
         self.advance(value)
-        return extra
 
     def finish(self):
         while not self.over:
@@ -181,8 +180,8 @@
         return self.result
 
 
-def gather_group(ring, rows):
-    across = other_tensor(rows)
+def gather_group(ring, rows, before=()):
+    across = together((other_tensor(rows), before))[0]
     beside = ring.other_core(rows)
     return jnp.concatenate([rows, across, beside, ring.other_core(across)], axis=0)
 
@@ -495,10 +494,10 @@
     half_far = half_sum(hidden, down_far)
     half_near = half_sum(together((hidden, half_far))[0], down_near)
     result_far, error_far, delta_far, low_far = output(tensor_sum(half_far), slice(0, cut))
-    branch_far = gather_group(ring, low_far)
-    grad_far = down_grad_of(branch_far)
     shared_near = together((tensor_sum(half_near), low_far))[0]
     result_near, error_near, delta_near, low_near = output(shared_near, slice(cut, width))
+    branch_far = gather_group(ring, low_far, low_near)
+    grad_far = down_grad_of(branch_far)
     branch_near = gather_group(ring, low_near)
     down_sums = Scatter(ring, [grad_far], None, piece)
     result = jnp.concatenate([result_far, result_near], axis=1)
@@ -514,9 +513,7 @@
             delta_hidden * up * sigmoid_gate * (1.0 + gate * (1.0 - sigmoid_gate))
         ).astype(bf16)
         delta_up = (delta_hidden * gate * sigmoid_gate).astype(bf16)
-        delta_gate, delta_up, branch = yield Held(delta_gate, delta_up, branch_near)
-        near, delta_gate = yield Held(down_grad_of(branch), delta_gate)
-        down_sums.parts = ([near], down_sums.parts[1])
+        delta_gate, delta_up = yield Held(delta_gate, delta_up)
         grad_gate = lax.dot_general(
             normed_mlp, delta_gate, over_rows, preferred_element_type=f32
         ).astype(bf16)
@@ -524,9 +521,8 @@
         grad_up = lax.dot_general(
             normed_mlp, delta_up, over_rows, preferred_element_type=f32
         ).astype(bf16)
-        grad_up, delta_gate, delta_up = yield Held(grad_up, delta_gate, delta_up)
-        gate_up.append(grad_gate)
-        gate_up.append(grad_up)
+        gate_up.extend([grad_gate, grad_up])
+        delta_gate, delta_up = yield Held(delta_gate, delta_up)
         def from_hidden(rows):
             return lax.dot_general(
                 delta_gate[rows], gate_proj, over_last, preferred_element_type=f32
@@ -587,15 +583,18 @@
 
     gate_up = []
     stages = Stages(backward())
-    for k in range(5):
+    for k in range(3):
         stages.turn(down_sums)
     gate_up_sums = Scatter(ring, *halves(gate_up), piece)
+    grad_near = down_grad_of(together((branch_near, gate_up_sums.now))[0])
+    down_sums.parts = ([grad_near], down_sums.parts[1])
+    stages.turn(down_sums, gate_up_sums)
     while down_sums.left:
+        stages.turn(gate_up_sums, down_sums)
         stages.turn(down_sums, gate_up_sums)
-        stages.turn(gate_up_sums, down_sums)
     down_grad = whole(*finish(down_sums)).T
     while not stages.over and gate_up_sums.left:
-        down_grad = stages.turn(gate_up_sums, None, down_grad)
+        stages.turn(gate_up_sums, None, down_grad)
     assert stages.over
     activations, gain_mlp_part, delta_middle, delta_qkv, attn_grads = stages.finish()
     attn_sums = Scatter(ring, *halves(attn_grads), piece)
@@ -627,18 +626,18 @@
         sums = jnp.concatenate(
             [natural.reshape(2 * devices, piece), jnp.full((8, piece), squared)], axis=0
         )
-        input_grad = input_grad.astype(bf16)
-        sums, input_grad = yield Held(sums + other_tensor(sums), input_grad)
+        sums, input_grad = yield Held(sums + other_tensor(sums), input_grad.astype(bf16))
+        input_grad = reorder(input_grad, to_natural)
         step = 1
         while step < devices:
             pairs = [(d, d ^ step) for d in range(devices)]
-            sums = yield Held(sums + lax.ppermute(sums, "dp", pairs))
+            sums, _ = yield Held(sums + lax.ppermute(sums, "dp", pairs), input_grad)
             step *= 2
-        return reorder(input_grad, to_natural), sums
+        return input_grad, sums
 
     stages = Stages(closing())
     while gate_up_sums.left:
-        down_grad = stages.turn(gate_up_sums, attn_sums, down_grad)
+        stages.turn(gate_up_sums, attn_sums, down_grad)
         stages.turn(attn_sums, gate_up_sums)
     kept, taken = finish(gate_up_sums)
     gate_width = w_gate.shape[1] // 2
@@ -646,7 +645,7 @@
     up_grad = whole(kept[:, gate_width:], taken[:, gate_width:])
     stages.turn(attn_sums)
     while attn_sums.left:
-        gate_grad, up_grad = stages.turn(attn_sums, None, (gate_grad, up_grad))
+        stages.turn(attn_sums, None, (gate_grad, up_grad))
     input_grad, totals = stages.finish()
     gain_mlp_grad = lax.dynamic_slice_in_dim(totals, me, 1, 0)[0]
     gain_attn_grad = lax.dynamic_slice_in_dim(totals, devices + me, 1, 0)[0]

time: 834 us -> 851 us (1.020)
  other arithmetic: 95.1 us -> 117 us
    ppermute x11, waiting for transfers between devices: 51.7 us -> 77.6 us  [other_tensor(): return lax.ppermute(v, 'tensor', [(0, 1), (1, 0)])]
    ppermute x49, waiting for transfers between devices: 125 us -> 102 us  [back(): return lax.ppermute(v, 'dp', self.down)]
    convert_element_type x24, other arithmetic: 26.6 us -> 35.6 us  [take(): self.now = tuple(sums if self.left == 0 else [v.astype(bf16) for v in sums])]
    unnamed x204 -> x174, local copies, waits for them, and re-layouts: 22.7 us -> 16.8 us
  transfers between devices with their start and end apart: 135 -> 135, of which waited for: 74 -> 66; matrix products, arithmetic and copies ran while one was open for 38% -> 40% of each run, Pallas kernels for 4% -> 4%
where the time goes in v8:
time: 851 us; the launch traced here: 843 us
  waiting for transfers between devices  301 us (35%)
  matrix products  165 us (19%)
  starting transfers between devices  121 us (14%)
  other arithmetic  117 us (14%)
  local copies, waits for them, and re-layouts  102 us (12%)
  Pallas kernels  30.7 us (4%)
    ppermute x49, waiting for transfers between devices, back(): return lax.ppermute(v, 'dp', self.down)  102 us
    ppermute x49, waiting for transfers between devices, ahead(): return lax.ppermute(v, 'dp', self.up)  101 us
    ppermute x11, waiting for transfers between devices, other_tensor(): return lax.ppermute(v, 'tensor', [(0, 1), (1, 0)])  77.6 us
    ppermute x49, starting transfers between devices, ahead(): return lax.ppermute(v, 'dp', self.up)  65 us
    dynamic_update_slice x62, local copies, waits for them, and re-layouts, store(): lax.dynamic_update_slice(self.buffers[i], rows[:self.size, a:b], (at * se...  44.2 us
    ppermute x49, starting transfers between devices, back(): return lax.ppermute(v, 'dp', self.down)  37.2 us
    convert_element_type x24, other arithmetic, take(): self.now = tuple(sums if self.left == 0 else [v.astype(bf16) for v in sums])  35.6 us
    dot_general x2, matrix products, from_hidden(): lax.dot_general(delta_up[rows], up_proj, over_last, preferred_element_typ...  19.8 us
  transfers between devices with their start and end apart: 135, of which 66 were waited for; matrix products, arithmetic and copies ran while one was open for 40% of the time, Pallas kernels for 4%

profile of v8, /device:TPU:0, one launch (start us, length us, event | category | flops | bytes accessed | tf_op | source)
XLA Modules:
  0.0 843.2 jit_solution(3341875345738954608)
XLA Ops:
  96.6 15.4 %collective-permute-done.12 = bf16[128,2048]{1,0:T(8,128)(2,1)S(1)} collective-permute-done((bf16[128,2048]{1,0:T(8,128)(2,1)S(1)}, bf16[128,2048]{1,0:T(8,128)(2,1)S(1)}, u32[]{:S(2)}, u32[]{:S(2)}) %collective-permute-start.12) | collective-permute-done | bytes 524320 | tf_op jit(solution)/shard_map/ppermute | solution.py:50
  119.1 7.7 collective-permute-done.15
  243.7 10.8 %collective-permute-done.39 = bf16[128,2048]{1,0:T(8,128)(2,1)S(1)} collective-permute-done((bf16[128,2048]{1,0:T(8,128)(2,1)}, bf16[128,2048]{1,0:T(8,128)(2,1)S(1)}, u32[]{:S(2)}, u32[]{:S(2)}) %collective-permute-start.39) | collective-permute-done | bytes 524320 | tf_op jit(solution)/shard_map/ppermute | solution.py:47
  279.0 8.4 collective-permute-done.51
  315.5 11.1 %fusion.72 = f32[1024,2048]{1,0:T(8,128)} fusion(bf16[1024,2048]{1,0:T(8,128)(2,1)S(1)} %pad_maximum_fusion.1, bf16[2048,2048]{1,0:T(8,128)(2,1)S(1)} %constant_dynamic-update-slice_fusion.14), kind=kOutput, calls=%fused_computation.397 | convolution fusion | flops 8589934592 | bytes 20971520 | tf_op jit(solution)/shard_map/dot_general | solution.py:457
  368.5 15.3 %multiply_convert_fusion.2 = (bf16[1024,2048]{1,0:T(8,128)(2,1)S(1)}, f32[1024,2048]{1,0:T(8,128)}) fusion(f32[1024,2048]{1,0:T(8,128)} %fusion.72, bf16[1024,2048]{1,0:T(8,128)(2,1)S(1)} %pad_maximum_fusion.1, bf16[2048,2048]{1,0:T(8,128)(2,1)} %constant_dynamic-update-slice_fusion.4), kind=kOutput, calls=%fused_computation.40 | convolution fusion | flops 8602517504 | bytes 33554432 | tf_op jit(solution)/shard_map/dot_general | solution.py:476
  409.8 10.6 %collective-permute-done.69 = bf16[256,1024]{1,0:T(8,128)(2,1)S(1)} collective-permute-done((bf16[256,1024]{1,0:T(8,128)(2,1)S(1)}, bf16[256,1024]{1,0:T(8,128)(2,1)S(1)}, u32[]{:S(2)}, u32[]{:S(2)}) %collective-permute-start.69) | collective-permute-done | bytes 524320 | tf_op jit(solution)/shard_map/ppermute | solution.py:57
  423.0 8.7 %collective-permute-done.72 = bf16[256,1024]{1,0:T(8,128)(2,1)S(1)} collective-permute-done((bf16[256,1024]{1,0:T(8,128)(2,1)S(1)}, bf16[256,1024]{1,0:T(8,128)(2,1)S(1)}, u32[]{:S(2)}, u32[]{:S(2)}) %collective-permute-start.72) | collective-permute-done | bytes 524320 | tf_op jit(solution)/shard_map/ppermute | solution.py:57
  434.2 8.1 collective-permute-done.70
  446.7 7.4 convolution_convert_fusion.4
  473.6 16.5 %multiply_convert_fusion = (bf16[1024,2048]{1,0:T(8,128)(2,1)}, bf16[1024,2048]{1,0:T(8,128)(2,1)}) fusion(f32[1024,2048]{1,0:T(8,128)} %fusion.72, f32[1024,2048]{1,0:T(8,128)} %get-tuple-element.663, f32[1024,2048]{1,0:T(8,128)} %fusion.75, bf16[1024,2048]{1,0:T(8,128)(2,1)} %constant_dynamic-update-slice_fusion.18, bf16[256,1024]{1,0:T(8,128)(2,1)} %copy-done.58, ...), kind=kOutput, calls=%fused_computation.38 | convolution fusion | flops 4332716032 | bytes 39845888 | tf_op jit(solution)/shard_map/dot_general | solution.py:511
  495.4 12.4 %convolution_convert_fusion.1 = bf16[2048,2048]{1,0:T(8,128)(2,1)S(1)} fusion(bf16[1024,2048]{1,0:T(8,128)(2,1)} %copy-done.18, bf16[1024,2048]{1,0:T(8,128)(2,1)} %get-tuple-element.413), kind=kOutput, calls=%fused_computation.43 | convolution fusion | flops 8594128896 | bytes 16777216 | tf_op jit(solution)/shard_map/dot_general | solution.py:517
  510.3 11.1 %convolution_convert_fusion = bf16[2048,2048]{1,0:T(8,128)(2,1)S(1)} fusion(bf16[1024,2048]{1,0:T(8,128)(2,1)S(1)} %copy-done.19, bf16[1024,2048]{1,0:T(8,128)(2,1)} %get-tuple-element.414), kind=kOutput, calls=%fused_computation.42 | convolution fusion | flops 8594128896 | bytes 16777216 | tf_op jit(solution)/shard_map/dot_general | solution.py:521
  542.2 10.4 %fusion.14 = f32[512,2048]{1,0:T(8,128)} fusion(bf16[2048,2048]{1,0:T(8,128)(2,1)} %constant_dynamic-update-slice_fusion.4, bf16[1024,2048]{1,0:T(8,128)(2,1)S(1)} %copy-done.75), kind=kOutput, calls=%fused_computation.108 | convolution fusion | flops 4294967296 | bytes 14680064 | tf_op jit(solution)/shard_map/dot_general | solution.py:529
  552.5 8.0 add_convert_fusion
  568.3 9.4 %fusion.11 = f32[512,2048]{1,0:T(8,128)} fusion(bf16[2048,2048]{1,0:T(8,128)(2,1)} %constant_dynamic-update-slice_fusion.4, bf16[1024,2048]{1,0:T(8,128)(2,1)S(1)} %copy-done.76), kind=kOutput, calls=%fused_computation.103 | convolution fusion | flops 4294967296 | bytes 14680064 | tf_op jit(solution)/shard_map/dot_general | solution.py:529
  577.7 8.5 %convolution_add_fusion.1 = f32[512,2048]{1,0:T(8,128)} fusion(f32[512,2048]{1,0:T(8,128)} %fusion.11, bf16[2048,2048]{1,0:T(8,128)(2,1)S(1)} %bitcast.82, bf16[1024,2048]{1,0:T(8,128)(2,1)} %get-tuple-element.413), kind=kOutput, calls=%fused_computation.62 | convolution fusion | flops 4296015872 | bytes 18874368 | tf_op jit(solution)/shard_map/dot_general | solution.py:527
  607.6 16.2 %collective-permute-done.97 = bf16[256,2048]{1,0:T(8,128)(2,1)S(1)} collective-permute-done((bf16[256,2048]{1,0:T(8,128)(2,1)S(1)}, bf16[256,2048]{1,0:T(8,128)(2,1)S(1)}, u32[]{:S(2)}, u32[]{:S(2)}) %collective-permute-start.97) | collective-permute-done | bytes 1048608 | tf_op jit(solution)/shard_map/ppermute | solution.py:57
  636.4 18.3 %collective-permute-done.102 = bf16[256,2048]{1,0:T(8,128)(2,1)} collective-permute-done((bf16[256,2048]{1,0:T(8,128)(2,1)}, bf16[256,2048]{1,0:T(8,128)(2,1)}, u32[]{:S(2)}, u32[]{:S(2)}) %collective-permute-start.102) | collective-permute-done | bytes 1048608 | tf_op jit(solution)/shard_map/ppermute | solution.py:57
  669.8 7.9 attend_back.1
  694.9 7.4 convolution_convert_fusion.2
  730.4 15.4 %collective-permute-done.108 = bf16[128,4096]{1,0:T(8,128)(2,1)S(1)} collective-permute-done((bf16[128,4096]{1,0:T(8,128)(2,1)S(1)}, bf16[128,4096]{1,0:T(8,128)(2,1)S(1)}, u32[]{:S(2)}, u32[]{:S(2)}) %collective-permute-start.108) | collective-permute-done | bytes 1048608 | tf_op jit(solution)/shard_map/ppermute | solution.py:50
  791.8 9.3 %collective-permute-done.124 = f32[40,128]{1,0:T(8,128)S(1)} collective-permute-done((f32[40,128]{1,0:T(8,128)S(1)}, f32[40,128]{1,0:T(8,128)S(1)}, u32[]{:S(2)}, u32[]{:S(2)}) %collective-permute-start.124) | collective-permute-done | bytes 20512 | tf_op jit(solution)/shard_map/ppermute | solution.py:634
  816.6 7.5 collective-permute-done.131
  (691 shorter events, 575.0 us)
Async XLA Ops:
  2.6 31.9 %collective-permute-start.33 = (bf16[128,2048]{1,0:T(8,128)(2,1)}, bf16[128,2048]{1,0:T(8,128)(2,1)}, u32[]{:S(2)}, u32[]{:S(2)}) collective-permute-start(bf16[128,2048]{1,0:T(8,128)(2,1)} %constant_dynamic-slice_fusion.2), channel_id=1, source_target_pairs={{0,2},{2,0},{4,6},{6,4},{8,10},{10,8},{12,14},{14,12},{16,18},{18,... | collective-permute-start | bytes 1572872 | tf_op jit(solution)/shard_map/ppermute | solution.py:53
  8.8 28.8 %collective-permute-start.1 = (bf16[128,2048]{1,0:T(8,128)(2,1)}, bf16[128,2048]{1,0:T(8,128)(2,1)}, u32[]{:S(2)}, u32[]{:S(2)}) collective-permute-start(bf16[128,2048]{1,0:T(8,128)(2,1)} %bitcast.8), channel_id=1, source_target_pairs={{0,2},{2,0},{4,6},{6,4},{8,10},{10,8},{12,14},{14,12},{16,18},{18,... | collective-permute-start | bytes 1572872 | tf_op jit(solution)/shard_map/ppermute | solution.py:53
  60.3 33.1 %collective-permute-start.37 = (bf16[256,2048]{1,0:T(8,128)(2,1)S(1)}, bf16[256,2048]{1,0:T(8,128)(2,1)S(1)}, u32[]{:S(2)}, u32[]{:S(2)}) collective-permute-start(bf16[256,2048]{1,0:T(8,128)(2,1)S(1)} %copy-done.3), channel_id=1, source_target_pairs={{0,2},{2,0},{4,6},{6,4},{8,10},{10,8},{12,14},{14,12},{16,18},{18,... | collective-permute-start | bytes 3145736 | tf_op jit(solution)/shard_map/ppermute | solution.py:53
  169.8 30.0 %collective-permute-start.27 = (bf16[128,2048]{1,0:T(8,128)(2,1)S(1)}, bf16[128,2048]{1,0:T(8,128)(2,1)S(1)}, u32[]{:S(2)}, u32[]{:S(2)}) collective-permute-start(bf16[128,2048]{1,0:T(8,128)(2,1)S(1)} %collective-permute-done.23), channel_id=1, source_target_pairs={{0,8},{2,10},{8,16},{10,18},{16,24},{18,26},{24,28},{26,30},{28,20... | collective-permute-start | bytes 1572872 | tf_op jit(solution)/shard_map/ppermute | solution.py:47
  171.3 28.5 %collective-permute-start.28 = (bf16[128,2048]{1,0:T(8,128)(2,1)S(1)}, bf16[128,2048]{1,0:T(8,128)(2,1)S(1)}, u32[]{:S(2)}, u32[]{:S(2)}) collective-permute-start(bf16[128,2048]{1,0:T(8,128)(2,1)S(1)} %collective-permute-done.24), channel_id=1, source_target_pairs={{8,0},{10,2},{16,8},{18,10},{24,16},{26,18},{28,24},{30,26},{20,28... | collective-permute-start | bytes 1572872 | tf_op jit(solution)/shard_map/ppermute | solution.py:50
  228.8 29.3 %collective-permute-start.45 = (bf16[128,2048]{1,0:T(8,128)(2,1)}, bf16[128,2048]{1,0:T(8,128)(2,1)S(1)}, u32[]{:S(2)}, u32[]{:S(2)}) collective-permute-start(bf16[128,2048]{1,0:T(8,128)(2,1)} %collective-permute-done.41), channel_id=1, source_target_pairs={{0,8},{2,10},{8,16},{10,18},{16,24},{18,26},{24,28},{26,30},{28,20... | collective-permute-start | bytes 1572872 | tf_op jit(solution)/shard_map/ppermute | solution.py:47
  508.2 29.0 %collective-permute-start.86 = (bf16[128,2048]{1,0:T(8,128)(2,1)S(1)}, bf16[128,2048]{1,0:T(8,128)(2,1)S(1)}, u32[]{:S(2)}, u32[]{:S(2)}) collective-permute-start(bf16[128,2048]{1,0:T(8,128)(2,1)S(1)} %get-tuple-element.615), channel_id=1, source_target_pairs={{8,0},{10,2},{16,8},{18,10},{24,16},{26,18},{28,24},{30,26},{20,28... | collective-permute-start | bytes 1572872 | tf_op jit(solution)/shard_map/ppermute | solution.py:50
  529.3 31.3 %collective-permute-start.84 = (bf16[128,4096]{1,0:T(8,128)(2,1)}, bf16[128,4096]{1,0:T(8,128)(2,1)}, u32[]{:S(2)}, u32[]{:S(2)}) collective-permute-start(bf16[128,4096]{1,0:T(8,128)(2,1)} %pad_maximum_fusion.7), channel_id=1, source_target_pairs={{8,0},{10,2},{16,8},{18,10},{24,16},{26,18},{28,24},{30,26},{20,28... | collective-permute-start | bytes 3145736 | tf_op jit(solution)/shard_map/ppermute | solution.py:50
  530.9 29.6 %collective-permute-start.85 = (bf16[128,4096]{1,0:T(8,128)(2,1)}, bf16[128,4096]{1,0:T(8,128)(2,1)}, u32[]{:S(2)}, u32[]{:S(2)}) collective-permute-start(bf16[128,4096]{1,0:T(8,128)(2,1)} %pad_maximum_fusion.8), channel_id=1, source_target_pairs={{0,8},{2,10},{8,16},{10,18},{16,24},{18,26},{24,28},{26,30},{28,20... | collective-permute-start | bytes 3145736 | tf_op jit(solution)/shard_map/ppermute | solution.py:47
  540.1 46.0 %collective-permute-start.90 = (bf16[128,2048]{1,0:T(8,128)(2,1)}, bf16[128,2048]{1,0:T(8,128)(2,1)}, u32[]{:S(2)}, u32[]{:S(2)}) collective-permute-start(bf16[128,2048]{1,0:T(8,128)(2,1)} %get-tuple-element.613), channel_id=1, source_target_pairs={{8,0},{10,2},{16,8},{18,10},{24,16},{26,18},{28,24},{30,26},{20,28... | collective-permute-start | bytes 1572872 | tf_op jit(solution)/shard_map/ppermute | solution.py:50
  540.7 45.4 %collective-permute-start.91 = (bf16[128,2048]{1,0:T(8,128)(2,1)}, bf16[128,2048]{1,0:T(8,128)(2,1)}, u32[]{:S(2)}, u32[]{:S(2)}) collective-permute-start(bf16[128,2048]{1,0:T(8,128)(2,1)} %get-tuple-element.612), channel_id=1, source_target_pairs={{0,8},{2,10},{8,16},{10,18},{16,24},{18,26},{24,28},{26,30},{28,20... | collective-permute-start | bytes 1572872 | tf_op jit(solution)/shard_map/ppermute | solution.py:47
  563.5 31.5 %collective-permute-start.88 = (bf16[128,4096]{1,0:T(8,128)(2,1)}, bf16[128,4096]{1,0:T(8,128)(2,1)}, u32[]{:S(2)}, u32[]{:S(2)}) collective-permute-start(bf16[128,4096]{1,0:T(8,128)(2,1)} %add_convert_fusion.12), channel_id=1, source_target_pairs={{8,0},{10,2},{16,8},{18,10},{24,16},{26,18},{28,24},{30,26},{20,28... | collective-permute-start | bytes 3145736 | tf_op jit(solution)/shard_map/ppermute | solution.py:50
  588.8 35.3 %collective-permute-start.94 = (bf16[128,2048]{1,0:T(8,128)(2,1)}, bf16[128,2048]{1,0:T(8,128)(2,1)}, u32[]{:S(2)}, u32[]{:S(2)}) collective-permute-start(bf16[128,2048]{1,0:T(8,128)(2,1)} %get-tuple-element.611), channel_id=1, source_target_pairs={{8,0},{10,2},{16,8},{18,10},{24,16},{26,18},{28,24},{30,26},{20,28... | collective-permute-start | bytes 1572872 | tf_op jit(solution)/shard_map/ppermute | solution.py:50
  589.4 34.8 %collective-permute-start.95 = (bf16[128,2048]{1,0:T(8,128)(2,1)}, bf16[128,2048]{1,0:T(8,128)(2,1)}, u32[]{:S(2)}, u32[]{:S(2)}) collective-permute-start(bf16[128,2048]{1,0:T(8,128)(2,1)} %get-tuple-element.610), channel_id=1, source_target_pairs={{0,8},{2,10},{8,16},{10,18},{16,24},{18,26},{24,28},{26,30},{28,20... | collective-permute-start | bytes 1572872 | tf_op jit(solution)/shard_map/ppermute | solution.py:47
  602.7 33.6 %collective-permute-start.92 = (bf16[128,4096]{1,0:T(8,128)(2,1)}, bf16[128,4096]{1,0:T(8,128)(2,1)}, u32[]{:S(2)}, u32[]{:S(2)}) collective-permute-start(bf16[128,4096]{1,0:T(8,128)(2,1)} %add_convert_fusion.10), channel_id=1, source_target_pairs={{8,0},{10,2},{16,8},{18,10},{24,16},{26,18},{28,24},{30,26},{20,28... | collective-permute-start | bytes 3145736 | tf_op jit(solution)/shard_map/ppermute | solution.py:50
  606.0 30.4 %collective-permute-start.93 = (bf16[128,4096]{1,0:T(8,128)(2,1)}, bf16[128,4096]{1,0:T(8,128)(2,1)}, u32[]{:S(2)}, u32[]{:S(2)}) collective-permute-start(bf16[128,4096]{1,0:T(8,128)(2,1)} %add_convert_fusion.9), channel_id=1, source_target_pairs={{0,8},{2,10},{8,16},{10,18},{16,24},{18,26},{24,28},{26,30},{28,20... | collective-permute-start | bytes 3145736 | tf_op jit(solution)/shard_map/ppermute | solution.py:47
  634.3 29.8 %collective-permute-start.100 = (bf16[128,2048]{1,0:T(8,128)(2,1)}, bf16[128,2048]{1,0:T(8,128)(2,1)S(1)}, u32[]{:S(2)}, u32[]{:S(2)}) collective-permute-start(bf16[128,2048]{1,0:T(8,128)(2,1)} %get-tuple-element.609), channel_id=1, source_target_pairs={{8,0},{10,2},{16,8},{18,10},{24,16},{26,18},{28,24},{30,26},{20,28... | collective-permute-start | bytes 1572872 | tf_op jit(solution)/shard_map/ppermute | solution.py:50
  635.1 29.0 %collective-permute-start.101 = (bf16[128,2048]{1,0:T(8,128)(2,1)}, bf16[128,2048]{1,0:T(8,128)(2,1)S(1)}, u32[]{:S(2)}, u32[]{:S(2)}) collective-permute-start(bf16[128,2048]{1,0:T(8,128)(2,1)} %get-tuple-element.608), channel_id=1, source_target_pairs={{0,8},{2,10},{8,16},{10,18},{16,24},{18,26},{24,28},{26,30},{28,20... | collective-permute-start | bytes 1572872 | tf_op jit(solution)/shard_map/ppermute | solution.py:47
  657.5 29.9 %collective-permute-start.98 = (bf16[128,4096]{1,0:T(8,128)(2,1)}, bf16[128,4096]{1,0:T(8,128)(2,1)S(1)}, u32[]{:S(2)}, u32[]{:S(2)}) collective-permute-start(bf16[128,4096]{1,0:T(8,128)(2,1)} %add_convert_fusion.8), channel_id=1, source_target_pairs={{8,0},{10,2},{16,8},{18,10},{24,16},{26,18},{28,24},{30,26},{20,28... | collective-permute-start | bytes 3145736 | tf_op jit(solution)/shard_map/ppermute | solution.py:50
  719.0 28.7 %collective-permute-start.109 = (bf16[128,4096]{1,0:T(8,128)(2,1)S(1)}, bf16[128,4096]{1,0:T(8,128)(2,1)S(1)}, u32[]{:S(2)}, u32[]{:S(2)}) collective-permute-start(bf16[128,4096]{1,0:T(8,128)(2,1)S(1)} %add_convert_fusion.3), channel_id=1, source_target_pairs={{0,8},{2,10},{8,16},{10,18},{16,24},{18,26},{24,28},{26,30},{28,20... | collective-permute-start | bytes 3145736 | tf_op jit(solution)/shard_map/ppermute | solution.py:47
  725.4 28.7 %collective-permute-start.114 = (bf16[128,1536]{0,1:T(8,128)(2,1)S(1)}, bf16[128,1536]{0,1:T(8,128)(2,1)S(1)}, u32[]{:S(2)}, u32[]{:S(2)}) collective-permute-start(bf16[128,1536]{0,1:T(8,128)(2,1)S(1)} %get-tuple-element.595), channel_id=1, source_target_pairs={{8,0},{10,2},{16,8},{18,10},{24,16},{26,18},{28,24},{30,26},{20,28... | collective-permute-start | bytes 1179656 | tf_op jit(solution)/shard_map/ppermute | solution.py:50
  725.9 30.2 %collective-permute-start.115 = (bf16[128,1536]{0,1:T(8,128)(2,1)S(1)}, bf16[128,1536]{0,1:T(8,128)(2,1)S(1)}, u32[]{:S(2)}, u32[]{:S(2)}) collective-permute-start(bf16[128,1536]{0,1:T(8,128)(2,1)S(1)} %get-tuple-element.594), channel_id=1, source_target_pairs={{0,8},{2,10},{8,16},{10,18},{16,24},{18,26},{24,28},{26,30},{28,20... | collective-permute-start | bytes 1179656 | tf_op jit(solution)/shard_map/ppermute | solution.py:47
  757.2 30.7 %collective-permute-start.119 = (bf16[128,1536]{0,1:T(8,128)(2,1)}, bf16[128,1536]{0,1:T(8,128)(2,1)S(1)}, u32[]{:S(2)}, u32[]{:S(2)}) collective-permute-start(bf16[128,1536]{0,1:T(8,128)(2,1)} %get-tuple-element.593), channel_id=1, source_target_pairs={{8,0},{10,2},{16,8},{18,10},{24,16},{26,18},{28,24},{30,26},{20,28... | collective-permute-start | bytes 1179656 | tf_op jit(solution)/shard_map/ppermute | solution.py:50
  757.6 30.3 %collective-permute-start.120 = (bf16[128,1536]{0,1:T(8,128)(2,1)}, bf16[128,1536]{0,1:T(8,128)(2,1)}, u32[]{:S(2)}, u32[]{:S(2)}) collective-permute-start(bf16[128,1536]{0,1:T(8,128)(2,1)} %get-tuple-element.592), channel_id=1, source_target_pairs={{0,8},{2,10},{8,16},{10,18},{16,24},{18,26},{24,28},{26,30},{28,20... | collective-permute-start | bytes 1179656 | tf_op jit(solution)/shard_map/ppermute | solution.py:47
  (192 other events, 3036.7 us)

commit v9 on v8

--- a/solution.py
+++ b/solution.py
@@ -402,6 +402,8 @@
     group_rows = gather_group(ring, own_input)
     for k in range(hops):
         turn(attn_weights, gate_weights)
+        if k == hops - 2:
+            group_rows = together((group_rows, attn_weights.now))[0]
         turn(gate_weights, attn_weights)
     up_weights = Gather(
         ring, "up_rows", *together((both_rows([w_up]), attn_weights.now))[0], piece
@@ -494,10 +496,10 @@
     half_far = half_sum(hidden, down_far)
     half_near = half_sum(together((hidden, half_far))[0], down_near)
     result_far, error_far, delta_far, low_far = output(tensor_sum(half_far), slice(0, cut))
+    branch_far = gather_group(ring, low_far)
+    grad_far = down_grad_of(branch_far)
     shared_near = together((tensor_sum(half_near), low_far))[0]
     result_near, error_near, delta_near, low_near = output(shared_near, slice(cut, width))
-    branch_far = gather_group(ring, low_far, low_near)
-    grad_far = down_grad_of(branch_far)
     branch_near = gather_group(ring, low_near)
     down_sums = Scatter(ring, [grad_far], None, piece)
     result = jnp.concatenate([result_far, result_near], axis=1)
@@ -533,10 +535,11 @@
         )
         taken = ring.other_core(given)
         parts = yield Held(from_hidden(slice(0, slots)))
-        delta_normed_mlp = tensor_sum(parts + taken.astype(f32))
-        placed = together((result.astype(bf16), parts))[0]
-        activations = yield Held(reorder(placed, to_natural))
-        delta_normed_mlp = yield Held(delta_normed_mlp)
+        parts = parts + taken.astype(f32)
+        delta_normed_mlp = tensor_sum(parts)
+        activations = reorder(together((result.astype(bf16), parts))[0], to_natural)
+        yield ()
+        delta_normed_mlp, activations = yield Held(delta_normed_mlp, activations)
         gain_mlp_part = jnp.sum(delta_normed_mlp * middle * mlp_scale, axis=0)
         weighted_mlp = mlp_gain * delta_normed_mlp
         delta_middle = (
@@ -545,6 +548,7 @@
             - middle * mlp_scale**3 * jnp.mean(middle * weighted_mlp, axis=-1, keepdims=True)
         )
         attn_low_rows = gather_group(ring, delta_middle.astype(bf16))
+        yield ()
         yield ()
         attn_low_rows = yield Held(attn_low_rows)
         grad_out_t = lax.dot_general(attn_low_rows, mixed, over_rows, preferred_element_type=f32)
@@ -589,9 +593,12 @@
     grad_near = down_grad_of(together((branch_near, gate_up_sums.now))[0])
     down_sums.parts = ([grad_near], down_sums.parts[1])
     stages.turn(down_sums, gate_up_sums)
-    while down_sums.left:
+    while down_sums.left > 1:
         stages.turn(gate_up_sums, down_sums)
         stages.turn(down_sums, gate_up_sums)
+    stages.turn(gate_up_sums, down_sums)
+    stages.turn(gate_up_sums, down_sums)
+    stages.turn(down_sums, gate_up_sums)
     down_grad = whole(*finish(down_sums)).T
     while not stages.over and gate_up_sums.left:
         stages.turn(gate_up_sums, None, down_grad)

time: 851 us -> 833 us (0.979)
  waiting for transfers between devices: 301 us -> 277 us
    ppermute x49, waiting for transfers between devices: 101 us -> 84.8 us  [ahead(): return lax.ppermute(v, 'dp', self.up)]
    ppermute x11, waiting for transfers between devices: 77.6 us -> 65.7 us  [other_tensor(): return lax.ppermute(v, 'tensor', [(0, 1), (1, 0)])]
    unnamed x174 -> x188, local copies, waits for them, and re-layouts: 16.8 us -> 20.2 us
  transfers between devices with their start and end apart: 135 -> 135, of which waited for: 66 -> 71; matrix products, arithmetic and copies ran while one was open for 40% -> 41% of each run, Pallas kernels for 4% -> 4%
where the time goes in v9:
time: 833 us; the launch traced here: 824 us
  waiting for transfers between devices  277 us (33%)
  matrix products  164 us (20%)
  other arithmetic  122 us (15%)
  starting transfers between devices  119 us (14%)
  local copies, waits for them, and re-layouts  105 us (13%)
  Pallas kernels  30.7 us (4%)
    ppermute x49, waiting for transfers between devices, back(): return lax.ppermute(v, 'dp', self.down)  103 us
    ppermute x49, waiting for transfers between devices, ahead(): return lax.ppermute(v, 'dp', self.up)  84.8 us
    ppermute x49, starting transfers between devices, ahead(): return lax.ppermute(v, 'dp', self.up)  67.3 us
    ppermute x11, waiting for transfers between devices, other_tensor(): return lax.ppermute(v, 'tensor', [(0, 1), (1, 0)])  65.7 us
    dynamic_update_slice x62, local copies, waits for them, and re-layouts, store(): lax.dynamic_update_slice(self.buffers[i], rows[:self.size, a:b], (at * se...  46.3 us
    convert_element_type x24, other arithmetic, take(): self.now = tuple(sums if self.left == 0 else [v.astype(bf16) for v in sums])  43.9 us
    ppermute x49, starting transfers between devices, back(): return lax.ppermute(v, 'dp', self.down)  35.2 us
    ppermute x4, waiting for transfers between devices, closing(): sums, _ = (yield Held(sums + lax.ppermute(sums, 'dp', pairs), input_grad))  20.3 us
  transfers between devices with their start and end apart: 135, of which 71 were waited for; matrix products, arithmetic and copies ran while one was open for 41% of the time, Pallas kernels for 4%

profile of v9, /device:TPU:0, one launch (start us, length us, event | category | flops | bytes accessed | tf_op | source)
XLA Modules:
  0.0 824.4 jit_solution(15681101757270690739)
XLA Ops:
  49.4 7.1 collective-permute-done.36
  237.2 7.6 collective-permute-done.45
  267.3 16.6 %collective-permute-done.57 = bf16[256,2048]{1,0:T(8,128)(2,1)S(1)} collective-permute-done((bf16[256,2048]{1,0:T(8,128)(2,1)S(1)}, bf16[256,2048]{1,0:T(8,128)(2,1)S(1)}, u32[]{:S(2)}, u32[]{:S(2)}) %collective-permute-start.57) | collective-permute-done | bytes 1048608 | tf_op jit(solution)/shard_map/ppermute | solution.py:57
  291.7 8.5 %collective-permute-done.55 = bf16[128,2048]{1,0:T(8,128)(2,1)S(1)} collective-permute-done((bf16[128,2048]{1,0:T(8,128)(2,1)S(1)}, bf16[128,2048]{1,0:T(8,128)(2,1)S(1)}, u32[]{:S(2)}, u32[]{:S(2)}) %collective-permute-start.55) | collective-permute-done | bytes 524320 | tf_op jit(solution)/shard_map/ppermute | solution.py:47
  305.9 11.0 %fusion.71 = f32[1024,2048]{1,0:T(8,128)} fusion(bf16[1024,2048]{1,0:T(8,128)(2,1)S(1)} %pad_maximum_fusion.1, bf16[2048,2048]{1,0:T(8,128)(2,1)S(1)} %constant_dynamic-update-slice_fusion.14), kind=kOutput, calls=%fused_computation.397 | convolution fusion | flops 8589934592 | bytes 20971520 | tf_op jit(solution)/shard_map/dot_general | solution.py:459
  358.4 15.0 %multiply_convert_fusion.2 = (bf16[1024,2048]{1,0:T(8,128)(2,1)S(1)}, f32[1024,2048]{1,0:T(8,128)}) fusion(f32[1024,2048]{1,0:T(8,128)} %fusion.71, bf16[1024,2048]{1,0:T(8,128)(2,1)S(1)} %pad_maximum_fusion.1, bf16[2048,2048]{1,0:T(8,128)(2,1)} %constant_dynamic-update-slice_fusion.4), kind=kOutput, calls=%fused_computation.40 | convolution fusion | flops 8602517504 | bytes 33554432 | tf_op jit(solution)/shard_map/dot_general | solution.py:478
  383.4 6.5 fusion.74
  409.1 7.8 collective-permute-done.70
  416.9 9.5 %collective-permute-done.78 = bf16[256,1024]{1,0:T(8,128)(2,1)} collective-permute-done((bf16[256,1024]{1,0:T(8,128)(2,1)}, bf16[256,1024]{1,0:T(8,128)(2,1)}, u32[]{:S(2)}, u32[]{:S(2)}) %collective-permute-start.78) | collective-permute-done | bytes 524320 | tf_op jit(solution)/shard_map/ppermute | solution.py:57
  442.4 6.7 fusion.73
  455.4 17.5 %multiply_convert_fusion = (bf16[1024,2048]{1,0:T(8,128)(2,1)}, bf16[1024,2048]{1,0:T(8,128)(2,1)}) fusion(f32[1024,2048]{1,0:T(8,128)} %fusion.71, f32[1024,2048]{1,0:T(8,128)} %get-tuple-element.664, f32[1024,2048]{1,0:T(8,128)} %fusion.73, bf16[1024,2048]{1,0:T(8,128)(2,1)} %constant_dynamic-update-slice_fusion.18, ...), kind=kOutput, calls=%fused_computation.38 | convolution fusion | flops 4332716032 | bytes 39845888 | tf_op jit(solution)/shard_map/dot_general | solution.py:513
  476.6 12.2 %convolution_convert_fusion.1 = bf16[2048,2048]{1,0:T(8,128)(2,1)S(1)} fusion(bf16[1024,2048]{1,0:T(8,128)(2,1)} %copy-done.22, bf16[1024,2048]{1,0:T(8,128)(2,1)} %get-tuple-element.413), kind=kOutput, calls=%fused_computation.43 | convolution fusion | flops 8594128896 | bytes 16777216 | tf_op jit(solution)/shard_map/dot_general | solution.py:519
  494.5 11.0 %convolution_convert_fusion = bf16[2048,2048]{1,0:T(8,128)(2,1)S(1)} fusion(bf16[1024,2048]{1,0:T(8,128)(2,1)S(1)} %copy-done.23, bf16[1024,2048]{1,0:T(8,128)(2,1)} %get-tuple-element.414), kind=kOutput, calls=%fused_computation.42 | convolution fusion | flops 8594128896 | bytes 16777216 | tf_op jit(solution)/shard_map/dot_general | solution.py:523
  526.2 10.1 %fusion.14 = f32[512,2048]{1,0:T(8,128)} fusion(bf16[2048,2048]{1,0:T(8,128)(2,1)} %constant_dynamic-update-slice_fusion.4, bf16[1024,2048]{1,0:T(8,128)(2,1)S(1)} %copy-done.82), kind=kOutput, calls=%fused_computation.108 | convolution fusion | flops 4294967296 | bytes 14680064 | tf_op jit(solution)/shard_map/dot_general | solution.py:531
  536.3 8.0 add_convert_fusion
  552.0 9.6 %fusion.11 = f32[512,2048]{1,0:T(8,128)} fusion(bf16[2048,2048]{1,0:T(8,128)(2,1)} %constant_dynamic-update-slice_fusion.4, bf16[1024,2048]{1,0:T(8,128)(2,1)S(1)} %copy-done.83), kind=kOutput, calls=%fused_computation.103 | convolution fusion | flops 4294967296 | bytes 14680064 | tf_op jit(solution)/shard_map/dot_general | solution.py:531
  561.6 8.4 %convolution_add_fusion.1 = f32[512,2048]{1,0:T(8,128)} fusion(f32[512,2048]{1,0:T(8,128)} %fusion.11, bf16[2048,2048]{1,0:T(8,128)(2,1)S(1)} %bitcast.82, bf16[1024,2048]{1,0:T(8,128)(2,1)} %get-tuple-element.413), kind=kOutput, calls=%fused_computation.62 | convolution fusion | flops 4296015872 | bytes 18874368 | tf_op jit(solution)/shard_map/dot_general | solution.py:529
  589.7 14.2 %collective-permute-done.95 = bf16[256,2048]{1,0:T(8,128)(2,1)} collective-permute-done((bf16[256,2048]{1,0:T(8,128)(2,1)}, bf16[256,2048]{1,0:T(8,128)(2,1)}, u32[]{:S(2)}, u32[]{:S(2)}) %collective-permute-start.95) | collective-permute-done | bytes 1048608 | tf_op jit(solution)/shard_map/ppermute | solution.py:57
  623.5 15.1 %collective-permute-done.98 = bf16[128,4096]{1,0:T(8,128)(2,1)} collective-permute-done((bf16[128,4096]{1,0:T(8,128)(2,1)}, bf16[128,4096]{1,0:T(8,128)(2,1)}, u32[]{:S(2)}, u32[]{:S(2)}) %collective-permute-start.98) | collective-permute-done | bytes 1048608 | tf_op jit(solution)/shard_map/ppermute | solution.py:50
  658.1 7.9 attend_back.1
  684.8 7.4 convolution_convert_fusion.2
  728.3 13.5 %collective-permute-done.114 = bf16[128,4096]{1,0:T(8,128)(2,1)S(1)} collective-permute-done((bf16[128,4096]{1,0:T(8,128)(2,1)S(1)}, bf16[128,4096]{1,0:T(8,128)(2,1)S(1)}, u32[]{:S(2)}, u32[]{:S(2)}) %collective-permute-start.114) | collective-permute-done | bytes 1048608 | tf_op jit(solution)/shard_map/ppermute | solution.py:50
  787.4 7.5 collective-permute-done.127
  797.3 6.6 collective-permute-done.130
  (706 shorter events, 572.5 us)
Async XLA Ops:
  3.1 30.6 %collective-permute-start.1 = (bf16[128,2048]{1,0:T(8,128)(2,1)}, bf16[128,2048]{1,0:T(8,128)(2,1)}, u32[]{:S(2)}, u32[]{:S(2)}) collective-permute-start(bf16[128,2048]{1,0:T(8,128)(2,1)} %bitcast.8), channel_id=1, source_target_pairs={{0,2},{2,0},{4,6},{6,4},{8,10},{10,8},{12,14},{14,12},{16,18},{18,... | collective-permute-start | bytes 1572872 | tf_op jit(solution)/shard_map/ppermute | solution.py:53
  13.7 27.2 %collective-permute-start.5 = (bf16[144,1536]{1,0:T(8,128)(2,1)}, bf16[144,1536]{1,0:T(8,128)(2,1)}, u32[]{:S(2)}, u32[]{:S(2)}) collective-permute-start(bf16[144,1536]{1,0:T(8,128)(2,1)} %get-tuple-element.640), channel_id=1, source_target_pairs={{0,8},{2,10},{8,16},{10,18},{16,24},{18,26},{24,28},{26,30},{28,20... | collective-permute-start | bytes 1327112 | tf_op jit(solution)/shard_map/ppermute | solution.py:47
  56.5 32.6 %collective-permute-start.37 = (bf16[256,2048]{1,0:T(8,128)(2,1)S(1)}, bf16[256,2048]{1,0:T(8,128)(2,1)S(1)}, u32[]{:S(2)}, u32[]{:S(2)}) collective-permute-start(bf16[256,2048]{1,0:T(8,128)(2,1)S(1)} %copy-done.5), channel_id=1, source_target_pairs={{0,2},{2,0},{4,6},{6,4},{8,10},{10,8},{12,14},{14,12},{16,18},{18,... | collective-permute-start | bytes 3145736 | tf_op jit(solution)/shard_map/ppermute | solution.py:53
  289.1 29.5 %collective-permute-start.53 = (bf16[128,2048]{1,0:T(8,128)(2,1)S(1)}, bf16[128,2048]{1,0:T(8,128)(2,1)S(1)}, u32[]{:S(2)}, u32[]{:S(2)}) collective-permute-start(bf16[128,2048]{1,0:T(8,128)(2,1)S(1)} %collective-permute-done.49), channel_id=1, source_target_pairs={{0,8},{2,10},{8,16},{10,18},{16,24},{18,26},{24,28},{26,30},{28,20... | collective-permute-start | bytes 1572872 | tf_op jit(solution)/shard_map/ppermute | solution.py:47
  290.8 27.8 %collective-permute-start.54 = (bf16[128,2048]{1,0:T(8,128)(2,1)S(1)}, bf16[128,2048]{1,0:T(8,128)(2,1)S(1)}, u32[]{:S(2)}, u32[]{:S(2)}) collective-permute-start(bf16[128,2048]{1,0:T(8,128)(2,1)S(1)} %collective-permute-done.50), channel_id=1, source_target_pairs={{8,0},{10,2},{16,8},{18,10},{24,16},{26,18},{28,24},{30,26},{20,28... | collective-permute-start | bytes 1572872 | tf_op jit(solution)/shard_map/ppermute | solution.py:50
  492.4 28.9 %collective-permute-start.84 = (bf16[128,2048]{1,0:T(8,128)(2,1)S(1)}, bf16[128,2048]{1,0:T(8,128)(2,1)S(1)}, u32[]{:S(2)}, u32[]{:S(2)}) collective-permute-start(bf16[128,2048]{1,0:T(8,128)(2,1)S(1)} %get-tuple-element.616), channel_id=1, source_target_pairs={{8,0},{10,2},{16,8},{18,10},{24,16},{26,18},{28,24},{30,26},{20,28... | collective-permute-start | bytes 1572872 | tf_op jit(solution)/shard_map/ppermute | solution.py:50
  493.0 28.4 %collective-permute-start.85 = (bf16[128,2048]{1,0:T(8,128)(2,1)S(1)}, bf16[128,2048]{1,0:T(8,128)(2,1)}, u32[]{:S(2)}, u32[]{:S(2)}) collective-permute-start(bf16[128,2048]{1,0:T(8,128)(2,1)S(1)} %get-tuple-element.615), channel_id=1, source_target_pairs={{0,8},{2,10},{8,16},{10,18},{16,24},{18,26},{24,28},{26,30},{28,20... | collective-permute-start | bytes 1572872 | tf_op jit(solution)/shard_map/ppermute | solution.py:47
  513.0 31.4 %collective-permute-start.88 = (bf16[128,4096]{1,0:T(8,128)(2,1)}, bf16[128,4096]{1,0:T(8,128)(2,1)}, u32[]{:S(2)}, u32[]{:S(2)}) collective-permute-start(bf16[128,4096]{1,0:T(8,128)(2,1)} %pad_maximum_fusion.7), channel_id=1, source_target_pairs={{8,0},{10,2},{16,8},{18,10},{24,16},{26,18},{28,24},{30,26},{20,28... | collective-permute-start | bytes 3145736 | tf_op jit(solution)/shard_map/ppermute | solution.py:50
  514.5 29.8 %collective-permute-start.89 = (bf16[128,4096]{1,0:T(8,128)(2,1)}, bf16[128,4096]{1,0:T(8,128)(2,1)}, u32[]{:S(2)}, u32[]{:S(2)}) collective-permute-start(bf16[128,4096]{1,0:T(8,128)(2,1)} %pad_maximum_fusion.8), channel_id=1, source_target_pairs={{0,8},{2,10},{8,16},{10,18},{16,24},{18,26},{24,28},{26,30},{28,20... | collective-permute-start | bytes 3145736 | tf_op jit(solution)/shard_map/ppermute | solution.py:47
  524.2 45.8 %collective-permute-start.86 = (bf16[128,2048]{1,0:T(8,128)(2,1)}, bf16[128,2048]{1,0:T(8,128)(2,1)}, u32[]{:S(2)}, u32[]{:S(2)}) collective-permute-start(bf16[128,2048]{1,0:T(8,128)(2,1)} %get-tuple-element.614), channel_id=1, source_target_pairs={{8,0},{10,2},{16,8},{18,10},{24,16},{26,18},{28,24},{30,26},{20,28... | collective-permute-start | bytes 1572872 | tf_op jit(solution)/shard_map/ppermute | solution.py:50
  524.7 45.3 %collective-permute-start.87 = (bf16[128,2048]{1,0:T(8,128)(2,1)}, bf16[128,2048]{1,0:T(8,128)(2,1)}, u32[]{:S(2)}, u32[]{:S(2)}) collective-permute-start(bf16[128,2048]{1,0:T(8,128)(2,1)} %get-tuple-element.613), channel_id=1, source_target_pairs={{0,8},{2,10},{8,16},{10,18},{16,24},{18,26},{24,28},{26,30},{28,20... | collective-permute-start | bytes 1572872 | tf_op jit(solution)/shard_map/ppermute | solution.py:47
  547.2 27.4 %collective-permute-start.92 = (bf16[128,4096]{1,0:T(8,128)(2,1)}, bf16[128,4096]{1,0:T(8,128)(2,1)S(1)}, u32[]{:S(2)}, u32[]{:S(2)}) collective-permute-start(bf16[128,4096]{1,0:T(8,128)(2,1)} %add_convert_fusion.12), channel_id=1, source_target_pairs={{8,0},{10,2},{16,8},{18,10},{24,16},{26,18},{28,24},{30,26},{20,28... | collective-permute-start | bytes 3145736 | tf_op jit(solution)/shard_map/ppermute | solution.py:50
  572.6 33.5 %collective-permute-start.90 = (bf16[128,2048]{1,0:T(8,128)(2,1)}, bf16[128,2048]{1,0:T(8,128)(2,1)}, u32[]{:S(2)}, u32[]{:S(2)}) collective-permute-start(bf16[128,2048]{1,0:T(8,128)(2,1)} %get-tuple-element.612), channel_id=1, source_target_pairs={{8,0},{10,2},{16,8},{18,10},{24,16},{26,18},{28,24},{30,26},{20,28... | collective-permute-start | bytes 1572872 | tf_op jit(solution)/shard_map/ppermute | solution.py:50
  572.6 33.5 %collective-permute-start.91 = (bf16[128,2048]{1,0:T(8,128)(2,1)}, bf16[128,2048]{1,0:T(8,128)(2,1)}, u32[]{:S(2)}, u32[]{:S(2)}) collective-permute-start(bf16[128,2048]{1,0:T(8,128)(2,1)} %get-tuple-element.611), channel_id=1, source_target_pairs={{0,8},{2,10},{8,16},{10,18},{16,24},{18,26},{24,28},{26,30},{28,20... | collective-permute-start | bytes 1572872 | tf_op jit(solution)/shard_map/ppermute | solution.py:47
  581.1 28.6 %collective-permute-start.96 = (bf16[128,4096]{1,0:T(8,128)(2,1)}, bf16[128,4096]{1,0:T(8,128)(2,1)}, u32[]{:S(2)}, u32[]{:S(2)}) collective-permute-start(bf16[128,4096]{1,0:T(8,128)(2,1)} %add_convert_fusion.10), channel_id=1, source_target_pairs={{8,0},{10,2},{16,8},{18,10},{24,16},{26,18},{28,24},{30,26},{20,28... | collective-permute-start | bytes 3145736 | tf_op jit(solution)/shard_map/ppermute | solution.py:50
  612.2 26.3 %collective-permute-start.98 = (bf16[128,4096]{1,0:T(8,128)(2,1)}, bf16[128,4096]{1,0:T(8,128)(2,1)}, u32[]{:S(2)}, u32[]{:S(2)}) collective-permute-start(bf16[128,4096]{1,0:T(8,128)(2,1)} %add_convert_fusion.8), channel_id=1, source_target_pairs={{8,0},{10,2},{16,8},{18,10},{24,16},{26,18},{28,24},{30,26},{20,28... | collective-permute-start | bytes 3145736 | tf_op jit(solution)/shard_map/ppermute | solution.py:50
  616.0 26.3 %collective-permute-start.99 = (bf16[128,4096]{1,0:T(8,128)(2,1)}, bf16[128,4096]{1,0:T(8,128)(2,1)}, u32[]{:S(2)}, u32[]{:S(2)}) collective-permute-start(bf16[128,4096]{1,0:T(8,128)(2,1)} %add_convert_fusion.7), channel_id=1, source_target_pairs={{0,8},{2,10},{8,16},{10,18},{16,24},{18,26},{24,28},{26,30},{28,20... | collective-permute-start | bytes 3145736 | tf_op jit(solution)/shard_map/ppermute | solution.py:47
  621.5 31.7 %collective-permute-start.102 = (bf16[128,2048]{1,0:T(8,128)(2,1)}, bf16[128,2048]{1,0:T(8,128)(2,1)S(1)}, u32[]{:S(2)}, u32[]{:S(2)}) collective-permute-start(bf16[128,2048]{1,0:T(8,128)(2,1)} %get-tuple-element.610), channel_id=1, source_target_pairs={{8,0},{10,2},{16,8},{18,10},{24,16},{26,18},{28,24},{30,26},{20,28... | collective-permute-start | bytes 1572872 | tf_op jit(solution)/shard_map/ppermute | solution.py:50
  622.6 30.6 %collective-permute-start.103 = (bf16[128,2048]{1,0:T(8,128)(2,1)}, bf16[128,2048]{1,0:T(8,128)(2,1)S(1)}, u32[]{:S(2)}, u32[]{:S(2)}) collective-permute-start(bf16[128,2048]{1,0:T(8,128)(2,1)} %get-tuple-element.609), channel_id=1, source_target_pairs={{0,8},{2,10},{8,16},{10,18},{16,24},{18,26},{24,28},{26,30},{28,20... | collective-permute-start | bytes 1572872 | tf_op jit(solution)/shard_map/ppermute | solution.py:47
  646.5 29.0 %collective-permute-start.100 = (bf16[128,4096]{1,0:T(8,128)(2,1)}, bf16[128,4096]{1,0:T(8,128)(2,1)S(1)}, u32[]{:S(2)}, u32[]{:S(2)}) collective-permute-start(bf16[128,4096]{1,0:T(8,128)(2,1)} %add_convert_fusion.6), channel_id=1, source_target_pairs={{8,0},{10,2},{16,8},{18,10},{24,16},{26,18},{28,24},{30,26},{20,28... | collective-permute-start | bytes 3145736 | tf_op jit(solution)/shard_map/ppermute | solution.py:50
  677.0 32.2 %collective-permute-start.110 = (bf16[128,4096]{1,0:T(8,128)(2,1)}, bf16[128,4096]{1,0:T(8,128)(2,1)}, u32[]{:S(2)}, u32[]{:S(2)}) collective-permute-start(bf16[128,4096]{1,0:T(8,128)(2,1)} %add_convert_fusion.4), channel_id=1, source_target_pairs={{8,0},{10,2},{16,8},{18,10},{24,16},{26,18},{28,24},{30,26},{20,28... | collective-permute-start | bytes 3145736 | tf_op jit(solution)/shard_map/ppermute | solution.py:50
  681.2 28.0 %collective-permute-start.111 = (bf16[128,4096]{1,0:T(8,128)(2,1)}, bf16[128,4096]{1,0:T(8,128)(2,1)}, u32[]{:S(2)}, u32[]{:S(2)}) collective-permute-start(bf16[128,4096]{1,0:T(8,128)(2,1)} %add_convert_fusion.3), channel_id=1, source_target_pairs={{0,8},{2,10},{8,16},{10,18},{16,24},{18,26},{24,28},{26,30},{28,20... | collective-permute-start | bytes 3145736 | tf_op jit(solution)/shard_map/ppermute | solution.py:47
  710.8 31.0 %collective-permute-start.114 = (bf16[128,4096]{1,0:T(8,128)(2,1)S(1)}, bf16[128,4096]{1,0:T(8,128)(2,1)S(1)}, u32[]{:S(2)}, u32[]{:S(2)}) collective-permute-start(bf16[128,4096]{1,0:T(8,128)(2,1)S(1)} %add_convert_fusion.2), channel_id=1, source_target_pairs={{8,0},{10,2},{16,8},{18,10},{24,16},{26,18},{28,24},{30,26},{20,28... | collective-permute-start | bytes 3145736 | tf_op jit(solution)/shard_map/ppermute | solution.py:50
  714.2 29.1 %collective-permute-start.115 = (bf16[128,4096]{1,0:T(8,128)(2,1)S(1)}, bf16[128,4096]{1,0:T(8,128)(2,1)S(1)}, u32[]{:S(2)}, u32[]{:S(2)}) collective-permute-start(bf16[128,4096]{1,0:T(8,128)(2,1)S(1)} %add_convert_fusion.1), channel_id=1, source_target_pairs={{0,8},{2,10},{8,16},{10,18},{16,24},{18,26},{24,28},{26,30},{28,20... | collective-permute-start | bytes 3145736 | tf_op jit(solution)/shard_map/ppermute | solution.py:47
  (199 other events, 2779.6 us)

commit v10 on v9

--- a/solution.py
+++ b/solution.py
@@ -467,17 +467,14 @@
     stages = Stages(forward())
     for k in range(hops):
         stages.turn(up_weights, down_weights)
-        stages.turn(down_weights, up_weights)
+        if k % 2:
+            stages.turn(down_weights, up_weights)
     own_teacher, attn_kept, mlp_kept = stages.finish()
     normed, rot_queries, rot_keys, values, mixed = attn_kept
     middle, mlp_scale, normed_mlp, gate = mlp_kept
     up_proj = up_weights.buffers[0]
-    down_far, down_near = down_weights.buffers
+    down_near = down_weights.buffers.pop()
     count = jnp.sum(lengths).astype(f32)
-
-    up = jnp.dot(normed_mlp, up_proj, preferred_element_type=f32)
-    sigmoid_gate = jax.nn.sigmoid(gate)
-    hidden = (gate * sigmoid_gate * up).astype(bf16)
     cut = width // 2
 
     def half_sum(rows, proj_t):
@@ -493,24 +490,39 @@
     def down_grad_of(branch):
         return lax.dot_general(branch, hidden, over_rows, preferred_element_type=f32).astype(bf16)
 
+    def near_half():
+        up = jnp.dot(normed_mlp, up_proj, preferred_element_type=f32)
+        sigmoid_gate = jax.nn.sigmoid(gate)
+        hidden = yield Held((gate * sigmoid_gate * up).astype(bf16))
+        half = yield Held(half_sum(hidden, down_near))
+        result, error, delta, low = output(tensor_sum(half), slice(cut, width))
+        low = yield Held(low)
+        across, beside = yield Held(other_tensor(low), ring.other_core(low))
+        branch = jnp.concatenate([low, across, beside, ring.other_core(across)], axis=0)
+        first = jnp.dot(branch, down_near, preferred_element_type=f32)
+        return up, sigmoid_gate, hidden, result, error, delta, branch, first
+
+    stages = Stages(near_half())
+    while down_weights.hops < ring.chips:
+        stages.turn(down_weights)
+    up, sigmoid_gate, hidden, result_near, error_near, delta_near, branch_near, first = (
+        stages.finish()
+    )
+    down_far = down_weights.buffers[0]
     half_far = half_sum(hidden, down_far)
-    half_near = half_sum(together((hidden, half_far))[0], down_near)
     result_far, error_far, delta_far, low_far = output(tensor_sum(half_far), slice(0, cut))
     branch_far = gather_group(ring, low_far)
     grad_far = down_grad_of(branch_far)
-    shared_near = together((tensor_sum(half_near), low_far))[0]
-    result_near, error_near, delta_near, low_near = output(shared_near, slice(cut, width))
-    branch_near = gather_group(ring, low_near)
     down_sums = Scatter(ring, [grad_far], None, piece)
     result = jnp.concatenate([result_far, result_near], axis=1)
     delta_result = jnp.concatenate([delta_far, delta_near], axis=1)
     squared = jnp.sum(error_far * error_far) + jnp.sum(error_near * error_near)
 
     def backward():
-        branch = together((branch_far, grad_far))[0]
-        first = jnp.dot(branch, down_far, preferred_element_type=f32)
-        first = yield Held(first)
-        delta_hidden = first + jnp.dot(branch_near, down_near, preferred_element_type=f32)
+        branch, near_part, _ = together((branch_far, first, grad_far))
+        delta_hidden = yield Held(
+            near_part + jnp.dot(branch, down_far, preferred_element_type=f32)
+        )
         delta_gate = (
             delta_hidden * up * sigmoid_gate * (1.0 + gate * (1.0 - sigmoid_gate))
         ).astype(bf16)
@@ -599,9 +611,8 @@
     stages.turn(gate_up_sums, down_sums)
     stages.turn(gate_up_sums, down_sums)
     stages.turn(down_sums, gate_up_sums)
-    down_grad = whole(*finish(down_sums)).T
     while not stages.over and gate_up_sums.left:
-        stages.turn(gate_up_sums, None, down_grad)
+        stages.turn(gate_up_sums, down_sums)
     assert stages.over
     activations, gain_mlp_part, delta_middle, delta_qkv, attn_grads = stages.finish()
     attn_sums = Scatter(ring, *halves(attn_grads), piece)
@@ -643,6 +654,9 @@
         return input_grad, sums
 
     stages = Stages(closing())
+    while down_sums.left:
+        stages.turn(down_sums, gate_up_sums)
+    down_grad = whole(*finish(down_sums)).T
     while gate_up_sums.left:
         stages.turn(gate_up_sums, attn_sums, down_grad)
         stages.turn(attn_sums, gate_up_sums)

time: 833 us -> 860 us (1.032)
  waiting for transfers between devices: 277 us -> 290 us
  other arithmetic: 122 us -> 132 us
  local copies, waits for them, and re-layouts: 105 us -> 115 us
    ppermute x49, waiting for transfers between devices: 84.8 us -> 120 us  [ahead(): return lax.ppermute(v, 'dp', self.up)]
    ppermute x49, waiting for transfers between devices: 103 us -> 70.8 us  [back(): return lax.ppermute(v, 'dp', self.down)]
    convert_element_type x0 -> x1, other arithmetic: none -> 12.4 us  [backward(): delta_up = (delta_hidden * gate * sigmoid_gate).astype(bf16)]
    add x0 -> x1, other arithmetic: none -> 11.7 us  [backward(): near_part + jnp.dot(branch, down_far, preferred_element_type=f32)]
    ppermute x49, starting transfers between devices: 35.2 us -> 44.4 us  [back(): return lax.ppermute(v, 'dp', self.down)]
    unnamed x188 -> x207, local copies, waits for them, and re-layouts: 20.2 us -> 22.2 us
  transfers between devices with their start and end apart: 135 -> 135, of which waited for: 71 -> 60; matrix products, arithmetic and copies ran while one was open for 41% -> 41% of each run, Pallas kernels for 4% -> 4%
where the time goes in v10:
time: 860 us; the launch traced here: 851 us
  waiting for transfers between devices  290 us (34%)
  matrix products  156 us (18%)
  other arithmetic  132 us (15%)
  starting transfers between devices  120 us (14%)
  local copies, waits for them, and re-layouts  115 us (13%)
  Pallas kernels  30.9 us (4%)
    ppermute x49, waiting for transfers between devices, ahead(): return lax.ppermute(v, 'dp', self.up)  120 us
    ppermute x11, waiting for transfers between devices, other_tensor(): return lax.ppermute(v, 'tensor', [(0, 1), (1, 0)])  72.6 us
    ppermute x49, waiting for transfers between devices, back(): return lax.ppermute(v, 'dp', self.down)  70.8 us
    ppermute x49, starting transfers between devices, ahead(): return lax.ppermute(v, 'dp', self.up)  60.3 us
    dynamic_update_slice x62, local copies, waits for them, and re-layouts, store(): lax.dynamic_update_slice(self.buffers[i], rows[:self.size, a:b], (at * se...  48.4 us
    ppermute x49, starting transfers between devices, back(): return lax.ppermute(v, 'dp', self.down)  44.4 us
    convert_element_type x24, other arithmetic, take(): self.now = tuple(sums if self.left == 0 else [v.astype(bf16) for v in sums])  41.9 us
    ppermute x4, waiting for transfers between devices, closing(): sums, _ = (yield Held(sums + lax.ppermute(sums, 'dp', pairs), input_grad))  24.2 us
  transfers between devices with their start and end apart: 135, of which 60 were waited for; matrix products, arithmetic and copies ran while one was open for 41% of the time, Pallas kernels for 4%

profile of v10, /device:TPU:0, one launch (start us, length us, event | category | flops | bytes accessed | tf_op | source)
XLA Modules:
  0.0 851.3 jit_solution(12224516695667838748)
XLA Ops:
  80.2 9.0 %collective-permute-done.13 = bf16[144,1536]{1,0:T(8,128)(2,1)S(1)} collective-permute-done((bf16[144,1536]{1,0:T(8,128)(2,1)S(1)}, bf16[144,1536]{1,0:T(8,128)(2,1)S(1)}, u32[]{:S(2)}, u32[]{:S(2)}) %collective-permute-start.13) | collective-permute-done | bytes 442400 | tf_op jit(solution)/shard_map/ppermute | solution.py:47
  252.1 17.0 %collective-permute-done.45 = bf16[128,2048]{1,0:T(8,128)(2,1)S(1)} collective-permute-done((bf16[128,2048]{1,0:T(8,128)(2,1)S(1)}, bf16[128,2048]{1,0:T(8,128)(2,1)S(1)}, u32[]{:S(2)}, u32[]{:S(2)}) %collective-permute-start.45) | collective-permute-done | bytes 524320 | tf_op jit(solution)/shard_map/ppermute | solution.py:47
  279.1 8.6 %collective-permute-done.51 = bf16[128,2048]{1,0:T(8,128)(2,1)S(1)} collective-permute-done((bf16[128,2048]{1,0:T(8,128)(2,1)S(1)}, bf16[128,2048]{1,0:T(8,128)(2,1)S(1)}, u32[]{:S(2)}, u32[]{:S(2)}) %collective-permute-start.51) | collective-permute-done | bytes 524320 | tf_op jit(solution)/shard_map/ppermute | solution.py:47
  298.6 9.7 %collective-permute-done.53 = bf16[128,2048]{1,0:T(8,128)(2,1)S(1)} collective-permute-done((bf16[128,2048]{1,0:T(8,128)(2,1)S(1)}, bf16[128,2048]{1,0:T(8,128)(2,1)S(1)}, u32[]{:S(2)}, u32[]{:S(2)}) %collective-permute-start.53) | collective-permute-done | bytes 524320 | tf_op jit(solution)/shard_map/ppermute | solution.py:47
  314.3 8.8 %collective-permute-done.50 = bf16[128,2048]{1,0:T(8,128)(2,1)S(1)} collective-permute-done((bf16[128,2048]{1,0:T(8,128)(2,1)S(1)}, bf16[128,2048]{1,0:T(8,128)(2,1)S(1)}, u32[]{:S(2)}, u32[]{:S(2)}) %collective-permute-start.50) | collective-permute-done | bytes 524320 | tf_op jit(solution)/shard_map/ppermute | solution.py:50
  325.4 11.2 %fusion.70 = f32[1024,2048]{1,0:T(8,128)S(1)} fusion(bf16[1024,2048]{1,0:T(8,128)(2,1)S(1)} %pad_maximum_fusion.1, bf16[2048,2048]{1,0:T(8,128)(2,1)} %constant_dynamic-update-slice_fusion.14), kind=kOutput, calls=%fused_computation.397 | convolution fusion | flops 8589934592 | bytes 20971520 | tf_op jit(solution)/shard_map/dot_general | solution.py:459
  338.9 15.5 %multiply_convert_fusion.2 = (bf16[1024,2048]{1,0:T(8,128)(2,1)}, f32[1024,2048]{1,0:T(8,128)}) fusion(f32[1024,2048]{1,0:T(8,128)S(1)} %fusion.70, bf16[1024,2048]{1,0:T(8,128)(2,1)S(1)} %pad_maximum_fusion.1, bf16[2048,2048]{1,0:T(8,128)(2,1)} %constant_dynamic-update-slice_fusion.10), kind=kOutput, calls=%fused_computation.40 | convolution fusion | flops 8602517504 | bytes 33554432 | tf_op jit(solution)/shard_map/dot_general | solution.py:494
  368.1 10.2 %collective-permute-done.62 = bf16[128,2048]{1,0:T(8,128)(2,1)S(1)} collective-permute-done((bf16[128,2048]{1,0:T(8,128)(2,1)S(1)}, bf16[128,2048]{1,0:T(8,128)(2,1)S(1)}, u32[]{:S(2)}, u32[]{:S(2)}) %collective-permute-start.62) | collective-permute-done | bytes 524320 | tf_op jit(solution)/shard_map/ppermute | solution.py:47
  401.7 8.3 collective-permute-done.70
  424.7 12.6 %collective-permute-done.73 = bf16[256,1024]{1,0:T(8,128)(2,1)S(1)} collective-permute-done((bf16[256,1024]{1,0:T(8,128)(2,1)S(1)}, bf16[256,1024]{1,0:T(8,128)(2,1)S(1)}, u32[]{:S(2)}, u32[]{:S(2)}) %collective-permute-start.73) | collective-permute-done | bytes 524320 | tf_op jit(solution)/shard_map/ppermute | solution.py:57
  453.6 8.8 %fusion.73 = f32[1024,2048]{1,0:T(8,128)} fusion(bf16[1024,1024]{1,0:T(8,128)(2,1)S(1)} %constant_dynamic-update-slice_fusion.64, bf16[1024,2048]{1,0:T(8,128)(2,1)} %constant_dynamic-update-slice_fusion.8), kind=kOutput, calls=%fused_computation.400 | convolution fusion | flops 4294967296 | bytes 14680064 | tf_op jit(solution)/shard_map/dot_general | solution.py:502
  481.8 11.7 %add.416 = f32[1024,2048]{1,0:T(8,128)} add(f32[1024,2048]{1,0:T(8,128)} %fusion.73, f32[1024,2048]{1,0:T(8,128)} %fusion.74) | non-fusion elementwise | flops 2097152 | bytes 25165824 | tf_op jit(solution)/shard_map/add | solution.py:524
  497.2 12.4 %multiply_convert_fusion = (bf16[1024,2048]{1,0:T(8,128)(2,1)}, bf16[1024,2048]{1,0:T(8,128)(2,1)S(1)}) fusion(f32[1024,2048]{1,0:T(8,128)} %add.416, f32[1024,2048]{1,0:T(8,128)} %copy-done.11, f32[1024,2048]{1,0:T(8,128)} %get-tuple-element.675), kind=kLoop, calls=%fused_computation.38 | loop fusion | flops 27262976 | bytes 33554432 | tf_op jit(solution)/shard_map/convert_element_type | solution.py:529
  512.1 9.8 %convolution_convert_fusion.1 = bf16[2048,2048]{1,0:T(8,128)(2,1)S(1)} fusion(bf16[1024,2048]{1,0:T(8,128)(2,1)S(1)} %copy-done.25, bf16[1024,2048]{1,0:T(8,128)(2,1)S(1)} %get-tuple-element.423), kind=kOutput, calls=%fused_computation.43 | convolution fusion | flops 8594128896 | bytes 16777216 | tf_op jit(solution)/shard_map/dot_general | solution.py:531
  527.0 11.0 %convolution_convert_fusion = bf16[2048,2048]{1,0:T(8,128)(2,1)S(1)} fusion(bf16[1024,2048]{1,0:T(8,128)(2,1)S(1)} %copy-done.25, bf16[1024,2048]{1,0:T(8,128)(2,1)} %get-tuple-element.424), kind=kOutput, calls=%fused_computation.42 | convolution fusion | flops 8594128896 | bytes 16777216 | tf_op jit(solution)/shard_map/dot_general | solution.py:535
  559.3 9.6 %fusion.14 = f32[512,2048]{1,0:T(8,128)} fusion(bf16[2048,2048]{1,0:T(8,128)(2,1)} %constant_dynamic-update-slice_fusion.10, bf16[1024,2048]{1,0:T(8,128)(2,1)S(1)} %copy-done.30), kind=kOutput, calls=%fused_computation.106 | convolution fusion | flops 4294967296 | bytes 14680064 | tf_op jit(solution)/shard_map/dot_general | solution.py:543
  569.0 10.0 %add_convert_fusion = bf16[512,2048]{1,0:T(8,128)(2,1)} fusion(f32[512,2048]{1,0:T(8,128)} %fusion.14, bf16[2048,2048]{1,0:T(8,128)(2,1)} %constant_dynamic-update-slice_fusion.14, bf16[1024,2048]{1,0:T(8,128)(2,1)S(1)} %get-tuple-element.423), kind=kOutput, calls=%fused_computation.51 | convolution fusion | flops 4297064448 | bytes 16777216 | tf_op jit(solution)/shard_map/dot_general | solution.py:541
  586.5 9.7 %fusion.11 = f32[512,2048]{1,0:T(8,128)} fusion(bf16[2048,2048]{1,0:T(8,128)(2,1)} %constant_dynamic-update-slice_fusion.10, bf16[1024,2048]{1,0:T(8,128)(2,1)S(1)} %copy-done.30), kind=kOutput, calls=%fused_computation.101 | convolution fusion | flops 4294967296 | bytes 14680064 | tf_op jit(solution)/shard_map/dot_general | solution.py:543
  596.2 9.0 %convolution_add_fusion = f32[512,2048]{1,0:T(8,128)S(1)} fusion(f32[512,2048]{1,0:T(8,128)} %fusion.11, bf16[2048,2048]{1,0:T(8,128)(2,1)} %constant_dynamic-update-slice_fusion.14, bf16[1024,2048]{1,0:T(8,128)(2,1)S(1)} %get-tuple-element.423), kind=kOutput, calls=%fused_computation.61 | convolution fusion | flops 4296015872 | bytes 18874368 | tf_op jit(solution)/shard_map/dot_general | solution.py:541
  622.3 14.6 %collective-permute-done.95 = bf16[256,2048]{1,0:T(8,128)(2,1)} collective-permute-done((bf16[256,2048]{1,0:T(8,128)(2,1)}, bf16[256,2048]{1,0:T(8,128)(2,1)}, u32[]{:S(2)}, u32[]{:S(2)}) %collective-permute-start.95) | collective-permute-done | bytes 1048608 | tf_op jit(solution)/shard_map/ppermute | solution.py:57
  656.8 12.4 %collective-permute-done.104 = bf16[256,2048]{1,0:T(8,128)(2,1)} collective-permute-done((bf16[256,2048]{1,0:T(8,128)(2,1)S(1)}, bf16[256,2048]{1,0:T(8,128)(2,1)}, u32[]{:S(2)}, u32[]{:S(2)}) %collective-permute-start.104) | collective-permute-done | bytes 1048608 | tf_op jit(solution)/shard_map/ppermute | solution.py:57
  693.1 8.0 attend_back.1
  752.3 15.8 %collective-permute-done.115 = bf16[128,4096]{1,0:T(8,128)(2,1)S(1)} collective-permute-done((bf16[128,4096]{1,0:T(8,128)(2,1)S(1)}, bf16[128,4096]{1,0:T(8,128)(2,1)S(1)}, u32[]{:S(2)}, u32[]{:S(2)}) %collective-permute-start.115) | collective-permute-done | bytes 1048608 | tf_op jit(solution)/shard_map/ppermute | solution.py:47
  809.1 9.5 %collective-permute-done.127 = f32[40,128]{1,0:T(8,128)S(1)} collective-permute-done((f32[40,128]{1,0:T(8,128)S(1)}, f32[40,128]{1,0:T(8,128)S(1)}, u32[]{:S(2)}, u32[]{:S(2)}) %collective-permute-start.127) | collective-permute-done | bytes 20512 | tf_op jit(solution)/shard_map/ppermute | solution.py:652
  (726 shorter events, 581.2 us)
Async XLA Ops:
  8.8 28.7 %collective-permute-start.1 = (bf16[128,2048]{1,0:T(8,128)(2,1)}, bf16[128,2048]{1,0:T(8,128)(2,1)}, u32[]{:S(2)}, u32[]{:S(2)}) collective-permute-start(bf16[128,2048]{1,0:T(8,128)(2,1)} %bitcast.8), channel_id=1, source_target_pairs={{0,2},{2,0},{4,6},{6,4},{8,10},{10,8},{12,14},{14,12},{16,18},{18,... | collective-permute-start | bytes 1572872 | tf_op jit(solution)/shard_map/ppermute | solution.py:53
  16.4 28.3 %collective-permute-start.5 = (bf16[144,1536]{1,0:T(8,128)(2,1)}, bf16[144,1536]{1,0:T(8,128)(2,1)}, u32[]{:S(2)}, u32[]{:S(2)}) collective-permute-start(bf16[144,1536]{1,0:T(8,128)(2,1)} %get-tuple-element.651), channel_id=1, source_target_pairs={{0,8},{2,10},{8,16},{10,18},{16,24},{18,26},{24,28},{26,30},{28,20... | collective-permute-start | bytes 1327112 | tf_op jit(solution)/shard_map/ppermute | solution.py:47
  60.3 34.0 %collective-permute-start.37 = (bf16[256,2048]{1,0:T(8,128)(2,1)S(1)}, bf16[256,2048]{1,0:T(8,128)(2,1)S(1)}, u32[]{:S(2)}, u32[]{:S(2)}) collective-permute-start(bf16[256,2048]{1,0:T(8,128)(2,1)S(1)} %copy-done.4), channel_id=1, source_target_pairs={{0,2},{2,0},{4,6},{6,4},{8,10},{10,8},{12,14},{14,12},{16,18},{18,... | collective-permute-start | bytes 3145736 | tf_op jit(solution)/shard_map/ppermute | solution.py:53
  189.9 32.2 %collective-permute-start.31 = (bf16[128,2048]{1,0:T(8,128)(2,1)}, bf16[128,2048]{1,0:T(8,128)(2,1)S(1)}, u32[]{:S(2)}, u32[]{:S(2)}) collective-permute-start(bf16[128,2048]{1,0:T(8,128)(2,1)} %get-tuple-element.306), channel_id=1, source_target_pairs={{0,8},{2,10},{8,16},{10,18},{16,24},{18,26},{24,28},{26,30},{28,20... | collective-permute-start | bytes 1572872 | tf_op jit(solution)/shard_map/ppermute | solution.py:47
  190.4 31.7 %collective-permute-start.32 = (bf16[128,2048]{1,0:T(8,128)(2,1)S(1)}, bf16[128,2048]{1,0:T(8,128)(2,1)S(1)}, u32[]{:S(2)}, u32[]{:S(2)}) collective-permute-start(bf16[128,2048]{1,0:T(8,128)(2,1)S(1)} %get-tuple-element.307), channel_id=1, source_target_pairs={{8,0},{10,2},{16,8},{18,10},{24,16},{26,18},{28,24},{30,26},{20,28... | collective-permute-start | bytes 1572872 | tf_op jit(solution)/shard_map/ppermute | solution.py:50
  234.1 35.4 %collective-permute-start.41 = (bf16[128,2048]{1,0:T(8,128)(2,1)}, bf16[128,2048]{1,0:T(8,128)(2,1)S(1)}, u32[]{:S(2)}, u32[]{:S(2)}) collective-permute-start(bf16[128,2048]{1,0:T(8,128)(2,1)} %copy-done.65), channel_id=1, source_target_pairs={{0,8},{2,10},{8,16},{10,18},{16,24},{18,26},{24,28},{26,30},{28,20... | collective-permute-start | bytes 1572872 | tf_op jit(solution)/shard_map/ppermute | solution.py:47
  234.5 35.0 %collective-permute-start.42 = (bf16[128,2048]{1,0:T(8,128)(2,1)}, bf16[128,2048]{1,0:T(8,128)(2,1)S(1)}, u32[]{:S(2)}, u32[]{:S(2)}) collective-permute-start(bf16[128,2048]{1,0:T(8,128)(2,1)} %copy-done.67), channel_id=1, source_target_pairs={{8,0},{10,2},{16,8},{18,10},{24,16},{26,18},{28,24},{30,26},{20,28... | collective-permute-start | bytes 1572872 | tf_op jit(solution)/shard_map/ppermute | solution.py:50
  241.1 28.2 %collective-permute-start.48 = (bf16[256,2048]{1,0:T(8,128)(2,1)S(1)}, bf16[256,2048]{1,0:T(8,128)(2,1)S(1)}, u32[]{:S(2)}, u32[]{:S(2)}) collective-permute-start(bf16[256,2048]{1,0:T(8,128)(2,1)S(1)} %slice.1087), channel_id=1, source_target_pairs={{0,1},{1,0},{2,3},{3,2},{4,5},{5,4},{6,7},{7,6},{8,9},{9,8},{10,11... | collective-permute-start | bytes 3145736 | tf_op jit(solution)/shard_map/ppermute | solution.py:57
  277.5 34.5 %collective-permute-start.56 = (bf16[256,2048]{1,0:T(8,128)(2,1)S(1)}, bf16[256,2048]{1,0:T(8,128)(2,1)S(1)}, u32[]{:S(2)}, u32[]{:S(2)}) collective-permute-start(bf16[256,2048]{1,0:T(8,128)(2,1)S(1)} %multiply_convert_fusion.3), channel_id=1, source_target_pairs={{0,2},{2,0},{4,6},{6,4},{8,10},{10,8},{12,14},{14,12},{16,18},{18,... | collective-permute-start | bytes 3145736 | tf_op jit(solution)/shard_map/ppermute | solution.py:53
  277.5 36.8 %collective-permute-start.49 = (bf16[128,2048]{1,0:T(8,128)(2,1)S(1)}, bf16[128,2048]{1,0:T(8,128)(2,1)S(1)}, u32[]{:S(2)}, u32[]{:S(2)}) collective-permute-start(bf16[128,2048]{1,0:T(8,128)(2,1)S(1)} %collective-permute-done.41), channel_id=1, source_target_pairs={{0,8},{2,10},{8,16},{10,18},{16,24},{18,26},{24,28},{26,30},{28,20... | collective-permute-start | bytes 1572872 | tf_op jit(solution)/shard_map/ppermute | solution.py:47
  323.2 33.0 %collective-permute-start.58 = (bf16[128,2048]{1,0:T(8,128)(2,1)S(1)}, bf16[128,2048]{1,0:T(8,128)(2,1)S(1)}, u32[]{:S(2)}, u32[]{:S(2)}) collective-permute-start(bf16[128,2048]{1,0:T(8,128)(2,1)S(1)} %collective-permute-done.49), channel_id=1, source_target_pairs={{0,8},{2,10},{8,16},{10,18},{16,24},{18,26},{24,28},{26,30},{28,20... | collective-permute-start | bytes 1572872 | tf_op jit(solution)/shard_map/ppermute | solution.py:47
  324.7 31.4 %collective-permute-start.59 = (bf16[128,2048]{1,0:T(8,128)(2,1)S(1)}, bf16[128,2048]{1,0:T(8,128)(2,1)S(1)}, u32[]{:S(2)}, u32[]{:S(2)}) collective-permute-start(bf16[128,2048]{1,0:T(8,128)(2,1)S(1)} %collective-permute-done.50), channel_id=1, source_target_pairs={{8,0},{10,2},{16,8},{18,10},{24,16},{26,18},{28,24},{30,26},{20,28... | collective-permute-start | bytes 1572872 | tf_op jit(solution)/shard_map/ppermute | solution.py:50
  524.7 28.8 %collective-permute-start.84 = (bf16[128,2048]{1,0:T(8,128)(2,1)}, bf16[128,2048]{1,0:T(8,128)(2,1)}, u32[]{:S(2)}, u32[]{:S(2)}) collective-permute-start(bf16[128,2048]{1,0:T(8,128)(2,1)} %get-tuple-element.627), channel_id=1, source_target_pairs={{8,0},{10,2},{16,8},{18,10},{24,16},{26,18},{28,24},{30,26},{20,28... | collective-permute-start | bytes 1572872 | tf_op jit(solution)/shard_map/ppermute | solution.py:50
  525.4 28.1 %collective-permute-start.85 = (bf16[128,2048]{1,0:T(8,128)(2,1)}, bf16[128,2048]{1,0:T(8,128)(2,1)}, u32[]{:S(2)}, u32[]{:S(2)}) collective-permute-start(bf16[128,2048]{1,0:T(8,128)(2,1)} %get-tuple-element.626), channel_id=1, source_target_pairs={{0,8},{2,10},{8,16},{10,18},{16,24},{18,26},{24,28},{26,30},{28,20... | collective-permute-start | bytes 1572872 | tf_op jit(solution)/shard_map/ppermute | solution.py:47
  545.5 33.5 %collective-permute-start.89 = (bf16[128,4096]{1,0:T(8,128)(2,1)}, bf16[128,4096]{1,0:T(8,128)(2,1)}, u32[]{:S(2)}, u32[]{:S(2)}) collective-permute-start(bf16[128,4096]{1,0:T(8,128)(2,1)} %pad_maximum_fusion.7), channel_id=1, source_target_pairs={{0,8},{2,10},{8,16},{10,18},{16,24},{18,26},{24,28},{26,30},{28,20... | collective-permute-start | bytes 3145736 | tf_op jit(solution)/shard_map/ppermute | solution.py:47
  548.1 30.8 %collective-permute-start.88 = (bf16[128,4096]{1,0:T(8,128)(2,1)}, bf16[128,4096]{1,0:T(8,128)(2,1)}, u32[]{:S(2)}, u32[]{:S(2)}) collective-permute-start(bf16[128,4096]{1,0:T(8,128)(2,1)} %pad_maximum_fusion.6), channel_id=1, source_target_pairs={{8,0},{10,2},{16,8},{18,10},{24,16},{26,18},{28,24},{30,26},{20,28... | collective-permute-start | bytes 3145736 | tf_op jit(solution)/shard_map/ppermute | solution.py:50
  556.9 48.3 %collective-permute-start.86 = (bf16[128,2048]{1,0:T(8,128)(2,1)}, bf16[128,2048]{1,0:T(8,128)(2,1)}, u32[]{:S(2)}, u32[]{:S(2)}) collective-permute-start(bf16[128,2048]{1,0:T(8,128)(2,1)} %get-tuple-element.625), channel_id=1, source_target_pairs={{8,0},{10,2},{16,8},{18,10},{24,16},{26,18},{28,24},{30,26},{20,28... | collective-permute-start | bytes 1572872 | tf_op jit(solution)/shard_map/ppermute | solution.py:50
  557.6 47.6 %collective-permute-start.87 = (bf16[128,2048]{1,0:T(8,128)(2,1)}, bf16[128,2048]{1,0:T(8,128)(2,1)}, u32[]{:S(2)}, u32[]{:S(2)}) collective-permute-start(bf16[128,2048]{1,0:T(8,128)(2,1)} %get-tuple-element.624), channel_id=1, source_target_pairs={{0,8},{2,10},{8,16},{10,18},{16,24},{18,26},{24,28},{26,30},{28,20... | collective-permute-start | bytes 1572872 | tf_op jit(solution)/shard_map/ppermute | solution.py:47
  607.8 31.3 %collective-permute-start.90 = (bf16[128,2048]{1,0:T(8,128)(2,1)}, bf16[128,2048]{1,0:T(8,128)(2,1)}, u32[]{:S(2)}, u32[]{:S(2)}) collective-permute-start(bf16[128,2048]{1,0:T(8,128)(2,1)} %get-tuple-element.623), channel_id=1, source_target_pairs={{8,0},{10,2},{16,8},{18,10},{24,16},{26,18},{28,24},{30,26},{20,28... | collective-permute-start | bytes 1572872 | tf_op jit(solution)/shard_map/ppermute | solution.py:50
  608.5 30.6 %collective-permute-start.91 = (bf16[128,2048]{1,0:T(8,128)(2,1)}, bf16[128,2048]{1,0:T(8,128)(2,1)}, u32[]{:S(2)}, u32[]{:S(2)}) collective-permute-start(bf16[128,2048]{1,0:T(8,128)(2,1)} %get-tuple-element.622), channel_id=1, source_target_pairs={{0,8},{2,10},{8,16},{10,18},{16,24},{18,26},{24,28},{26,30},{28,20... | collective-permute-start | bytes 1572872 | tf_op jit(solution)/shard_map/ppermute | solution.py:47
  613.5 32.0 %collective-permute-start.97 = (bf16[128,4096]{1,0:T(8,128)(2,1)}, bf16[128,4096]{1,0:T(8,128)(2,1)}, u32[]{:S(2)}, u32[]{:S(2)}) collective-permute-start(bf16[128,4096]{1,0:T(8,128)(2,1)} %add_convert_fusion.9), channel_id=1, source_target_pairs={{0,8},{2,10},{8,16},{10,18},{16,24},{18,26},{24,28},{26,30},{28,20... | collective-permute-start | bytes 3145736 | tf_op jit(solution)/shard_map/ppermute | solution.py:47
  655.3 29.7 %collective-permute-start.105 = (bf16[256,2048]{1,0:T(8,128)(2,1)S(1)}, bf16[256,2048]{1,0:T(8,128)(2,1)S(1)}, u32[]{:S(2)}, u32[]{:S(2)}) collective-permute-start(bf16[256,2048]{1,0:T(8,128)(2,1)S(1)} %get-tuple-element.548), channel_id=1, source_target_pairs={{0,2},{2,0},{4,6},{6,4},{8,10},{10,8},{12,14},{14,12},{16,18},{18,... | collective-permute-start | bytes 3145736 | tf_op jit(solution)/shard_map/ppermute | solution.py:53
  655.4 34.4 %collective-permute-start.102 = (bf16[128,2048]{1,0:T(8,128)(2,1)}, bf16[128,2048]{1,0:T(8,128)(2,1)}, u32[]{:S(2)}, u32[]{:S(2)}) collective-permute-start(bf16[128,2048]{1,0:T(8,128)(2,1)} %get-tuple-element.621), channel_id=1, source_target_pairs={{8,0},{10,2},{16,8},{18,10},{24,16},{26,18},{28,24},{30,26},{20,28... | collective-permute-start | bytes 1572872 | tf_op jit(solution)/shard_map/ppermute | solution.py:50
  681.0 28.8 %collective-permute-start.101 = (bf16[128,4096]{1,0:T(8,128)(2,1)}, bf16[128,4096]{1,0:T(8,128)(2,1)}, u32[]{:S(2)}, u32[]{:S(2)}) collective-permute-start(bf16[128,4096]{1,0:T(8,128)(2,1)} %add_convert_fusion.5), channel_id=1, source_target_pairs={{0,8},{2,10},{8,16},{10,18},{16,24},{18,26},{24,28},{26,30},{28,20... | collective-permute-start | bytes 3145736 | tf_op jit(solution)/shard_map/ppermute | solution.py:47
  (208 other events, 3451.3 us)

commit v11 on v9

--- a/solution.py
+++ b/solution.py
@@ -121,21 +121,30 @@
         self.ring, self.parts, self.size = ring, (near, far), rows
         self.buffers = []
         self.left = ring.chips - 1
-        self.now = (self.block(0), self.block(1))
+        self.now = tuple(jnp.concatenate(self.block(side), axis=1) for side in range(2))
 
     def block(self, side):
         half = self.ring.chips // 2
         grads = self.parts[self.left // half]
         start = (side * half + self.left % half) * self.size
-        return jnp.concatenate([g[start : start + self.size] for g in grads], axis=1)
+        return [g[start : start + self.size] for g in grads]
 
     def move(self):
         return self.ring.back(self.now[0]), self.ring.ahead(self.now[1])
 
     def take(self, moved):
         self.left -= 1
-        sums = [m.astype(f32) + self.block(side).astype(f32) for side, m in enumerate(moved)]
-        self.now = tuple(sums if self.left == 0 else [v.astype(bf16) for v in sums])
+        kind = f32 if self.left == 0 else bf16
+
+        def added(side):
+            column, sums = 0, []
+            for part in self.block(side):
+                taken = moved[side][:, column : column + part.shape[1]]
+                sums.append((taken.astype(f32) + part.astype(f32)).astype(kind))
+                column += part.shape[1]
+            return jnp.concatenate(sums, axis=1)
+
+        self.now = (added(0), added(1))
 
 
 class Held:

time: 833 us -> 829 us (level)
    convert_element_type x24 -> x18, other arithmetic: 43.9 us -> 37.7 us  [added(): sums.append((taken.astype(f32) + part.astype(f32)).astype(kind))]
    unnamed x188 -> x162, local copies, waits for them, and re-layouts: 20.2 us -> 22.8 us
  transfers between devices with their start and end apart: 135 -> 135, of which waited for: 71 -> 71; matrix products, arithmetic and copies ran while one was open for 41% -> 40% of each run, Pallas kernels for 4% -> 4%
where the time goes in v11:
time: 829 us; the launch traced here: 821 us
  waiting for transfers between devices  275 us (33%)
  matrix products  164 us (20%)
  other arithmetic  124 us (15%)
  starting transfers between devices  118 us (14%)
  local copies, waits for them, and re-layouts  102 us (12%)
  Pallas kernels  30.7 us (4%)
    ppermute x49, waiting for transfers between devices, back(): return lax.ppermute(v, 'dp', self.down)  106 us
    ppermute x49, waiting for transfers between devices, ahead(): return lax.ppermute(v, 'dp', self.up)  83.5 us
    ppermute x49, starting transfers between devices, ahead(): return lax.ppermute(v, 'dp', self.up)  66.9 us
    ppermute x11, waiting for transfers between devices, other_tensor(): return lax.ppermute(v, 'tensor', [(0, 1), (1, 0)])  62.1 us
    dynamic_update_slice x62, local copies, waits for them, and re-layouts, store(): lax.dynamic_update_slice(self.buffers[i], rows[:self.size, a:b], (at * se...  46.4 us
    convert_element_type x18, other arithmetic, added(): sums.append((taken.astype(f32) + part.astype(f32)).astype(kind))  37.7 us
    ppermute x49, starting transfers between devices, back(): return lax.ppermute(v, 'dp', self.down)  35.9 us
    unnamed x162, local copies, waits for them, and re-layouts  22.8 us
  transfers between devices with their start and end apart: 135, of which 71 were waited for; matrix products, arithmetic and copies ran while one was open for 40% of the time, Pallas kernels for 4%

profile of v11, /device:TPU:0, one launch (start us, length us, event | category | flops | bytes accessed | tf_op | source)
XLA Modules:
  0.0 820.5 jit_solution(3829349670328923053)
XLA Ops:
  49.4 7.1 collective-permute-done.36
  237.2 7.6 collective-permute-done.45
  267.3 16.6 %collective-permute-done.57 = bf16[256,2048]{1,0:T(8,128)(2,1)S(1)} collective-permute-done((bf16[256,2048]{1,0:T(8,128)(2,1)S(1)}, bf16[256,2048]{1,0:T(8,128)(2,1)S(1)}, u32[]{:S(2)}, u32[]{:S(2)}) %collective-permute-start.57) | collective-permute-done | bytes 1048608 | tf_op jit(solution)/shard_map/ppermute | solution.py:57
  291.6 8.5 %collective-permute-done.55 = bf16[128,2048]{1,0:T(8,128)(2,1)S(1)} collective-permute-done((bf16[128,2048]{1,0:T(8,128)(2,1)S(1)}, bf16[128,2048]{1,0:T(8,128)(2,1)S(1)}, u32[]{:S(2)}, u32[]{:S(2)}) %collective-permute-start.55) | collective-permute-done | bytes 524320 | tf_op jit(solution)/shard_map/ppermute | solution.py:47
  305.8 11.0 %fusion.71 = f32[1024,2048]{1,0:T(8,128)} fusion(bf16[1024,2048]{1,0:T(8,128)(2,1)S(1)} %pad_maximum_fusion.1, bf16[2048,2048]{1,0:T(8,128)(2,1)S(1)} %constant_dynamic-update-slice_fusion.14), kind=kOutput, calls=%fused_computation.425 | convolution fusion | flops 8589934592 | bytes 20971520 | tf_op jit(solution)/shard_map/dot_general | solution.py:468
  358.3 15.1 %multiply_convert_fusion.2 = (bf16[1024,2048]{1,0:T(8,128)(2,1)S(1)}, f32[1024,2048]{1,0:T(8,128)}) fusion(f32[1024,2048]{1,0:T(8,128)} %fusion.71, bf16[1024,2048]{1,0:T(8,128)(2,1)S(1)} %pad_maximum_fusion.1, bf16[2048,2048]{1,0:T(8,128)(2,1)} %constant_dynamic-update-slice_fusion.4), kind=kOutput, calls=%fused_computation.40 | convolution fusion | flops 8602517504 | bytes 33554432 | tf_op jit(solution)/shard_map/dot_general | solution.py:487
  383.4 6.5 fusion.74
  409.1 7.8 collective-permute-done.70
  416.9 9.5 %collective-permute-done.78 = bf16[256,1024]{1,0:T(8,128)(2,1)} collective-permute-done((bf16[256,1024]{1,0:T(8,128)(2,1)}, bf16[256,1024]{1,0:T(8,128)(2,1)}, u32[]{:S(2)}, u32[]{:S(2)}) %collective-permute-start.78) | collective-permute-done | bytes 524320 | tf_op jit(solution)/shard_map/ppermute | solution.py:57
  442.5 6.7 fusion.73
  455.5 17.5 %multiply_convert_fusion = (bf16[1024,2048]{1,0:T(8,128)(2,1)}, bf16[1024,2048]{1,0:T(8,128)(2,1)}) fusion(f32[1024,2048]{1,0:T(8,128)} %fusion.71, f32[1024,2048]{1,0:T(8,128)} %get-tuple-element.676, f32[1024,2048]{1,0:T(8,128)} %fusion.73, bf16[1024,2048]{1,0:T(8,128)(2,1)} %constant_dynamic-update-slice_fusion.18, ...), kind=kOutput, calls=%fused_computation.38 | convolution fusion | flops 4332716032 | bytes 39845888 | tf_op jit(solution)/shard_map/dot_general | solution.py:522
  476.7 12.2 %convolution_convert_fusion.1 = bf16[2048,2048]{1,0:T(8,128)(2,1)S(1)} fusion(bf16[1024,2048]{1,0:T(8,128)(2,1)} %copy-done.25, bf16[1024,2048]{1,0:T(8,128)(2,1)} %get-tuple-element.413), kind=kOutput, calls=%fused_computation.43 | convolution fusion | flops 8594128896 | bytes 16777216 | tf_op jit(solution)/shard_map/dot_general | solution.py:528
  497.5 11.0 %convolution_convert_fusion = bf16[2048,2048]{1,0:T(8,128)(2,1)S(1)} fusion(bf16[1024,2048]{1,0:T(8,128)(2,1)S(1)} %copy-done.26, bf16[1024,2048]{1,0:T(8,128)(2,1)} %get-tuple-element.414), kind=kOutput, calls=%fused_computation.42 | convolution fusion | flops 8594128896 | bytes 16777216 | tf_op jit(solution)/shard_map/dot_general | solution.py:532
  525.1 10.1 %fusion.14 = f32[512,2048]{1,0:T(8,128)} fusion(bf16[2048,2048]{1,0:T(8,128)(2,1)} %constant_dynamic-update-slice_fusion.4, bf16[1024,2048]{1,0:T(8,128)(2,1)S(1)} %copy-done.69), kind=kOutput, calls=%fused_computation.96 | convolution fusion | flops 4294967296 | bytes 14680064 | tf_op jit(solution)/shard_map/dot_general | solution.py:540
  535.2 8.0 add_convert_fusion
  548.7 9.6 %fusion.11 = f32[512,2048]{1,0:T(8,128)} fusion(bf16[2048,2048]{1,0:T(8,128)(2,1)} %constant_dynamic-update-slice_fusion.4, bf16[1024,2048]{1,0:T(8,128)(2,1)S(1)} %copy-done.70), kind=kOutput, calls=%fused_computation.93 | convolution fusion | flops 4294967296 | bytes 14680064 | tf_op jit(solution)/shard_map/dot_general | solution.py:540
  558.2 8.4 %convolution_add_fusion.1 = f32[512,2048]{1,0:T(8,128)} fusion(f32[512,2048]{1,0:T(8,128)} %fusion.11, bf16[2048,2048]{1,0:T(8,128)(2,1)S(1)} %bitcast.82, bf16[1024,2048]{1,0:T(8,128)(2,1)} %get-tuple-element.413), kind=kOutput, calls=%fused_computation.62 | convolution fusion | flops 4296015872 | bytes 18874368 | tf_op jit(solution)/shard_map/dot_general | solution.py:538
  587.9 12.8 %collective-permute-done.95 = bf16[256,2048]{1,0:T(8,128)(2,1)S(1)} collective-permute-done((bf16[256,2048]{1,0:T(8,128)(2,1)}, bf16[256,2048]{1,0:T(8,128)(2,1)S(1)}, u32[]{:S(2)}, u32[]{:S(2)}) %collective-permute-start.95) | collective-permute-done | bytes 1048608 | tf_op jit(solution)/shard_map/ppermute | solution.py:57
  620.1 17.1 %collective-permute-done.98 = bf16[128,4096]{1,0:T(8,128)(2,1)} collective-permute-done((bf16[128,4096]{1,0:T(8,128)(2,1)}, bf16[128,4096]{1,0:T(8,128)(2,1)}, u32[]{:S(2)}, u32[]{:S(2)}) %collective-permute-start.98) | collective-permute-done | bytes 1048608 | tf_op jit(solution)/shard_map/ppermute | solution.py:50
  654.2 7.9 attend_back.1
  680.7 7.4 convolution_convert_fusion.2
  722.8 14.9 %collective-permute-done.114 = bf16[128,4096]{1,0:T(8,128)(2,1)S(1)} collective-permute-done((bf16[128,4096]{1,0:T(8,128)(2,1)S(1)}, bf16[128,4096]{1,0:T(8,128)(2,1)S(1)}, u32[]{:S(2)}, u32[]{:S(2)}) %collective-permute-start.114) | collective-permute-done | bytes 1048608 | tf_op jit(solution)/shard_map/ppermute | solution.py:50
  782.9 7.6 collective-permute-done.127
  792.8 6.7 collective-permute-done.130
  (688 shorter events, 566.2 us)
Async XLA Ops:
  3.1 30.6 %collective-permute-start.1 = (bf16[128,2048]{1,0:T(8,128)(2,1)}, bf16[128,2048]{1,0:T(8,128)(2,1)}, u32[]{:S(2)}, u32[]{:S(2)}) collective-permute-start(bf16[128,2048]{1,0:T(8,128)(2,1)} %bitcast.8), channel_id=1, source_target_pairs={{0,2},{2,0},{4,6},{6,4},{8,10},{10,8},{12,14},{14,12},{16,18},{18,... | collective-permute-start | bytes 1572872 | tf_op jit(solution)/shard_map/ppermute | solution.py:53
  13.7 27.2 %collective-permute-start.5 = (bf16[144,1536]{1,0:T(8,128)(2,1)}, bf16[144,1536]{1,0:T(8,128)(2,1)}, u32[]{:S(2)}, u32[]{:S(2)}) collective-permute-start(bf16[144,1536]{1,0:T(8,128)(2,1)} %get-tuple-element.652), channel_id=1, source_target_pairs={{0,8},{2,10},{8,16},{10,18},{16,24},{18,26},{24,28},{26,30},{28,20... | collective-permute-start | bytes 1327112 | tf_op jit(solution)/shard_map/ppermute | solution.py:47
  30.7 25.8 %collective-permute-start.36 = (bf16[256,2048]{1,0:T(8,128)(2,1)}, bf16[256,2048]{1,0:T(8,128)(2,1)S(1)}, u32[]{:S(2)}, u32[]{:S(2)}) collective-permute-start(bf16[256,2048]{1,0:T(8,128)(2,1)} %reorder.4), channel_id=1, source_target_pairs={{0,1},{1,0},{2,3},{3,2},{4,5},{5,4},{6,7},{7,6},{8,9},{9,8},{10,11... | collective-permute-start | bytes 3145736 | tf_op jit(solution)/shard_map/ppermute | solution.py:57
  56.5 32.6 %collective-permute-start.37 = (bf16[256,2048]{1,0:T(8,128)(2,1)S(1)}, bf16[256,2048]{1,0:T(8,128)(2,1)S(1)}, u32[]{:S(2)}, u32[]{:S(2)}) collective-permute-start(bf16[256,2048]{1,0:T(8,128)(2,1)S(1)} %copy-done.5), channel_id=1, source_target_pairs={{0,2},{2,0},{4,6},{6,4},{8,10},{10,8},{12,14},{14,12},{16,18},{18,... | collective-permute-start | bytes 3145736 | tf_op jit(solution)/shard_map/ppermute | solution.py:53
  289.0 29.5 %collective-permute-start.53 = (bf16[128,2048]{1,0:T(8,128)(2,1)S(1)}, bf16[128,2048]{1,0:T(8,128)(2,1)S(1)}, u32[]{:S(2)}, u32[]{:S(2)}) collective-permute-start(bf16[128,2048]{1,0:T(8,128)(2,1)S(1)} %collective-permute-done.49), channel_id=1, source_target_pairs={{0,8},{2,10},{8,16},{10,18},{16,24},{18,26},{24,28},{26,30},{28,20... | collective-permute-start | bytes 1572872 | tf_op jit(solution)/shard_map/ppermute | solution.py:47
  290.7 27.8 %collective-permute-start.54 = (bf16[128,2048]{1,0:T(8,128)(2,1)S(1)}, bf16[128,2048]{1,0:T(8,128)(2,1)S(1)}, u32[]{:S(2)}, u32[]{:S(2)}) collective-permute-start(bf16[128,2048]{1,0:T(8,128)(2,1)S(1)} %collective-permute-done.50), channel_id=1, source_target_pairs={{8,0},{10,2},{16,8},{18,10},{24,16},{26,18},{28,24},{30,26},{20,28... | collective-permute-start | bytes 1572872 | tf_op jit(solution)/shard_map/ppermute | solution.py:50
  508.9 34.4 %collective-permute-start.88 = (bf16[128,4096]{1,0:T(8,128)(2,1)S(1)}, bf16[128,4096]{1,0:T(8,128)(2,1)}, u32[]{:S(2)}, u32[]{:S(2)}) collective-permute-start(bf16[128,4096]{1,0:T(8,128)(2,1)S(1)} %pad_maximum_fusion.9), channel_id=1, source_target_pairs={{8,0},{10,2},{16,8},{18,10},{24,16},{26,18},{28,24},{30,26},{20,28... | collective-permute-start | bytes 3145736 | tf_op jit(solution)/shard_map/ppermute | solution.py:50
  513.3 30.0 %collective-permute-start.89 = (bf16[128,4096]{1,0:T(8,128)(2,1)}, bf16[128,4096]{1,0:T(8,128)(2,1)}, u32[]{:S(2)}, u32[]{:S(2)}) collective-permute-start(bf16[128,4096]{1,0:T(8,128)(2,1)} %pad_maximum_fusion.10), channel_id=1, source_target_pairs={{0,8},{2,10},{8,16},{10,18},{16,24},{18,26},{24,28},{26,30},{28,20... | collective-permute-start | bytes 3145736 | tf_op jit(solution)/shard_map/ppermute | solution.py:47
  523.1 43.6 %collective-permute-start.86 = (bf16[128,2048]{1,0:T(8,128)(2,1)}, bf16[128,2048]{1,0:T(8,128)(2,1)}, u32[]{:S(2)}, u32[]{:S(2)}) collective-permute-start(bf16[128,2048]{1,0:T(8,128)(2,1)} %get-tuple-element.612), channel_id=1, source_target_pairs={{8,0},{10,2},{16,8},{18,10},{24,16},{26,18},{28,24},{30,26},{20,28... | collective-permute-start | bytes 1572872 | tf_op jit(solution)/shard_map/ppermute | solution.py:50
  523.5 43.2 %collective-permute-start.87 = (bf16[128,2048]{1,0:T(8,128)(2,1)}, bf16[128,2048]{1,0:T(8,128)(2,1)}, u32[]{:S(2)}, u32[]{:S(2)}) collective-permute-start(bf16[128,2048]{1,0:T(8,128)(2,1)} %get-tuple-element.611), channel_id=1, source_target_pairs={{0,8},{2,10},{8,16},{10,18},{16,24},{18,26},{24,28},{26,30},{28,20... | collective-permute-start | bytes 1572872 | tf_op jit(solution)/shard_map/ppermute | solution.py:47
  569.3 33.2 %collective-permute-start.90 = (bf16[128,2048]{1,0:T(8,128)(2,1)}, bf16[128,2048]{1,0:T(8,128)(2,1)}, u32[]{:S(2)}, u32[]{:S(2)}) collective-permute-start(bf16[128,2048]{1,0:T(8,128)(2,1)} %get-tuple-element.610), channel_id=1, source_target_pairs={{8,0},{10,2},{16,8},{18,10},{24,16},{26,18},{28,24},{30,26},{20,28... | collective-permute-start | bytes 1572872 | tf_op jit(solution)/shard_map/ppermute | solution.py:50
  569.3 33.2 %collective-permute-start.91 = (bf16[128,2048]{1,0:T(8,128)(2,1)}, bf16[128,2048]{1,0:T(8,128)(2,1)}, u32[]{:S(2)}, u32[]{:S(2)}) collective-permute-start(bf16[128,2048]{1,0:T(8,128)(2,1)} %get-tuple-element.609), channel_id=1, source_target_pairs={{0,8},{2,10},{8,16},{10,18},{16,24},{18,26},{24,28},{26,30},{28,20... | collective-permute-start | bytes 1572872 | tf_op jit(solution)/shard_map/ppermute | solution.py:47
  580.7 25.7 %collective-permute-start.96 = (bf16[128,4096]{1,0:T(8,128)(2,1)}, bf16[128,4096]{1,0:T(8,128)(2,1)}, u32[]{:S(2)}, u32[]{:S(2)}) collective-permute-start(bf16[128,4096]{1,0:T(8,128)(2,1)} %pad_maximum_fusion.13), channel_id=1, source_target_pairs={{8,0},{10,2},{16,8},{18,10},{24,16},{26,18},{28,24},{30,26},{20,28... | collective-permute-start | bytes 3145736 | tf_op jit(solution)/shard_map/ppermute | solution.py:50
  610.9 26.3 %collective-permute-start.98 = (bf16[128,4096]{1,0:T(8,128)(2,1)}, bf16[128,4096]{1,0:T(8,128)(2,1)}, u32[]{:S(2)}, u32[]{:S(2)}) collective-permute-start(bf16[128,4096]{1,0:T(8,128)(2,1)} %pad_maximum_fusion.16), channel_id=1, source_target_pairs={{8,0},{10,2},{16,8},{18,10},{24,16},{26,18},{28,24},{30,26},{20,28... | collective-permute-start | bytes 3145736 | tf_op jit(solution)/shard_map/ppermute | solution.py:50
  613.1 26.3 %collective-permute-start.99 = (bf16[128,4096]{1,0:T(8,128)(2,1)}, bf16[128,4096]{1,0:T(8,128)(2,1)}, u32[]{:S(2)}, u32[]{:S(2)}) collective-permute-start(bf16[128,4096]{1,0:T(8,128)(2,1)} %pad_maximum_fusion.17), channel_id=1, source_target_pairs={{0,8},{2,10},{8,16},{10,18},{16,24},{18,26},{24,28},{26,30},{28,20... | collective-permute-start | bytes 3145736 | tf_op jit(solution)/shard_map/ppermute | solution.py:47
  618.1 31.1 %collective-permute-start.102 = (bf16[128,2048]{1,0:T(8,128)(2,1)}, bf16[128,2048]{1,0:T(8,128)(2,1)S(1)}, u32[]{:S(2)}, u32[]{:S(2)}) collective-permute-start(bf16[128,2048]{1,0:T(8,128)(2,1)} %get-tuple-element.608), channel_id=1, source_target_pairs={{8,0},{10,2},{16,8},{18,10},{24,16},{26,18},{28,24},{30,26},{20,28... | collective-permute-start | bytes 1572872 | tf_op jit(solution)/shard_map/ppermute | solution.py:50
  619.3 29.9 %collective-permute-start.103 = (bf16[128,2048]{1,0:T(8,128)(2,1)}, bf16[128,2048]{1,0:T(8,128)(2,1)S(1)}, u32[]{:S(2)}, u32[]{:S(2)}) collective-permute-start(bf16[128,2048]{1,0:T(8,128)(2,1)} %get-tuple-element.607), channel_id=1, source_target_pairs={{0,8},{2,10},{8,16},{10,18},{16,24},{18,26},{24,28},{26,30},{28,20... | collective-permute-start | bytes 1572872 | tf_op jit(solution)/shard_map/ppermute | solution.py:47
  644.3 27.1 %collective-permute-start.100 = (bf16[128,4096]{1,0:T(8,128)(2,1)}, bf16[128,4096]{1,0:T(8,128)(2,1)}, u32[]{:S(2)}, u32[]{:S(2)}) collective-permute-start(bf16[128,4096]{1,0:T(8,128)(2,1)} %pad_maximum_fusion.18), channel_id=1, source_target_pairs={{8,0},{10,2},{16,8},{18,10},{24,16},{26,18},{28,24},{30,26},{20,28... | collective-permute-start | bytes 3145736 | tf_op jit(solution)/shard_map/ppermute | solution.py:50
  674.3 30.8 %collective-permute-start.110 = (bf16[128,4096]{1,0:T(8,128)(2,1)S(1)}, bf16[128,4096]{1,0:T(8,128)(2,1)}, u32[]{:S(2)}, u32[]{:S(2)}) collective-permute-start(bf16[128,4096]{1,0:T(8,128)(2,1)S(1)} %pad_maximum_fusion.20), channel_id=1, source_target_pairs={{8,0},{10,2},{16,8},{18,10},{24,16},{26,18},{28,24},{30,26},{20,28... | collective-permute-start | bytes 3145736 | tf_op jit(solution)/shard_map/ppermute | solution.py:50
  677.1 28.0 %collective-permute-start.111 = (bf16[128,4096]{1,0:T(8,128)(2,1)}, bf16[128,4096]{1,0:T(8,128)(2,1)}, u32[]{:S(2)}, u32[]{:S(2)}) collective-permute-start(bf16[128,4096]{1,0:T(8,128)(2,1)} %pad_maximum_fusion.21), channel_id=1, source_target_pairs={{0,8},{2,10},{8,16},{10,18},{16,24},{18,26},{24,28},{26,30},{28,20... | collective-permute-start | bytes 3145736 | tf_op jit(solution)/shard_map/ppermute | solution.py:47
  708.0 29.7 %collective-permute-start.114 = (bf16[128,4096]{1,0:T(8,128)(2,1)S(1)}, bf16[128,4096]{1,0:T(8,128)(2,1)S(1)}, u32[]{:S(2)}, u32[]{:S(2)}) collective-permute-start(bf16[128,4096]{1,0:T(8,128)(2,1)S(1)} %pad_maximum_fusion.22), channel_id=1, source_target_pairs={{8,0},{10,2},{16,8},{18,10},{24,16},{26,18},{28,24},{30,26},{20,28... | collective-permute-start | bytes 3145736 | tf_op jit(solution)/shard_map/ppermute | solution.py:50
  709.9 29.3 %collective-permute-start.115 = (bf16[128,4096]{1,0:T(8,128)(2,1)S(1)}, bf16[128,4096]{1,0:T(8,128)(2,1)S(1)}, u32[]{:S(2)}, u32[]{:S(2)}) collective-permute-start(bf16[128,4096]{1,0:T(8,128)(2,1)S(1)} %pad_maximum_fusion.23), channel_id=1, source_target_pairs={{0,8},{2,10},{8,16},{10,18},{16,24},{18,26},{24,28},{26,30},{28,20... | collective-permute-start | bytes 3145736 | tf_op jit(solution)/shard_map/ppermute | solution.py:47
  717.0 28.7 %collective-permute-start.112 = (bf16[128,1536]{0,1:T(8,128)(2,1)S(1)}, bf16[128,1536]{0,1:T(8,128)(2,1)S(1)}, u32[]{:S(2)}, u32[]{:S(2)}) collective-permute-start(bf16[128,1536]{0,1:T(8,128)(2,1)S(1)} %get-tuple-element.596), channel_id=1, source_target_pairs={{8,0},{10,2},{16,8},{18,10},{24,16},{26,18},{28,24},{30,26},{20,28... | collective-permute-start | bytes 1179656 | tf_op jit(solution)/shard_map/ppermute | solution.py:50
  718.8 28.1 %collective-permute-start.113 = (bf16[128,1536]{0,1:T(8,128)(2,1)S(1)}, bf16[128,1536]{0,1:T(8,128)(2,1)S(1)}, u32[]{:S(2)}, u32[]{:S(2)}) collective-permute-start(bf16[128,1536]{0,1:T(8,128)(2,1)S(1)} %get-tuple-element.595), channel_id=1, source_target_pairs={{0,8},{2,10},{8,16},{10,18},{16,24},{18,26},{24,28},{26,30},{28,20... | collective-permute-start | bytes 1179656 | tf_op jit(solution)/shard_map/ppermute | solution.py:47
  (186 other events, 2639.3 us)

commit v12 on v11

--- a/solution.py
+++ b/solution.py
@@ -660,8 +660,10 @@
     gate_grad = whole(kept[:, :gate_width], taken[:, :gate_width])
     up_grad = whole(kept[:, gate_width:], taken[:, gate_width:])
     stages.turn(attn_sums)
+    stages.turn(attn_sums)
+    finished = [gate_grad, up_grad]
     while attn_sums.left:
-        stages.turn(attn_sums, None, (gate_grad, up_grad))
+        stages.turn(attn_sums, None, finished.pop(0) if finished else ())
     input_grad, totals = stages.finish()
     gain_mlp_grad = lax.dynamic_slice_in_dim(totals, me, 1, 0)[0]
     gain_attn_grad = lax.dynamic_slice_in_dim(totals, devices + me, 1, 0)[0]

time: 829 us -> 827 us (level)
    unnamed x162 -> x168, local copies, waits for them, and re-layouts: 22.8 us -> 21.9 us
where the time goes in v12:
time: 827 us; the launch traced here: 818 us
  waiting for transfers between devices  272 us (33%)
  matrix products  164 us (20%)
  other arithmetic  126 us (15%)
  starting transfers between devices  118 us (14%)
  local copies, waits for them, and re-layouts  101 us (12%)
  Pallas kernels  30.7 us (4%)
    ppermute x49, waiting for transfers between devices, back(): return lax.ppermute(v, 'dp', self.down)  105 us
    ppermute x49, waiting for transfers between devices, ahead(): return lax.ppermute(v, 'dp', self.up)  83.9 us
    ppermute x49, starting transfers between devices, ahead(): return lax.ppermute(v, 'dp', self.up)  66.9 us
    ppermute x11, waiting for transfers between devices, other_tensor(): return lax.ppermute(v, 'tensor', [(0, 1), (1, 0)])  62 us
    dynamic_update_slice x62, local copies, waits for them, and re-layouts, store(): lax.dynamic_update_slice(self.buffers[i], rows[:self.size, a:b], (at * se...  46.5 us
    convert_element_type x18, other arithmetic, added(): sums.append((taken.astype(f32) + part.astype(f32)).astype(kind))  38 us
    ppermute x49, starting transfers between devices, back(): return lax.ppermute(v, 'dp', self.down)  35.9 us
    unnamed x168, local copies, waits for them, and re-layouts  21.9 us
  transfers between devices with their start and end apart: 135, of which 71 were waited for; matrix products, arithmetic and copies ran while one was open for 40% of the time, Pallas kernels for 4%

profile of v12, /device:TPU:0, one launch (start us, length us, event | category | flops | bytes accessed | tf_op | source)
XLA Modules:
  0.0 818.3 jit_solution(4979730471557752571)
XLA Ops:
  49.5 7.1 collective-permute-done.36
  196.4 6.3 attend.1
  237.3 7.6 collective-permute-done.45
  267.4 16.6 %collective-permute-done.57 = bf16[256,2048]{1,0:T(8,128)(2,1)S(1)} collective-permute-done((bf16[256,2048]{1,0:T(8,128)(2,1)S(1)}, bf16[256,2048]{1,0:T(8,128)(2,1)S(1)}, u32[]{:S(2)}, u32[]{:S(2)}) %collective-permute-start.57) | collective-permute-done | bytes 1048608 | tf_op jit(solution)/shard_map/ppermute | solution.py:57
  291.6 8.5 %collective-permute-done.55 = bf16[128,2048]{1,0:T(8,128)(2,1)S(1)} collective-permute-done((bf16[128,2048]{1,0:T(8,128)(2,1)S(1)}, bf16[128,2048]{1,0:T(8,128)(2,1)S(1)}, u32[]{:S(2)}, u32[]{:S(2)}) %collective-permute-start.55) | collective-permute-done | bytes 524320 | tf_op jit(solution)/shard_map/ppermute | solution.py:47
  305.8 11.0 %fusion.71 = f32[1024,2048]{1,0:T(8,128)} fusion(bf16[1024,2048]{1,0:T(8,128)(2,1)S(1)} %pad_maximum_fusion.1, bf16[2048,2048]{1,0:T(8,128)(2,1)S(1)} %constant_dynamic-update-slice_fusion.14), kind=kOutput, calls=%fused_computation.425 | convolution fusion | flops 8589934592 | bytes 20971520 | tf_op jit(solution)/shard_map/dot_general | solution.py:468
  358.3 15.1 %multiply_convert_fusion.2 = (bf16[1024,2048]{1,0:T(8,128)(2,1)S(1)}, f32[1024,2048]{1,0:T(8,128)}) fusion(f32[1024,2048]{1,0:T(8,128)} %fusion.71, bf16[1024,2048]{1,0:T(8,128)(2,1)S(1)} %pad_maximum_fusion.1, bf16[2048,2048]{1,0:T(8,128)(2,1)} %constant_dynamic-update-slice_fusion.4), kind=kOutput, calls=%fused_computation.40 | convolution fusion | flops 8602517504 | bytes 33554432 | tf_op jit(solution)/shard_map/dot_general | solution.py:487
  383.4 6.5 fusion.74
  409.1 7.8 collective-permute-done.70
  417.0 9.5 %collective-permute-done.78 = bf16[256,1024]{1,0:T(8,128)(2,1)} collective-permute-done((bf16[256,1024]{1,0:T(8,128)(2,1)}, bf16[256,1024]{1,0:T(8,128)(2,1)}, u32[]{:S(2)}, u32[]{:S(2)}) %collective-permute-start.78) | collective-permute-done | bytes 524320 | tf_op jit(solution)/shard_map/ppermute | solution.py:57
  442.4 6.7 fusion.73
  455.4 17.5 %multiply_convert_fusion = (bf16[1024,2048]{1,0:T(8,128)(2,1)}, bf16[1024,2048]{1,0:T(8,128)(2,1)}) fusion(f32[1024,2048]{1,0:T(8,128)} %fusion.71, f32[1024,2048]{1,0:T(8,128)} %get-tuple-element.676, f32[1024,2048]{1,0:T(8,128)} %fusion.73, bf16[1024,2048]{1,0:T(8,128)(2,1)} %constant_dynamic-update-slice_fusion.18, ...), kind=kOutput, calls=%fused_computation.38 | convolution fusion | flops 4332716032 | bytes 39845888 | tf_op jit(solution)/shard_map/dot_general | solution.py:522
  476.6 12.2 %convolution_convert_fusion.1 = bf16[2048,2048]{1,0:T(8,128)(2,1)S(1)} fusion(bf16[1024,2048]{1,0:T(8,128)(2,1)} %copy-done.25, bf16[1024,2048]{1,0:T(8,128)(2,1)} %get-tuple-element.413), kind=kOutput, calls=%fused_computation.43 | convolution fusion | flops 8594128896 | bytes 16777216 | tf_op jit(solution)/shard_map/dot_general | solution.py:528
  497.5 11.0 %convolution_convert_fusion = bf16[2048,2048]{1,0:T(8,128)(2,1)S(1)} fusion(bf16[1024,2048]{1,0:T(8,128)(2,1)S(1)} %copy-done.26, bf16[1024,2048]{1,0:T(8,128)(2,1)} %get-tuple-element.414), kind=kOutput, calls=%fused_computation.42 | convolution fusion | flops 8594128896 | bytes 16777216 | tf_op jit(solution)/shard_map/dot_general | solution.py:532
  525.1 10.1 %fusion.14 = f32[512,2048]{1,0:T(8,128)} fusion(bf16[2048,2048]{1,0:T(8,128)(2,1)} %constant_dynamic-update-slice_fusion.4, bf16[1024,2048]{1,0:T(8,128)(2,1)S(1)} %copy-done.72), kind=kOutput, calls=%fused_computation.96 | convolution fusion | flops 4294967296 | bytes 14680064 | tf_op jit(solution)/shard_map/dot_general | solution.py:540
  535.2 8.0 add_convert_fusion
  548.6 9.6 %fusion.11 = f32[512,2048]{1,0:T(8,128)} fusion(bf16[2048,2048]{1,0:T(8,128)(2,1)} %constant_dynamic-update-slice_fusion.4, bf16[1024,2048]{1,0:T(8,128)(2,1)S(1)} %copy-done.73), kind=kOutput, calls=%fused_computation.93 | convolution fusion | flops 4294967296 | bytes 14680064 | tf_op jit(solution)/shard_map/dot_general | solution.py:540
  558.2 8.3 %convolution_add_fusion.1 = f32[512,2048]{1,0:T(8,128)} fusion(f32[512,2048]{1,0:T(8,128)} %fusion.11, bf16[2048,2048]{1,0:T(8,128)(2,1)S(1)} %bitcast.82, bf16[1024,2048]{1,0:T(8,128)(2,1)} %get-tuple-element.413), kind=kOutput, calls=%fused_computation.62 | convolution fusion | flops 4296015872 | bytes 18874368 | tf_op jit(solution)/shard_map/dot_general | solution.py:538
  587.8 12.8 %collective-permute-done.95 = bf16[256,2048]{1,0:T(8,128)(2,1)S(1)} collective-permute-done((bf16[256,2048]{1,0:T(8,128)(2,1)}, bf16[256,2048]{1,0:T(8,128)(2,1)S(1)}, u32[]{:S(2)}, u32[]{:S(2)}) %collective-permute-start.95) | collective-permute-done | bytes 1048608 | tf_op jit(solution)/shard_map/ppermute | solution.py:57
  620.0 17.1 %collective-permute-done.98 = bf16[128,4096]{1,0:T(8,128)(2,1)} collective-permute-done((bf16[128,4096]{1,0:T(8,128)(2,1)}, bf16[128,4096]{1,0:T(8,128)(2,1)}, u32[]{:S(2)}, u32[]{:S(2)}) %collective-permute-start.98) | collective-permute-done | bytes 1048608 | tf_op jit(solution)/shard_map/ppermute | solution.py:50
  654.0 7.9 attend_back.1
  680.6 7.4 convolution_convert_fusion.2
  722.6 14.9 %collective-permute-done.114 = bf16[128,4096]{1,0:T(8,128)(2,1)S(1)} collective-permute-done((bf16[128,4096]{1,0:T(8,128)(2,1)S(1)}, bf16[128,4096]{1,0:T(8,128)(2,1)S(1)}, u32[]{:S(2)}, u32[]{:S(2)}) %collective-permute-start.114) | collective-permute-done | bytes 1048608 | tf_op jit(solution)/shard_map/ppermute | solution.py:50
  781.8 6.2 collective-permute-done.126
  (694 shorter events, 566.1 us)
Async XLA Ops:
  3.1 30.7 %collective-permute-start.1 = (bf16[128,2048]{1,0:T(8,128)(2,1)}, bf16[128,2048]{1,0:T(8,128)(2,1)}, u32[]{:S(2)}, u32[]{:S(2)}) collective-permute-start(bf16[128,2048]{1,0:T(8,128)(2,1)} %bitcast.8), channel_id=1, source_target_pairs={{0,2},{2,0},{4,6},{6,4},{8,10},{10,8},{12,14},{14,12},{16,18},{18,... | collective-permute-start | bytes 1572872 | tf_op jit(solution)/shard_map/ppermute | solution.py:53
  13.7 27.3 %collective-permute-start.5 = (bf16[144,1536]{1,0:T(8,128)(2,1)}, bf16[144,1536]{1,0:T(8,128)(2,1)}, u32[]{:S(2)}, u32[]{:S(2)}) collective-permute-start(bf16[144,1536]{1,0:T(8,128)(2,1)} %get-tuple-element.652), channel_id=1, source_target_pairs={{0,8},{2,10},{8,16},{10,18},{16,24},{18,26},{24,28},{26,30},{28,20... | collective-permute-start | bytes 1327112 | tf_op jit(solution)/shard_map/ppermute | solution.py:47
  30.8 25.8 %collective-permute-start.36 = (bf16[256,2048]{1,0:T(8,128)(2,1)}, bf16[256,2048]{1,0:T(8,128)(2,1)S(1)}, u32[]{:S(2)}, u32[]{:S(2)}) collective-permute-start(bf16[256,2048]{1,0:T(8,128)(2,1)} %reorder.4), channel_id=1, source_target_pairs={{0,1},{1,0},{2,3},{3,2},{4,5},{5,4},{6,7},{7,6},{8,9},{9,8},{10,11... | collective-permute-start | bytes 3145736 | tf_op jit(solution)/shard_map/ppermute | solution.py:57
  56.5 32.7 %collective-permute-start.37 = (bf16[256,2048]{1,0:T(8,128)(2,1)S(1)}, bf16[256,2048]{1,0:T(8,128)(2,1)S(1)}, u32[]{:S(2)}, u32[]{:S(2)}) collective-permute-start(bf16[256,2048]{1,0:T(8,128)(2,1)S(1)} %copy-done.5), channel_id=1, source_target_pairs={{0,2},{2,0},{4,6},{6,4},{8,10},{10,8},{12,14},{14,12},{16,18},{18,... | collective-permute-start | bytes 3145736 | tf_op jit(solution)/shard_map/ppermute | solution.py:53
  289.0 29.5 %collective-permute-start.53 = (bf16[128,2048]{1,0:T(8,128)(2,1)S(1)}, bf16[128,2048]{1,0:T(8,128)(2,1)S(1)}, u32[]{:S(2)}, u32[]{:S(2)}) collective-permute-start(bf16[128,2048]{1,0:T(8,128)(2,1)S(1)} %collective-permute-done.49), channel_id=1, source_target_pairs={{0,8},{2,10},{8,16},{10,18},{16,24},{18,26},{24,28},{26,30},{28,20... | collective-permute-start | bytes 1572872 | tf_op jit(solution)/shard_map/ppermute | solution.py:47
  290.7 27.8 %collective-permute-start.54 = (bf16[128,2048]{1,0:T(8,128)(2,1)S(1)}, bf16[128,2048]{1,0:T(8,128)(2,1)S(1)}, u32[]{:S(2)}, u32[]{:S(2)}) collective-permute-start(bf16[128,2048]{1,0:T(8,128)(2,1)S(1)} %collective-permute-done.50), channel_id=1, source_target_pairs={{8,0},{10,2},{16,8},{18,10},{24,16},{26,18},{28,24},{30,26},{20,28... | collective-permute-start | bytes 1572872 | tf_op jit(solution)/shard_map/ppermute | solution.py:50
  508.8 34.4 %collective-permute-start.88 = (bf16[128,4096]{1,0:T(8,128)(2,1)S(1)}, bf16[128,4096]{1,0:T(8,128)(2,1)}, u32[]{:S(2)}, u32[]{:S(2)}) collective-permute-start(bf16[128,4096]{1,0:T(8,128)(2,1)S(1)} %pad_maximum_fusion.9), channel_id=1, source_target_pairs={{8,0},{10,2},{16,8},{18,10},{24,16},{26,18},{28,24},{30,26},{20,28... | collective-permute-start | bytes 3145736 | tf_op jit(solution)/shard_map/ppermute | solution.py:50
  513.3 30.0 %collective-permute-start.89 = (bf16[128,4096]{1,0:T(8,128)(2,1)}, bf16[128,4096]{1,0:T(8,128)(2,1)}, u32[]{:S(2)}, u32[]{:S(2)}) collective-permute-start(bf16[128,4096]{1,0:T(8,128)(2,1)} %pad_maximum_fusion.10), channel_id=1, source_target_pairs={{0,8},{2,10},{8,16},{10,18},{16,24},{18,26},{24,28},{26,30},{28,20... | collective-permute-start | bytes 3145736 | tf_op jit(solution)/shard_map/ppermute | solution.py:47
  523.0 43.5 %collective-permute-start.86 = (bf16[128,2048]{1,0:T(8,128)(2,1)}, bf16[128,2048]{1,0:T(8,128)(2,1)}, u32[]{:S(2)}, u32[]{:S(2)}) collective-permute-start(bf16[128,2048]{1,0:T(8,128)(2,1)} %get-tuple-element.612), channel_id=1, source_target_pairs={{8,0},{10,2},{16,8},{18,10},{24,16},{26,18},{28,24},{30,26},{20,28... | collective-permute-start | bytes 1572872 | tf_op jit(solution)/shard_map/ppermute | solution.py:50
  523.5 43.1 %collective-permute-start.87 = (bf16[128,2048]{1,0:T(8,128)(2,1)}, bf16[128,2048]{1,0:T(8,128)(2,1)}, u32[]{:S(2)}, u32[]{:S(2)}) collective-permute-start(bf16[128,2048]{1,0:T(8,128)(2,1)} %get-tuple-element.611), channel_id=1, source_target_pairs={{0,8},{2,10},{8,16},{10,18},{16,24},{18,26},{24,28},{26,30},{28,20... | collective-permute-start | bytes 1572872 | tf_op jit(solution)/shard_map/ppermute | solution.py:47
  569.2 33.3 %collective-permute-start.90 = (bf16[128,2048]{1,0:T(8,128)(2,1)}, bf16[128,2048]{1,0:T(8,128)(2,1)}, u32[]{:S(2)}, u32[]{:S(2)}) collective-permute-start(bf16[128,2048]{1,0:T(8,128)(2,1)} %get-tuple-element.610), channel_id=1, source_target_pairs={{8,0},{10,2},{16,8},{18,10},{24,16},{26,18},{28,24},{30,26},{20,28... | collective-permute-start | bytes 1572872 | tf_op jit(solution)/shard_map/ppermute | solution.py:50
  569.2 33.2 %collective-permute-start.91 = (bf16[128,2048]{1,0:T(8,128)(2,1)}, bf16[128,2048]{1,0:T(8,128)(2,1)}, u32[]{:S(2)}, u32[]{:S(2)}) collective-permute-start(bf16[128,2048]{1,0:T(8,128)(2,1)} %get-tuple-element.609), channel_id=1, source_target_pairs={{0,8},{2,10},{8,16},{10,18},{16,24},{18,26},{24,28},{26,30},{28,20... | collective-permute-start | bytes 1572872 | tf_op jit(solution)/shard_map/ppermute | solution.py:47
  580.6 25.7 %collective-permute-start.96 = (bf16[128,4096]{1,0:T(8,128)(2,1)}, bf16[128,4096]{1,0:T(8,128)(2,1)}, u32[]{:S(2)}, u32[]{:S(2)}) collective-permute-start(bf16[128,4096]{1,0:T(8,128)(2,1)} %pad_maximum_fusion.13), channel_id=1, source_target_pairs={{8,0},{10,2},{16,8},{18,10},{24,16},{26,18},{28,24},{30,26},{20,28... | collective-permute-start | bytes 3145736 | tf_op jit(solution)/shard_map/ppermute | solution.py:50
  610.7 26.3 %collective-permute-start.98 = (bf16[128,4096]{1,0:T(8,128)(2,1)}, bf16[128,4096]{1,0:T(8,128)(2,1)}, u32[]{:S(2)}, u32[]{:S(2)}) collective-permute-start(bf16[128,4096]{1,0:T(8,128)(2,1)} %pad_maximum_fusion.16), channel_id=1, source_target_pairs={{8,0},{10,2},{16,8},{18,10},{24,16},{26,18},{28,24},{30,26},{20,28... | collective-permute-start | bytes 3145736 | tf_op jit(solution)/shard_map/ppermute | solution.py:50
  613.0 26.3 %collective-permute-start.99 = (bf16[128,4096]{1,0:T(8,128)(2,1)}, bf16[128,4096]{1,0:T(8,128)(2,1)}, u32[]{:S(2)}, u32[]{:S(2)}) collective-permute-start(bf16[128,4096]{1,0:T(8,128)(2,1)} %pad_maximum_fusion.17), channel_id=1, source_target_pairs={{0,8},{2,10},{8,16},{10,18},{16,24},{18,26},{24,28},{26,30},{28,20... | collective-permute-start | bytes 3145736 | tf_op jit(solution)/shard_map/ppermute | solution.py:47
  618.0 31.1 %collective-permute-start.102 = (bf16[128,2048]{1,0:T(8,128)(2,1)}, bf16[128,2048]{1,0:T(8,128)(2,1)S(1)}, u32[]{:S(2)}, u32[]{:S(2)}) collective-permute-start(bf16[128,2048]{1,0:T(8,128)(2,1)} %get-tuple-element.608), channel_id=1, source_target_pairs={{8,0},{10,2},{16,8},{18,10},{24,16},{26,18},{28,24},{30,26},{20,28... | collective-permute-start | bytes 1572872 | tf_op jit(solution)/shard_map/ppermute | solution.py:50
  619.2 29.9 %collective-permute-start.103 = (bf16[128,2048]{1,0:T(8,128)(2,1)}, bf16[128,2048]{1,0:T(8,128)(2,1)S(1)}, u32[]{:S(2)}, u32[]{:S(2)}) collective-permute-start(bf16[128,2048]{1,0:T(8,128)(2,1)} %get-tuple-element.607), channel_id=1, source_target_pairs={{0,8},{2,10},{8,16},{10,18},{16,24},{18,26},{24,28},{26,30},{28,20... | collective-permute-start | bytes 1572872 | tf_op jit(solution)/shard_map/ppermute | solution.py:47
  644.1 27.1 %collective-permute-start.100 = (bf16[128,4096]{1,0:T(8,128)(2,1)}, bf16[128,4096]{1,0:T(8,128)(2,1)}, u32[]{:S(2)}, u32[]{:S(2)}) collective-permute-start(bf16[128,4096]{1,0:T(8,128)(2,1)} %pad_maximum_fusion.18), channel_id=1, source_target_pairs={{8,0},{10,2},{16,8},{18,10},{24,16},{26,18},{28,24},{30,26},{20,28... | collective-permute-start | bytes 3145736 | tf_op jit(solution)/shard_map/ppermute | solution.py:50
  674.1 30.8 %collective-permute-start.110 = (bf16[128,4096]{1,0:T(8,128)(2,1)S(1)}, bf16[128,4096]{1,0:T(8,128)(2,1)}, u32[]{:S(2)}, u32[]{:S(2)}) collective-permute-start(bf16[128,4096]{1,0:T(8,128)(2,1)S(1)} %pad_maximum_fusion.20), channel_id=1, source_target_pairs={{8,0},{10,2},{16,8},{18,10},{24,16},{26,18},{28,24},{30,26},{20,28... | collective-permute-start | bytes 3145736 | tf_op jit(solution)/shard_map/ppermute | solution.py:50
  676.9 27.9 %collective-permute-start.111 = (bf16[128,4096]{1,0:T(8,128)(2,1)}, bf16[128,4096]{1,0:T(8,128)(2,1)}, u32[]{:S(2)}, u32[]{:S(2)}) collective-permute-start(bf16[128,4096]{1,0:T(8,128)(2,1)} %pad_maximum_fusion.21), channel_id=1, source_target_pairs={{0,8},{2,10},{8,16},{10,18},{16,24},{18,26},{24,28},{26,30},{28,20... | collective-permute-start | bytes 3145736 | tf_op jit(solution)/shard_map/ppermute | solution.py:47
  707.9 29.7 %collective-permute-start.114 = (bf16[128,4096]{1,0:T(8,128)(2,1)S(1)}, bf16[128,4096]{1,0:T(8,128)(2,1)S(1)}, u32[]{:S(2)}, u32[]{:S(2)}) collective-permute-start(bf16[128,4096]{1,0:T(8,128)(2,1)S(1)} %pad_maximum_fusion.22), channel_id=1, source_target_pairs={{8,0},{10,2},{16,8},{18,10},{24,16},{26,18},{28,24},{30,26},{20,28... | collective-permute-start | bytes 3145736 | tf_op jit(solution)/shard_map/ppermute | solution.py:50
  709.7 29.3 %collective-permute-start.115 = (bf16[128,4096]{1,0:T(8,128)(2,1)S(1)}, bf16[128,4096]{1,0:T(8,128)(2,1)S(1)}, u32[]{:S(2)}, u32[]{:S(2)}) collective-permute-start(bf16[128,4096]{1,0:T(8,128)(2,1)S(1)} %pad_maximum_fusion.23), channel_id=1, source_target_pairs={{0,8},{2,10},{8,16},{10,18},{16,24},{18,26},{24,28},{26,30},{28,20... | collective-permute-start | bytes 3145736 | tf_op jit(solution)/shard_map/ppermute | solution.py:47
  716.8 28.7 %collective-permute-start.112 = (bf16[128,1536]{0,1:T(8,128)(2,1)S(1)}, bf16[128,1536]{0,1:T(8,128)(2,1)S(1)}, u32[]{:S(2)}, u32[]{:S(2)}) collective-permute-start(bf16[128,1536]{0,1:T(8,128)(2,1)S(1)} %get-tuple-element.596), channel_id=1, source_target_pairs={{8,0},{10,2},{16,8},{18,10},{24,16},{26,18},{28,24},{30,26},{20,28... | collective-permute-start | bytes 1179656 | tf_op jit(solution)/shard_map/ppermute | solution.py:50
  718.6 28.1 %collective-permute-start.113 = (bf16[128,1536]{0,1:T(8,128)(2,1)S(1)}, bf16[128,1536]{0,1:T(8,128)(2,1)S(1)}, u32[]{:S(2)}, u32[]{:S(2)}) collective-permute-start(bf16[128,1536]{0,1:T(8,128)(2,1)S(1)} %get-tuple-element.595), channel_id=1, source_target_pairs={{0,8},{2,10},{8,16},{10,18},{16,24},{18,26},{24,28},{26,30},{28,20... | collective-permute-start | bytes 1179656 | tf_op jit(solution)/shard_map/ppermute | solution.py:47
  (189 other events, 2660.1 us)
